TPU v7x, 512 devices: a whole 4x4x16 slice. The times are simulated.
512 devices in a mesh: nodes: 128 (over z, x, core), mp: 4 (over y).
Axes of the slice: x: 4, y: 4, z: 16, core: 2. Of those that a mesh axis runs over, the one named last changes fastest.
Arguments:
- grid_in: bfloat16 [131072, 1024], P('nodes', 'mp'), may hold values from -2200 to 2200
- mesh_in: bfloat16 [32768, 1024], P('nodes', 'mp'), may hold values from -2200 to 2200
- w_query: bfloat16 [4, 1024, 512], P(None, None, 'mp'), as said below
- w_key: bfloat16 [4, 1024, 512], P(None, None, 'mp'), may hold values from -8 to 8
- w_value: bfloat16 [4, 1024, 512], P(None, None, 'mp'), may hold values from -0.1875 to 0.1875
- w_out: bfloat16 [4, 512, 1024], P(None, 'mp'), may hold values from -1 to 1
- norm_gains: float32 [6, 1024], replicated, may hold values from 0.25 to 1.75
- enc_list: int32 [256, 4], P('nodes'), may hold values from 0 to 1023, as said below
- proc_list: int32 [256, 3], P('nodes'), may hold values from 0 to 255, as said below
- dec_list: int32 [1024, 2], P('nodes'), may hold values from 0 to 255, as said below
- grid_count: int32 [1024], replicated, may hold values from 1 to 128
Outputs:
- grid_out: bfloat16 [131072, 1024], P('nodes', 'mp')
- mesh_out: bfloat16 [32768, 1024], P('nodes', 'mp')
Inputs may be any that keep to these rules, and one draw needn't show every extreme that they name: `enc_list`: mesh block b lies with node index b // 2; its 4 entries are distinct grid blocks held by node indices at most 2 from it (grid block c lies with node index c // 8). `proc_list`: entry 0 of row b is b; the others are distinct mesh blocks other than b held by node indices at most 2 from b's. `dec_list`: grid block c's 2 entries are distinct mesh blocks held by node indices at most 2 from c's. `w_query`: entries within 6 / sqrt(1024) of zero.
All inputs are finite; a program needn't handle non-finite values.
Results may differ from a plain program's by a relative error of at most 0.019.
Values may be sent and summed in bfloat16 or wider, within the bound.
No kernel may reach another device: no remote copies, remote signals or barrier semaphores. Data moves between devices by JAX's collectives and lax.ppermute only.
A program may use at most 64 MiB of HBM per device.

v0:
```python
import jax
import jax.numpy as jnp
from jax import lax
from jax.sharding import PartitionSpec as P

HEAD_DIM = 64
BLOCK = 128
REACH = 2


epsilon = 1e-05


def in_blocks(value, dim, count):
    lengths = value.shape
    pieces = value.reshape(*lengths[:dim], count, lengths[dim] // count, *lengths[dim + 1 :])
    return jnp.moveaxis(pieces, dim, 0)


def summed_on_arrival(value, axis, dim):
    pieces = in_blocks(value, dim, lax.axis_size(axis))
    arrived = lax.all_to_all(pieces, axis, split_axis=0, concat_axis=0, tiled=True)
    return arrived.astype(jnp.float32).sum(axis=0)


def from_behind(value, axis, steps):
    count = lax.axis_size(axis)
    first, last = (max(0, -steps), min(count, count - steps))
    return lax.ppermute(value, axis, [(source, source + steps) for source in range(first, last)])


def normalize(states, gains):
    values = states.astype(jnp.float32)
    average = jnp.mean(values, axis=-1, keepdims=True)
    centred = values - average
    spread = jnp.mean(centred * centred, axis=-1, keepdims=True)
    return (centred * lax.rsqrt(spread + epsilon) * gains).astype(jnp.bfloat16)


def project(inputs, weight):
    return jnp.dot(inputs, weight, preferred_element_type=jnp.float32).astype(jnp.bfloat16)


def attend(queries, key_rows, values, key_ok):
    batch_count, row_count, head_width = queries.shape
    key_count = key_rows.shape[1]
    head_count = head_width // HEAD_DIM
    query_heads = queries.reshape(batch_count, row_count, head_count, HEAD_DIM)
    key_heads = key_rows.reshape(batch_count, key_count, head_count, HEAD_DIM)
    value_heads = values.reshape(batch_count, key_count, head_count, HEAD_DIM)
    scores = jnp.einsum(
        "brhd,bkhd->bhrk", query_heads, key_heads, preferred_element_type=jnp.float32
    ) * HEAD_DIM ** (-0.5)
    if key_ok is not None:
        scores = jnp.where(key_ok[:, None, None, :], scores, -1e30)
    highest = jnp.max(scores, axis=-1, keepdims=True)
    weights = jnp.exp(scores - highest)
    chances = (weights / jnp.sum(weights, axis=-1, keepdims=True)).astype(jnp.bfloat16)
    blended = jnp.einsum(
        "bhrk,bkhd->brhd", chances, value_heads, preferred_element_type=jnp.float32
    )
    return blended.astype(jnp.bfloat16).reshape(batch_count * row_count, head_width)


def window(inputs, fetch):
    pieces = []
    for offset in range(-REACH, REACH + 1):
        pieces.append(inputs if offset == 0 else fetch(inputs, offset))
    return jnp.concatenate(pieces, axis=0)


def pick(beside_all, listed, window_start):
    blocks = beside_all.reshape(-1, BLOCK, beside_all.shape[1])
    local_ids = listed - window_start
    chosen = jnp.take(blocks, local_ids, axis=0)
    return chosen.reshape(listed.shape[0], listed.shape[1] * BLOCK, beside_all.shape[1])


def keys_values(normed, key_weight, value_weight):
    return jnp.concatenate([project(normed, key_weight), project(normed, value_weight)], axis=1)


def listed_valid(listed, grid_count):
    every_block = jnp.arange(grid_count.shape[0])
    counts = jnp.sum(
        jnp.where(listed[:, :, None] == every_block[None, None, :], grid_count[None, None, :], 0),
        axis=-1,
    )
    return jnp.arange(BLOCK)[None, None, :] < counts[:, :, None]


def per_device(
    grid_in,
    mesh_in,
    w_query,
    w_key,
    w_value,
    w_out,
    norm_gains,
    enc_list,
    proc_list,
    dec_list,
    grid_count,
):
    node_index = lax.axis_index("nodes")
    head_width = w_query.shape[2]
    grid_blocks = grid_in.shape[0] // BLOCK
    mesh_blocks = mesh_in.shape[0] // BLOCK
    grid_full, mesh_full = (
        lax.all_gather(grid_in, "mp", axis=1, tiled=True),
        lax.all_gather(mesh_in, "mp", axis=1, tiled=True),
    )
    own_counts = lax.dynamic_slice_in_dim(grid_count, node_index * grid_blocks, grid_blocks)
    row_ok = (jnp.arange(BLOCK)[None, :] < own_counts[:, None]).reshape(-1, 1)

    def mesh_update(blended, layer_index, state_part):
        whole_new = None
        terms = jnp.dot(blended, w_out[layer_index], preferred_element_type=jnp.float32)
        shares = summed_on_arrival(terms.astype(jnp.bfloat16), "mp", 1)
        part_new = (state_part.astype(jnp.float32) + shares).astype(jnp.bfloat16)
        whole_new = lax.all_gather(part_new, "mp", axis=1, tiled=True)
        return (part_new, whole_new)

    mesh_queries = project(normalize(mesh_full, norm_gains[0]), w_query[0]).reshape(
        mesh_blocks, BLOCK, head_width
    )
    grid_normed = normalize(grid_full, norm_gains[1])
    grid_kv = keys_values(grid_normed, w_key[0], w_value[0])
    listed_ok = listed_valid(enc_list, grid_count).reshape(enc_list.shape[0], -1)
    beside_all = window(grid_kv, lambda inputs, offset: from_behind(inputs, "nodes", -offset))
    chosen = pick(beside_all, enc_list, (node_index - REACH) * grid_blocks)
    blended = attend(mesh_queries, chosen[:, :, :head_width], chosen[:, :, head_width:], listed_ok)
    state_part, state_whole = mesh_update(blended, 0, mesh_in)
    for layer_index in (1, 2):
        normed = normalize(state_whole, norm_gains[layer_index + 1])
        queries = project(normed, w_query[layer_index]).reshape(mesh_blocks, BLOCK, head_width)
        mesh_kv = keys_values(normed, w_key[layer_index], w_value[layer_index])
        beside_all = window(mesh_kv, lambda inputs, offset: from_behind(inputs, "nodes", -offset))
        chosen = pick(beside_all, proc_list, (node_index - REACH) * mesh_blocks)
        blended = attend(queries, chosen[:, :, :head_width], chosen[:, :, head_width:], None)
        state_part, state_whole = mesh_update(blended, layer_index, state_part)
    grid_queries = project(normalize(grid_full, norm_gains[4]), w_query[3]).reshape(
        grid_blocks, BLOCK, head_width
    )
    mesh_normed = normalize(state_whole, norm_gains[5])
    mesh_kv = keys_values(mesh_normed, w_key[3], w_value[3])
    beside_all = window(mesh_kv, lambda inputs, offset: from_behind(inputs, "nodes", -offset))
    chosen = pick(beside_all, dec_list, (node_index - REACH) * mesh_blocks)
    blended = attend(grid_queries, chosen[:, :, :head_width], chosen[:, :, head_width:], None)
    terms = jnp.dot(blended, w_out[3], preferred_element_type=jnp.float32)
    update = lax.psum_scatter(
        terms.astype(jnp.bfloat16), "mp", scatter_dimension=1, tiled=True
    ).astype(jnp.float32)
    grid_out = grid_in.astype(jnp.float32) + update
    grid_out = jnp.where(row_ok, grid_out, 0.0).astype(jnp.bfloat16)
    return (grid_out, state_part)


def solution(mesh):
    placed = (
        P("nodes", "mp"),
        P("nodes", "mp"),
        P(None, None, "mp"),
        P(None, None, "mp"),
        P(None, None, "mp"),
        P(None, "mp", None),
        P(),
        P("nodes", None),
        P("nodes", None),
        P("nodes", None),
        P(),
    )
    return jax.shard_map(
        per_device,
        mesh=mesh,
        in_specs=placed,
        out_specs=(P("nodes", "mp"), P("nodes", "mp")),
        check_vma=False,
    )
```

profile of v0, /device:TPU:1, one launch (start us, length us, event | category | flops | bytes accessed | tf_op | source)
XLA Modules:
  0.0 329.7 jit_solution(16877713221942611837)
XLA Ops:
  8.8 11.4 %all_gather.16 = bf16[256,1024]{1,0:T(8,128)(2,1)S(1)} all-gather(bf16[256,256]{1,0:T(8,128)(2,1)} %param.14), channel_id=1, replica_groups=mesh['nodes'=128,'mp'=4] {'mp'}, dimensions={1}, use_global_device_ids=true | all-gather | bytes 655360 | tf_op jit(solution)/shard_map/all_gather | solution.py:111
  20.8 1.6 fusion.139
  22.4 1.3 convolution_convert_fusion.18
  23.7 31.9 %all-gather.2.cloned.1.call-done = bf16[1024,1024]{1,0:T(8,128)(2,1)} async-done(((bf16[1024,256]{1,0:T(8,128)(2,1)}), bf16[1024,1024]{1,0:T(8,128)(2,1)}) %all-gather.2.cloned.1.call-update) | async-done | bytes 2097168 | tf_op jit(solution)/shard_map/all_gather | solution.py:110
  55.7 2.1 convert_reduce_fusion
  59.3 1.8 convolution_convert_fusion.5
  61.1 1.8 convolution_convert_fusion.6
  62.9 5.0 %collective-permute-start.1 = (bf16[1024,256]{0,1:T(8,128)(2,1)S(1)}, bf16[1024,256]{0,1:T(8,128)(2,1)}, u32[]{:S(2)}, u32[]{:S(2)}) collective-permute-start(bf16[1024,256]{0,1:T(8,128)(2,1)S(1)} %pad_maximum_fusion), channel_id=1, source_target_pairs={{0,4},{4,8},{8,12},{12,16},{16,20},{20,24},{24,28},{28,32},{32,36}... | collective-permute-start | bytes 1572872 | tf_op jit(solution)/shard_map/ppermute | solution.py:29
  68.0 3.9 %collective-permute-start = (bf16[1024,256]{0,1:T(8,128)(2,1)S(1)}, bf16[1024,256]{0,1:T(8,128)(2,1)}, u32[]{:S(2)}, u32[]{:S(2)}) collective-permute-start(bf16[1024,256]{0,1:T(8,128)(2,1)S(1)} %pad_maximum_fusion), channel_id=1, source_target_pairs={{0,8},{4,12},{8,16},{12,20},{16,24},{20,28},{24,32},{28,36},{32,40... | collective-permute-start | bytes 1572872 | tf_op jit(solution)/shard_map/ppermute | solution.py:29
  71.9 1.9 collective-permute-start.2
  75.4 9.9 %collective-permute-done = bf16[1024,256]{0,1:T(8,128)(2,1)} collective-permute-done((bf16[1024,256]{0,1:T(8,128)(2,1)S(1)}, bf16[1024,256]{0,1:T(8,128)(2,1)}, u32[]{:S(2)}, u32[]{:S(2)}) %collective-permute-start) | collective-permute-done | bytes 524320 | tf_op jit(solution)/shard_map/ppermute | solution.py:29
  85.3 1.9 constant_dynamic-update-slice_fusion.4
  87.2 1.9 constant_dynamic-update-slice_fusion.3
  90.0 1.9 constant_dynamic-update-slice_fusion.1
  91.9 1.9 constant_dynamic-update-slice_fusion
  93.8 4.4 %copy.97 = bf16[5120,256]{1,0:T(8,128)(2,1)} copy(bf16[5120,256]{0,1:T(8,128)(2,1)} %constant_dynamic-update-slice_fusion) | data formatting | bytes 5242880 | tf_op jit(solution)/shard_map/reshape | solution.py:73
  98.2 2.3 gather_fusion
  103.6 2.0 fusion.36
  107.8 3.7 %all-to-all-start = ((bf16[4,256,256]{2,1,0:T(8,128)(2,1)}), bf16[4,256,256]{2,1,0:T(8,128)(2,1)S(1)}, u32[]{:S(2)}, u32[]{:S(2)}) async-start(bf16[4,256,256]{2,1,0:T(8,128)(2,1)} %bitcast.165), calls=%async_computation | async-start | bytes 1048576 | tf_op jit(solution)/shard_map/all_to_all | solution.py:22
  112.9 5.5 %all-to-all-done = bf16[4,256,256]{2,1,0:T(8,128)(2,1)S(1)} async-done(((bf16[4,256,256]{2,1,0:T(8,128)(2,1)}), bf16[4,256,256]{2,1,0:T(8,128)(2,1)S(1)}, u32[]{:S(2)}, u32[]{:S(2)}) %all-to-all-start) | async-done | bytes 524320 | tf_op jit(solution)/shard_map/all_to_all | solution.py:22
  118.5 10.1 %all_gather.17 = bf16[256,1024]{1,0:T(8,128)(2,1)S(1)} all-gather(bf16[256,256]{1,0:T(8,128)(2,1)S(1)} %add_convert_fusion.2), channel_id=1, replica_groups=mesh['nodes'=128,'mp'=4] {'mp'}, dimensions={1}, use_global_device_ids=true | all-gather | bytes 655360 | tf_op jit(solution)/shard_map/all_gather | solution.py:121
  131.9 10.9 %collective-permute-start.5 = (bf16[256,256]{0,1:T(8,128)(2,1)S(1)}, bf16[256,256]{0,1:T(8,128)(2,1)S(1)}, u32[]{:S(2)}, u32[]{:S(2)}) collective-permute-start(bf16[256,256]{0,1:T(8,128)(2,1)S(1)} %pad_maximum_fusion.1), channel_id=1, source_target_pairs={{0,4},{4,8},{8,12},{12,16},{16,20},{20,24},{24,28},{28,32},{32,36}... | collective-permute-start | bytes 393224 | tf_op jit(solution)/shard_map/ppermute | solution.py:29
  142.9 3.2 collective-permute-start.4
  148.6 1.9 collective-permute-start.6
  153.3 2.1 collective-permute-done.6
  156.8 1.4 copy.77
  159.1 1.4 fusion.143
  163.3 10.8 %all_to_all.15 = bf16[4,256,256]{2,1,0:T(8,128)(2,1)S(1)} all-to-all(bf16[4,256,256]{2,1,0:T(8,128)(2,1)S(1)} %bitcast.173), channel_id=1, replica_groups=mesh['nodes'=128,'mp'=4] {'mp'}, dimensions={0} | all-to-all | bytes 1048576 | tf_op jit(solution)/shard_map/all_to_all | solution.py:22
  174.2 11.8 %all_gather.18 = bf16[256,1024]{1,0:T(8,128)(2,1)S(1)} all-gather(bf16[256,256]{1,0:T(8,128)(2,1)S(1)} %add_convert_fusion.1), channel_id=1, replica_groups=mesh['nodes'=128,'mp'=4] {'mp'}, dimensions={1}, use_global_device_ids=true | all-gather | bytes 655360 | tf_op jit(solution)/shard_map/all_gather | solution.py:121
  189.4 5.1 %collective-permute-start.9 = (bf16[256,256]{0,1:T(8,128)(2,1)S(1)}, bf16[256,256]{0,1:T(8,128)(2,1)S(1)}, u32[]{:S(2)}, u32[]{:S(2)}) collective-permute-start(bf16[256,256]{0,1:T(8,128)(2,1)S(1)} %pad_maximum_fusion.2), channel_id=1, source_target_pairs={{0,4},{4,8},{8,12},{12,16},{16,20},{20,24},{24,28},{28,32},{32,36}... | collective-permute-start | bytes 393224 | tf_op jit(solution)/shard_map/ppermute | solution.py:29
  194.5 4.2 %collective-permute-start.8 = (bf16[256,256]{0,1:T(8,128)(2,1)S(1)}, bf16[256,256]{0,1:T(8,128)(2,1)S(1)}, u32[]{:S(2)}, u32[]{:S(2)}) collective-permute-start(bf16[256,256]{0,1:T(8,128)(2,1)S(1)} %pad_maximum_fusion.2), channel_id=1, source_target_pairs={{0,8},{4,12},{8,16},{12,20},{16,24},{20,28},{24,32},{28,36},{32,40... | collective-permute-start | bytes 393224 | tf_op jit(solution)/shard_map/ppermute | solution.py:29
  201.2 1.9 collective-permute-start.10
  205.3 2.3 collective-permute-done.10
  208.9 1.3 copy.84
  215.4 3.5 %all-to-all-start.2 = ((bf16[4,256,256]{2,1,0:T(8,128)(2,1)}), bf16[4,256,256]{2,1,0:T(8,128)(2,1)S(1)}, u32[]{:S(2)}, u32[]{:S(2)}) async-start(bf16[4,256,256]{2,1,0:T(8,128)(2,1)} %bitcast.161), calls=%async_computation.2 | async-start | bytes 1048576 | tf_op jit(solution)/shard_map/all_to_all | solution.py:22
  219.0 7.6 %all-to-all-done.2 = bf16[4,256,256]{2,1,0:T(8,128)(2,1)S(1)} async-done(((bf16[4,256,256]{2,1,0:T(8,128)(2,1)}), bf16[4,256,256]{2,1,0:T(8,128)(2,1)S(1)}, u32[]{:S(2)}, u32[]{:S(2)}) %all-to-all-start.2) | async-done | bytes 524320 | tf_op jit(solution)/shard_map/all_to_all | solution.py:22
  226.7 11.1 %all_gather.19 = bf16[256,1024]{1,0:T(8,128)(2,1)S(1)} all-gather(bf16[256,256]{1,0:T(8,128)(2,1)S(1)} %add_convert_fusion), channel_id=1, replica_groups=mesh['nodes'=128,'mp'=4] {'mp'}, dimensions={1}, use_global_device_ids=true | all-gather | bytes 655360 | tf_op jit(solution)/shard_map/all_gather | solution.py:121
  238.3 1.4 convolution_convert_fusion.7
  239.6 1.4 convolution_convert_fusion.8
  241.0 4.5 %collective-permute-start.13 = (bf16[256,256]{0,1:T(8,128)(2,1)S(1)}, bf16[256,256]{0,1:T(8,128)(2,1)S(1)}, u32[]{:S(2)}, u32[]{:S(2)}) collective-permute-start(bf16[256,256]{0,1:T(8,128)(2,1)S(1)} %pad_maximum_fusion.3), channel_id=1, source_target_pairs={{0,4},{4,8},{8,12},{12,16},{16,20},{20,24},{24,28},{28,32},{32,36}... | collective-permute-start | bytes 393224 | tf_op jit(solution)/shard_map/ppermute | solution.py:29
  245.5 5.6 %collective-permute-start.12 = (bf16[256,256]{0,1:T(8,128)(2,1)S(1)}, bf16[256,256]{0,1:T(8,128)(2,1)S(1)}, u32[]{:S(2)}, u32[]{:S(2)}) collective-permute-start(bf16[256,256]{0,1:T(8,128)(2,1)S(1)} %pad_maximum_fusion.3), channel_id=1, source_target_pairs={{0,8},{4,12},{8,16},{12,20},{16,24},{20,28},{24,32},{28,36},{32,40... | collective-permute-start | bytes 393224 | tf_op jit(solution)/shard_map/ppermute | solution.py:29
  251.2 1.8 fusion.32
  255.3 1.9 collective-permute-start.14
  257.3 5.2 %collective-permute-done.14 = bf16[256,256]{0,1:T(8,128)(2,1)S(1)} collective-permute-done((bf16[256,256]{0,1:T(8,128)(2,1)S(1)}, bf16[256,256]{0,1:T(8,128)(2,1)S(1)}, u32[]{:S(2)}, u32[]{:S(2)}) %collective-permute-start.14) | collective-permute-done | bytes 131104 | tf_op jit(solution)/shard_map/ppermute | solution.py:29
  266.4 3.7 %fusion.35 = bf16[8,128,2,64]{1,3,2,0:T(8,128)(2,1)S(1)} fusion(bf16[8,256,2,64]{1,3,2,0:T(8,128)(2,1)S(1)} %bitcast.190, f32[8,2,128]{2,1,0:T(2,128)S(1)} %fusion.149, bf16[8,256,2,64]{1,3,2,0:T(8,128)(2,1)S(1)} %bitcast.189, bf16[8,128,2,64]{3,2,1,0:T(2,128)(2,1)S(1)} %copy-done.3), kind=kOutput, calls=%fused_computation.59 | convolution fusion | flops 136448256 | bytes 1581056 | tf_op jit(solution)/shard_map/bhrk,bkhd->brhd/dot_general | solution.py:59
  270.3 3.0 convolution_convert_fusion
  274.2 46.6 %reduce-scatter.2.cloned.1.call-done = bf16[1024,256]{1,0:T(8,128)(2,1)} async-done(((bf16[1024,1024]{1,0:T(8,128)(2,1)}), bf16[1024,256]{1,0:T(8,128)(2,1)}) %reduce-scatter.2.cloned.1.call-update) | async-done | bytes 524304 | tf_op jit(solution)/shard_map/reduce_scatter | solution.py:151
  320.9 2.0 select_convert_fusion
  (166 shorter events, 49.0 us)
Async XLA Ops:
  7.2 48.5 %all-gather.2.cloned.1.call-start = ((), (), s32[]{:S(2)}) async-start(), calls=%async_computation.4 | async-start | bytes 2621440 | tf_op jit(solution)/shard_map/all_gather | solution.py:110
  20.8 80.7 %copy-start.8 = (pred[2,512]{1,0:T(4,128)(4,1)}, pred[2,512]{1,0:T(4,128)(4,1)S(1)}, u32[]{:S(2)}) copy-start(pred[2,512]{1,0:T(4,128)(4,1)S(1)} %bitcast_compare_fusion) | copy-start | bytes 3076
  55.7 2.2 copy-start
  59.3 12.6 %copy-start.13 = (s32[2,4]{1,0:T(2,128)S(1)}, s32[2,4]{1,0:T(2,128)}, u32[]{:S(2)}) copy-start(s32[2,4]{1,0:T(2,128)} %param.20) | copy-start | bytes 100
  62.9 24.3 %collective-permute-start.1 = (bf16[1024,256]{0,1:T(8,128)(2,1)S(1)}, bf16[1024,256]{0,1:T(8,128)(2,1)}, u32[]{:S(2)}, u32[]{:S(2)}) collective-permute-start(bf16[1024,256]{0,1:T(8,128)(2,1)S(1)} %pad_maximum_fusion), channel_id=1, source_target_pairs={{0,4},{4,8},{8,12},{12,16},{16,20},{20,24},{24,28},{28,32},{32,36}... | collective-permute-start | bytes 1572872 | tf_op jit(solution)/shard_map/ppermute | solution.py:29
  68.0 17.3 %collective-permute-start = (bf16[1024,256]{0,1:T(8,128)(2,1)S(1)}, bf16[1024,256]{0,1:T(8,128)(2,1)}, u32[]{:S(2)}, u32[]{:S(2)}) collective-permute-start(bf16[1024,256]{0,1:T(8,128)(2,1)S(1)} %pad_maximum_fusion), channel_id=1, source_target_pairs={{0,8},{4,12},{8,16},{12,20},{16,24},{20,28},{24,32},{28,36},{32,40... | collective-permute-start | bytes 1572872 | tf_op jit(solution)/shard_map/ppermute | solution.py:29
  71.9 18.1 %collective-permute-start.2 = (bf16[1024,256]{0,1:T(8,128)(2,1)S(1)}, bf16[1024,256]{0,1:T(8,128)(2,1)}, u32[]{:S(2)}, u32[]{:S(2)}) collective-permute-start(bf16[1024,256]{0,1:T(8,128)(2,1)S(1)} %pad_maximum_fusion), channel_id=1, source_target_pairs={{4,0},{8,4},{12,8},{16,12},{20,16},{24,20},{28,24},{32,28},{36,32}... | collective-permute-start | bytes 1572872 | tf_op jit(solution)/shard_map/ppermute | solution.py:29
  73.9 17.9 %collective-permute-start.3 = (bf16[1024,256]{0,1:T(8,128)(2,1)S(1)}, bf16[1024,256]{0,1:T(8,128)(2,1)}, u32[]{:S(2)}, u32[]{:S(2)}) collective-permute-start(bf16[1024,256]{0,1:T(8,128)(2,1)S(1)} %pad_maximum_fusion), channel_id=1, source_target_pairs={{8,0},{12,4},{16,8},{20,12},{24,16},{28,20},{32,24},{36,28},{40,32... | collective-permute-start | bytes 1572872 | tf_op jit(solution)/shard_map/ppermute | solution.py:29
  105.6 5.9 %copy-start.15 = (s32[2,3]{1,0:T(2,128)S(1)}, s32[2,3]{1,0:T(2,128)}, u32[]{:S(2)}) copy-start(s32[2,3]{1,0:T(2,128)} %param.21) | copy-start | bytes 76
  105.6 6.0 %copy-start.16 = (s32[8,2]{0,1:T(2,128)S(1)}, s32[8,2]{0,1:T(2,128)}, u32[]{:S(2)}) copy-start(s32[8,2]{0,1:T(2,128)} %param.22) | copy-start | bytes 196
  105.6 12.9 %copy-start.4 = (bf16[256,256]{1,0:T(8,128)(2,1)S(1)}, bf16[256,256]{1,0:T(8,128)(2,1)}, u32[]{:S(2)}) copy-start(bf16[256,256]{1,0:T(8,128)(2,1)} %param.14) | copy-start | bytes 393220
  107.8 10.6 %all-to-all-start = ((bf16[4,256,256]{2,1,0:T(8,128)(2,1)}), bf16[4,256,256]{2,1,0:T(8,128)(2,1)S(1)}, u32[]{:S(2)}, u32[]{:S(2)}) async-start(bf16[4,256,256]{2,1,0:T(8,128)(2,1)} %bitcast.165), calls=%async_computation | async-start | bytes 1048576 | tf_op jit(solution)/shard_map/all_to_all | solution.py:22
  111.5 47.2 %copy-start.9 = (pred[2,3]{1,0:T(4,128)(4,1)}, pred[2,3]{1,0:T(4,128)(4,1)S(1)}, u32[]{:S(2)}) copy-start(pred[2,3]{1,0:T(4,128)(4,1)S(1)} %get-tuple-element.5) | copy-start | bytes 22
  112.9 45.3 %copy-start.7 = (s32[1024]{0:T(1024)}, s32[1024]{0:T(1024)S(1)}, u32[]{:S(2)}) copy-start(s32[1024]{0:T(1024)S(1)} %get-tuple-element.24) | copy-start | bytes 12292
  131.9 20.0 %collective-permute-start.5 = (bf16[256,256]{0,1:T(8,128)(2,1)S(1)}, bf16[256,256]{0,1:T(8,128)(2,1)S(1)}, u32[]{:S(2)}, u32[]{:S(2)}) collective-permute-start(bf16[256,256]{0,1:T(8,128)(2,1)S(1)} %pad_maximum_fusion.1), channel_id=1, source_target_pairs={{0,4},{4,8},{8,12},{12,16},{16,20},{20,24},{24,28},{28,32},{32,36}... | collective-permute-start | bytes 393224 | tf_op jit(solution)/shard_map/ppermute | solution.py:29
  142.9 8.4 %collective-permute-start.4 = (bf16[256,256]{0,1:T(8,128)(2,1)S(1)}, bf16[256,256]{0,1:T(8,128)(2,1)S(1)}, u32[]{:S(2)}, u32[]{:S(2)}) collective-permute-start(bf16[256,256]{0,1:T(8,128)(2,1)S(1)} %pad_maximum_fusion.1), channel_id=1, source_target_pairs={{0,8},{4,12},{8,16},{12,20},{16,24},{20,28},{24,32},{28,36},{32,40... | collective-permute-start | bytes 393224 | tf_op jit(solution)/shard_map/ppermute | solution.py:29
  147.3 8.8 %collective-permute-start.7 = (bf16[256,256]{0,1:T(8,128)(2,1)S(1)}, bf16[256,256]{0,1:T(8,128)(2,1)S(1)}, u32[]{:S(2)}, u32[]{:S(2)}) collective-permute-start(bf16[256,256]{0,1:T(8,128)(2,1)S(1)} %pad_maximum_fusion.1), channel_id=1, source_target_pairs={{8,0},{12,4},{16,8},{20,12},{24,16},{28,20},{32,24},{36,28},{40,32... | collective-permute-start | bytes 393224 | tf_op jit(solution)/shard_map/ppermute | solution.py:29
  148.6 6.8 %collective-permute-start.6 = (bf16[256,256]{0,1:T(8,128)(2,1)S(1)}, bf16[256,256]{0,1:T(8,128)(2,1)S(1)}, u32[]{:S(2)}, u32[]{:S(2)}) collective-permute-start(bf16[256,256]{0,1:T(8,128)(2,1)S(1)} %pad_maximum_fusion.1), channel_id=1, source_target_pairs={{4,0},{8,4},{12,8},{16,12},{20,16},{24,20},{28,24},{32,28},{36,32}... | collective-permute-start | bytes 393224 | tf_op jit(solution)/shard_map/ppermute | solution.py:29
  156.8 3.7 %copy-start.2 = (bf16[2,128,2,64]{3,2,1,0:T(2,128)(2,1)S(1)}, bf16[2,128,2,64]{3,2,1,0:T(2,128)(2,1)}, u32[]{:S(2)}) copy-start(bf16[2,128,2,64]{3,2,1,0:T(2,128)(2,1)} %reshape.261) | copy-start | bytes 196612
  188.1 22.8 %copy-start.10 = (pred[2,3]{1,0:T(4,128)(4,1)S(1)}, pred[2,3]{1,0:T(4,128)(4,1)}, u32[]{:S(2)}) copy-start(pred[2,3]{1,0:T(4,128)(4,1)} %copy-done.9) | copy-start | bytes 22
  189.4 14.5 %collective-permute-start.9 = (bf16[256,256]{0,1:T(8,128)(2,1)S(1)}, bf16[256,256]{0,1:T(8,128)(2,1)S(1)}, u32[]{:S(2)}, u32[]{:S(2)}) collective-permute-start(bf16[256,256]{0,1:T(8,128)(2,1)S(1)} %pad_maximum_fusion.2), channel_id=1, source_target_pairs={{0,4},{4,8},{8,12},{12,16},{16,20},{20,24},{24,28},{28,32},{32,36}... | collective-permute-start | bytes 393224 | tf_op jit(solution)/shard_map/ppermute | solution.py:29
  194.5 8.8 %collective-permute-start.8 = (bf16[256,256]{0,1:T(8,128)(2,1)S(1)}, bf16[256,256]{0,1:T(8,128)(2,1)S(1)}, u32[]{:S(2)}, u32[]{:S(2)}) collective-permute-start(bf16[256,256]{0,1:T(8,128)(2,1)S(1)} %pad_maximum_fusion.2), channel_id=1, source_target_pairs={{0,8},{4,12},{8,16},{12,20},{16,24},{20,28},{24,32},{28,36},{32,40... | collective-permute-start | bytes 393224 | tf_op jit(solution)/shard_map/ppermute | solution.py:29
  199.9 8.3 %collective-permute-start.11 = (bf16[256,256]{0,1:T(8,128)(2,1)S(1)}, bf16[256,256]{0,1:T(8,128)(2,1)S(1)}, u32[]{:S(2)}, u32[]{:S(2)}) collective-permute-start(bf16[256,256]{0,1:T(8,128)(2,1)S(1)} %pad_maximum_fusion.2), channel_id=1, source_target_pairs={{8,0},{12,4},{16,8},{20,12},{24,16},{28,20},{32,24},{36,28},{40,32... | collective-permute-start | bytes 393224 | tf_op jit(solution)/shard_map/ppermute | solution.py:29
  201.2 6.4 %collective-permute-start.10 = (bf16[256,256]{0,1:T(8,128)(2,1)S(1)}, bf16[256,256]{0,1:T(8,128)(2,1)S(1)}, u32[]{:S(2)}, u32[]{:S(2)}) collective-permute-start(bf16[256,256]{0,1:T(8,128)(2,1)S(1)} %pad_maximum_fusion.2), channel_id=1, source_target_pairs={{4,0},{8,4},{12,8},{16,12},{20,16},{24,20},{28,24},{32,28},{36,32}... | collective-permute-start | bytes 393224 | tf_op jit(solution)/shard_map/ppermute | solution.py:29
  212.2 6.8 %copy-start.14 = (pred[8,2]{0,1:T(4,128)(4,1)S(1)}, pred[8,2]{0,1:T(4,128)(4,1)}, u32[]{:S(2)}) copy-start(pred[8,2]{0,1:T(4,128)(4,1)} %get-tuple-element.3) | copy-start | bytes 52
  214.6 23.7 %copy-start.12 = (f32[1,1024]{1,0:T(1,128)S(1)}, f32[1,1024]{1,0:T(1,128)}, u32[]{:S(2)}) copy-start(f32[1,1024]{1,0:T(1,128)} %get-tuple-element.22) | copy-start | bytes 12292
  215.4 11.2 %all-to-all-start.2 = ((bf16[4,256,256]{2,1,0:T(8,128)(2,1)}), bf16[4,256,256]{2,1,0:T(8,128)(2,1)S(1)}, u32[]{:S(2)}, u32[]{:S(2)}) async-start(bf16[4,256,256]{2,1,0:T(8,128)(2,1)} %bitcast.161), calls=%async_computation.2 | async-start | bytes 1048576 | tf_op jit(solution)/shard_map/all_to_all | solution.py:22
  218.9 102.0 %reduce-scatter.2.cloned.1.call-start = ((), (), s32[]{:S(2)}) async-start(), calls=%async_computation.5 | async-start | bytes 2621440 | tf_op jit(solution)/shard_map/reduce_scatter | solution.py:151
  226.7 26.3 %copy-start.5 = (bf16[256,256]{1,0:T(8,128)(2,1)}, bf16[256,256]{1,0:T(8,128)(2,1)S(1)}, u32[]{:S(2)}) copy-start(bf16[256,256]{1,0:T(8,128)(2,1)S(1)} %add_convert_fusion) | copy-start | bytes 393220
  226.7 24.4 %copy-start.11 = (f32[1,1024]{1,0:T(1,128)S(1)}, f32[1,1024]{1,0:T(1,128)}, u32[]{:S(2)}) copy-start(f32[1,1024]{1,0:T(1,128)} %get-tuple-element.17) | copy-start | bytes 12292
  241.0 16.2 %collective-permute-start.13 = (bf16[256,256]{0,1:T(8,128)(2,1)S(1)}, bf16[256,256]{0,1:T(8,128)(2,1)S(1)}, u32[]{:S(2)}, u32[]{:S(2)}) collective-permute-start(bf16[256,256]{0,1:T(8,128)(2,1)S(1)} %pad_maximum_fusion.3), channel_id=1, source_target_pairs={{0,4},{4,8},{8,12},{12,16},{16,20},{20,24},{24,28},{28,32},{32,36}... | collective-permute-start | bytes 393224 | tf_op jit(solution)/shard_map/ppermute | solution.py:29
  245.5 11.7 %collective-permute-start.12 = (bf16[256,256]{0,1:T(8,128)(2,1)S(1)}, bf16[256,256]{0,1:T(8,128)(2,1)S(1)}, u32[]{:S(2)}, u32[]{:S(2)}) collective-permute-start(bf16[256,256]{0,1:T(8,128)(2,1)S(1)} %pad_maximum_fusion.3), channel_id=1, source_target_pairs={{0,8},{4,12},{8,16},{12,20},{16,24},{20,28},{24,32},{28,36},{32,40... | collective-permute-start | bytes 393224 | tf_op jit(solution)/shard_map/ppermute | solution.py:29
  253.0 10.3 %copy-start.6 = (s32[1024]{0:T(1024)S(1)}, s32[1024]{0:T(1024)}, u32[]{:S(2)}) copy-start(s32[1024]{0:T(1024)} %get-tuple-element.23) | copy-start | bytes 12292
  254.0 9.0 %collective-permute-start.15 = (bf16[256,256]{0,1:T(8,128)(2,1)S(1)}, bf16[256,256]{0,1:T(8,128)(2,1)S(1)}, u32[]{:S(2)}, u32[]{:S(2)}) collective-permute-start(bf16[256,256]{0,1:T(8,128)(2,1)S(1)} %pad_maximum_fusion.3), channel_id=1, source_target_pairs={{8,0},{12,4},{16,8},{20,12},{24,16},{28,20},{32,24},{36,28},{40,32... | collective-permute-start | bytes 393224 | tf_op jit(solution)/shard_map/ppermute | solution.py:29
  255.3 7.2 %collective-permute-start.14 = (bf16[256,256]{0,1:T(8,128)(2,1)S(1)}, bf16[256,256]{0,1:T(8,128)(2,1)S(1)}, u32[]{:S(2)}, u32[]{:S(2)}) collective-permute-start(bf16[256,256]{0,1:T(8,128)(2,1)S(1)} %pad_maximum_fusion.3), channel_id=1, source_target_pairs={{4,0},{8,4},{12,8},{16,12},{20,16},{24,20},{28,24},{32,28},{36,32}... | collective-permute-start | bytes 393224 | tf_op jit(solution)/shard_map/ppermute | solution.py:29
  264.4 1.0 copy-start.3
  270.1 50.7 %copy-start.1 = (bf16[1024,256]{1,0:T(8,128)(2,1)S(1)}, bf16[1024,256]{1,0:T(8,128)(2,1)}, u32[]{:S(2)}) copy-start(bf16[1024,256]{1,0:T(8,128)(2,1)} %param.13) | copy-start | bytes 1572868
Sparse Core Ops, SparseCore 0:
  10.1 45.5 all-gather.1
  273.5 47.2 reduce-scatter.1
where the time goes:
time: 332 us; the launch traced here: 330 us
  waiting for transfers between devices  112 us (34%)
  starting transfers between devices  62.4 us (19%)
  blocking collectives  55.2 us (17%)
  matrix products  36.8 us (11%)
  local copies, waits for them, and re-layouts  35 us (11%)
  between operations  14.9 us (4%)
  other arithmetic  13.1 us (4%)
    ppermute x16, starting transfers between devices, from_behind(): lax.ppermute(value, axis, [(source, source + steps) for source in range(f...  55.2 us
    reduce_scatter x1, waiting for transfers between devices, per_device(): lax.psum_scatter(terms.astype(jnp.bfloat16), 'mp', scatter_dimension=1, t...  46.6 us
    all_gather x3, blocking collectives, mesh_update(): whole_new = lax.all_gather(part_new, 'mp', axis=1, tiled=True)  33 us
    all_gather x1, waiting for transfers between devices, per_device(): lax.all_gather(grid_in, 'mp', axis=1, tiled=True)  31.9 us
    ppermute x16, waiting for transfers between devices, from_behind(): lax.ppermute(value, axis, [(source, source + steps) for source in range(f...  20 us
    dot_general x12, matrix products, project(): jnp.dot(inputs, weight, preferred_element_type=jnp.float32)  16.9 us
    all_to_all x2, waiting for transfers between devices, summed_on_arrival(): lax.all_to_all(pieces, axis, split_axis=0, concat_axis=0, tiled=True)  13.1 us
    all_gather x1, blocking collectives, per_device(): lax.all_gather(mesh_in, 'mp', axis=1, tiled=True)  11.4 us
  transfers between devices with their start and end apart: 20, of which 9 were waited for; matrix products, arithmetic and copies ran while one was open for 8% of the time, Pallas kernels for 0%

commit v1 on v0

v1 whole, which is shorter than its diff:
```python
import jax
import jax.numpy as jnp
from jax import lax
from jax.experimental import pallas as pl
from jax.experimental.pallas import tpu as pltpu
from jax.sharding import PartitionSpec as P


BLOCK = 128
REACH = 2
EPS = 1e-05
MP = 4
F32 = jnp.float32
BF16 = jnp.bfloat16

ENC0, PROC0, DEC0 = 2, 10, 16


PARAMS = pltpu.CompilerParams(vmem_limit_bytes=16 * 1024 * 1024)


def shift_mp(value, steps):
    return lax.ppermute(value, "mp", [(s, (s + steps) % MP) for s in range(MP)])


def from_node(value, offset):
    count = lax.axis_size("nodes")
    pairs = [(s, s - offset) for s in range(count) if 0 <= s - offset < count]
    return lax.ppermute(value, "nodes", pairs)


def swap_cores(value):
    count = lax.axis_size("nodes")
    return lax.ppermute(value, "nodes", [(s, s ^ 1) for s in range(count)])


def smem():
    return pl.BlockSpec(memory_space=pltpu.SMEM)


def vmem():
    return pl.BlockSpec(memory_space=pltpu.VMEM)


def source(meta, k):
    return (meta[0] + MP - k) % MP


def normed(pieces):
    width = sum(p.shape[-1] for p in pieces)
    values = [p.astype(F32) for p in pieces]
    mean = sum(jnp.sum(v, axis=-1, keepdims=True) for v in values) * (1.0 / width)
    centred = [v - mean for v in values]
    spread = sum(jnp.sum(c * c, axis=-1, keepdims=True) for c in centred) * (1.0 / width)
    scale = lax.rsqrt(spread + EPS)
    return [c * scale for c in centred]


def dot(a, b):
    return jnp.dot(a, b, preferred_element_type=F32)


def grid_kernel(meta, x0, x1, x2, x3, gains, w_k, w_v, w_q, kv_out, q_out):
    rows = normed([x[...] for x in (x0, x1, x2, x3)])
    kv = q = None
    for k in range(MP):
        src = source(meta, k)
        at = pl.ds(pl.multiple_of(src * 256, 256), 256)
        for_kv = (rows[k] * gains[1, pl.ds(src, 1), :]).astype(BF16)
        for_q = (rows[k] * gains[4, pl.ds(src, 1), :]).astype(BF16)
        kv_part = dot(for_kv, jnp.concatenate([w_k[at, :], w_v[at, :]], axis=1))
        q_part = dot(for_q, w_q[at, :])
        kv = kv_part if kv is None else kv + kv_part
        q = q_part if q is None else q + q_part
    kv_out[...] = kv.astype(BF16)
    q_out[...] = q.astype(BF16)


def grid_project(meta, pieces, gains, w_k, w_v, w_q):
    rows = pieces[0].shape[0]
    tile = 256
    return pl.pallas_call(
        grid_kernel,
        grid=(rows // tile,),
        in_specs=[smem()]
        + [pl.BlockSpec((tile, 256), lambda i: (i, 0))] * MP
        + [vmem()] * 4,
        out_specs=[
            pl.BlockSpec((tile, 256), lambda i: (i, 0)),
            pl.BlockSpec((tile, 128), lambda i: (i, 0)),
        ],
        out_shape=[
            jax.ShapeDtypeStruct((rows, 256), BF16),
            jax.ShapeDtypeStruct((rows, 128), BF16),
        ],
        cost_estimate=pl.CostEstimate(flops=rows * 1024 * 384 * 2, transcendentals=0, bytes_accessed=rows * 4096),
        compiler_params=PARAMS,
        name="grid_project",
    )(meta, *pieces, gains, w_k, w_v, w_q)


def mesh_kernel(meta, x0, x1, x2, x3, gains, w_q, state_out, q_out):
    pieces = [x[...] for x in (x0, x1, x2, x3)]
    rows = normed(pieces)
    q = None
    for k in range(MP):
        src = source(meta, k)
        at = pl.ds(pl.multiple_of(src * 256, 256), 256)
        part = dot((rows[k] * gains[0, pl.ds(src, 1), :]).astype(BF16), w_q[at, :])
        q = part if q is None else q + part
        state_out[src] = pieces[k]
    q_out[...] = q.astype(BF16)


def mesh_start(meta, pieces, gains, w_q):
    rows = pieces[0].shape[0]
    return pl.pallas_call(
        mesh_kernel,
        in_specs=[smem()] + [vmem()] * 6,
        out_specs=[vmem(), vmem()],
        out_shape=[
            jax.ShapeDtypeStruct((MP, rows, 256), BF16),
            jax.ShapeDtypeStruct((rows, 128), BF16),
        ],
        cost_estimate=pl.CostEstimate(flops=rows * 1024 * 128 * 2, transcendentals=0, bytes_accessed=rows * 4096),
        compiler_params=PARAMS,
        name="mesh_start",
    )(meta, *pieces, gains, w_q)


def head_rows():
    lane = lax.broadcasted_iota(jnp.int32, (1, 128), 1)
    first = jnp.where(lane < 64, 0.125, 0.0).astype(BF16)
    second = jnp.where(lane < 64, 0.0, 0.125).astype(BF16)
    return first, second


def attend_block(q, keys, values, key_ok):
    outs = []
    for row in head_rows():
        scores = lax.dot_general(
            q * row, keys, (((1,), (1,)), ((), ())), preferred_element_type=F32
        )
        if key_ok is not None:
            scores = jnp.where(key_ok, scores, -1e30)
        highest = jnp.max(scores, axis=-1, keepdims=True)
        weights = jnp.exp(scores - highest)
        total = jnp.sum(weights, axis=-1, keepdims=True)
        outs.append(dot(weights.astype(BF16), values) / total)
    lane = lax.broadcasted_iota(jnp.int32, outs[0].shape, 1)
    return jnp.where(lane < 64, outs[0], outs[1]).astype(BF16)


def enc_kernel(meta, listed, counts, q, *rest):
    windows, o_out, kept = rest[:-2], rest[-2], rest[-1]
    blocks_each = windows[0].shape[0] // BLOCK
    for slot in range(8):
        place = meta[ENC0 + slot]
        which = place // blocks_each
        start = pl.multiple_of((place % blocks_each) * BLOCK, BLOCK)
        for i, array in enumerate(windows):

            @pl.when(which == i)
            def _():
                kept[slot] = array[pl.ds(start, BLOCK), :]

    lane = lax.broadcasted_iota(jnp.int32, (1, BLOCK), 1)
    for b in range(2):
        key_ok = jnp.concatenate(
            [lane < counts[listed[b, j]] for j in range(4)], axis=1
        )
        kv = kept[b * 4 : b * 4 + 4].reshape(4 * BLOCK, 256)
        o = attend_block(q[b * BLOCK : (b + 1) * BLOCK, :], kv[:, :128], kv[:, 128:], key_ok)
        for j in range(MP):
            o_out[j, b * BLOCK : (b + 1) * BLOCK, :] = o


def enc_attend(meta, listed, counts, q, windows):
    return pl.pallas_call(
        enc_kernel,
        in_specs=[smem(), smem(), smem()] + [vmem()] * (1 + len(windows)),
        out_specs=vmem(),
        out_shape=jax.ShapeDtypeStruct((MP,) + q.shape, BF16),
        scratch_shapes=[pltpu.VMEM((8, BLOCK, 256), BF16)],
        compiler_params=PARAMS,
        name="enc_attend",
    )(meta, listed, counts, q, *windows)


def near_kernel(first_entry, per_block, meta, q, a0, a1, a2, a3, a4, o_out, kept):
    for i, array in enumerate((a0, a1, a2, a3, a4)):
        kept[2 * i] = array[0:BLOCK, :]
        kept[2 * i + 1] = array[BLOCK : 2 * BLOCK, :]
    for b in range(q.shape[0] // BLOCK):
        kv = jnp.concatenate(
            [kept[meta[first_entry + b * per_block + j]] for j in range(per_block)], axis=0
        )
        o = attend_block(q[b * BLOCK : (b + 1) * BLOCK, :], kv[:, :128], kv[:, 128:], None)
        for j in range(MP):
            o_out[j, b * BLOCK : (b + 1) * BLOCK, :] = o


def near_attend(first_entry, per_block, meta, q, windows):
    def body(*refs):
        near_kernel(first_entry, per_block, *refs)

    return pl.pallas_call(
        body,
        in_specs=[smem()] + [vmem()] * 6,
        out_specs=vmem(),
        out_shape=jax.ShapeDtypeStruct((MP,) + q.shape, BF16),
        scratch_shapes=[pltpu.VMEM((10, BLOCK, 256), BF16)],
        compiler_params=PARAMS,
        name="near_attend",
    )(meta, q, *windows)


def layer_kernel(index, gain_row, with_query, meta, o, state, w_own, a1, a2, a3, other, gains, *rest):
    projections, outs = rest[: 2 + with_query], rest[2 + with_query :]
    heads = jnp.concatenate([o[source(meta, k)] for k in range(MP)], axis=1)
    core = meta[1] % 2
    for part in range(4):
        at = 2 * index + part % 2
        if part < 2:
            g = 2 * core + part
            fetched = [a1[at], a2[at], a3[at]]
        else:
            g = 2 * (1 - core) + part - 2
            fetched = [other[k, at] for k in range(MP - 1)]
        w_out = jnp.concatenate([w_own[index, g]] + fetched, axis=0)
        outs[0][g] = (state[g].astype(F32) + dot(heads, w_out)).astype(BF16)
    rows = normed([outs[0][g] for g in range(MP)])
    row = jnp.concatenate(
        [(rows[g] * gains[gain_row, g : g + 1, :]).astype(BF16) for g in range(MP)], axis=1
    )
    result = dot(row, jnp.concatenate([w[...] for w in projections], axis=1)).astype(BF16)
    outs[1][...] = result[:, :256]
    if with_query:
        outs[2][...] = result[:, 256:]


def layer(index, gain_row, with_query, meta, o, state, w_own, fetched, other, gains, projections):
    def body(*refs):
        layer_kernel(index, gain_row, with_query, *refs)

    rows = state.shape[1]
    shapes = [
        jax.ShapeDtypeStruct(state.shape, BF16),
        jax.ShapeDtypeStruct((rows, 256), BF16),
    ]
    if with_query:
        shapes.append(jax.ShapeDtypeStruct((rows, 128), BF16))
    operands = (o, state, w_own, *fetched, other, gains, *projections)
    return pl.pallas_call(
        body,
        in_specs=[smem()] + [vmem()] * len(operands),
        out_specs=[vmem()] * len(shapes),
        out_shape=shapes,
        compiler_params=PARAMS,
        name="mesh_layer",
    )(meta, *operands)


def final_kernel(meta, counts, o, w_out, grid_in, out):
    tile = grid_in.shape[0]
    heads = jnp.concatenate([o[source(meta, k)] for k in range(MP)], axis=1)
    value = grid_in[...].astype(F32) + dot(heads, w_out[...])
    row = lax.broadcasted_iota(jnp.int32, (BLOCK, 256), 0)
    for b in range(tile // BLOCK):
        count = counts[meta[1] * 8 + pl.program_id(0) * (tile // BLOCK) + b]
        part = value[b * BLOCK : (b + 1) * BLOCK, :]
        out[b * BLOCK : (b + 1) * BLOCK, :] = jnp.where(row < count, part, 0.0).astype(BF16)


def final(meta, counts, o, w_out, grid_in):
    rows = grid_in.shape[0]
    tile = 256
    return pl.pallas_call(
        final_kernel,
        grid=(rows // tile,),
        in_specs=[
            smem(),
            smem(),
            pl.BlockSpec((MP, tile, 128), lambda i: (0, i, 0)),
            vmem(),
            pl.BlockSpec((tile, 256), lambda i: (i, 0)),
        ],
        out_specs=pl.BlockSpec((tile, 256), lambda i: (i, 0)),
        out_shape=jax.ShapeDtypeStruct((rows, 256), BF16),
        compiler_params=PARAMS,
        name="grid_final",
    )(meta, counts, o, w_out, grid_in)


def gather_heads(copies):
    return lax.all_to_all(copies, "mp", split_axis=0, concat_axis=0, tiled=True)


def program(
    grid_in, mesh_in, w_query, w_key, w_value, w_out, norm_gains,
    enc_list, proc_list, dec_list, grid_count,
):
    own_mp, own_node = lax.axis_index("mp"), lax.axis_index("nodes")
    core = own_node % 2
    meta = jnp.concatenate([
        own_mp[None].astype(jnp.int32),
        own_node[None].astype(jnp.int32),
        enc_list.reshape(-1) - (own_node - REACH) * 8,
        proc_list.reshape(-1) - (own_node - REACH) * 2,
        dec_list.reshape(-1) - (own_node - REACH) * 2,
    ])
    gains = norm_gains.reshape(6, MP, 256)

    def gathered(part, name):
        pieces = [part, None, None, None]
        for k in (1, 3, 2):
            pieces[k] = shift_mp(part if name != "w" else part[k], k)
        return pieces

    def window(part):
        pieces = []
        for d in range(-REACH, REACH + 1):
            pieces.append(from_node(part, d) if d else part)
        return pieces

    grid_pieces = gathered(grid_in, "g")
    mesh_pieces = gathered(mesh_in, "m")

    w_groups = w_out.reshape(4, 128, MP, 256).transpose(0, 2, 1, 3)
    own_half = lax.dynamic_slice_in_dim(w_groups[:3], core * 2, 2, axis=1)
    sent = [None] * MP
    for k in (1, 2, 3):
        last = lax.dynamic_index_in_dim(w_groups[3], (own_mp + k) % MP, 0, keepdims=True)
        sent[k] = jnp.concatenate([own_half.reshape(6, 128, 256), last], axis=0)
    sent[0] = sent[1]
    arrived = gathered(sent, "w")[1:]

    kv, grid_q = grid_project(meta, grid_pieces, gains, w_key[0], w_value[0], w_query[3])
    grid_windows = window(kv)
    state, mesh_q = mesh_start(meta, mesh_pieces, gains, w_query[0])
    o = enc_attend(meta, enc_list, grid_count, mesh_q, grid_windows)

    arrived = lax.optimization_barrier((*arrived, o))[:3]
    other = swap_cores(jnp.stack([a[:6] for a in arrived]))
    w_last = jnp.concatenate(
        [lax.dynamic_index_in_dim(w_groups[3], own_mp, 0, keepdims=True)] + [a[6:] for a in arrived], axis=0
    ).reshape(512, 256)

    for index in range(3):
        heads = gather_heads(o)
        projections = [w_key[index + 1], w_value[index + 1]] + ([w_query[index + 1]] if index < 2 else [])
        made = layer(
            index, index + 2 if index < 2 else 5, index < 2, meta, heads, state, w_groups[:3], arrived, other, gains, projections
        )
        state, kv = made[0], made[1]
        near = window(kv)
        if index < 2:
            o = near_attend(PROC0, 3, meta, made[2], near)
    o = near_attend(DEC0, 2, meta, grid_q, near)
    heads = gather_heads(o)
    grid_out = final(meta, grid_count, heads, w_last, grid_in)
    mesh_out = lax.dynamic_index_in_dim(state, own_mp, 0, keepdims=False)
    return grid_out, mesh_out


def solution(mesh):
    placed = (
        P("nodes", "mp"),
        P("nodes", "mp"),
        P(None, None, "mp"),
        P(None, None, "mp"),
        P(None, None, "mp"),
        P(None, "mp", None),
        P(),
        P("nodes", None),
        P("nodes", None),
        P("nodes", None),
        P(),
    )
    return jax.shard_map(
        program,
        mesh=mesh,
        in_specs=placed,
        out_specs=(P("nodes", "mp"), P("nodes", "mp")),
        check_vma=False,
    )
```

time: 332 us -> 221 us (0.67)
  the two profiles are of different devices: /device:TPU:1 before, /device:TPU:70 now
where the time goes in v1:
time: 221 us; the launch traced here: 219 us
  starting transfers between devices  84.1 us (38%)
  waiting for transfers between devices  59.8 us (27%)
  blocking collectives  29.2 us (13%)
  Pallas kernels  22.4 us (10%)
  local copies, waits for them, and re-layouts  20.3 us (9%)
  other arithmetic  2.31 us (1%)
    ppermute x16, starting transfers between devices, from_node(): return lax.ppermute(value, 'nodes', pairs)  46.6 us
    ppermute x9, starting transfers between devices, shift_mp(): return lax.ppermute(value, 'mp', [(s, (s + steps) % MP) for s in range(MP)])  32 us
    all_to_all x3, blocking collectives, gather_heads(): return lax.all_to_all(copies, 'mp', split_axis=0, concat_axis=0, tiled=True)  29.2 us
    ppermute x16, waiting for transfers between devices, from_node(): return lax.ppermute(value, 'nodes', pairs)  27.9 us
    ppermute x9, waiting for transfers between devices, shift_mp(): return lax.ppermute(value, 'mp', [(s, (s + steps) % MP) for s in range(MP)])  18.5 us
    all_to_all x1, waiting for transfers between devices, gather_heads(): return lax.all_to_all(copies, 'mp', split_axis=0, concat_axis=0, tiled=True)  13.4 us
    unnamed x53, local copies, waits for them, and re-layouts  9.04 us
    pallas_call x3, Pallas kernels, near_attend(): pl.pallas_call(body, in_specs=[smem()] + [vmem()] * 6, out_specs=vmem(),...  6.28 us
  transfers between devices with their start and end apart: 27, of which 11 were waited for; matrix products, arithmetic and copies ran while one was open for 7% of the time, Pallas kernels for 2%

profile of v1, /device:TPU:70, one launch (start us, length us, event | category | flops | bytes accessed | tf_op | source)
XLA Modules:
  0.0 219.4 jit_solution(14684154570581939896)
XLA Ops:
  0.6 3.5 %collective-permute-start = (bf16[1024,256]{1,0:T(8,128)(2,1)}, bf16[1024,256]{1,0:T(8,128)(2,1)S(1)}, u32[]{:S(2)}, u32[]{:S(2)}) collective-permute-start(bf16[1024,256]{1,0:T(8,128)(2,1)} %grid_in.1), channel_id=1, source_target_pairs={{0,1},{1,2},{2,3},{3,0},{4,5},{5,6},{6,7},{7,4},{8,9},{9,10},{10,1... | collective-permute-start | bytes 1572872 | tf_op jit(solution)/shard_map/ppermute | solution.py:23
  4.1 4.8 %collective-permute-start.1 = (bf16[1024,256]{1,0:T(8,128)(2,1)}, bf16[1024,256]{1,0:T(8,128)(2,1)S(1)}, u32[]{:S(2)}, u32[]{:S(2)}) collective-permute-start(bf16[1024,256]{1,0:T(8,128)(2,1)} %grid_in.1), channel_id=1, source_target_pairs={{0,2},{1,3},{2,0},{3,1},{4,6},{5,7},{6,4},{7,5},{8,10},{9,11},{10,... | collective-permute-start | bytes 1572872 | tf_op jit(solution)/shard_map/ppermute | solution.py:23
  8.9 3.3 %collective-permute-start.2 = (bf16[1024,256]{1,0:T(8,128)(2,1)}, bf16[1024,256]{1,0:T(8,128)(2,1)S(1)}, u32[]{:S(2)}, u32[]{:S(2)}) collective-permute-start(bf16[1024,256]{1,0:T(8,128)(2,1)} %grid_in.1), channel_id=1, source_target_pairs={{0,3},{1,0},{2,1},{3,2},{4,7},{5,4},{6,5},{7,6},{8,11},{9,8},{10,9... | collective-permute-start | bytes 1572872 | tf_op jit(solution)/shard_map/ppermute | solution.py:23
  15.5 2.3 %slice_bitcast_fusion.5 = (bf16[1024,128]{1,0:T(8,128)(2,1)}, bf16[1024,128]{1,0:T(8,128)(2,1)}, bf16[1024,128]{1,0:T(8,128)(2,1)S(1)}, bf16[1024,128]{1,0:T(8,128)(2,1)}) fusion(bf16[4,1024,128]{2,1,0:T(8,128)(2,1)} %param.13), kind=kLoop, calls=%fused_computation.10 | loop fusion | bytes 2097152 | tf_op jit(solution)/shard_map/squeeze | solution.py:351
  18.6 11.5 %collective-permute-done.1.x2 = bf16[1024,256]{1,0:T(8,128)(2,1)S(1)} collective-permute-done((bf16[1024,256]{1,0:T(8,128)(2,1)}, bf16[1024,256]{1,0:T(8,128)(2,1)S(1)}, u32[]{:S(2)}, u32[]{:S(2)}) %collective-permute-start.1) | collective-permute-done | bytes 524320 | tf_op jit(solution)/shard_map/ppermute | solution.py:23
  31.5 4.3 %grid_project.1 = (bf16[1024,256]{1,0:T(8,128)(2,1)}, bf16[1024,128]{1,0:T(8,128)(2,1)S(1)}) custom-call(s32[32]{0:T(128)S(1)} %concatenate.15.meta.refs_0_, bf16[1024,256]{1,0:T(8,128)(2,1)S(1)} %copy-done.4, bf16[1024,256]{1,0:T(8,128)(2,1)S(1)} %collective-permute-done.x1, bf16[1024,256]{1,0:T(8,128)(2,1)S(1)} %collective-permute-done.1.x2, ...), custom_call_target="tpu_custom_call" | custom-call | flops 805306368 | bytes 4194304 | tf_op jit(solution)/shard_map/grid_project/pallas_call | solution.py:82
  36.5 3.7 %collective-permute-start.6 = (bf16[1024,256]{1,0:T(8,128)(2,1)}, bf16[1024,256]{1,0:T(8,128)(2,1)S(1)}, u32[]{:S(2)}, u32[]{:S(2)}) collective-permute-start(bf16[1024,256]{1,0:T(8,128)(2,1)} %get-tuple-element.19.rest_2_), channel_id=1, source_target_pairs={{0,8},{4,12},{8,16},{12,20},{16,24},{20,28},{24,32},{28,36},{32,40... | collective-permute-start | bytes 1572872 | tf_op jit(solution)/shard_map/ppermute | solution.py:29
  40.2 1.9 collective-permute-start.7
  42.1 4.4 %collective-permute-start.3 = (bf16[256,256]{1,0:T(8,128)(2,1)S(1)}, bf16[256,256]{1,0:T(8,128)(2,1)S(1)}, u32[]{:S(2)}, u32[]{:S(2)}) collective-permute-start(bf16[256,256]{1,0:T(8,128)(2,1)S(1)} %copy-done.10), channel_id=1, source_target_pairs={{0,1},{1,2},{2,3},{3,0},{4,5},{5,6},{6,7},{7,4},{8,9},{9,10},{10,1... | collective-permute-start | bytes 393224 | tf_op jit(solution)/shard_map/ppermute | solution.py:23
  46.5 3.5 %collective-permute-start.4 = (bf16[256,256]{1,0:T(8,128)(2,1)S(1)}, bf16[256,256]{1,0:T(8,128)(2,1)S(1)}, u32[]{:S(2)}, u32[]{:S(2)}) collective-permute-start(bf16[256,256]{1,0:T(8,128)(2,1)S(1)} %copy-done.10), channel_id=1, source_target_pairs={{0,2},{1,3},{2,0},{3,1},{4,6},{5,7},{6,4},{7,5},{8,10},{9,11},{10,... | collective-permute-start | bytes 393224 | tf_op jit(solution)/shard_map/ppermute | solution.py:23
  50.1 3.6 %collective-permute-start.5 = (bf16[256,256]{1,0:T(8,128)(2,1)S(1)}, bf16[256,256]{1,0:T(8,128)(2,1)S(1)}, u32[]{:S(2)}, u32[]{:S(2)}) collective-permute-start(bf16[256,256]{1,0:T(8,128)(2,1)S(1)} %copy-done.10), channel_id=1, source_target_pairs={{0,3},{1,0},{2,1},{3,2},{4,7},{5,4},{6,5},{7,6},{8,11},{9,8},{10,9... | collective-permute-start | bytes 393224 | tf_op jit(solution)/shard_map/ppermute | solution.py:23
  53.7 2.3 %copy.15 = bf16[4,128,1024]{1,2,0:T(8,128)(2,1)} copy(bf16[4,128,1024]{2,1,0:T(8,128)(2,1)} %param.16) | data formatting | bytes 2097152 | tf_op args[5]
  56.0 2.3 %copy.16 = bf16[4,128,4,256]{3,1,2,0:T(8,128)(2,1)} copy(bf16[4,128,4,256]{1,3,2,0:T(8,128)(2,1)} %bitcast.49) | data formatting | bytes 2097152 | tf_op jit(solution)/shard_map/reshape | solution.py:329
  61.3 2.9 %collective-permute-start.8 = (bf16[1024,256]{1,0:T(8,128)(2,1)}, bf16[1024,256]{1,0:T(8,128)(2,1)S(1)}, u32[]{:S(2)}, u32[]{:S(2)}) collective-permute-start(bf16[1024,256]{1,0:T(8,128)(2,1)} %get-tuple-element.19.rest_2_), channel_id=1, source_target_pairs={{4,0},{8,4},{12,8},{16,12},{20,16},{24,20},{28,24},{32,28},{36,32}... | collective-permute-start | bytes 1572872 | tf_op jit(solution)/shard_map/ppermute | solution.py:29
  64.2 2.1 collective-permute-start.9
  67.2 2.3 %collective-permute-start.10 = (bf16[7,128,256]{2,1,0:T(8,128)(2,1)S(1)}, bf16[7,128,256]{2,1,0:T(8,128)(2,1)S(1)}, u32[]{:S(2)}, u32[]{:S(2)}) collective-permute-start(bf16[7,128,256]{2,1,0:T(8,128)(2,1)S(1)} %get-tuple-element.46), channel_id=1, source_target_pairs={{0,1},{1,2},{2,3},{3,0},{4,5},{5,6},{6,7},{7,4},{8,9},{9,10},{10,1... | collective-permute-start | bytes 1376264 | tf_op jit(solution)/shard_map/ppermute | solution.py:23
  70.2 3.8 %collective-permute-start.11 = (bf16[7,128,256]{2,1,0:T(8,128)(2,1)S(1)}, bf16[7,128,256]{2,1,0:T(8,128)(2,1)S(1)}, u32[]{:S(2)}, u32[]{:S(2)}) collective-permute-start(bf16[7,128,256]{2,1,0:T(8,128)(2,1)S(1)} %get-tuple-element.45), channel_id=1, source_target_pairs={{0,2},{1,3},{2,0},{3,1},{4,6},{5,7},{6,4},{7,5},{8,10},{9,11},{10,... | collective-permute-start | bytes 1376264 | tf_op jit(solution)/shard_map/ppermute | solution.py:23
  74.1 2.9 %collective-permute-start.12 = (bf16[7,128,256]{2,1,0:T(8,128)(2,1)S(1)}, bf16[7,128,256]{2,1,0:T(8,128)(2,1)S(1)}, u32[]{:S(2)}, u32[]{:S(2)}) collective-permute-start(bf16[7,128,256]{2,1,0:T(8,128)(2,1)S(1)} %get-tuple-element.44), channel_id=1, source_target_pairs={{0,3},{1,0},{2,1},{3,2},{4,7},{5,4},{6,5},{7,6},{8,11},{9,8},{10,9... | collective-permute-start | bytes 1376264 | tf_op jit(solution)/shard_map/ppermute | solution.py:23
  80.9 5.5 %collective-permute-done.9.rest_4_ = bf16[1024,256]{1,0:T(8,128)(2,1)S(1)} collective-permute-done((bf16[1024,256]{1,0:T(8,128)(2,1)}, bf16[1024,256]{1,0:T(8,128)(2,1)S(1)}, u32[]{:S(2)}, u32[]{:S(2)}) %collective-permute-start.9) | collective-permute-done | bytes 524320 | tf_op jit(solution)/shard_map/ppermute | solution.py:29
  87.4 2.7 %enc_attend.1 = bf16[4,256,128]{2,1,0:T(8,128)(2,1)S(1)} custom-call(s32[32]{0:T(128)S(1)} %concatenate.15.meta.refs_0_, s32[2,4]{1,0:T(2,128)S(1)} %copy-done.20, s32[1024]{0:T(1024)S(1)} %copy-done.19, bf16[256,128]{1,0:T(8,128)(2,1)S(1)} %get-tuple-element.18.q, bf16[1024,256]{1,0:T(8,128)(2,1)S(1)} %copy-done.7, ...), custom_call_target="tpu_custom_call" | custom-call | tf_op jit(solution)/shard_map/enc_attend/pallas_call | solution.py:179
  90.1 2.3 %collective-permute-done.10.refs_4_ = bf16[7,128,256]{2,1,0:T(8,128)(2,1)S(1)} collective-permute-done((bf16[7,128,256]{2,1,0:T(8,128)(2,1)S(1)}, bf16[7,128,256]{2,1,0:T(8,128)(2,1)S(1)}, u32[]{:S(2)}, u32[]{:S(2)}) %collective-permute-start.10) | collective-permute-done | bytes 458784 | tf_op jit(solution)/shard_map/ppermute | solution.py:23
  92.5 3.3 %collective-permute-done.12.refs_6_ = bf16[7,128,256]{2,1,0:T(8,128)(2,1)S(1)} collective-permute-done((bf16[7,128,256]{2,1,0:T(8,128)(2,1)S(1)}, bf16[7,128,256]{2,1,0:T(8,128)(2,1)S(1)}, u32[]{:S(2)}, u32[]{:S(2)}) %collective-permute-start.12) | collective-permute-done | bytes 458784 | tf_op jit(solution)/shard_map/ppermute | solution.py:23
  96.1 1.9 collective-permute-start.13
  98.0 11.0 %all_to_all.20.refs_1_ = bf16[4,256,128]{2,1,0:T(8,128)(2,1)S(1)} all-to-all(bf16[4,256,128]{2,1,0:T(8,128)(2,1)S(1)} %enc_attend.1), channel_id=1, replica_groups=mesh['nodes'=128,'mp'=4] {'mp'}, dimensions={0} | all-to-all | bytes 524288 | tf_op jit(solution)/shard_map/all_to_all | solution.py:296
  110.8 5.6 %collective-permute-start.14 = (bf16[256,256]{1,0:T(8,128)(2,1)S(1)}, bf16[256,256]{1,0:T(8,128)(2,1)S(1)}, u32[]{:S(2)}, u32[]{:S(2)}) collective-permute-start(bf16[256,256]{1,0:T(8,128)(2,1)S(1)} %get-tuple-element.25.refs_4_), channel_id=1, source_target_pairs={{0,8},{4,12},{8,16},{12,20},{16,24},{20,28},{24,32},{28,36},{32,40... | collective-permute-start | bytes 393224 | tf_op jit(solution)/shard_map/ppermute | solution.py:29
  116.4 1.9 collective-permute-start.15
  118.4 3.6 %collective-permute-start.16 = (bf16[256,256]{1,0:T(8,128)(2,1)S(1)}, bf16[256,256]{1,0:T(8,128)(2,1)S(1)}, u32[]{:S(2)}, u32[]{:S(2)}) collective-permute-start(bf16[256,256]{1,0:T(8,128)(2,1)S(1)} %get-tuple-element.25.refs_4_), channel_id=1, source_target_pairs={{4,0},{8,4},{12,8},{16,12},{20,16},{24,20},{28,24},{32,28},{36,32}... | collective-permute-start | bytes 393224 | tf_op jit(solution)/shard_map/ppermute | solution.py:29
  122.0 1.9 collective-permute-start.17
  124.5 6.5 %collective-permute-done.17.refs_6_ = bf16[256,256]{1,0:T(8,128)(2,1)S(1)} collective-permute-done((bf16[256,256]{1,0:T(8,128)(2,1)S(1)}, bf16[256,256]{1,0:T(8,128)(2,1)S(1)}, u32[]{:S(2)}, u32[]{:S(2)}) %collective-permute-start.17) | collective-permute-done | bytes 131104 | tf_op jit(solution)/shard_map/ppermute | solution.py:29
  131.0 1.8 near_attend.3
  132.7 9.1 %all_to_all.21.refs_1_ = bf16[4,256,128]{2,1,0:T(8,128)(2,1)S(1)} all-to-all(bf16[4,256,128]{2,1,0:T(8,128)(2,1)S(1)} %near_attend.3), channel_id=1, replica_groups=mesh['nodes'=128,'mp'=4] {'mp'}, dimensions={0} | all-to-all | bytes 524288 | tf_op jit(solution)/shard_map/all_to_all | solution.py:296
  143.6 1.9 collective-permute-start.18
  145.5 1.9 collective-permute-start.19
  147.4 3.6 %collective-permute-start.20 = (bf16[256,256]{1,0:T(8,128)(2,1)S(1)}, bf16[256,256]{1,0:T(8,128)(2,1)S(1)}, u32[]{:S(2)}, u32[]{:S(2)}) collective-permute-start(bf16[256,256]{1,0:T(8,128)(2,1)S(1)} %get-tuple-element.28.refs_4_), channel_id=1, source_target_pairs={{4,0},{8,4},{12,8},{16,12},{20,16},{24,20},{28,24},{32,28},{36,32}... | collective-permute-start | bytes 393224 | tf_op jit(solution)/shard_map/ppermute | solution.py:29
  151.1 3.9 %collective-permute-start.21 = (bf16[256,256]{1,0:T(8,128)(2,1)S(1)}, bf16[256,256]{1,0:T(8,128)(2,1)S(1)}, u32[]{:S(2)}, u32[]{:S(2)}) collective-permute-start(bf16[256,256]{1,0:T(8,128)(2,1)S(1)} %get-tuple-element.28.refs_4_), channel_id=1, source_target_pairs={{8,0},{12,4},{16,8},{20,12},{24,16},{28,20},{32,24},{36,28},{40,32... | collective-permute-start | bytes 393224 | tf_op jit(solution)/shard_map/ppermute | solution.py:29
  155.0 5.2 %collective-permute-done.21.refs_6_ = bf16[256,256]{1,0:T(8,128)(2,1)S(1)} collective-permute-done((bf16[256,256]{1,0:T(8,128)(2,1)S(1)}, bf16[256,256]{1,0:T(8,128)(2,1)S(1)}, u32[]{:S(2)}, u32[]{:S(2)}) %collective-permute-start.21) | collective-permute-done | bytes 131104 | tf_op jit(solution)/shard_map/ppermute | solution.py:29
  160.2 1.8 near_attend.4
  162.0 9.1 %all_to_all.22.refs_1_ = bf16[4,256,128]{2,1,0:T(8,128)(2,1)S(1)} all-to-all(bf16[4,256,128]{2,1,0:T(8,128)(2,1)S(1)} %near_attend.4), channel_id=1, replica_groups=mesh['nodes'=128,'mp'=4] {'mp'}, dimensions={0} | all-to-all | bytes 524288 | tf_op jit(solution)/shard_map/all_to_all | solution.py:296
  171.0 1.8 mesh_layer.5
  173.7 3.2 %collective-permute-start.22 = (bf16[256,256]{1,0:T(8,128)(2,1)S(1)}, bf16[256,256]{1,0:T(8,128)(2,1)S(1)}, u32[]{:S(2)}, u32[]{:S(2)}) collective-permute-start(bf16[256,256]{1,0:T(8,128)(2,1)S(1)} %get-tuple-element.30.refs_4_), channel_id=1, source_target_pairs={{0,8},{4,12},{8,16},{12,20},{16,24},{20,28},{24,32},{28,36},{32,40... | collective-permute-start | bytes 393224 | tf_op jit(solution)/shard_map/ppermute | solution.py:29
  176.9 2.4 %collective-permute-start.23 = (bf16[256,256]{1,0:T(8,128)(2,1)S(1)}, bf16[256,256]{1,0:T(8,128)(2,1)S(1)}, u32[]{:S(2)}, u32[]{:S(2)}) collective-permute-start(bf16[256,256]{1,0:T(8,128)(2,1)S(1)} %get-tuple-element.30.refs_4_), channel_id=1, source_target_pairs={{0,4},{4,8},{8,12},{12,16},{16,20},{20,24},{24,28},{28,32},{32,36}... | collective-permute-start | bytes 393224 | tf_op jit(solution)/shard_map/ppermute | solution.py:29
  179.3 3.1 %collective-permute-start.24 = (bf16[256,256]{1,0:T(8,128)(2,1)S(1)}, bf16[256,256]{1,0:T(8,128)(2,1)S(1)}, u32[]{:S(2)}, u32[]{:S(2)}) collective-permute-start(bf16[256,256]{1,0:T(8,128)(2,1)S(1)} %get-tuple-element.30.refs_4_), channel_id=1, source_target_pairs={{4,0},{8,4},{12,8},{16,12},{20,16},{24,20},{28,24},{32,28},{36,32}... | collective-permute-start | bytes 393224 | tf_op jit(solution)/shard_map/ppermute | solution.py:29
  182.5 2.6 %collective-permute-start.25 = (bf16[256,256]{1,0:T(8,128)(2,1)S(1)}, bf16[256,256]{1,0:T(8,128)(2,1)S(1)}, u32[]{:S(2)}, u32[]{:S(2)}) collective-permute-start(bf16[256,256]{1,0:T(8,128)(2,1)S(1)} %get-tuple-element.30.refs_4_), channel_id=1, source_target_pairs={{8,0},{12,4},{16,8},{20,12},{24,16},{28,20},{32,24},{36,28},{40,32... | collective-permute-start | bytes 393224 | tf_op jit(solution)/shard_map/ppermute | solution.py:29
  186.6 8.6 %collective-permute-done.25.refs_6_ = bf16[256,256]{1,0:T(8,128)(2,1)S(1)} collective-permute-done((bf16[256,256]{1,0:T(8,128)(2,1)S(1)}, bf16[256,256]{1,0:T(8,128)(2,1)S(1)}, u32[]{:S(2)}, u32[]{:S(2)}) %collective-permute-start.25) | collective-permute-done | bytes 131104 | tf_op jit(solution)/shard_map/ppermute | solution.py:29
  195.2 2.8 %near_attend.5 = bf16[4,1024,128]{2,1,0:T(8,128)(2,1)} custom-call(s32[32]{0:T(128)S(1)} %concatenate.15.meta.refs_0_, bf16[1024,128]{1,0:T(8,128)(2,1)S(1)} %copy-done.9, bf16[256,256]{1,0:T(8,128)(2,1)S(1)} %collective-permute-done.22.refs_2_, bf16[256,256]{1,0:T(8,128)(2,1)S(1)} %collective-permute-done.23.refs_3_, ...), custom_call_target="tpu_custom_call" | custom-call | tf_op jit(solution)/shard_map/near_attend/pallas_call | solution.py:207
  198.0 3.6 %all-to-all-start.3 = ((bf16[4,1024,128]{2,1,0:T(8,128)(2,1)}), bf16[4,1024,128]{2,1,0:T(8,128)(2,1)S(1)}, u32[]{:S(2)}, u32[]{:S(2)}) async-start(bf16[4,1024,128]{2,1,0:T(8,128)(2,1)} %near_attend.5), calls=%async_computation.3 | async-start | bytes 2097152 | tf_op jit(solution)/shard_map/all_to_all | solution.py:296
  203.3 13.4 %all-to-all-done.3.o = bf16[4,1024,128]{2,1,0:T(8,128)(2,1)S(1)} async-done(((bf16[4,1024,128]{2,1,0:T(8,128)(2,1)}), bf16[4,1024,128]{2,1,0:T(8,128)(2,1)S(1)}, u32[]{:S(2)}, u32[]{:S(2)}) %all-to-all-start.3) | async-done | bytes 1048608 | tf_op jit(solution)/shard_map/all_to_all | solution.py:296
  216.7 2.7 %grid_final.1 = bf16[1024,256]{1,0:T(8,128)(2,1)} custom-call(s32[32]{0:T(128)S(1)} %concatenate.15.meta.refs_0_, s32[1024]{0:T(1024)S(1)} %copy-done.19, bf16[4,1024,128]{2,1,0:T(8,128)(2,1)S(1)} %all-to-all-done.3.o, bf16[512,256]{1,0:T(8,128)(2,1)S(1)} %bitcast.46, bf16[1024,256]{1,0:T(8,128)(2,1)S(1)} %copy-done.5), custom_call_target="tpu_custom_call" | custom-call | tf_op jit(solution)/shard_map/grid_final/pallas_call | solution.py:278
  (98 shorter events, 23.7 us)
Async XLA Ops:
  0.6 18.0 %collective-permute-start = (bf16[1024,256]{1,0:T(8,128)(2,1)}, bf16[1024,256]{1,0:T(8,128)(2,1)S(1)}, u32[]{:S(2)}, u32[]{:S(2)}) collective-permute-start(bf16[1024,256]{1,0:T(8,128)(2,1)} %grid_in.1), channel_id=1, source_target_pairs={{0,1},{1,2},{2,3},{3,0},{4,5},{5,6},{6,7},{7,4},{8,9},{9,10},{10,1... | collective-permute-start | bytes 1572872 | tf_op jit(solution)/shard_map/ppermute | solution.py:23
  4.1 26.0 %collective-permute-start.1 = (bf16[1024,256]{1,0:T(8,128)(2,1)}, bf16[1024,256]{1,0:T(8,128)(2,1)S(1)}, u32[]{:S(2)}, u32[]{:S(2)}) collective-permute-start(bf16[1024,256]{1,0:T(8,128)(2,1)} %grid_in.1), channel_id=1, source_target_pairs={{0,2},{1,3},{2,0},{3,1},{4,6},{5,7},{6,4},{7,5},{8,10},{9,11},{10,... | collective-permute-start | bytes 1572872 | tf_op jit(solution)/shard_map/ppermute | solution.py:23
  8.9 22.5 %collective-permute-start.2 = (bf16[1024,256]{1,0:T(8,128)(2,1)}, bf16[1024,256]{1,0:T(8,128)(2,1)S(1)}, u32[]{:S(2)}, u32[]{:S(2)}) collective-permute-start(bf16[1024,256]{1,0:T(8,128)(2,1)} %grid_in.1), channel_id=1, source_target_pairs={{0,3},{1,0},{2,1},{3,2},{4,7},{5,4},{6,5},{7,6},{8,11},{9,8},{10,9... | collective-permute-start | bytes 1572872 | tf_op jit(solution)/shard_map/ppermute | solution.py:23
  15.5 2.3 %copy-start.21 = (bf16[4,1024,128]{2,1,0:T(8,128)(2,1)S(1)}, bf16[4,1024,128]{2,1,0:T(8,128)(2,1)}, u32[]{:S(2)}) copy-start(bf16[4,1024,128]{2,1,0:T(8,128)(2,1)} %param.15) | copy-start | bytes 3145732
  15.5 2.3 %copy-start.22 = (bf16[4,1024,128]{2,1,0:T(8,128)(2,1)S(1)}, bf16[4,1024,128]{2,1,0:T(8,128)(2,1)}, u32[]{:S(2)}) copy-start(bf16[4,1024,128]{2,1,0:T(8,128)(2,1)} %param.14) | copy-start | bytes 3145732
  17.8 13.7 %copy-start.4 = (bf16[1024,256]{1,0:T(8,128)(2,1)S(1)}, bf16[1024,256]{1,0:T(8,128)(2,1)}, u32[]{:S(2)}) copy-start(bf16[1024,256]{1,0:T(8,128)(2,1)} %grid_in.1) | copy-start | bytes 1572868
  31.5 10.7 %copy-start.10 = (bf16[256,256]{1,0:T(8,128)(2,1)S(1)}, bf16[256,256]{1,0:T(8,128)(2,1)}, u32[]{:S(2)}) copy-start(bf16[256,256]{1,0:T(8,128)(2,1)} %x0.3) | copy-start | bytes 393220
  36.5 33.0 %collective-permute-start.6 = (bf16[1024,256]{1,0:T(8,128)(2,1)}, bf16[1024,256]{1,0:T(8,128)(2,1)S(1)}, u32[]{:S(2)}, u32[]{:S(2)}) collective-permute-start(bf16[1024,256]{1,0:T(8,128)(2,1)} %get-tuple-element.19.rest_2_), channel_id=1, source_target_pairs={{0,8},{4,12},{8,16},{12,20},{16,24},{20,28},{24,32},{28,36},{32,40... | collective-permute-start | bytes 1572872 | tf_op jit(solution)/shard_map/ppermute | solution.py:29
  40.2 33.9 %collective-permute-start.7 = (bf16[1024,256]{1,0:T(8,128)(2,1)}, bf16[1024,256]{1,0:T(8,128)(2,1)}, u32[]{:S(2)}, u32[]{:S(2)}) collective-permute-start(bf16[1024,256]{1,0:T(8,128)(2,1)} %get-tuple-element.19.rest_2_), channel_id=1, source_target_pairs={{0,4},{4,8},{8,12},{12,16},{16,20},{20,24},{24,28},{28,32},{32,36}... | collective-permute-start | bytes 1572872 | tf_op jit(solution)/shard_map/ppermute | solution.py:29
  42.1 19.1 %collective-permute-start.3 = (bf16[256,256]{1,0:T(8,128)(2,1)S(1)}, bf16[256,256]{1,0:T(8,128)(2,1)S(1)}, u32[]{:S(2)}, u32[]{:S(2)}) collective-permute-start(bf16[256,256]{1,0:T(8,128)(2,1)S(1)} %copy-done.10), channel_id=1, source_target_pairs={{0,1},{1,2},{2,3},{3,0},{4,5},{5,6},{6,7},{7,4},{8,9},{9,10},{10,1... | collective-permute-start | bytes 393224 | tf_op jit(solution)/shard_map/ppermute | solution.py:23
  46.5 17.7 %collective-permute-start.4 = (bf16[256,256]{1,0:T(8,128)(2,1)S(1)}, bf16[256,256]{1,0:T(8,128)(2,1)S(1)}, u32[]{:S(2)}, u32[]{:S(2)}) collective-permute-start(bf16[256,256]{1,0:T(8,128)(2,1)S(1)} %copy-done.10), channel_id=1, source_target_pairs={{0,2},{1,3},{2,0},{3,1},{4,6},{5,7},{6,4},{7,5},{8,10},{9,11},{10,... | collective-permute-start | bytes 393224 | tf_op jit(solution)/shard_map/ppermute | solution.py:23
  50.1 16.4 %collective-permute-start.5 = (bf16[256,256]{1,0:T(8,128)(2,1)S(1)}, bf16[256,256]{1,0:T(8,128)(2,1)S(1)}, u32[]{:S(2)}, u32[]{:S(2)}) collective-permute-start(bf16[256,256]{1,0:T(8,128)(2,1)S(1)} %copy-done.10), channel_id=1, source_target_pairs={{0,3},{1,0},{2,1},{3,2},{4,7},{5,4},{6,5},{7,6},{8,11},{9,8},{10,9... | collective-permute-start | bytes 393224 | tf_op jit(solution)/shard_map/ppermute | solution.py:23
  60.0 6.4 %copy-start.23 = (bf16[1,128,256]{2,1,0:T(8,128)(2,1)S(1)}, bf16[1,128,256]{2,1,0:T(8,128)(2,1)}, u32[]{:S(2)}) copy-start(bf16[1,128,256]{2,1,0:T(8,128)(2,1)} %get-tuple-element.49) | copy-start | bytes 196612
  60.0 6.4 %copy-start.24 = (bf16[1,128,256]{2,1,0:T(8,128)(2,1)S(1)}, bf16[1,128,256]{2,1,0:T(8,128)(2,1)}, u32[]{:S(2)}) copy-start(bf16[1,128,256]{2,1,0:T(8,128)(2,1)} %get-tuple-element.50) | copy-start | bytes 196612
  61.2 15.7 %copy-start.3 = (bf16[1024,128]{1,0:T(8,128)(2,1)S(1)}, bf16[1024,128]{1,0:T(8,128)(2,1)}, u32[]{:S(2)}) copy-start(bf16[1024,128]{1,0:T(8,128)(2,1)} %get-tuple-element.41.w_q) | copy-start | bytes 786436
  61.3 15.7 %copy-start.11 = (bf16[256,256]{1,0:T(8,128)(2,1)S(1)}, bf16[256,256]{1,0:T(8,128)(2,1)}, u32[]{:S(2)}) copy-start(bf16[256,256]{1,0:T(8,128)(2,1)} %x0.3) | copy-start | bytes 393220
  61.3 12.8 %copy-start.12 = (bf16[256,256]{1,0:T(8,128)(2,1)}, bf16[256,256]{1,0:T(8,128)(2,1)S(1)}, u32[]{:S(2)}) copy-start(bf16[256,256]{1,0:T(8,128)(2,1)S(1)} %collective-permute-done.3.x1) | copy-start | bytes 393220
  61.3 19.6 %collective-permute-start.8 = (bf16[1024,256]{1,0:T(8,128)(2,1)}, bf16[1024,256]{1,0:T(8,128)(2,1)S(1)}, u32[]{:S(2)}, u32[]{:S(2)}) collective-permute-start(bf16[1024,256]{1,0:T(8,128)(2,1)} %get-tuple-element.19.rest_2_), channel_id=1, source_target_pairs={{4,0},{8,4},{12,8},{16,12},{20,16},{24,20},{28,24},{32,28},{36,32}... | collective-permute-start | bytes 1572872 | tf_op jit(solution)/shard_map/ppermute | solution.py:29
  64.2 9.8 %copy-start.14 = (bf16[256,256]{1,0:T(8,128)(2,1)}, bf16[256,256]{1,0:T(8,128)(2,1)S(1)}, u32[]{:S(2)}) copy-start(bf16[256,256]{1,0:T(8,128)(2,1)S(1)} %collective-permute-done.4.x2) | copy-start | bytes 393220
  64.2 22.1 %collective-permute-start.9 = (bf16[1024,256]{1,0:T(8,128)(2,1)}, bf16[1024,256]{1,0:T(8,128)(2,1)S(1)}, u32[]{:S(2)}, u32[]{:S(2)}) collective-permute-start(bf16[1024,256]{1,0:T(8,128)(2,1)} %get-tuple-element.19.rest_2_), channel_id=1, source_target_pairs={{8,0},{12,4},{16,8},{20,12},{24,16},{28,20},{32,24},{36,28},{40,32... | collective-permute-start | bytes 1572872 | tf_op jit(solution)/shard_map/ppermute | solution.py:29
  66.4 20.0 %copy-start.19 = (s32[1024]{0:T(1024)S(1)}, s32[1024]{0:T(1024)}, u32[]{:S(2)}) copy-start(s32[1024]{0:T(1024)} %counts.3) | copy-start | bytes 12292
  66.4 20.0 %copy-start.20 = (s32[2,4]{1,0:T(2,128)S(1)}, s32[2,4]{1,0:T(2,128)}, u32[]{:S(2)}) copy-start(s32[2,4]{1,0:T(2,128)} %listed.1) | copy-start | bytes 100
  67.2 25.3 %collective-permute-start.10 = (bf16[7,128,256]{2,1,0:T(8,128)(2,1)S(1)}, bf16[7,128,256]{2,1,0:T(8,128)(2,1)S(1)}, u32[]{:S(2)}, u32[]{:S(2)}) collective-permute-start(bf16[7,128,256]{2,1,0:T(8,128)(2,1)S(1)} %get-tuple-element.46), channel_id=1, source_target_pairs={{0,1},{1,2},{2,3},{3,0},{4,5},{5,6},{6,7},{7,4},{8,9},{9,10},{10,1... | collective-permute-start | bytes 1376264 | tf_op jit(solution)/shard_map/ppermute | solution.py:23
  70.2 22.2 %collective-permute-start.11 = (bf16[7,128,256]{2,1,0:T(8,128)(2,1)S(1)}, bf16[7,128,256]{2,1,0:T(8,128)(2,1)S(1)}, u32[]{:S(2)}, u32[]{:S(2)}) collective-permute-start(bf16[7,128,256]{2,1,0:T(8,128)(2,1)S(1)} %get-tuple-element.45), channel_id=1, source_target_pairs={{0,2},{1,3},{2,0},{3,1},{4,6},{5,7},{6,4},{7,5},{8,10},{9,11},{10,... | collective-permute-start | bytes 1376264 | tf_op jit(solution)/shard_map/ppermute | solution.py:23
  74.1 21.7 %collective-permute-start.12 = (bf16[7,128,256]{2,1,0:T(8,128)(2,1)S(1)}, bf16[7,128,256]{2,1,0:T(8,128)(2,1)S(1)}, u32[]{:S(2)}, u32[]{:S(2)}) collective-permute-start(bf16[7,128,256]{2,1,0:T(8,128)(2,1)S(1)} %get-tuple-element.44), channel_id=1, source_target_pairs={{0,3},{1,0},{2,1},{3,2},{4,7},{5,4},{6,5},{7,6},{8,11},{9,8},{10,9... | collective-permute-start | bytes 1376264 | tf_op jit(solution)/shard_map/ppermute | solution.py:23
  77.0 0.9 copy-start.13
  77.9 0.9 copy-start.15
  86.4 1.0 copy-start.7
  95.9 13.1 %copy-start = (bf16[1024,128]{1,0:T(8,128)(2,1)S(1)}, bf16[1024,128]{1,0:T(8,128)(2,1)}, u32[]{:S(2)}) copy-start(bf16[1024,128]{1,0:T(8,128)(2,1)} %get-tuple-element.53.refs_9_) | copy-start | bytes 786436
  95.9 13.1 %copy-start.2 = (bf16[1024,128]{1,0:T(8,128)(2,1)S(1)}, bf16[1024,128]{1,0:T(8,128)(2,1)}, u32[]{:S(2)}) copy-start(bf16[1024,128]{1,0:T(8,128)(2,1)} %get-tuple-element.43.refs_11_) | copy-start | bytes 786436
  96.1 13.0 %collective-permute-start.13 = (bf16[3,6,128,256]{3,2,1,0:T(8,128)(2,1)S(1)}, bf16[3,6,128,256]{3,2,1,0:T(8,128)(2,1)S(1)}, u32[]{:S(2)}, u32[]{:S(2)}) collective-permute-start(bf16[3,6,128,256]{3,2,1,0:T(8,128)(2,1)S(1)} %pad_maximum_fusion), channel_id=1, source_target_pairs={{0,4},{4,0},{8,12},{12,8},{16,20},{20,16},{24,28},{28,24},{32,36},... | collective-permute-start | bytes 3538952 | tf_op jit(solution)/shard_map/ppermute | solution.py:34
  110.8 31.0 %copy-start.1 = (bf16[1024,128]{1,0:T(8,128)(2,1)S(1)}, bf16[1024,128]{1,0:T(8,128)(2,1)}, u32[]{:S(2)}) copy-start(bf16[1024,128]{1,0:T(8,128)(2,1)} %get-tuple-element.40.refs_11_) | copy-start | bytes 786436
  110.8 13.2 %collective-permute-start.14 = (bf16[256,256]{1,0:T(8,128)(2,1)S(1)}, bf16[256,256]{1,0:T(8,128)(2,1)S(1)}, u32[]{:S(2)}, u32[]{:S(2)}) collective-permute-start(bf16[256,256]{1,0:T(8,128)(2,1)S(1)} %get-tuple-element.25.refs_4_), channel_id=1, source_target_pairs={{0,8},{4,12},{8,16},{12,20},{16,24},{20,28},{24,32},{28,36},{32,40... | collective-permute-start | bytes 393224 | tf_op jit(solution)/shard_map/ppermute | solution.py:29
  116.4 7.5 %collective-permute-start.15 = (bf16[256,256]{1,0:T(8,128)(2,1)S(1)}, bf16[256,256]{1,0:T(8,128)(2,1)S(1)}, u32[]{:S(2)}, u32[]{:S(2)}) collective-permute-start(bf16[256,256]{1,0:T(8,128)(2,1)S(1)} %get-tuple-element.25.refs_4_), channel_id=1, source_target_pairs={{0,4},{4,8},{8,12},{12,16},{16,20},{20,24},{24,28},{28,32},{32,36}... | collective-permute-start | bytes 393224 | tf_op jit(solution)/shard_map/ppermute | solution.py:29
  118.4 6.1 %collective-permute-start.16 = (bf16[256,256]{1,0:T(8,128)(2,1)S(1)}, bf16[256,256]{1,0:T(8,128)(2,1)S(1)}, u32[]{:S(2)}, u32[]{:S(2)}) collective-permute-start(bf16[256,256]{1,0:T(8,128)(2,1)S(1)} %get-tuple-element.25.refs_4_), channel_id=1, source_target_pairs={{4,0},{8,4},{12,8},{16,12},{20,16},{24,20},{28,24},{32,28},{36,32}... | collective-permute-start | bytes 393224 | tf_op jit(solution)/shard_map/ppermute | solution.py:29
  122.0 9.0 %collective-permute-start.17 = (bf16[256,256]{1,0:T(8,128)(2,1)S(1)}, bf16[256,256]{1,0:T(8,128)(2,1)S(1)}, u32[]{:S(2)}, u32[]{:S(2)}) collective-permute-start(bf16[256,256]{1,0:T(8,128)(2,1)S(1)} %get-tuple-element.25.refs_4_), channel_id=1, source_target_pairs={{8,0},{12,4},{16,8},{20,12},{24,16},{28,20},{32,24},{36,28},{40,32... | collective-permute-start | bytes 393224 | tf_op jit(solution)/shard_map/ppermute | solution.py:29
  143.6 11.4 %collective-permute-start.18 = (bf16[256,256]{1,0:T(8,128)(2,1)S(1)}, bf16[256,256]{1,0:T(8,128)(2,1)S(1)}, u32[]{:S(2)}, u32[]{:S(2)}) collective-permute-start(bf16[256,256]{1,0:T(8,128)(2,1)S(1)} %get-tuple-element.28.refs_4_), channel_id=1, source_target_pairs={{0,8},{4,12},{8,16},{12,20},{16,24},{20,28},{24,32},{28,36},{32,40... | collective-permute-start | bytes 393224 | tf_op jit(solution)/shard_map/ppermute | solution.py:29
  145.5 9.5 %collective-permute-start.19 = (bf16[256,256]{1,0:T(8,128)(2,1)S(1)}, bf16[256,256]{1,0:T(8,128)(2,1)S(1)}, u32[]{:S(2)}, u32[]{:S(2)}) collective-permute-start(bf16[256,256]{1,0:T(8,128)(2,1)S(1)} %get-tuple-element.28.refs_4_), channel_id=1, source_target_pairs={{0,4},{4,8},{8,12},{12,16},{16,20},{20,24},{24,28},{28,32},{32,36}... | collective-permute-start | bytes 393224 | tf_op jit(solution)/shard_map/ppermute | solution.py:29
  147.4 7.6 %collective-permute-start.20 = (bf16[256,256]{1,0:T(8,128)(2,1)S(1)}, bf16[256,256]{1,0:T(8,128)(2,1)S(1)}, u32[]{:S(2)}, u32[]{:S(2)}) collective-permute-start(bf16[256,256]{1,0:T(8,128)(2,1)S(1)} %get-tuple-element.28.refs_4_), channel_id=1, source_target_pairs={{4,0},{8,4},{12,8},{16,12},{20,16},{24,20},{28,24},{32,28},{36,32}... | collective-permute-start | bytes 393224 | tf_op jit(solution)/shard_map/ppermute | solution.py:29
  151.1 9.1 %collective-permute-start.21 = (bf16[256,256]{1,0:T(8,128)(2,1)S(1)}, bf16[256,256]{1,0:T(8,128)(2,1)S(1)}, u32[]{:S(2)}, u32[]{:S(2)}) collective-permute-start(bf16[256,256]{1,0:T(8,128)(2,1)S(1)} %get-tuple-element.28.refs_4_), channel_id=1, source_target_pairs={{8,0},{12,4},{16,8},{20,12},{24,16},{28,20},{32,24},{36,28},{40,32... | collective-permute-start | bytes 393224 | tf_op jit(solution)/shard_map/ppermute | solution.py:29
  171.0 24.2 %copy-start.9 = (bf16[1024,128]{1,0:T(8,128)(2,1)S(1)}, bf16[1024,128]{1,0:T(8,128)(2,1)}, u32[]{:S(2)}) copy-start(bf16[1024,128]{1,0:T(8,128)(2,1)} %copy-done.8) | copy-start | bytes 786436
  173.7 11.4 %collective-permute-start.22 = (bf16[256,256]{1,0:T(8,128)(2,1)S(1)}, bf16[256,256]{1,0:T(8,128)(2,1)S(1)}, u32[]{:S(2)}, u32[]{:S(2)}) collective-permute-start(bf16[256,256]{1,0:T(8,128)(2,1)S(1)} %get-tuple-element.30.refs_4_), channel_id=1, source_target_pairs={{0,8},{4,12},{8,16},{12,20},{16,24},{20,28},{24,32},{28,36},{32,40... | collective-permute-start | bytes 393224 | tf_op jit(solution)/shard_map/ppermute | solution.py:29
  176.9 8.2 %collective-permute-start.23 = (bf16[256,256]{1,0:T(8,128)(2,1)S(1)}, bf16[256,256]{1,0:T(8,128)(2,1)S(1)}, u32[]{:S(2)}, u32[]{:S(2)}) collective-permute-start(bf16[256,256]{1,0:T(8,128)(2,1)S(1)} %get-tuple-element.30.refs_4_), channel_id=1, source_target_pairs={{0,4},{4,8},{8,12},{12,16},{16,20},{20,24},{24,28},{28,32},{32,36}... | collective-permute-start | bytes 393224 | tf_op jit(solution)/shard_map/ppermute | solution.py:29
  179.3 7.2 %collective-permute-start.24 = (bf16[256,256]{1,0:T(8,128)(2,1)S(1)}, bf16[256,256]{1,0:T(8,128)(2,1)S(1)}, u32[]{:S(2)}, u32[]{:S(2)}) collective-permute-start(bf16[256,256]{1,0:T(8,128)(2,1)S(1)} %get-tuple-element.30.refs_4_), channel_id=1, source_target_pairs={{4,0},{8,4},{12,8},{16,12},{20,16},{24,20},{28,24},{32,28},{36,32}... | collective-permute-start | bytes 393224 | tf_op jit(solution)/shard_map/ppermute | solution.py:29
  182.5 12.7 %collective-permute-start.25 = (bf16[256,256]{1,0:T(8,128)(2,1)S(1)}, bf16[256,256]{1,0:T(8,128)(2,1)S(1)}, u32[]{:S(2)}, u32[]{:S(2)}) collective-permute-start(bf16[256,256]{1,0:T(8,128)(2,1)S(1)} %get-tuple-element.30.refs_4_), channel_id=1, source_target_pairs={{8,0},{12,4},{16,8},{20,12},{24,16},{28,20},{32,24},{36,28},{40,32... | collective-permute-start | bytes 393224 | tf_op jit(solution)/shard_map/ppermute | solution.py:29
  198.0 3.7 %copy-start.25 = (bf16[1,128,256]{2,1,0:T(8,128)(2,1)S(1)}, bf16[1,128,256]{2,1,0:T(8,128)(2,1)}, u32[]{:S(2)}) copy-start(bf16[1,128,256]{2,1,0:T(8,128)(2,1)} %get-tuple-element.47) | copy-start | bytes 196612
  198.0 18.8 %copy-start.5 = (bf16[1024,256]{1,0:T(8,128)(2,1)S(1)}, bf16[1024,256]{1,0:T(8,128)(2,1)}, u32[]{:S(2)}) copy-start(bf16[1024,256]{1,0:T(8,128)(2,1)} %grid_in.1) | copy-start | bytes 1572868
  198.0 18.7 %all-to-all-start.3 = ((bf16[4,1024,128]{2,1,0:T(8,128)(2,1)}), bf16[4,1024,128]{2,1,0:T(8,128)(2,1)S(1)}, u32[]{:S(2)}, u32[]{:S(2)}) async-start(bf16[4,1024,128]{2,1,0:T(8,128)(2,1)} %near_attend.5), calls=%async_computation.3 | async-start | bytes 2097152 | tf_op jit(solution)/shard_map/all_to_all | solution.py:296
  (5 other events, 3.9 us)

commit v2 on v1

--- a/solution.py
+++ b/solution.py
@@ -40,6 +40,17 @@
 
 def vmem():
     return pl.BlockSpec(memory_space=pltpu.VMEM)
+
+
+def hbm():
+    return pl.BlockSpec(memory_space=pltpu.HBM)
+
+
+def copies_of(pairs, kept, sems):
+    return [
+        pltpu.make_async_copy(w.at[layer_index], kept.at[i], sems.at[i])
+        for i, (w, layer_index) in enumerate(pairs)
+    ]
 
 
 def source(meta, k):
@@ -60,16 +71,29 @@
     return jnp.dot(a, b, preferred_element_type=F32)
 
 
-def grid_kernel(meta, x0, x1, x2, x3, gains, w_k, w_v, w_q, kv_out, q_out):
+def grid_kernel(meta, x0, x1, x2, x3, gains, w_k, w_v, w_q, kv_out, q_out, kept, sems):
+    copies = copies_of([(w_k, 0), (w_v, 0), (w_q, 3)], kept, sems)
+
+    @pl.when(pl.program_id(0) == 0)
+    def _():
+        for copy in copies:
+            copy.start()
+
     rows = normed([x[...] for x in (x0, x1, x2, x3)])
+
+    @pl.when(pl.program_id(0) == 0)
+    def _():
+        for copy in copies:
+            copy.wait()
+
     kv = q = None
     for k in range(MP):
         src = source(meta, k)
         at = pl.ds(pl.multiple_of(src * 256, 256), 256)
         for_kv = (rows[k] * gains[1, pl.ds(src, 1), :]).astype(BF16)
         for_q = (rows[k] * gains[4, pl.ds(src, 1), :]).astype(BF16)
-        kv_part = dot(for_kv, jnp.concatenate([w_k[at, :], w_v[at, :]], axis=1))
-        q_part = dot(for_q, w_q[at, :])
+        kv_part = dot(for_kv, jnp.concatenate([kept[0, at, :], kept[1, at, :]], axis=1))
+        q_part = dot(for_q, kept[2, at, :])
         kv = kv_part if kv is None else kv + kv_part
         q = q_part if q is None else q + q_part
     kv_out[...] = kv.astype(BF16)
@@ -84,7 +108,7 @@
         grid=(rows // tile,),
         in_specs=[smem()]
         + [pl.BlockSpec((tile, 256), lambda i: (i, 0))] * MP
-        + [vmem()] * 4,
+        + [vmem(), hbm(), hbm(), hbm()],
         out_specs=[
             pl.BlockSpec((tile, 256), lambda i: (i, 0)),
             pl.BlockSpec((tile, 128), lambda i: (i, 0)),
@@ -93,39 +117,42 @@
             jax.ShapeDtypeStruct((rows, 256), BF16),
             jax.ShapeDtypeStruct((rows, 128), BF16),
         ],
+        scratch_shapes=[pltpu.VMEM((3, 1024, 128), BF16), pltpu.SemaphoreType.DMA((3,))],
         cost_estimate=pl.CostEstimate(flops=rows * 1024 * 384 * 2, transcendentals=0, bytes_accessed=rows * 4096),
         compiler_params=PARAMS,
         name="grid_project",
     )(meta, *pieces, gains, w_k, w_v, w_q)
 
 
-def mesh_kernel(meta, x0, x1, x2, x3, gains, w_q, state_out, q_out):
-    pieces = [x[...] for x in (x0, x1, x2, x3)]
-    rows = normed(pieces)
+def mesh_kernel(meta, x0, a1, a2, a3, gains, w_q, q_out, kept, sems):
+    copies = copies_of([(w_q, 0)], kept, sems)
+    copies[0].start()
+    rows = normed([x0[...]] + [a[...].reshape(2 * BLOCK, 256) for a in (a1, a2, a3)])
+    copies[0].wait()
     q = None
     for k in range(MP):
         src = source(meta, k)
         at = pl.ds(pl.multiple_of(src * 256, 256), 256)
-        part = dot((rows[k] * gains[0, pl.ds(src, 1), :]).astype(BF16), w_q[at, :])
+        part = dot((rows[k] * gains[0, pl.ds(src, 1), :]).astype(BF16), kept[0, at, :])
         q = part if q is None else q + part
-        state_out[src] = pieces[k]
     q_out[...] = q.astype(BF16)
 
 
-def mesh_start(meta, pieces, gains, w_q):
-    rows = pieces[0].shape[0]
+def mesh_start(meta, mesh_in, arrived, gains, w_q):
+    rows = mesh_in.shape[0]
     return pl.pallas_call(
         mesh_kernel,
-        in_specs=[smem()] + [vmem()] * 6,
-        out_specs=[vmem(), vmem()],
-        out_shape=[
-            jax.ShapeDtypeStruct((MP, rows, 256), BF16),
-            jax.ShapeDtypeStruct((rows, 128), BF16),
-        ],
+        grid=(1,),
+        in_specs=[smem(), vmem()]
+        + [pl.BlockSpec((2, BLOCK, 256), lambda i: (0, 0, 0))] * 3
+        + [vmem(), hbm()],
+        out_specs=vmem(),
+        out_shape=jax.ShapeDtypeStruct((rows, 128), BF16),
+        scratch_shapes=[pltpu.VMEM((1, 1024, 128), BF16), pltpu.SemaphoreType.DMA((1,))],
         cost_estimate=pl.CostEstimate(flops=rows * 1024 * 128 * 2, transcendentals=0, bytes_accessed=rows * 4096),
         compiler_params=PARAMS,
         name="mesh_start",
-    )(meta, *pieces, gains, w_q)
+    )(meta, mesh_in, *arrived, gains, w_q)
 
 
 def head_rows():
@@ -215,50 +242,75 @@
     )(meta, q, *windows)
 
 
-def layer_kernel(index, gain_row, with_query, meta, o, state, w_own, a1, a2, a3, other, gains, *rest):
-    projections, outs = rest[: 2 + with_query], rest[2 + with_query :]
+def layer_kernel(index, gain_row, meta, o, state, w_own, a1, a2, a3, other, gains, w_k, w_v, w_q, *rest):
+    last = index == 2
+    state_out, kv_out = rest[0], rest[1]
+    new, kept, sems = rest[2 + (not last) :]
+    weights = (w_k, w_v) if last else (w_k, w_v, w_q)
+    copies = copies_of([(w, index + 1) for w in weights], kept, sems)
+    for copy in copies:
+        copy.start()
+    if index == 0:
+        new[meta[0]] = state[...]
+        for k, a in enumerate((a1, a2, a3)):
+            new[source(meta, k + 1)] = a[0:2].reshape(2 * BLOCK, 256)
+        state = new
     heads = jnp.concatenate([o[source(meta, k)] for k in range(MP)], axis=1)
     core = meta[1] % 2
     for part in range(4):
-        at = 2 * index + part % 2
+        at = index + 3 * (part % 2)
         if part < 2:
             g = 2 * core + part
-            fetched = [a1[at], a2[at], a3[at]]
+            fetched = [a[2 + at] for a in (a1, a2, a3)]
         else:
             g = 2 * (1 - core) + part - 2
             fetched = [other[k, at] for k in range(MP - 1)]
-        w_out = jnp.concatenate([w_own[index, g]] + fetched, axis=0)
-        outs[0][g] = (state[g].astype(F32) + dot(heads, w_out)).astype(BF16)
-    rows = normed([outs[0][g] for g in range(MP)])
+        own = w_own[index, :, pl.ds(pl.multiple_of(g * 256, 256), 256)]
+        w_out = jnp.concatenate([own] + fetched, axis=0)
+        new[g] = (state[g].astype(F32) + dot(heads, w_out)).astype(BF16)
+    if last:
+        state_out[...] = new[meta[0]]
+    else:
+        for g in range(MP):
+            state_out[g] = new[g]
+    rows = normed([new[g] for g in range(MP)])
     row = jnp.concatenate(
         [(rows[g] * gains[gain_row, g : g + 1, :]).astype(BF16) for g in range(MP)], axis=1
     )
-    result = dot(row, jnp.concatenate([w[...] for w in projections], axis=1)).astype(BF16)
-    outs[1][...] = result[:, :256]
-    if with_query:
-        outs[2][...] = result[:, 256:]
-
-
-def layer(index, gain_row, with_query, meta, o, state, w_own, fetched, other, gains, projections):
+    for copy in copies:
+        copy.wait()
+    result = dot(row, jnp.concatenate([kept[i] for i in range(len(weights))], axis=1)).astype(BF16)
+    kv_out[...] = result[:, :256]
+    if not last:
+        rest[2][...] = result[:, 256:]
+
+
+def layer(index, gain_row, meta, o, state, w_own, fetched, other, gains, w_key, w_value, w_query):
     def body(*refs):
-        layer_kernel(index, gain_row, with_query, *refs)
-
-    rows = state.shape[1]
+        layer_kernel(index, gain_row, *refs)
+
+    last = index == 2
+    rows = o.shape[1]
     shapes = [
-        jax.ShapeDtypeStruct(state.shape, BF16),
+        jax.ShapeDtypeStruct((rows, 256) if last else (MP, rows, 256), BF16),
         jax.ShapeDtypeStruct((rows, 256), BF16),
     ]
-    if with_query:
+    if not last:
         shapes.append(jax.ShapeDtypeStruct((rows, 128), BF16))
-    operands = (o, state, w_own, *fetched, other, gains, *projections)
+    operands = (o, state, w_own, *fetched, other, gains)
     return pl.pallas_call(
         body,
-        in_specs=[smem()] + [vmem()] * len(operands),
+        in_specs=[smem()] + [vmem()] * len(operands) + [hbm()] * 3,
         out_specs=[vmem()] * len(shapes),
         out_shape=shapes,
+        scratch_shapes=[
+            pltpu.VMEM((MP, rows, 256), BF16),
+            pltpu.VMEM((3, 1024, 128), BF16),
+            pltpu.SemaphoreType.DMA((3,)),
+        ],
         compiler_params=PARAMS,
         name="mesh_layer",
-    )(meta, *operands)
+    )(meta, *operands, w_key, w_value, w_query)
 
 
 def final_kernel(meta, counts, o, w_out, grid_in, out):
@@ -310,6 +362,9 @@
         dec_list.reshape(-1) - (own_node - REACH) * 2,
     ])
     gains = norm_gains.reshape(6, MP, 256)
+    w_query, w_key, w_value = (
+        pltpu.with_memory_space_constraint(w, pltpu.HBM) for w in (w_query, w_key, w_value)
+    )
 
     def gathered(part, name):
         pieces = [part, None, None, None]
@@ -324,33 +379,32 @@
         return pieces
 
     grid_pieces = gathered(grid_in, "g")
-    mesh_pieces = gathered(mesh_in, "m")
-
-    w_groups = w_out.reshape(4, 128, MP, 256).transpose(0, 2, 1, 3)
-    own_half = lax.dynamic_slice_in_dim(w_groups[:3], core * 2, 2, axis=1)
+    grid_pieces[0] = pltpu.with_memory_space_constraint(grid_in, pltpu.HBM)
+
+    halves = [lax.dynamic_slice_in_dim(w_out[:3], core * 512 + part * 256, 256, axis=2) for part in range(2)]
     sent = [None] * MP
     for k in (1, 2, 3):
-        last = lax.dynamic_index_in_dim(w_groups[3], (own_mp + k) % MP, 0, keepdims=True)
-        sent[k] = jnp.concatenate([own_half.reshape(6, 128, 256), last], axis=0)
+        last = lax.dynamic_slice_in_dim(w_out[3:], (own_mp + k) % MP * 256, 256, axis=2)
+        sent[k] = jnp.concatenate([mesh_in.reshape(2, BLOCK, 256)] + halves + [last], axis=0)
     sent[0] = sent[1]
     arrived = gathered(sent, "w")[1:]
 
-    kv, grid_q = grid_project(meta, grid_pieces, gains, w_key[0], w_value[0], w_query[3])
+    kv, grid_q = grid_project(meta, grid_pieces, gains, w_key, w_value, w_query)
     grid_windows = window(kv)
-    state, mesh_q = mesh_start(meta, mesh_pieces, gains, w_query[0])
+    mesh_q = mesh_start(meta, mesh_in, arrived, gains, w_query)
     o = enc_attend(meta, enc_list, grid_count, mesh_q, grid_windows)
 
     arrived = lax.optimization_barrier((*arrived, o))[:3]
-    other = swap_cores(jnp.stack([a[:6] for a in arrived]))
+    other = swap_cores(jnp.stack([a[2:8] for a in arrived]))
     w_last = jnp.concatenate(
-        [lax.dynamic_index_in_dim(w_groups[3], own_mp, 0, keepdims=True)] + [a[6:] for a in arrived], axis=0
+        [lax.dynamic_slice_in_dim(w_out[3:], own_mp * 256, 256, axis=2)] + [a[8:] for a in arrived], axis=0
     ).reshape(512, 256)
 
+    state = mesh_in
     for index in range(3):
         heads = gather_heads(o)
-        projections = [w_key[index + 1], w_value[index + 1]] + ([w_query[index + 1]] if index < 2 else [])
         made = layer(
-            index, index + 2 if index < 2 else 5, index < 2, meta, heads, state, w_groups[:3], arrived, other, gains, projections
+            index, index + 2 if index < 2 else 5, meta, heads, state, w_out, arrived, other, gains, w_key, w_value, w_query
         )
         state, kv = made[0], made[1]
         near = window(kv)
@@ -359,8 +413,7 @@
     o = near_attend(DEC0, 2, meta, grid_q, near)
     heads = gather_heads(o)
     grid_out = final(meta, grid_count, heads, w_last, grid_in)
-    mesh_out = lax.dynamic_index_in_dim(state, own_mp, 0, keepdims=False)
-    return grid_out, mesh_out
+    return grid_out, state
 
 
 def solution(mesh):

time: 221 us -> 195 us (0.88)
  the two profiles are of different devices: /device:TPU:70 before, /device:TPU:230 now
where the time goes in v2:
time: 195 us; the launch traced here: 194 us
  starting transfers between devices  73.9 us (38%)
  waiting for transfers between devices  60.5 us (31%)
  blocking collectives  28.2 us (14%)
  Pallas kernels  26 us (13%)
  other arithmetic  2.34 us (1%)
  local copies, waits for them, and re-layouts  2.13 us (1%)
    ppermute x16, starting transfers between devices, from_node(): return lax.ppermute(value, 'nodes', pairs)  47.5 us
    ppermute x16, waiting for transfers between devices, from_node(): return lax.ppermute(value, 'nodes', pairs)  33.5 us
    all_to_all x3, blocking collectives, gather_heads(): return lax.all_to_all(copies, 'mp', split_axis=0, concat_axis=0, tiled=True)  28.2 us
    ppermute x6, starting transfers between devices, shift_mp(): return lax.ppermute(value, 'mp', [(s, (s + steps) % MP) for s in range(MP)])  20.8 us
    ppermute x6, waiting for transfers between devices, shift_mp(): return lax.ppermute(value, 'mp', [(s, (s + steps) % MP) for s in range(MP)])  14.7 us
    all_to_all x1, waiting for transfers between devices, gather_heads(): return lax.all_to_all(copies, 'mp', split_axis=0, concat_axis=0, tiled=True)  12.2 us
    pallas_call x3, Pallas kernels, layer(): pl.pallas_call(body, in_specs=[smem()] + [vmem()] * len(operands) + [hbm(...  7.77 us
    pallas_call x3, Pallas kernels, near_attend(): pl.pallas_call(body, in_specs=[smem()] + [vmem()] * 6, out_specs=vmem(),...  6.23 us
  transfers between devices with their start and end apart: 24, of which 8 were waited for; matrix products, arithmetic and copies ran while one was open for 2% of the time, Pallas kernels for 4%

profile of v2, /device:TPU:230, one launch (start us, length us, event | category | flops | bytes accessed | tf_op | source)
XLA Modules:
  0.0 194.2 jit_solution(13310483367047862729)
XLA Ops:
  0.6 3.6 %collective-permute-start = (bf16[1024,256]{1,0:T(8,128)(2,1)}, bf16[1024,256]{1,0:T(8,128)(2,1)S(1)}, u32[]{:S(2)}, u32[]{:S(2)}) collective-permute-start(bf16[1024,256]{1,0:T(8,128)(2,1)} %grid_in.1), channel_id=1, source_target_pairs={{0,1},{1,2},{2,3},{3,0},{4,5},{5,6},{6,7},{7,4},{8,9},{9,10},{10,1... | collective-permute-start | bytes 1572872 | tf_op jit(solution)/shard_map/ppermute | solution.py:23
  4.3 4.8 %collective-permute-start.1 = (bf16[1024,256]{1,0:T(8,128)(2,1)}, bf16[1024,256]{1,0:T(8,128)(2,1)S(1)}, u32[]{:S(2)}, u32[]{:S(2)}) collective-permute-start(bf16[1024,256]{1,0:T(8,128)(2,1)} %grid_in.1), channel_id=1, source_target_pairs={{0,2},{1,3},{2,0},{3,1},{4,6},{5,7},{6,4},{7,5},{8,10},{9,11},{10,... | collective-permute-start | bytes 1572872 | tf_op jit(solution)/shard_map/ppermute | solution.py:23
  9.1 3.3 %collective-permute-start.2 = (bf16[1024,256]{1,0:T(8,128)(2,1)}, bf16[1024,256]{1,0:T(8,128)(2,1)S(1)}, u32[]{:S(2)}, u32[]{:S(2)}) collective-permute-start(bf16[1024,256]{1,0:T(8,128)(2,1)} %grid_in.1), channel_id=1, source_target_pairs={{0,3},{1,0},{2,1},{3,2},{4,7},{5,4},{6,5},{7,6},{8,11},{9,8},{10,9... | collective-permute-start | bytes 1572872 | tf_op jit(solution)/shard_map/ppermute | solution.py:23
  12.5 0.8 slice-done
  14.0 1.3 pad_maximum_fusion.4
  15.4 2.6 %collective-permute-start.3 = (bf16[9,128,256]{2,1,0:T(8,128)(2,1)}, bf16[9,128,256]{2,1,0:T(8,128)(2,1)S(1)}, u32[]{:S(2)}, u32[]{:S(2)}) collective-permute-start(bf16[9,128,256]{2,1,0:T(8,128)(2,1)} %get-tuple-element.32), channel_id=1, source_target_pairs={{0,1},{1,2},{2,3},{3,0},{4,5},{5,6},{6,7},{7,4},{8,9},{9,10},{10,1... | collective-permute-start | bytes 1769480 | tf_op jit(solution)/shard_map/ppermute | solution.py:23
  17.9 2.7 %collective-permute-start.4 = (bf16[9,128,256]{2,1,0:T(8,128)(2,1)}, bf16[9,128,256]{2,1,0:T(8,128)(2,1)S(1)}, u32[]{:S(2)}, u32[]{:S(2)}) collective-permute-start(bf16[9,128,256]{2,1,0:T(8,128)(2,1)} %get-tuple-element.31), channel_id=1, source_target_pairs={{0,2},{1,3},{2,0},{3,1},{4,6},{5,7},{6,4},{7,5},{8,10},{9,11},{10,... | collective-permute-start | bytes 1769480 | tf_op jit(solution)/shard_map/ppermute | solution.py:23
  21.1 3.8 %collective-permute-start.5 = (bf16[9,128,256]{2,1,0:T(8,128)(2,1)}, bf16[9,128,256]{2,1,0:T(8,128)(2,1)S(1)}, u32[]{:S(2)}, u32[]{:S(2)}) collective-permute-start(bf16[9,128,256]{2,1,0:T(8,128)(2,1)} %get-tuple-element.30), channel_id=1, source_target_pairs={{0,3},{1,0},{2,1},{3,2},{4,7},{5,4},{6,5},{7,6},{8,11},{9,8},{10,9... | collective-permute-start | bytes 1769480 | tf_op jit(solution)/shard_map/ppermute | solution.py:23
  24.9 6.5 %collective-permute-done.1.x2 = bf16[1024,256]{1,0:T(8,128)(2,1)S(1)} collective-permute-done((bf16[1024,256]{1,0:T(8,128)(2,1)}, bf16[1024,256]{1,0:T(8,128)(2,1)S(1)}, u32[]{:S(2)}, u32[]{:S(2)}) %collective-permute-start.1) | collective-permute-done | bytes 524320 | tf_op jit(solution)/shard_map/ppermute | solution.py:23
  31.4 1.5 collective-permute-done.2.x3
  32.9 5.3 %grid_project.1 = (bf16[1024,256]{1,0:T(8,128)(2,1)S(1)}, bf16[1024,128]{1,0:T(8,128)(2,1)S(1)}) custom-call(s32[32]{0:T(128)S(1)} %concatenate.15.meta.refs_0_, bf16[1024,256]{1,0:T(8,128)(2,1)} %grid_in.1, bf16[1024,256]{1,0:T(8,128)(2,1)S(1)} %collective-permute-done.x1, bf16[1024,256]{1,0:T(8,128)(2,1)S(1)} %collective-permute-done.1.x2, ...), custom_call_target="tpu_custom_call" | custom-call | flops 805306368 | bytes 4194304 | tf_op jit(solution)/shard_map/grid_project/pallas_call | solution.py:106
  38.3 4.9 %collective-permute-start.6 = (bf16[1024,256]{1,0:T(8,128)(2,1)S(1)}, bf16[1024,256]{1,0:T(8,128)(2,1)S(1)}, u32[]{:S(2)}, u32[]{:S(2)}) collective-permute-start(bf16[1024,256]{1,0:T(8,128)(2,1)S(1)} %get-tuple-element.16.rest_2_), channel_id=1, source_target_pairs={{0,8},{4,12},{8,16},{12,20},{16,24},{20,28},{24,32},{28,36},{32,40... | collective-permute-start | bytes 1572872 | tf_op jit(solution)/shard_map/ppermute | solution.py:29
  43.2 1.9 collective-permute-start.7
  45.2 3.6 %collective-permute-start.8 = (bf16[1024,256]{1,0:T(8,128)(2,1)S(1)}, bf16[1024,256]{1,0:T(8,128)(2,1)S(1)}, u32[]{:S(2)}, u32[]{:S(2)}) collective-permute-start(bf16[1024,256]{1,0:T(8,128)(2,1)S(1)} %get-tuple-element.16.rest_2_), channel_id=1, source_target_pairs={{4,0},{8,4},{12,8},{16,12},{20,16},{24,20},{28,24},{32,28},{36,32}... | collective-permute-start | bytes 1572872 | tf_op jit(solution)/shard_map/ppermute | solution.py:29
  48.8 6.7 %collective-permute-done.4.a2.refs_5_ = bf16[9,128,256]{2,1,0:T(8,128)(2,1)S(1)} collective-permute-done((bf16[9,128,256]{2,1,0:T(8,128)(2,1)}, bf16[9,128,256]{2,1,0:T(8,128)(2,1)S(1)}, u32[]{:S(2)}, u32[]{:S(2)}) %collective-permute-start.4) | collective-permute-done | bytes 589856 | tf_op jit(solution)/shard_map/ppermute | solution.py:23
  55.6 2.7 %collective-permute-start.9 = (bf16[1024,256]{1,0:T(8,128)(2,1)S(1)}, bf16[1024,256]{1,0:T(8,128)(2,1)S(1)}, u32[]{:S(2)}, u32[]{:S(2)}) collective-permute-start(bf16[1024,256]{1,0:T(8,128)(2,1)S(1)} %get-tuple-element.16.rest_2_), channel_id=1, source_target_pairs={{8,0},{12,4},{16,8},{20,12},{24,16},{28,20},{32,24},{36,28},{40,32... | collective-permute-start | bytes 1572872 | tf_op jit(solution)/shard_map/ppermute | solution.py:29
  58.3 1.9 mesh_start.1.q
  60.3 13.3 %collective-permute-done.9.rest_4_ = bf16[1024,256]{1,0:T(8,128)(2,1)S(1)} collective-permute-done((bf16[1024,256]{1,0:T(8,128)(2,1)S(1)}, bf16[1024,256]{1,0:T(8,128)(2,1)S(1)}, u32[]{:S(2)}, u32[]{:S(2)}) %collective-permute-start.9) | collective-permute-done | bytes 524320 | tf_op jit(solution)/shard_map/ppermute | solution.py:29
  73.6 2.1 %enc_attend.1 = bf16[4,256,128]{2,1,0:T(8,128)(2,1)S(1)} custom-call(s32[32]{0:T(128)S(1)} %concatenate.15.meta.refs_0_, s32[2,4]{1,0:T(2,128)S(1)} %copy-done.4, s32[1024]{0:T(1024)S(1)} %copy-done.3, bf16[256,128]{1,0:T(8,128)(2,1)S(1)} %mesh_start.1.q, bf16[1024,256]{1,0:T(8,128)(2,1)S(1)} %collective-permute-done.6.rest_0_, ...), custom_call_target="tpu_custom_call" | custom-call | tf_op jit(solution)/shard_map/enc_attend/pallas_call | solution.py:206
  75.9 2.1 %collective-permute-start.10 = (bf16[3,6,128,256]{3,2,1,0:T(8,128)(2,1)S(1)}, bf16[3,6,128,256]{3,2,1,0:T(8,128)(2,1)S(1)}, u32[]{:S(2)}, u32[]{:S(2)}) collective-permute-start(bf16[3,6,128,256]{3,2,1,0:T(8,128)(2,1)S(1)} %pad_maximum_fusion), channel_id=1, source_target_pairs={{0,4},{4,0},{8,12},{12,8},{16,20},{20,16},{24,28},{28,24},{32,36},... | collective-permute-start | bytes 3538952 | tf_op jit(solution)/shard_map/ppermute | solution.py:34
  78.0 10.0 %all_to_all.20.refs_1_ = bf16[4,256,128]{2,1,0:T(8,128)(2,1)S(1)} all-to-all(bf16[4,256,128]{2,1,0:T(8,128)(2,1)S(1)} %enc_attend.1), channel_id=1, replica_groups=mesh['nodes'=128,'mp'=4] {'mp'}, dimensions={0} | all-to-all | bytes 524288 | tf_op jit(solution)/shard_map/all_to_all | solution.py:348
  88.0 2.6 %mesh_layer.3 = (bf16[4,256,256]{2,1,0:T(8,128)(2,1)S(1)}, bf16[256,256]{1,0:T(8,128)(2,1)S(1)}, bf16[256,128]{1,0:T(8,128)(2,1)S(1)}) custom-call(s32[32]{0:T(128)S(1)} %concatenate.15.meta.refs_0_, bf16[4,256,128]{2,1,0:T(8,128)(2,1)S(1)} %all_to_all.20.refs_1_, bf16[256,256]{1,0:T(8,128)(2,1)S(1)} %copy-done.2, bf16[4,128,1024]{2,1,0:T(8,128)(2,1)S(1)} %copy-done, ...), custom_call_target="tpu_custom_call" | custom-call | tf_op jit(solution)/shard_map/mesh_layer/pallas_call | solution.py:301
  90.7 1.9 collective-permute-start.11
  92.6 1.9 collective-permute-start.12
  94.5 3.6 %collective-permute-start.13 = (bf16[256,256]{1,0:T(8,128)(2,1)S(1)}, bf16[256,256]{1,0:T(8,128)(2,1)S(1)}, u32[]{:S(2)}, u32[]{:S(2)}) collective-permute-start(bf16[256,256]{1,0:T(8,128)(2,1)S(1)} %get-tuple-element.21.refs_4_), channel_id=1, source_target_pairs={{4,0},{8,4},{12,8},{16,12},{20,16},{24,20},{28,24},{32,28},{36,32}... | collective-permute-start | bytes 393224 | tf_op jit(solution)/shard_map/ppermute | solution.py:29
  98.2 3.9 %collective-permute-start.14 = (bf16[256,256]{1,0:T(8,128)(2,1)S(1)}, bf16[256,256]{1,0:T(8,128)(2,1)S(1)}, u32[]{:S(2)}, u32[]{:S(2)}) collective-permute-start(bf16[256,256]{1,0:T(8,128)(2,1)S(1)} %get-tuple-element.21.refs_4_), channel_id=1, source_target_pairs={{8,0},{12,4},{16,8},{20,12},{24,16},{28,20},{32,24},{36,28},{40,32... | collective-permute-start | bytes 393224 | tf_op jit(solution)/shard_map/ppermute | solution.py:29
  102.1 6.3 %collective-permute-done.14.refs_6_ = bf16[256,256]{1,0:T(8,128)(2,1)S(1)} collective-permute-done((bf16[256,256]{1,0:T(8,128)(2,1)S(1)}, bf16[256,256]{1,0:T(8,128)(2,1)S(1)}, u32[]{:S(2)}, u32[]{:S(2)}) %collective-permute-start.14) | collective-permute-done | bytes 131104 | tf_op jit(solution)/shard_map/ppermute | solution.py:29
  108.4 1.8 near_attend.3
  110.2 9.1 %all_to_all.21.refs_1_ = bf16[4,256,128]{2,1,0:T(8,128)(2,1)S(1)} all-to-all(bf16[4,256,128]{2,1,0:T(8,128)(2,1)S(1)} %near_attend.3), channel_id=1, replica_groups=mesh['nodes'=128,'mp'=4] {'mp'}, dimensions={0} | all-to-all | bytes 524288 | tf_op jit(solution)/shard_map/all_to_all | solution.py:348
  119.2 2.7 %mesh_layer.4 = (bf16[4,256,256]{2,1,0:T(8,128)(2,1)S(1)}, bf16[256,256]{1,0:T(8,128)(2,1)S(1)}, bf16[256,128]{1,0:T(8,128)(2,1)S(1)}) custom-call(s32[32]{0:T(128)S(1)} %concatenate.15.meta.refs_0_, bf16[4,256,128]{2,1,0:T(8,128)(2,1)S(1)} %all_to_all.21.refs_1_, bf16[4,256,256]{2,1,0:T(8,128)(2,1)S(1)} %get-tuple-element.22.refs_2_, ...), custom_call_target="tpu_custom_call" | custom-call | tf_op jit(solution)/shard_map/mesh_layer/pallas_call | solution.py:301
  121.9 3.0 %collective-permute-start.15 = (bf16[256,256]{1,0:T(8,128)(2,1)S(1)}, bf16[256,256]{1,0:T(8,128)(2,1)S(1)}, u32[]{:S(2)}, u32[]{:S(2)}) collective-permute-start(bf16[256,256]{1,0:T(8,128)(2,1)S(1)} %get-tuple-element.24.refs_4_), channel_id=1, source_target_pairs={{0,8},{4,12},{8,16},{12,20},{16,24},{20,28},{24,32},{28,36},{32,40... | collective-permute-start | bytes 393224 | tf_op jit(solution)/shard_map/ppermute | solution.py:29
  125.0 1.9 collective-permute-start.16
  126.9 3.6 %collective-permute-start.17 = (bf16[256,256]{1,0:T(8,128)(2,1)S(1)}, bf16[256,256]{1,0:T(8,128)(2,1)S(1)}, u32[]{:S(2)}, u32[]{:S(2)}) collective-permute-start(bf16[256,256]{1,0:T(8,128)(2,1)S(1)} %get-tuple-element.24.refs_4_), channel_id=1, source_target_pairs={{4,0},{8,4},{12,8},{16,12},{20,16},{24,20},{28,24},{32,28},{36,32}... | collective-permute-start | bytes 393224 | tf_op jit(solution)/shard_map/ppermute | solution.py:29
  130.5 2.8 %collective-permute-start.18 = (bf16[256,256]{1,0:T(8,128)(2,1)S(1)}, bf16[256,256]{1,0:T(8,128)(2,1)S(1)}, u32[]{:S(2)}, u32[]{:S(2)}) collective-permute-start(bf16[256,256]{1,0:T(8,128)(2,1)S(1)} %get-tuple-element.24.refs_4_), channel_id=1, source_target_pairs={{8,0},{12,4},{16,8},{20,12},{24,16},{28,20},{32,24},{36,28},{40,32... | collective-permute-start | bytes 393224 | tf_op jit(solution)/shard_map/ppermute | solution.py:29
  133.4 7.3 %collective-permute-done.18.refs_6_ = bf16[256,256]{1,0:T(8,128)(2,1)S(1)} collective-permute-done((bf16[256,256]{1,0:T(8,128)(2,1)S(1)}, bf16[256,256]{1,0:T(8,128)(2,1)S(1)}, u32[]{:S(2)}, u32[]{:S(2)}) %collective-permute-start.18) | collective-permute-done | bytes 131104 | tf_op jit(solution)/shard_map/ppermute | solution.py:29
  140.7 1.8 near_attend.4
  142.5 9.1 %all_to_all.22.refs_1_ = bf16[4,256,128]{2,1,0:T(8,128)(2,1)S(1)} all-to-all(bf16[4,256,128]{2,1,0:T(8,128)(2,1)S(1)} %near_attend.4), channel_id=1, replica_groups=mesh['nodes'=128,'mp'=4] {'mp'}, dimensions={0} | all-to-all | bytes 524288 | tf_op jit(solution)/shard_map/all_to_all | solution.py:348
  151.5 2.5 %mesh_layer.5 = (bf16[256,256]{1,0:T(8,128)(2,1)}, bf16[256,256]{1,0:T(8,128)(2,1)S(1)}) custom-call(s32[32]{0:T(128)S(1)} %concatenate.15.meta.refs_0_, bf16[4,256,128]{2,1,0:T(8,128)(2,1)S(1)} %all_to_all.22.refs_1_, bf16[4,256,256]{2,1,0:T(8,128)(2,1)S(1)} %get-tuple-element.25.refs_2_, bf16[4,128,1024]{2,1,0:T(8,128)(2,1)S(1)} %copy-done, ...), custom_call_target="tpu_custom_call" | custom-call | tf_op jit(solution)/shard_map/mesh_layer/pallas_call | solution.py:301
  154.0 2.3 %collective-permute-start.19 = (bf16[256,256]{1,0:T(8,128)(2,1)S(1)}, bf16[256,256]{1,0:T(8,128)(2,1)S(1)}, u32[]{:S(2)}, u32[]{:S(2)}) collective-permute-start(bf16[256,256]{1,0:T(8,128)(2,1)S(1)} %get-tuple-element.26.refs_4_), channel_id=1, source_target_pairs={{0,8},{4,12},{8,16},{12,20},{16,24},{20,28},{24,32},{28,36},{32,40... | collective-permute-start | bytes 393224 | tf_op jit(solution)/shard_map/ppermute | solution.py:29
  156.3 1.9 collective-permute-start.20
  158.2 3.6 %collective-permute-start.21 = (bf16[256,256]{1,0:T(8,128)(2,1)S(1)}, bf16[256,256]{1,0:T(8,128)(2,1)S(1)}, u32[]{:S(2)}, u32[]{:S(2)}) collective-permute-start(bf16[256,256]{1,0:T(8,128)(2,1)S(1)} %get-tuple-element.26.refs_4_), channel_id=1, source_target_pairs={{4,0},{8,4},{12,8},{16,12},{20,16},{24,20},{28,24},{32,28},{36,32}... | collective-permute-start | bytes 393224 | tf_op jit(solution)/shard_map/ppermute | solution.py:29
  161.9 3.6 %collective-permute-start.22 = (bf16[256,256]{1,0:T(8,128)(2,1)S(1)}, bf16[256,256]{1,0:T(8,128)(2,1)S(1)}, u32[]{:S(2)}, u32[]{:S(2)}) collective-permute-start(bf16[256,256]{1,0:T(8,128)(2,1)S(1)} %get-tuple-element.26.refs_4_), channel_id=1, source_target_pairs={{8,0},{12,4},{16,8},{20,12},{24,16},{28,20},{32,24},{36,28},{40,32... | collective-permute-start | bytes 393224 | tf_op jit(solution)/shard_map/ppermute | solution.py:29
  165.5 6.6 %collective-permute-done.22.refs_6_ = bf16[256,256]{1,0:T(8,128)(2,1)S(1)} collective-permute-done((bf16[256,256]{1,0:T(8,128)(2,1)S(1)}, bf16[256,256]{1,0:T(8,128)(2,1)S(1)}, u32[]{:S(2)}, u32[]{:S(2)}) %collective-permute-start.22) | collective-permute-done | bytes 131104 | tf_op jit(solution)/shard_map/ppermute | solution.py:29
  172.1 2.7 %near_attend.5 = bf16[4,1024,128]{2,1,0:T(8,128)(2,1)} custom-call(s32[32]{0:T(128)S(1)} %concatenate.15.meta.refs_0_, bf16[1024,128]{1,0:T(8,128)(2,1)S(1)} %get-tuple-element.15.refs_1_, bf16[256,256]{1,0:T(8,128)(2,1)S(1)} %collective-permute-done.19.refs_2_, bf16[256,256]{1,0:T(8,128)(2,1)S(1)} %collective-permute-done.20.refs_3_, ...), custom_call_target="tpu_custom_call" | custom-call | tf_op jit(solution)/shard_map/near_attend/pallas_call | solution.py:234
  174.8 3.6 %all-to-all-start.3 = ((bf16[4,1024,128]{2,1,0:T(8,128)(2,1)}), bf16[4,1024,128]{2,1,0:T(8,128)(2,1)S(1)}, u32[]{:S(2)}, u32[]{:S(2)}) async-start(bf16[4,1024,128]{2,1,0:T(8,128)(2,1)} %near_attend.5), calls=%async_computation.3 | async-start | bytes 2097152 | tf_op jit(solution)/shard_map/all_to_all | solution.py:348
  178.5 0.9 pad_maximum_fusion.5
  179.3 12.2 %all-to-all-done.3.o = bf16[4,1024,128]{2,1,0:T(8,128)(2,1)S(1)} async-done(((bf16[4,1024,128]{2,1,0:T(8,128)(2,1)}), bf16[4,1024,128]{2,1,0:T(8,128)(2,1)S(1)}, u32[]{:S(2)}, u32[]{:S(2)}) %all-to-all-start.3) | async-done | bytes 1048608 | tf_op jit(solution)/shard_map/all_to_all | solution.py:348
  191.6 2.7 %grid_final.1 = bf16[1024,256]{1,0:T(8,128)(2,1)} custom-call(s32[32]{0:T(128)S(1)} %concatenate.15.meta.refs_0_, s32[1024]{0:T(1024)S(1)} %copy-done.3, bf16[4,1024,128]{2,1,0:T(8,128)(2,1)S(1)} %all-to-all-done.3.o, bf16[512,256]{1,0:T(8,128)(2,1)S(1)} %bitcast.11, bf16[1024,256]{1,0:T(8,128)(2,1)S(1)} %copy-done.1), custom_call_target="tpu_custom_call" | custom-call | tf_op jit(solution)/shard_map/grid_final/pallas_call | solution.py:330
  (52 shorter events, 1.5 us)
Async XLA Ops:
  0.6 11.8 %slice-start.1 = ((bf16[4,128,1024]{2,1,0:T(8,128)(2,1)}), bf16[3,128,1024]{2,1,0:T(8,128)(2,1)S(1)}, s32[]{:S(2)}) async-start(bf16[4,128,1024]{2,1,0:T(8,128)(2,1)} %refs_3_.5), calls=%async_computation.5 | async-start | bytes 1572864 | tf_op jit(solution)/shard_map/slice | solution.py:384
  0.6 20.5 %collective-permute-start = (bf16[1024,256]{1,0:T(8,128)(2,1)}, bf16[1024,256]{1,0:T(8,128)(2,1)S(1)}, u32[]{:S(2)}, u32[]{:S(2)}) collective-permute-start(bf16[1024,256]{1,0:T(8,128)(2,1)} %grid_in.1), channel_id=1, source_target_pairs={{0,1},{1,2},{2,3},{3,0},{4,5},{5,6},{6,7},{7,4},{8,9},{9,10},{10,1... | collective-permute-start | bytes 1572872 | tf_op jit(solution)/shard_map/ppermute | solution.py:23
  4.3 27.1 %collective-permute-start.1 = (bf16[1024,256]{1,0:T(8,128)(2,1)}, bf16[1024,256]{1,0:T(8,128)(2,1)S(1)}, u32[]{:S(2)}, u32[]{:S(2)}) collective-permute-start(bf16[1024,256]{1,0:T(8,128)(2,1)} %grid_in.1), channel_id=1, source_target_pairs={{0,2},{1,3},{2,0},{3,1},{4,6},{5,7},{6,4},{7,5},{8,10},{9,11},{10,... | collective-permute-start | bytes 1572872 | tf_op jit(solution)/shard_map/ppermute | solution.py:23
  9.1 23.9 %collective-permute-start.2 = (bf16[1024,256]{1,0:T(8,128)(2,1)}, bf16[1024,256]{1,0:T(8,128)(2,1)S(1)}, u32[]{:S(2)}, u32[]{:S(2)}) collective-permute-start(bf16[1024,256]{1,0:T(8,128)(2,1)} %grid_in.1), channel_id=1, source_target_pairs={{0,3},{1,0},{2,1},{3,2},{4,7},{5,4},{6,5},{7,6},{8,11},{9,8},{10,9... | collective-permute-start | bytes 1572872 | tf_op jit(solution)/shard_map/ppermute | solution.py:23
  12.4 1.0 slice-start
  12.4 1.6 copy-start.2
  14.0 6.6 %copy-start.4 = (s32[2,4]{1,0:T(2,128)S(1)}, s32[2,4]{1,0:T(2,128)}, u32[]{:S(2)}) copy-start(s32[2,4]{1,0:T(2,128)} %listed.1) | copy-start | bytes 100
  14.0 6.7 %copy-start.6 = (s32[2,3]{1,0:T(2,128)S(1)}, s32[2,3]{1,0:T(2,128)}, u32[]{:S(2)}) copy-start(s32[2,3]{1,0:T(2,128)} %param.19) | copy-start | bytes 76
  14.0 6.8 %copy-start.7 = (s32[8,2]{0,1:T(2,128)S(1)}, s32[8,2]{0,1:T(2,128)}, u32[]{:S(2)}) copy-start(s32[8,2]{0,1:T(2,128)} %param.20) | copy-start | bytes 196
  14.0 7.0 %copy-start.5 = (f32[6,1024]{1,0:T(8,128)S(1)}, f32[6,1024]{1,0:T(8,128)}, u32[]{:S(2)}) copy-start(f32[6,1024]{1,0:T(8,128)} %param.17) | copy-start | bytes 73732
  15.4 29.8 %collective-permute-start.3 = (bf16[9,128,256]{2,1,0:T(8,128)(2,1)}, bf16[9,128,256]{2,1,0:T(8,128)(2,1)S(1)}, u32[]{:S(2)}, u32[]{:S(2)}) collective-permute-start(bf16[9,128,256]{2,1,0:T(8,128)(2,1)} %get-tuple-element.32), channel_id=1, source_target_pairs={{0,1},{1,2},{2,3},{3,0},{4,5},{5,6},{6,7},{7,4},{8,9},{9,10},{10,1... | collective-permute-start | bytes 1769480 | tf_op jit(solution)/shard_map/ppermute | solution.py:23
  17.9 37.6 %collective-permute-start.4 = (bf16[9,128,256]{2,1,0:T(8,128)(2,1)}, bf16[9,128,256]{2,1,0:T(8,128)(2,1)S(1)}, u32[]{:S(2)}, u32[]{:S(2)}) collective-permute-start(bf16[9,128,256]{2,1,0:T(8,128)(2,1)} %get-tuple-element.31), channel_id=1, source_target_pairs={{0,2},{1,3},{2,0},{3,1},{4,6},{5,7},{6,4},{7,5},{8,10},{9,11},{10,... | collective-permute-start | bytes 1769480 | tf_op jit(solution)/shard_map/ppermute | solution.py:23
  21.1 37.2 %collective-permute-start.5 = (bf16[9,128,256]{2,1,0:T(8,128)(2,1)}, bf16[9,128,256]{2,1,0:T(8,128)(2,1)S(1)}, u32[]{:S(2)}, u32[]{:S(2)}) collective-permute-start(bf16[9,128,256]{2,1,0:T(8,128)(2,1)} %get-tuple-element.30), channel_id=1, source_target_pairs={{0,3},{1,0},{2,1},{3,2},{4,7},{5,4},{6,5},{7,6},{8,11},{9,8},{10,9... | collective-permute-start | bytes 1769480 | tf_op jit(solution)/shard_map/ppermute | solution.py:23
  38.3 35.3 %copy-start.3 = (s32[1024]{0:T(1024)S(1)}, s32[1024]{0:T(1024)}, u32[]{:S(2)}) copy-start(s32[1024]{0:T(1024)} %counts.3) | copy-start | bytes 12292
  38.3 22.0 %collective-permute-start.6 = (bf16[1024,256]{1,0:T(8,128)(2,1)S(1)}, bf16[1024,256]{1,0:T(8,128)(2,1)S(1)}, u32[]{:S(2)}, u32[]{:S(2)}) collective-permute-start(bf16[1024,256]{1,0:T(8,128)(2,1)S(1)} %get-tuple-element.16.rest_2_), channel_id=1, source_target_pairs={{0,8},{4,12},{8,16},{12,20},{16,24},{20,28},{24,32},{28,36},{32,40... | collective-permute-start | bytes 1572872 | tf_op jit(solution)/shard_map/ppermute | solution.py:29
  43.2 17.0 %collective-permute-start.7 = (bf16[1024,256]{1,0:T(8,128)(2,1)S(1)}, bf16[1024,256]{1,0:T(8,128)(2,1)S(1)}, u32[]{:S(2)}, u32[]{:S(2)}) collective-permute-start(bf16[1024,256]{1,0:T(8,128)(2,1)S(1)} %get-tuple-element.16.rest_2_), channel_id=1, source_target_pairs={{0,4},{4,8},{8,12},{12,16},{16,20},{20,24},{24,28},{28,32},{32,36}... | collective-permute-start | bytes 1572872 | tf_op jit(solution)/shard_map/ppermute | solution.py:29
  45.2 15.1 %collective-permute-start.8 = (bf16[1024,256]{1,0:T(8,128)(2,1)S(1)}, bf16[1024,256]{1,0:T(8,128)(2,1)S(1)}, u32[]{:S(2)}, u32[]{:S(2)}) collective-permute-start(bf16[1024,256]{1,0:T(8,128)(2,1)S(1)} %get-tuple-element.16.rest_2_), channel_id=1, source_target_pairs={{4,0},{8,4},{12,8},{16,12},{20,16},{24,20},{28,24},{32,28},{36,32}... | collective-permute-start | bytes 1572872 | tf_op jit(solution)/shard_map/ppermute | solution.py:29
  55.6 18.0 %collective-permute-start.9 = (bf16[1024,256]{1,0:T(8,128)(2,1)S(1)}, bf16[1024,256]{1,0:T(8,128)(2,1)S(1)}, u32[]{:S(2)}, u32[]{:S(2)}) collective-permute-start(bf16[1024,256]{1,0:T(8,128)(2,1)S(1)} %get-tuple-element.16.rest_2_), channel_id=1, source_target_pairs={{8,0},{12,4},{16,8},{20,12},{24,16},{28,20},{32,24},{36,28},{40,32... | collective-permute-start | bytes 1572872 | tf_op jit(solution)/shard_map/ppermute | solution.py:29
  75.8 12.2 %copy-start = (bf16[4,128,1024]{2,1,0:T(8,128)(2,1)S(1)}, bf16[4,128,1024]{2,1,0:T(8,128)(2,1)}, u32[]{:S(2)}) copy-start(bf16[4,128,1024]{2,1,0:T(8,128)(2,1)} %refs_3_.5) | copy-start | bytes 3145732
  75.9 12.1 %collective-permute-start.10 = (bf16[3,6,128,256]{3,2,1,0:T(8,128)(2,1)S(1)}, bf16[3,6,128,256]{3,2,1,0:T(8,128)(2,1)S(1)}, u32[]{:S(2)}, u32[]{:S(2)}) collective-permute-start(bf16[3,6,128,256]{3,2,1,0:T(8,128)(2,1)S(1)} %pad_maximum_fusion), channel_id=1, source_target_pairs={{0,4},{4,0},{8,12},{12,8},{16,20},{20,16},{24,28},{28,24},{32,36},... | collective-permute-start | bytes 3538952 | tf_op jit(solution)/shard_map/ppermute | solution.py:34
  90.7 11.4 %collective-permute-start.11 = (bf16[256,256]{1,0:T(8,128)(2,1)S(1)}, bf16[256,256]{1,0:T(8,128)(2,1)S(1)}, u32[]{:S(2)}, u32[]{:S(2)}) collective-permute-start(bf16[256,256]{1,0:T(8,128)(2,1)S(1)} %get-tuple-element.21.refs_4_), channel_id=1, source_target_pairs={{0,8},{4,12},{8,16},{12,20},{16,24},{20,28},{24,32},{28,36},{32,40... | collective-permute-start | bytes 393224 | tf_op jit(solution)/shard_map/ppermute | solution.py:29
  92.6 9.5 %collective-permute-start.12 = (bf16[256,256]{1,0:T(8,128)(2,1)S(1)}, bf16[256,256]{1,0:T(8,128)(2,1)S(1)}, u32[]{:S(2)}, u32[]{:S(2)}) collective-permute-start(bf16[256,256]{1,0:T(8,128)(2,1)S(1)} %get-tuple-element.21.refs_4_), channel_id=1, source_target_pairs={{0,4},{4,8},{8,12},{12,16},{16,20},{20,24},{24,28},{28,32},{32,36}... | collective-permute-start | bytes 393224 | tf_op jit(solution)/shard_map/ppermute | solution.py:29
  94.5 7.6 %collective-permute-start.13 = (bf16[256,256]{1,0:T(8,128)(2,1)S(1)}, bf16[256,256]{1,0:T(8,128)(2,1)S(1)}, u32[]{:S(2)}, u32[]{:S(2)}) collective-permute-start(bf16[256,256]{1,0:T(8,128)(2,1)S(1)} %get-tuple-element.21.refs_4_), channel_id=1, source_target_pairs={{4,0},{8,4},{12,8},{16,12},{20,16},{24,20},{28,24},{32,28},{36,32}... | collective-permute-start | bytes 393224 | tf_op jit(solution)/shard_map/ppermute | solution.py:29
  98.2 10.2 %collective-permute-start.14 = (bf16[256,256]{1,0:T(8,128)(2,1)S(1)}, bf16[256,256]{1,0:T(8,128)(2,1)S(1)}, u32[]{:S(2)}, u32[]{:S(2)}) collective-permute-start(bf16[256,256]{1,0:T(8,128)(2,1)S(1)} %get-tuple-element.21.refs_4_), channel_id=1, source_target_pairs={{8,0},{12,4},{16,8},{20,12},{24,16},{28,20},{32,24},{36,28},{40,32... | collective-permute-start | bytes 393224 | tf_op jit(solution)/shard_map/ppermute | solution.py:29
  121.9 11.4 %collective-permute-start.15 = (bf16[256,256]{1,0:T(8,128)(2,1)S(1)}, bf16[256,256]{1,0:T(8,128)(2,1)S(1)}, u32[]{:S(2)}, u32[]{:S(2)}) collective-permute-start(bf16[256,256]{1,0:T(8,128)(2,1)S(1)} %get-tuple-element.24.refs_4_), channel_id=1, source_target_pairs={{0,8},{4,12},{8,16},{12,20},{16,24},{20,28},{24,32},{28,36},{32,40... | collective-permute-start | bytes 393224 | tf_op jit(solution)/shard_map/ppermute | solution.py:29
  125.0 8.4 %collective-permute-start.16 = (bf16[256,256]{1,0:T(8,128)(2,1)S(1)}, bf16[256,256]{1,0:T(8,128)(2,1)S(1)}, u32[]{:S(2)}, u32[]{:S(2)}) collective-permute-start(bf16[256,256]{1,0:T(8,128)(2,1)S(1)} %get-tuple-element.24.refs_4_), channel_id=1, source_target_pairs={{0,4},{4,8},{8,12},{12,16},{16,20},{20,24},{24,28},{28,32},{32,36}... | collective-permute-start | bytes 393224 | tf_op jit(solution)/shard_map/ppermute | solution.py:29
  126.9 6.5 %collective-permute-start.17 = (bf16[256,256]{1,0:T(8,128)(2,1)S(1)}, bf16[256,256]{1,0:T(8,128)(2,1)S(1)}, u32[]{:S(2)}, u32[]{:S(2)}) collective-permute-start(bf16[256,256]{1,0:T(8,128)(2,1)S(1)} %get-tuple-element.24.refs_4_), channel_id=1, source_target_pairs={{4,0},{8,4},{12,8},{16,12},{20,16},{24,20},{28,24},{32,28},{36,32}... | collective-permute-start | bytes 393224 | tf_op jit(solution)/shard_map/ppermute | solution.py:29
  130.5 10.2 %collective-permute-start.18 = (bf16[256,256]{1,0:T(8,128)(2,1)S(1)}, bf16[256,256]{1,0:T(8,128)(2,1)S(1)}, u32[]{:S(2)}, u32[]{:S(2)}) collective-permute-start(bf16[256,256]{1,0:T(8,128)(2,1)S(1)} %get-tuple-element.24.refs_4_), channel_id=1, source_target_pairs={{8,0},{12,4},{16,8},{20,12},{24,16},{28,20},{32,24},{36,28},{40,32... | collective-permute-start | bytes 393224 | tf_op jit(solution)/shard_map/ppermute | solution.py:29
  154.0 11.4 %collective-permute-start.19 = (bf16[256,256]{1,0:T(8,128)(2,1)S(1)}, bf16[256,256]{1,0:T(8,128)(2,1)S(1)}, u32[]{:S(2)}, u32[]{:S(2)}) collective-permute-start(bf16[256,256]{1,0:T(8,128)(2,1)S(1)} %get-tuple-element.26.refs_4_), channel_id=1, source_target_pairs={{0,8},{4,12},{8,16},{12,20},{16,24},{20,28},{24,32},{28,36},{32,40... | collective-permute-start | bytes 393224 | tf_op jit(solution)/shard_map/ppermute | solution.py:29
  156.3 9.2 %collective-permute-start.20 = (bf16[256,256]{1,0:T(8,128)(2,1)S(1)}, bf16[256,256]{1,0:T(8,128)(2,1)S(1)}, u32[]{:S(2)}, u32[]{:S(2)}) collective-permute-start(bf16[256,256]{1,0:T(8,128)(2,1)S(1)} %get-tuple-element.26.refs_4_), channel_id=1, source_target_pairs={{0,4},{4,8},{8,12},{12,16},{16,20},{20,24},{24,28},{28,32},{32,36}... | collective-permute-start | bytes 393224 | tf_op jit(solution)/shard_map/ppermute | solution.py:29
  158.2 7.2 %collective-permute-start.21 = (bf16[256,256]{1,0:T(8,128)(2,1)S(1)}, bf16[256,256]{1,0:T(8,128)(2,1)S(1)}, u32[]{:S(2)}, u32[]{:S(2)}) collective-permute-start(bf16[256,256]{1,0:T(8,128)(2,1)S(1)} %get-tuple-element.26.refs_4_), channel_id=1, source_target_pairs={{4,0},{8,4},{12,8},{16,12},{20,16},{24,20},{28,24},{32,28},{36,32}... | collective-permute-start | bytes 393224 | tf_op jit(solution)/shard_map/ppermute | solution.py:29
  161.9 10.2 %collective-permute-start.22 = (bf16[256,256]{1,0:T(8,128)(2,1)S(1)}, bf16[256,256]{1,0:T(8,128)(2,1)S(1)}, u32[]{:S(2)}, u32[]{:S(2)}) collective-permute-start(bf16[256,256]{1,0:T(8,128)(2,1)S(1)} %get-tuple-element.26.refs_4_), channel_id=1, source_target_pairs={{8,0},{12,4},{16,8},{20,12},{24,16},{28,20},{32,24},{36,28},{40,32... | collective-permute-start | bytes 393224 | tf_op jit(solution)/shard_map/ppermute | solution.py:29
  174.8 16.8 %copy-start.1 = (bf16[1024,256]{1,0:T(8,128)(2,1)S(1)}, bf16[1024,256]{1,0:T(8,128)(2,1)}, u32[]{:S(2)}) copy-start(bf16[1024,256]{1,0:T(8,128)(2,1)} %grid_in.1) | copy-start | bytes 1572868
  174.8 16.8 %all-to-all-start.3 = ((bf16[4,1024,128]{2,1,0:T(8,128)(2,1)}), bf16[4,1024,128]{2,1,0:T(8,128)(2,1)S(1)}, u32[]{:S(2)}, u32[]{:S(2)}) async-start(bf16[4,1024,128]{2,1,0:T(8,128)(2,1)} %near_attend.5), calls=%async_computation.3 | async-start | bytes 2097152 | tf_op jit(solution)/shard_map/all_to_all | solution.py:348

commit v3 on v2

--- a/solution.py
+++ b/solution.py
@@ -178,16 +178,21 @@
     return jnp.where(lane < 64, outs[0], outs[1]).astype(BF16)
 
 
-def enc_kernel(meta, listed, counts, q, *rest):
-    windows, o_out, kept = rest[:-2], rest[-2], rest[-1]
-    blocks_each = windows[0].shape[0] // BLOCK
+def window_places(meta):
+    core = meta[1] % 2
+    return 0, 2, 4, 3 - 2 * core, 1 + 2 * core
+
+
+def enc_kernel(meta, listed, counts, q, a0, a1, a2, a3, a4, o_out, kept):
+    blocks_each = a0.shape[0] // BLOCK
+    places = window_places(meta)
     for slot in range(8):
         place = meta[ENC0 + slot]
         which = place // blocks_each
         start = pl.multiple_of((place % blocks_each) * BLOCK, BLOCK)
-        for i, array in enumerate(windows):
-
-            @pl.when(which == i)
+        for w, array in zip(places, (a0, a1, a2, a3, a4)):
+
+            @pl.when(which == w)
             def _():
                 kept[slot] = array[pl.ds(start, BLOCK), :]
 
@@ -205,7 +210,7 @@
 def enc_attend(meta, listed, counts, q, windows):
     return pl.pallas_call(
         enc_kernel,
-        in_specs=[smem(), smem(), smem()] + [vmem()] * (1 + len(windows)),
+        in_specs=[smem(), smem(), smem()] + [vmem()] * 6,
         out_specs=vmem(),
         out_shape=jax.ShapeDtypeStruct((MP,) + q.shape, BF16),
         scratch_shapes=[pltpu.VMEM((8, BLOCK, 256), BF16)],
@@ -215,9 +220,9 @@
 
 
 def near_kernel(first_entry, per_block, meta, q, a0, a1, a2, a3, a4, o_out, kept):
-    for i, array in enumerate((a0, a1, a2, a3, a4)):
-        kept[2 * i] = array[0:BLOCK, :]
-        kept[2 * i + 1] = array[BLOCK : 2 * BLOCK, :]
+    for w, array in zip(window_places(meta), (a0, a1, a2, a3, a4)):
+        kept[2 * w] = array[0:BLOCK, :]
+        kept[2 * w + 1] = array[BLOCK : 2 * BLOCK, :]
     for b in range(q.shape[0] // BLOCK):
         kv = jnp.concatenate(
             [kept[meta[first_entry + b * per_block + j]] for j in range(per_block)], axis=0
@@ -242,10 +247,22 @@
     )(meta, q, *windows)
 
 
-def layer_kernel(index, gain_row, meta, o, state, w_own, a1, a2, a3, other, gains, w_k, w_v, w_q, *rest):
+def layer_kernel(index, gain_row, meta, o, state, a1, a2, a3, gains, w_own, b1, b2, b3, other, w_k, w_v, w_q, *rest):
     last = index == 2
     state_out, kv_out = rest[0], rest[1]
-    new, kept, sems = rest[2 + (not last) :]
+    new, w_out, kept, w_sems, sems = rest[2 + (not last) :]
+    core = meta[1] % 2
+    for g in range(MP):
+        pltpu.make_async_copy(
+            w_own.at[index, :, g * 256 : (g + 1) * 256], w_out.at[g, 0:BLOCK, :], w_sems.at[g, 0]
+        ).start()
+    for part in range(2):
+        at = index + 3 * part
+        for k, b in enumerate((b1, b2, b3)):
+            rows = w_out.at[2 * core + part, (k + 1) * BLOCK : (k + 2) * BLOCK, :]
+            pltpu.make_async_copy(b.at[2 + at], rows, w_sems.at[2 * core + part, k + 1]).start()
+            rows = w_out.at[2 * (1 - core) + part, (k + 1) * BLOCK : (k + 2) * BLOCK, :]
+            pltpu.make_async_copy(other.at[k, at], rows, w_sems.at[2 * (1 - core) + part, k + 1]).start()
     weights = (w_k, w_v) if last else (w_k, w_v, w_q)
     copies = copies_of([(w, index + 1) for w in weights], kept, sems)
     for copy in copies:
@@ -253,21 +270,14 @@
     if index == 0:
         new[meta[0]] = state[...]
         for k, a in enumerate((a1, a2, a3)):
-            new[source(meta, k + 1)] = a[0:2].reshape(2 * BLOCK, 256)
+            new[source(meta, k + 1)] = a[...].reshape(2 * BLOCK, 256)
         state = new
     heads = jnp.concatenate([o[source(meta, k)] for k in range(MP)], axis=1)
-    core = meta[1] % 2
-    for part in range(4):
-        at = index + 3 * (part % 2)
-        if part < 2:
-            g = 2 * core + part
-            fetched = [a[2 + at] for a in (a1, a2, a3)]
-        else:
-            g = 2 * (1 - core) + part - 2
-            fetched = [other[k, at] for k in range(MP - 1)]
-        own = w_own[index, :, pl.ds(pl.multiple_of(g * 256, 256), 256)]
-        w_out = jnp.concatenate([own] + fetched, axis=0)
-        new[g] = (state[g].astype(F32) + dot(heads, w_out)).astype(BF16)
+    for g in range(MP):
+        for k in range(MP):
+            rows = w_out.at[g, k * BLOCK : (k + 1) * BLOCK, :]
+            pltpu.make_async_copy(other.at[0, 0], rows, w_sems.at[g, k]).wait()
+        new[g] = (state[g].astype(F32) + dot(heads, w_out[g])).astype(BF16)
     if last:
         state_out[...] = new[meta[0]]
     else:
@@ -297,20 +307,25 @@
     ]
     if not last:
         shapes.append(jax.ShapeDtypeStruct((rows, 128), BF16))
-    operands = (o, state, w_own, *fetched, other, gains)
     return pl.pallas_call(
         body,
-        in_specs=[smem()] + [vmem()] * len(operands) + [hbm()] * 3,
+        grid=(1,),
+        in_specs=[smem(), vmem(), vmem()]
+        + [pl.BlockSpec((2, BLOCK, 256), lambda i: (0, 0, 0))] * 3
+        + [vmem()]
+        + [hbm()] * 8,
         out_specs=[vmem()] * len(shapes),
         out_shape=shapes,
         scratch_shapes=[
             pltpu.VMEM((MP, rows, 256), BF16),
+            pltpu.VMEM((MP, 4 * BLOCK, 256), BF16),
             pltpu.VMEM((3, 1024, 128), BF16),
+            pltpu.SemaphoreType.DMA((MP, MP)),
             pltpu.SemaphoreType.DMA((3,)),
         ],
         compiler_params=PARAMS,
         name="mesh_layer",
-    )(meta, *operands, w_key, w_value, w_query)
+    )(meta, o, state, *fetched, gains, w_own, *fetched, other, w_key, w_value, w_query)
 
 
 def final_kernel(meta, counts, o, w_out, grid_in, out):
@@ -326,7 +341,7 @@
 
 def final(meta, counts, o, w_out, grid_in):
     rows = grid_in.shape[0]
-    tile = 256
+    tile = 512
     return pl.pallas_call(
         final_kernel,
         grid=(rows // tile,),
@@ -373,10 +388,11 @@
         return pieces
 
     def window(part):
-        pieces = []
-        for d in range(-REACH, REACH + 1):
-            pieces.append(from_node(part, d) if d else part)
-        return pieces
+        low = from_node(part, -2)
+        high = from_node(part, 2)
+        beside = swap_cores(part)
+        beyond = swap_cores(jnp.where(core == 0, high, low))
+        return [low, part, high, beside, beyond]
 
     grid_pieces = gathered(grid_in, "g")
     grid_pieces[0] = pltpu.with_memory_space_constraint(grid_in, pltpu.HBM)
@@ -396,6 +412,8 @@
 
     arrived = lax.optimization_barrier((*arrived, o))[:3]
     other = swap_cores(jnp.stack([a[2:8] for a in arrived]))
+    other = pltpu.with_memory_space_constraint(other, pltpu.HBM)
+    w_own = pltpu.with_memory_space_constraint(w_out, pltpu.HBM)
     w_last = jnp.concatenate(
         [lax.dynamic_slice_in_dim(w_out[3:], own_mp * 256, 256, axis=2)] + [a[8:] for a in arrived], axis=0
     ).reshape(512, 256)
@@ -404,7 +422,7 @@
     for index in range(3):
         heads = gather_heads(o)
         made = layer(
-            index, index + 2 if index < 2 else 5, meta, heads, state, w_out, arrived, other, gains, w_key, w_value, w_query
+            index, index + 2 if index < 2 else 5, meta, heads, state, w_own, arrived, other, gains, w_key, w_value, w_query
         )
         state, kv = made[0], made[1]
         near = window(kv)

time: 195 us -> 209 us (1.072)
  the two profiles are of different devices: /device:TPU:230 before, /device:TPU:102 now
where the time goes in v3:
time: 209 us; the launch traced here: 208 us
  starting transfers between devices  72 us (34%)
  waiting for transfers between devices  67.2 us (32%)
  blocking collectives  30.8 us (15%)
  Pallas kernels  28.1 us (13%)
  other arithmetic  4.48 us (2%)
  local copies, waits for them, and re-layouts  4.21 us (2%)
    ppermute x6, waiting for transfers between devices, shift_mp(): return lax.ppermute(value, 'mp', [(s, (s + steps) % MP) for s in range(MP)])  33.2 us
    all_to_all x3, blocking collectives, gather_heads(): return lax.all_to_all(copies, 'mp', split_axis=0, concat_axis=0, tiled=True)  30.8 us
    ppermute x8, starting transfers between devices, from_node(): return lax.ppermute(value, 'nodes', pairs)  27.6 us
    ppermute x6, starting transfers between devices, shift_mp(): return lax.ppermute(value, 'mp', [(s, (s + steps) % MP) for s in range(MP)])  23 us
    ppermute x9, starting transfers between devices, swap_cores(): return lax.ppermute(value, 'nodes', [(s, s ^ 1) for s in range(count)])  17.8 us
    ppermute x8, waiting for transfers between devices, from_node(): return lax.ppermute(value, 'nodes', pairs)  15.3 us
    all_to_all x1, waiting for transfers between devices, gather_heads(): return lax.all_to_all(copies, 'mp', split_axis=0, concat_axis=0, tiled=True)  14.7 us
    pallas_call x3, Pallas kernels, layer(): pl.pallas_call(body, grid=(1,), in_specs=[smem(), vmem(), vmem()] + [pl.B...  10.6 us
  transfers between devices with their start and end apart: 24, of which 13 were waited for; matrix products, arithmetic and copies ran while one was open for 3% of the time, Pallas kernels for 1%

profile of v3, /device:TPU:102, one launch (start us, length us, event | category | flops | bytes accessed | tf_op | source)
XLA Modules:
  0.0 208.0 jit_solution(3650175684055895957)
XLA Ops:
  0.6 3.5 %collective-permute-start = (bf16[1024,256]{1,0:T(8,128)(2,1)}, bf16[1024,256]{1,0:T(8,128)(2,1)S(1)}, u32[]{:S(2)}, u32[]{:S(2)}) collective-permute-start(bf16[1024,256]{1,0:T(8,128)(2,1)} %grid_in.1), channel_id=1, source_target_pairs={{0,1},{1,2},{2,3},{3,0},{4,5},{5,6},{6,7},{7,4},{8,9},{9,10},{10,1... | collective-permute-start | bytes 1572872 | tf_op jit(solution)/shard_map/ppermute | solution.py:23
  4.1 4.8 %collective-permute-start.1 = (bf16[1024,256]{1,0:T(8,128)(2,1)}, bf16[1024,256]{1,0:T(8,128)(2,1)S(1)}, u32[]{:S(2)}, u32[]{:S(2)}) collective-permute-start(bf16[1024,256]{1,0:T(8,128)(2,1)} %grid_in.1), channel_id=1, source_target_pairs={{0,2},{1,3},{2,0},{3,1},{4,6},{5,7},{6,4},{7,5},{8,10},{9,11},{10,... | collective-permute-start | bytes 1572872 | tf_op jit(solution)/shard_map/ppermute | solution.py:23
  8.9 3.3 %collective-permute-start.2 = (bf16[1024,256]{1,0:T(8,128)(2,1)}, bf16[1024,256]{1,0:T(8,128)(2,1)S(1)}, u32[]{:S(2)}, u32[]{:S(2)}) collective-permute-start(bf16[1024,256]{1,0:T(8,128)(2,1)} %grid_in.1), channel_id=1, source_target_pairs={{0,3},{1,0},{2,1},{3,2},{4,7},{5,4},{6,5},{7,6},{8,11},{9,8},{10,9... | collective-permute-start | bytes 1572872 | tf_op jit(solution)/shard_map/ppermute | solution.py:23
  15.5 2.2 %collective-permute-done.x1 = bf16[1024,256]{1,0:T(8,128)(2,1)S(1)} collective-permute-done((bf16[1024,256]{1,0:T(8,128)(2,1)}, bf16[1024,256]{1,0:T(8,128)(2,1)S(1)}, u32[]{:S(2)}, u32[]{:S(2)}) %collective-permute-start) | collective-permute-done | bytes 524320 | tf_op jit(solution)/shard_map/ppermute | solution.py:23
  17.7 12.4 %collective-permute-done.1.x2 = bf16[1024,256]{1,0:T(8,128)(2,1)S(1)} collective-permute-done((bf16[1024,256]{1,0:T(8,128)(2,1)}, bf16[1024,256]{1,0:T(8,128)(2,1)S(1)}, u32[]{:S(2)}, u32[]{:S(2)}) %collective-permute-start.1) | collective-permute-done | bytes 524320 | tf_op jit(solution)/shard_map/ppermute | solution.py:23
  30.1 1.4 collective-permute-done.2.x3
  31.5 5.3 %grid_project.1 = (bf16[1024,256]{1,0:T(8,128)(2,1)S(1)}, bf16[1024,128]{1,0:T(8,128)(2,1)S(1)}) custom-call(s32[32]{0:T(128)S(1)} %concatenate.15.meta.refs_0_, bf16[1024,256]{1,0:T(8,128)(2,1)} %grid_in.1, bf16[1024,256]{1,0:T(8,128)(2,1)S(1)} %collective-permute-done.x1, bf16[1024,256]{1,0:T(8,128)(2,1)S(1)} %collective-permute-done.1.x2, ...), custom_call_target="tpu_custom_call" | custom-call | flops 805306368 | bytes 4194304 | tf_op jit(solution)/shard_map/grid_project/pallas_call | solution.py:106
  37.5 5.1 %collective-permute-start.6 = (bf16[1024,256]{1,0:T(8,128)(2,1)S(1)}, bf16[1024,256]{1,0:T(8,128)(2,1)S(1)}, u32[]{:S(2)}, u32[]{:S(2)}) collective-permute-start(bf16[1024,256]{1,0:T(8,128)(2,1)S(1)} %get-tuple-element.16.a1), channel_id=1, source_target_pairs={{0,8},{4,12},{8,16},{12,20},{16,24},{20,28},{24,32},{28,36},{32,40... | collective-permute-start | bytes 1572872 | tf_op jit(solution)/shard_map/ppermute | solution.py:29
  42.5 1.9 collective-permute-start.7
  45.8 1.3 pad_maximum_fusion.4
  47.1 4.4 %collective-permute-start.3 = (bf16[9,128,256]{2,1,0:T(8,128)(2,1)}, bf16[9,128,256]{2,1,0:T(8,128)(2,1)S(1)}, u32[]{:S(2)}, u32[]{:S(2)}) collective-permute-start(bf16[9,128,256]{2,1,0:T(8,128)(2,1)} %get-tuple-element.32), channel_id=1, source_target_pairs={{0,1},{1,2},{2,3},{3,0},{4,5},{5,6},{6,7},{7,4},{8,9},{9,10},{10,1... | collective-permute-start | bytes 1769480 | tf_op jit(solution)/shard_map/ppermute | solution.py:23
  51.5 3.5 %collective-permute-start.4 = (bf16[9,128,256]{2,1,0:T(8,128)(2,1)}, bf16[9,128,256]{2,1,0:T(8,128)(2,1)S(1)}, u32[]{:S(2)}, u32[]{:S(2)}) collective-permute-start(bf16[9,128,256]{2,1,0:T(8,128)(2,1)} %get-tuple-element.31), channel_id=1, source_target_pairs={{0,2},{1,3},{2,0},{3,1},{4,6},{5,7},{6,4},{7,5},{8,10},{9,11},{10,... | collective-permute-start | bytes 1769480 | tf_op jit(solution)/shard_map/ppermute | solution.py:23
  55.0 3.6 %collective-permute-start.5 = (bf16[9,128,256]{2,1,0:T(8,128)(2,1)}, bf16[9,128,256]{2,1,0:T(8,128)(2,1)S(1)}, u32[]{:S(2)}, u32[]{:S(2)}) collective-permute-start(bf16[9,128,256]{2,1,0:T(8,128)(2,1)} %get-tuple-element.30), channel_id=1, source_target_pairs={{0,3},{1,0},{2,1},{3,2},{4,7},{5,4},{6,5},{7,6},{8,11},{9,8},{10,9... | collective-permute-start | bytes 1769480 | tf_op jit(solution)/shard_map/ppermute | solution.py:23
  58.6 1.9 collective-permute-start.8
  60.6 2.4 %collective-permute-start.9 = (bf16[1024,256]{1,0:T(8,128)(2,1)S(1)}, bf16[1024,256]{1,0:T(8,128)(2,1)S(1)}, u32[]{:S(2)}, u32[]{:S(2)}) collective-permute-start(bf16[1024,256]{1,0:T(8,128)(2,1)S(1)} %broadcast_select_fusion), channel_id=1, source_target_pairs={{0,4},{4,0},{8,12},{12,8},{16,20},{20,16},{24,28},{28,24},{32,36},... | collective-permute-start | bytes 1572872 | tf_op jit(solution)/shard_map/ppermute | solution.py:34
  63.0 2.4 %collective-permute-done.3.a1.refs_3_.refs_8_ = bf16[9,128,256]{2,1,0:T(8,128)(2,1)S(1)} collective-permute-done((bf16[9,128,256]{2,1,0:T(8,128)(2,1)}, bf16[9,128,256]{2,1,0:T(8,128)(2,1)S(1)}, u32[]{:S(2)}, u32[]{:S(2)}) %collective-permute-start.3) | collective-permute-done | bytes 589856 | tf_op jit(solution)/shard_map/ppermute | solution.py:23
  65.5 13.4 %collective-permute-done.4.a2.refs_4_.refs_9_ = bf16[9,128,256]{2,1,0:T(8,128)(2,1)S(1)} collective-permute-done((bf16[9,128,256]{2,1,0:T(8,128)(2,1)}, bf16[9,128,256]{2,1,0:T(8,128)(2,1)S(1)}, u32[]{:S(2)}, u32[]{:S(2)}) %collective-permute-start.4) | collective-permute-done | bytes 589856 | tf_op jit(solution)/shard_map/ppermute | solution.py:23
  78.8 1.4 collective-permute-done.5.a3.refs_5_.refs_10_
  80.2 1.9 mesh_start.1.q
  82.2 2.1 %enc_attend.1 = bf16[4,256,128]{2,1,0:T(8,128)(2,1)S(1)} custom-call(s32[32]{0:T(128)S(1)} %concatenate.15.meta.refs_0_, s32[2,4]{1,0:T(2,128)S(1)} %copy-done.5, s32[1024]{0:T(1024)S(1)} %copy-done.4, bf16[256,128]{1,0:T(8,128)(2,1)S(1)} %mesh_start.1.q, bf16[1024,256]{1,0:T(8,128)(2,1)S(1)} %collective-permute-done.6.a0, ...), custom_call_target="tpu_custom_call" | custom-call | tf_op jit(solution)/shard_map/enc_attend/pallas_call | solution.py:211
  84.5 1.9 collective-permute-start.10
  86.5 11.5 %all_to_all.20.refs_1_ = bf16[4,256,128]{2,1,0:T(8,128)(2,1)S(1)} all-to-all(bf16[4,256,128]{2,1,0:T(8,128)(2,1)S(1)} %enc_attend.1), channel_id=1, replica_groups=mesh['nodes'=128,'mp'=4] {'mp'}, dimensions={0} | all-to-all | bytes 524288 | tf_op jit(solution)/shard_map/all_to_all | solution.py:363
  99.0 3.5 %mesh_layer.3 = (bf16[4,256,256]{2,1,0:T(8,128)(2,1)S(1)}, bf16[256,256]{1,0:T(8,128)(2,1)S(1)}, bf16[256,128]{1,0:T(8,128)(2,1)S(1)}) custom-call(s32[32]{0:T(128)S(1)} %concatenate.15.meta.refs_0_, bf16[4,256,128]{2,1,0:T(8,128)(2,1)S(1)} %all_to_all.20.refs_1_, bf16[256,256]{1,0:T(8,128)(2,1)S(1)} %copy-done.1, ...), custom_call_target="tpu_custom_call" | custom-call | tf_op jit(solution)/shard_map/mesh_layer/pallas_call | solution.py:310
  102.5 7.0 %collective-permute-start.11 = (bf16[256,256]{1,0:T(8,128)(2,1)S(1)}, bf16[256,256]{1,0:T(8,128)(2,1)S(1)}, u32[]{:S(2)}, u32[]{:S(2)}) collective-permute-start(bf16[256,256]{1,0:T(8,128)(2,1)S(1)} %get-tuple-element.21.refs_3_), channel_id=1, source_target_pairs={{0,8},{4,12},{8,16},{12,20},{16,24},{20,28},{24,32},{28,36},{32,40... | collective-permute-start | bytes 393224 | tf_op jit(solution)/shard_map/ppermute | solution.py:29
  109.5 1.9 collective-permute-start.12
  111.4 1.9 collective-permute-start.13
  113.4 6.4 %collective-permute-done.12.refs_4_ = bf16[256,256]{1,0:T(8,128)(2,1)S(1)} collective-permute-done((bf16[256,256]{1,0:T(8,128)(2,1)S(1)}, bf16[256,256]{1,0:T(8,128)(2,1)S(1)}, u32[]{:S(2)}, u32[]{:S(2)}) %collective-permute-start.12) | collective-permute-done | bytes 131104 | tf_op jit(solution)/shard_map/ppermute | solution.py:29
  119.7 1.9 collective-permute-start.14
  123.0 1.8 near_attend.3
  124.7 9.6 %all_to_all.21.refs_1_ = bf16[4,256,128]{2,1,0:T(8,128)(2,1)S(1)} all-to-all(bf16[4,256,128]{2,1,0:T(8,128)(2,1)S(1)} %near_attend.3), channel_id=1, replica_groups=mesh['nodes'=128,'mp'=4] {'mp'}, dimensions={0} | all-to-all | bytes 524288 | tf_op jit(solution)/shard_map/all_to_all | solution.py:363
  134.4 3.5 %mesh_layer.4 = (bf16[4,256,256]{2,1,0:T(8,128)(2,1)S(1)}, bf16[256,256]{1,0:T(8,128)(2,1)S(1)}, bf16[256,128]{1,0:T(8,128)(2,1)S(1)}) custom-call(s32[32]{0:T(128)S(1)} %concatenate.15.meta.refs_0_, bf16[4,256,128]{2,1,0:T(8,128)(2,1)S(1)} %all_to_all.21.refs_1_, bf16[4,256,256]{2,1,0:T(8,128)(2,1)S(1)} %get-tuple-element.22.refs_2_, ...), custom_call_target="tpu_custom_call" | custom-call | tf_op jit(solution)/shard_map/mesh_layer/pallas_call | solution.py:310
  137.9 1.9 collective-permute-start.15
  139.8 3.9 %collective-permute-start.16 = (bf16[256,256]{1,0:T(8,128)(2,1)S(1)}, bf16[256,256]{1,0:T(8,128)(2,1)S(1)}, u32[]{:S(2)}, u32[]{:S(2)}) collective-permute-start(bf16[256,256]{1,0:T(8,128)(2,1)S(1)} %get-tuple-element.24.refs_3_), channel_id=1, source_target_pairs={{8,0},{12,4},{16,8},{20,12},{24,16},{28,20},{32,24},{36,28},{40,32... | collective-permute-start | bytes 393224 | tf_op jit(solution)/shard_map/ppermute | solution.py:29
  143.7 1.9 collective-permute-start.17
  145.7 4.5 %collective-permute-done.16.refs_4_ = bf16[256,256]{1,0:T(8,128)(2,1)S(1)} collective-permute-done((bf16[256,256]{1,0:T(8,128)(2,1)S(1)}, bf16[256,256]{1,0:T(8,128)(2,1)S(1)}, u32[]{:S(2)}, u32[]{:S(2)}) %collective-permute-start.16) | collective-permute-done | bytes 131104 | tf_op jit(solution)/shard_map/ppermute | solution.py:29
  150.2 1.9 collective-permute-start.18
  153.5 1.8 near_attend.4
  155.2 9.6 %all_to_all.22.refs_1_ = bf16[4,256,128]{2,1,0:T(8,128)(2,1)S(1)} all-to-all(bf16[4,256,128]{2,1,0:T(8,128)(2,1)S(1)} %near_attend.4), channel_id=1, replica_groups=mesh['nodes'=128,'mp'=4] {'mp'}, dimensions={0} | all-to-all | bytes 524288 | tf_op jit(solution)/shard_map/all_to_all | solution.py:363
  164.9 3.6 %mesh_layer.5 = (bf16[256,256]{1,0:T(8,128)(2,1)}, bf16[256,256]{1,0:T(8,128)(2,1)S(1)}) custom-call(s32[32]{0:T(128)S(1)} %concatenate.15.meta.refs_0_, bf16[4,256,128]{2,1,0:T(8,128)(2,1)S(1)} %all_to_all.22.refs_1_, bf16[4,256,256]{2,1,0:T(8,128)(2,1)S(1)} %get-tuple-element.25.refs_2_, ...), custom_call_target="tpu_custom_call" | custom-call | tf_op jit(solution)/shard_map/mesh_layer/pallas_call | solution.py:310
  168.5 1.9 collective-permute-start.19
  170.4 3.9 %collective-permute-start.20 = (bf16[256,256]{1,0:T(8,128)(2,1)S(1)}, bf16[256,256]{1,0:T(8,128)(2,1)S(1)}, u32[]{:S(2)}, u32[]{:S(2)}) collective-permute-start(bf16[256,256]{1,0:T(8,128)(2,1)S(1)} %get-tuple-element.26.refs_3_), channel_id=1, source_target_pairs={{8,0},{12,4},{16,8},{20,12},{24,16},{28,20},{32,24},{36,28},{40,32... | collective-permute-start | bytes 393224 | tf_op jit(solution)/shard_map/ppermute | solution.py:29
  174.4 1.9 collective-permute-start.21
  176.3 4.4 %collective-permute-done.20.refs_4_ = bf16[256,256]{1,0:T(8,128)(2,1)S(1)} collective-permute-done((bf16[256,256]{1,0:T(8,128)(2,1)S(1)}, bf16[256,256]{1,0:T(8,128)(2,1)S(1)}, u32[]{:S(2)}, u32[]{:S(2)}) %collective-permute-start.20) | collective-permute-done | bytes 131104 | tf_op jit(solution)/shard_map/ppermute | solution.py:29
  180.8 1.9 collective-permute-start.22
  184.0 2.7 %near_attend.5 = bf16[4,1024,128]{2,1,0:T(8,128)(2,1)} custom-call(s32[32]{0:T(128)S(1)} %concatenate.15.meta.refs_0_, bf16[1024,128]{1,0:T(8,128)(2,1)S(1)} %copy-done.3, bf16[256,256]{1,0:T(8,128)(2,1)S(1)} %collective-permute-done.19.refs_2_, bf16[256,256]{1,0:T(8,128)(2,1)S(1)} %get-tuple-element.26.refs_3_, ...), custom_call_target="tpu_custom_call" | custom-call | tf_op jit(solution)/shard_map/near_attend/pallas_call | solution.py:239
  186.7 3.6 %all-to-all-start.3 = ((bf16[4,1024,128]{2,1,0:T(8,128)(2,1)}), bf16[4,1024,128]{2,1,0:T(8,128)(2,1)S(1)}, u32[]{:S(2)}, u32[]{:S(2)}) async-start(bf16[4,1024,128]{2,1,0:T(8,128)(2,1)} %near_attend.5), calls=%async_computation.3 | async-start | bytes 2097152 | tf_op jit(solution)/shard_map/all_to_all | solution.py:363
  191.3 14.7 %all-to-all-done.3.o = bf16[4,1024,128]{2,1,0:T(8,128)(2,1)S(1)} async-done(((bf16[4,1024,128]{2,1,0:T(8,128)(2,1)}), bf16[4,1024,128]{2,1,0:T(8,128)(2,1)S(1)}, u32[]{:S(2)}, u32[]{:S(2)}) %all-to-all-start.3) | async-done | bytes 1048608 | tf_op jit(solution)/shard_map/all_to_all | solution.py:363
  206.0 2.0 grid_final.1
  (54 shorter events, 11.3 us)
Async XLA Ops:
  0.6 17.1 %collective-permute-start = (bf16[1024,256]{1,0:T(8,128)(2,1)}, bf16[1024,256]{1,0:T(8,128)(2,1)S(1)}, u32[]{:S(2)}, u32[]{:S(2)}) collective-permute-start(bf16[1024,256]{1,0:T(8,128)(2,1)} %grid_in.1), channel_id=1, source_target_pairs={{0,1},{1,2},{2,3},{3,0},{4,5},{5,6},{6,7},{7,4},{8,9},{9,10},{10,1... | collective-permute-start | bytes 1572872 | tf_op jit(solution)/shard_map/ppermute | solution.py:23
  4.1 26.0 %collective-permute-start.1 = (bf16[1024,256]{1,0:T(8,128)(2,1)}, bf16[1024,256]{1,0:T(8,128)(2,1)S(1)}, u32[]{:S(2)}, u32[]{:S(2)}) collective-permute-start(bf16[1024,256]{1,0:T(8,128)(2,1)} %grid_in.1), channel_id=1, source_target_pairs={{0,2},{1,3},{2,0},{3,1},{4,6},{5,7},{6,4},{7,5},{8,10},{9,11},{10,... | collective-permute-start | bytes 1572872 | tf_op jit(solution)/shard_map/ppermute | solution.py:23
  8.9 22.5 %collective-permute-start.2 = (bf16[1024,256]{1,0:T(8,128)(2,1)}, bf16[1024,256]{1,0:T(8,128)(2,1)S(1)}, u32[]{:S(2)}, u32[]{:S(2)}) collective-permute-start(bf16[1024,256]{1,0:T(8,128)(2,1)} %grid_in.1), channel_id=1, source_target_pairs={{0,3},{1,0},{2,1},{3,2},{4,7},{5,4},{6,5},{7,6},{8,11},{9,8},{10,9... | collective-permute-start | bytes 1572872 | tf_op jit(solution)/shard_map/ppermute | solution.py:23
  36.8 0.7 copy-start.2
  37.5 7.1 %slice-start.1 = ((bf16[4,128,1024]{2,1,0:T(8,128)(2,1)}), bf16[1,128,1024]{2,1,0:T(8,128)(2,1)S(1)}, s32[]{:S(2)}) async-start(bf16[4,128,1024]{2,1,0:T(8,128)(2,1)} %refs_7_.5), calls=%async_computation.5 | async-start | bytes 524288 | tf_op jit(solution)/shard_map/slice | solution.py:403
  37.5 21.1 %collective-permute-start.6 = (bf16[1024,256]{1,0:T(8,128)(2,1)S(1)}, bf16[1024,256]{1,0:T(8,128)(2,1)S(1)}, u32[]{:S(2)}, u32[]{:S(2)}) collective-permute-start(bf16[1024,256]{1,0:T(8,128)(2,1)S(1)} %get-tuple-element.16.a1), channel_id=1, source_target_pairs={{0,8},{4,12},{8,16},{12,20},{16,24},{20,28},{24,32},{28,36},{32,40... | collective-permute-start | bytes 1572872 | tf_op jit(solution)/shard_map/ppermute | solution.py:29
  42.5 18.0 %collective-permute-start.7 = (bf16[1024,256]{1,0:T(8,128)(2,1)S(1)}, bf16[1024,256]{1,0:T(8,128)(2,1)S(1)}, u32[]{:S(2)}, u32[]{:S(2)}) collective-permute-start(bf16[1024,256]{1,0:T(8,128)(2,1)S(1)} %get-tuple-element.16.a1), channel_id=1, source_target_pairs={{8,0},{12,4},{16,8},{20,12},{24,16},{28,20},{32,24},{36,28},{40,32... | collective-permute-start | bytes 1572872 | tf_op jit(solution)/shard_map/ppermute | solution.py:29
  44.5 1.2 slice-start
  44.5 1.2 copy-start.1
  47.1 18.4 %collective-permute-start.3 = (bf16[9,128,256]{2,1,0:T(8,128)(2,1)}, bf16[9,128,256]{2,1,0:T(8,128)(2,1)S(1)}, u32[]{:S(2)}, u32[]{:S(2)}) collective-permute-start(bf16[9,128,256]{2,1,0:T(8,128)(2,1)} %get-tuple-element.32), channel_id=1, source_target_pairs={{0,1},{1,2},{2,3},{3,0},{4,5},{5,6},{6,7},{7,4},{8,9},{9,10},{10,1... | collective-permute-start | bytes 1769480 | tf_op jit(solution)/shard_map/ppermute | solution.py:23
  51.5 27.4 %collective-permute-start.4 = (bf16[9,128,256]{2,1,0:T(8,128)(2,1)}, bf16[9,128,256]{2,1,0:T(8,128)(2,1)S(1)}, u32[]{:S(2)}, u32[]{:S(2)}) collective-permute-start(bf16[9,128,256]{2,1,0:T(8,128)(2,1)} %get-tuple-element.31), channel_id=1, source_target_pairs={{0,2},{1,3},{2,0},{3,1},{4,6},{5,7},{6,4},{7,5},{8,10},{9,11},{10,... | collective-permute-start | bytes 1769480 | tf_op jit(solution)/shard_map/ppermute | solution.py:23
  55.0 25.2 %collective-permute-start.5 = (bf16[9,128,256]{2,1,0:T(8,128)(2,1)}, bf16[9,128,256]{2,1,0:T(8,128)(2,1)S(1)}, u32[]{:S(2)}, u32[]{:S(2)}) collective-permute-start(bf16[9,128,256]{2,1,0:T(8,128)(2,1)} %get-tuple-element.30), channel_id=1, source_target_pairs={{0,3},{1,0},{2,1},{3,2},{4,7},{5,4},{6,5},{7,6},{8,11},{9,8},{10,9... | collective-permute-start | bytes 1769480 | tf_op jit(solution)/shard_map/ppermute | solution.py:23
  58.6 23.6 %collective-permute-start.8 = (bf16[1024,256]{1,0:T(8,128)(2,1)S(1)}, bf16[1024,256]{1,0:T(8,128)(2,1)S(1)}, u32[]{:S(2)}, u32[]{:S(2)}) collective-permute-start(bf16[1024,256]{1,0:T(8,128)(2,1)S(1)} %get-tuple-element.16.a1), channel_id=1, source_target_pairs={{0,4},{4,0},{8,12},{12,8},{16,20},{20,16},{24,28},{28,24},{32,36},... | collective-permute-start | bytes 1572872 | tf_op jit(solution)/shard_map/ppermute | solution.py:34
  60.6 21.6 %copy-start.4 = (s32[1024]{0:T(1024)S(1)}, s32[1024]{0:T(1024)}, u32[]{:S(2)}) copy-start(s32[1024]{0:T(1024)} %counts.3) | copy-start | bytes 12292
  60.6 21.6 %copy-start.5 = (s32[2,4]{1,0:T(2,128)S(1)}, s32[2,4]{1,0:T(2,128)}, u32[]{:S(2)}) copy-start(s32[2,4]{1,0:T(2,128)} %listed.1) | copy-start | bytes 100
  60.6 21.5 %collective-permute-start.9 = (bf16[1024,256]{1,0:T(8,128)(2,1)S(1)}, bf16[1024,256]{1,0:T(8,128)(2,1)S(1)}, u32[]{:S(2)}, u32[]{:S(2)}) collective-permute-start(bf16[1024,256]{1,0:T(8,128)(2,1)S(1)} %broadcast_select_fusion), channel_id=1, source_target_pairs={{0,4},{4,0},{8,12},{12,8},{16,20},{20,16},{24,28},{28,24},{32,36},... | collective-permute-start | bytes 1572872 | tf_op jit(solution)/shard_map/ppermute | solution.py:34
  84.5 13.5 %collective-permute-start.10 = (bf16[3,6,128,256]{3,2,1,0:T(8,128)(2,1)S(1)}, bf16[3,6,128,256]{3,2,1,0:T(8,128)(2,1)S(1)}, u32[]{:S(2)}, u32[]{:S(2)}) collective-permute-start(bf16[3,6,128,256]{3,2,1,0:T(8,128)(2,1)S(1)} %pad_maximum_fusion), channel_id=1, source_target_pairs={{0,4},{4,0},{8,12},{12,8},{16,20},{20,16},{24,28},{28,24},{32,36},... | collective-permute-start | bytes 3538952 | tf_op jit(solution)/shard_map/ppermute | solution.py:34
  98.0 1.0 copy-start.6
  102.5 10.8 %collective-permute-start.11 = (bf16[256,256]{1,0:T(8,128)(2,1)S(1)}, bf16[256,256]{1,0:T(8,128)(2,1)S(1)}, u32[]{:S(2)}, u32[]{:S(2)}) collective-permute-start(bf16[256,256]{1,0:T(8,128)(2,1)S(1)} %get-tuple-element.21.refs_3_), channel_id=1, source_target_pairs={{0,8},{4,12},{8,16},{12,20},{16,24},{20,28},{24,32},{28,36},{32,40... | collective-permute-start | bytes 393224 | tf_op jit(solution)/shard_map/ppermute | solution.py:29
  109.5 10.2 %collective-permute-start.12 = (bf16[256,256]{1,0:T(8,128)(2,1)S(1)}, bf16[256,256]{1,0:T(8,128)(2,1)S(1)}, u32[]{:S(2)}, u32[]{:S(2)}) collective-permute-start(bf16[256,256]{1,0:T(8,128)(2,1)S(1)} %get-tuple-element.21.refs_3_), channel_id=1, source_target_pairs={{8,0},{12,4},{16,8},{20,12},{24,16},{28,20},{32,24},{36,28},{40,32... | collective-permute-start | bytes 393224 | tf_op jit(solution)/shard_map/ppermute | solution.py:29
  111.4 10.3 %collective-permute-start.13 = (bf16[256,256]{1,0:T(8,128)(2,1)S(1)}, bf16[256,256]{1,0:T(8,128)(2,1)S(1)}, u32[]{:S(2)}, u32[]{:S(2)}) collective-permute-start(bf16[256,256]{1,0:T(8,128)(2,1)S(1)} %get-tuple-element.21.refs_3_), channel_id=1, source_target_pairs={{0,4},{4,0},{8,12},{12,8},{16,20},{20,16},{24,28},{28,24},{32,36},... | collective-permute-start | bytes 393224 | tf_op jit(solution)/shard_map/ppermute | solution.py:34
  119.7 3.2 %collective-permute-start.14 = (bf16[256,256]{1,0:T(8,128)(2,1)S(1)}, bf16[256,256]{1,0:T(8,128)(2,1)S(1)}, u32[]{:S(2)}, u32[]{:S(2)}) collective-permute-start(bf16[256,256]{1,0:T(8,128)(2,1)S(1)} %broadcast_select_fusion.3), channel_id=1, source_target_pairs={{0,4},{4,0},{8,12},{12,8},{16,20},{20,16},{24,28},{28,24},{32,36},... | collective-permute-start | bytes 393224 | tf_op jit(solution)/shard_map/ppermute | solution.py:34
  137.9 7.8 %collective-permute-start.15 = (bf16[256,256]{1,0:T(8,128)(2,1)S(1)}, bf16[256,256]{1,0:T(8,128)(2,1)S(1)}, u32[]{:S(2)}, u32[]{:S(2)}) collective-permute-start(bf16[256,256]{1,0:T(8,128)(2,1)S(1)} %get-tuple-element.24.refs_3_), channel_id=1, source_target_pairs={{0,8},{4,12},{8,16},{12,20},{16,24},{20,28},{24,32},{28,36},{32,40... | collective-permute-start | bytes 393224 | tf_op jit(solution)/shard_map/ppermute | solution.py:29
  139.8 10.4 %collective-permute-start.16 = (bf16[256,256]{1,0:T(8,128)(2,1)S(1)}, bf16[256,256]{1,0:T(8,128)(2,1)S(1)}, u32[]{:S(2)}, u32[]{:S(2)}) collective-permute-start(bf16[256,256]{1,0:T(8,128)(2,1)S(1)} %get-tuple-element.24.refs_3_), channel_id=1, source_target_pairs={{8,0},{12,4},{16,8},{20,12},{24,16},{28,20},{32,24},{36,28},{40,32... | collective-permute-start | bytes 393224 | tf_op jit(solution)/shard_map/ppermute | solution.py:29
  143.7 8.4 %collective-permute-start.17 = (bf16[256,256]{1,0:T(8,128)(2,1)S(1)}, bf16[256,256]{1,0:T(8,128)(2,1)S(1)}, u32[]{:S(2)}, u32[]{:S(2)}) collective-permute-start(bf16[256,256]{1,0:T(8,128)(2,1)S(1)} %get-tuple-element.24.refs_3_), channel_id=1, source_target_pairs={{0,4},{4,0},{8,12},{12,8},{16,20},{20,16},{24,28},{28,24},{32,36},... | collective-permute-start | bytes 393224 | tf_op jit(solution)/shard_map/ppermute | solution.py:34
  150.2 3.2 %collective-permute-start.18 = (bf16[256,256]{1,0:T(8,128)(2,1)S(1)}, bf16[256,256]{1,0:T(8,128)(2,1)S(1)}, u32[]{:S(2)}, u32[]{:S(2)}) collective-permute-start(bf16[256,256]{1,0:T(8,128)(2,1)S(1)} %broadcast_select_fusion.2), channel_id=1, source_target_pairs={{0,4},{4,0},{8,12},{12,8},{16,20},{20,16},{24,28},{28,24},{32,36},... | collective-permute-start | bytes 393224 | tf_op jit(solution)/shard_map/ppermute | solution.py:34
  164.9 19.1 %copy-start.3 = (bf16[1024,128]{1,0:T(8,128)(2,1)S(1)}, bf16[1024,128]{1,0:T(8,128)(2,1)}, u32[]{:S(2)}) copy-start(bf16[1024,128]{1,0:T(8,128)(2,1)} %copy-done.2) | copy-start | bytes 786436
  168.5 7.8 %collective-permute-start.19 = (bf16[256,256]{1,0:T(8,128)(2,1)S(1)}, bf16[256,256]{1,0:T(8,128)(2,1)S(1)}, u32[]{:S(2)}, u32[]{:S(2)}) collective-permute-start(bf16[256,256]{1,0:T(8,128)(2,1)S(1)} %get-tuple-element.26.refs_3_), channel_id=1, source_target_pairs={{0,8},{4,12},{8,16},{12,20},{16,24},{20,28},{24,32},{28,36},{32,40... | collective-permute-start | bytes 393224 | tf_op jit(solution)/shard_map/ppermute | solution.py:29
  170.4 10.3 %collective-permute-start.20 = (bf16[256,256]{1,0:T(8,128)(2,1)S(1)}, bf16[256,256]{1,0:T(8,128)(2,1)S(1)}, u32[]{:S(2)}, u32[]{:S(2)}) collective-permute-start(bf16[256,256]{1,0:T(8,128)(2,1)S(1)} %get-tuple-element.26.refs_3_), channel_id=1, source_target_pairs={{8,0},{12,4},{16,8},{20,12},{24,16},{28,20},{32,24},{36,28},{40,32... | collective-permute-start | bytes 393224 | tf_op jit(solution)/shard_map/ppermute | solution.py:29
  174.4 8.3 %collective-permute-start.21 = (bf16[256,256]{1,0:T(8,128)(2,1)S(1)}, bf16[256,256]{1,0:T(8,128)(2,1)S(1)}, u32[]{:S(2)}, u32[]{:S(2)}) collective-permute-start(bf16[256,256]{1,0:T(8,128)(2,1)S(1)} %get-tuple-element.26.refs_3_), channel_id=1, source_target_pairs={{0,4},{4,0},{8,12},{12,8},{16,20},{20,16},{24,28},{28,24},{32,36},... | collective-permute-start | bytes 393224 | tf_op jit(solution)/shard_map/ppermute | solution.py:34
  180.8 3.2 %collective-permute-start.22 = (bf16[256,256]{1,0:T(8,128)(2,1)S(1)}, bf16[256,256]{1,0:T(8,128)(2,1)S(1)}, u32[]{:S(2)}, u32[]{:S(2)}) collective-permute-start(bf16[256,256]{1,0:T(8,128)(2,1)S(1)} %broadcast_select_fusion.1), channel_id=1, source_target_pairs={{0,4},{4,0},{8,12},{12,8},{16,20},{20,16},{24,28},{28,24},{32,36},... | collective-permute-start | bytes 393224 | tf_op jit(solution)/shard_map/ppermute | solution.py:34
  186.7 19.3 %copy-start = (bf16[1024,256]{1,0:T(8,128)(2,1)S(1)}, bf16[1024,256]{1,0:T(8,128)(2,1)}, u32[]{:S(2)}) copy-start(bf16[1024,256]{1,0:T(8,128)(2,1)} %grid_in.1) | copy-start | bytes 1572868
  186.7 19.3 %all-to-all-start.3 = ((bf16[4,1024,128]{2,1,0:T(8,128)(2,1)}), bf16[4,1024,128]{2,1,0:T(8,128)(2,1)S(1)}, u32[]{:S(2)}, u32[]{:S(2)}) async-start(bf16[4,1024,128]{2,1,0:T(8,128)(2,1)} %near_attend.5), calls=%async_computation.3 | async-start | bytes 2097152 | tf_op jit(solution)/shard_map/all_to_all | solution.py:363

commit v4 on v3

--- a/solution.py
+++ b/solution.py
@@ -71,8 +71,9 @@
     return jnp.dot(a, b, preferred_element_type=F32)
 
 
-def grid_kernel(meta, x0, x1, x2, x3, gains, w_k, w_v, w_q, kv_out, q_out, kept, sems):
-    copies = copies_of([(w_k, 0), (w_v, 0), (w_q, 3)], kept, sems)
+def grid_kernel(gain_row, count, layer_index, meta, x0, x1, x2, x3, gains, *rest):
+    weights, (out, kept, sems) = rest[:count], rest[count:]
+    copies = copies_of([(w, layer_index) for w in weights], kept, sems)
 
     @pl.when(pl.program_id(0) == 0)
     def _():
@@ -86,42 +87,38 @@
         for copy in copies:
             copy.wait()
 
-    kv = q = None
+    total = None
     for k in range(MP):
         src = source(meta, k)
         at = pl.ds(pl.multiple_of(src * 256, 256), 256)
-        for_kv = (rows[k] * gains[1, pl.ds(src, 1), :]).astype(BF16)
-        for_q = (rows[k] * gains[4, pl.ds(src, 1), :]).astype(BF16)
-        kv_part = dot(for_kv, jnp.concatenate([kept[0, at, :], kept[1, at, :]], axis=1))
-        q_part = dot(for_q, kept[2, at, :])
-        kv = kv_part if kv is None else kv + kv_part
-        q = q_part if q is None else q + q_part
-    kv_out[...] = kv.astype(BF16)
-    q_out[...] = q.astype(BF16)
-
-
-def grid_project(meta, pieces, gains, w_k, w_v, w_q):
+        row = (rows[k] * gains[gain_row, pl.ds(src, 1), :]).astype(BF16)
+        part = dot(row, jnp.concatenate([kept[i, at, :] for i in range(count)], axis=1))
+        total = part if total is None else total + part
+    out[...] = total.astype(BF16)
+
+
+def grid_project(gain_row, layer_index, meta, pieces, gains, *weights):
+    count = len(weights)
+
+    def body(*refs):
+        grid_kernel(gain_row, count, layer_index, *refs)
+
     rows = pieces[0].shape[0]
     tile = 256
     return pl.pallas_call(
-        grid_kernel,
+        body,
         grid=(rows // tile,),
         in_specs=[smem()]
         + [pl.BlockSpec((tile, 256), lambda i: (i, 0))] * MP
-        + [vmem(), hbm(), hbm(), hbm()],
-        out_specs=[
-            pl.BlockSpec((tile, 256), lambda i: (i, 0)),
-            pl.BlockSpec((tile, 128), lambda i: (i, 0)),
-        ],
-        out_shape=[
-            jax.ShapeDtypeStruct((rows, 256), BF16),
-            jax.ShapeDtypeStruct((rows, 128), BF16),
-        ],
-        scratch_shapes=[pltpu.VMEM((3, 1024, 128), BF16), pltpu.SemaphoreType.DMA((3,))],
-        cost_estimate=pl.CostEstimate(flops=rows * 1024 * 384 * 2, transcendentals=0, bytes_accessed=rows * 4096),
+        + [vmem()]
+        + [hbm()] * count,
+        out_specs=pl.BlockSpec((tile, 128 * count), lambda i: (i, 0)),
+        out_shape=jax.ShapeDtypeStruct((rows, 128 * count), BF16),
+        scratch_shapes=[pltpu.VMEM((count, 1024, 128), BF16), pltpu.SemaphoreType.DMA((count,))],
+        cost_estimate=pl.CostEstimate(flops=rows * 1024 * 128 * count * 2, transcendentals=0, bytes_accessed=rows * 4096),
         compiler_params=PARAMS,
         name="grid_project",
-    )(meta, *pieces, gains, w_k, w_v, w_q)
+    )(meta, *pieces, gains, *weights)
 
 
 def mesh_kernel(meta, x0, a1, a2, a3, gains, w_q, q_out, kept, sems):
@@ -212,7 +209,7 @@
         enc_kernel,
         in_specs=[smem(), smem(), smem()] + [vmem()] * 6,
         out_specs=vmem(),
-        out_shape=jax.ShapeDtypeStruct((MP,) + q.shape, BF16),
+        out_shape=pltpu.HBM((MP,) + q.shape, BF16),
         scratch_shapes=[pltpu.VMEM((8, BLOCK, 256), BF16)],
         compiler_params=PARAMS,
         name="enc_attend",
@@ -247,59 +244,129 @@
     )(meta, q, *windows)
 
 
-def layer_kernel(index, gain_row, meta, o, state, a1, a2, a3, gains, w_own, b1, b2, b3, other, w_k, w_v, w_q, *rest):
-    last = index == 2
-    state_out, kv_out = rest[0], rest[1]
-    new, w_out, kept, w_sems, sems = rest[2 + (not last) :]
+def prepare_kernel(index, meta, w_own, a1, a2, a3, other, *rest):
+    weights = rest[:-4]
+    w_out, w_next, w_sems, sems = rest[-4:]
     core = meta[1] % 2
-    for g in range(MP):
+    copies = [
         pltpu.make_async_copy(
             w_own.at[index, :, g * 256 : (g + 1) * 256], w_out.at[g, 0:BLOCK, :], w_sems.at[g, 0]
-        ).start()
+        )
+        for g in range(MP)
+    ]
     for part in range(2):
         at = index + 3 * part
-        for k, b in enumerate((b1, b2, b3)):
+        for k, a in enumerate((a1, a2, a3)):
             rows = w_out.at[2 * core + part, (k + 1) * BLOCK : (k + 2) * BLOCK, :]
-            pltpu.make_async_copy(b.at[2 + at], rows, w_sems.at[2 * core + part, k + 1]).start()
+            copies.append(pltpu.make_async_copy(a.at[2 + at], rows, w_sems.at[part, k + 1]))
             rows = w_out.at[2 * (1 - core) + part, (k + 1) * BLOCK : (k + 2) * BLOCK, :]
-            pltpu.make_async_copy(other.at[k, at], rows, w_sems.at[2 * (1 - core) + part, k + 1]).start()
-    weights = (w_k, w_v) if last else (w_k, w_v, w_q)
-    copies = copies_of([(w, index + 1) for w in weights], kept, sems)
+            copies.append(pltpu.make_async_copy(other.at[k, at], rows, w_sems.at[2 + part, k + 1]))
+    for i, w in enumerate(weights):
+        copies.append(
+            pltpu.make_async_copy(w.at[index + 1], w_next.at[:, i * 128 : (i + 1) * 128], sems.at[i])
+        )
     for copy in copies:
         copy.start()
-    if index == 0:
-        new[meta[0]] = state[...]
-        for k, a in enumerate((a1, a2, a3)):
-            new[source(meta, k + 1)] = a[...].reshape(2 * BLOCK, 256)
-        state = new
-    heads = jnp.concatenate([o[source(meta, k)] for k in range(MP)], axis=1)
-    for g in range(MP):
-        for k in range(MP):
-            rows = w_out.at[g, k * BLOCK : (k + 1) * BLOCK, :]
-            pltpu.make_async_copy(other.at[0, 0], rows, w_sems.at[g, k]).wait()
-        new[g] = (state[g].astype(F32) + dot(heads, w_out[g])).astype(BF16)
-    if last:
-        state_out[...] = new[meta[0]]
-    else:
-        for g in range(MP):
-            state_out[g] = new[g]
+    for copy in copies:
+        copy.wait()
+
+
+def prepare(index, meta, w_own, fetched, other, weights):
+    def body(*refs):
+        prepare_kernel(index, *refs)
+
+    operands = (w_own, *fetched, other, *weights)
+    return pl.pallas_call(
+        body,
+        in_specs=[smem()] + [pl.BlockSpec(memory_space=pl.ANY)] * len(operands),
+        out_specs=[vmem(), vmem()],
+        out_shape=[
+            jax.ShapeDtypeStruct((MP, 4 * BLOCK, 256), BF16),
+            jax.ShapeDtypeStruct((1024, 128 * len(weights)), BF16),
+        ],
+        scratch_shapes=[pltpu.SemaphoreType.DMA((MP, MP)), pltpu.SemaphoreType.DMA((3,))],
+        compiler_params=PARAMS,
+        name="layer_weights",
+    )(meta, *operands)
+
+
+def finish_layer(gain_row, gains, new, w_next):
     rows = normed([new[g] for g in range(MP)])
     row = jnp.concatenate(
         [(rows[g] * gains[gain_row, g : g + 1, :]).astype(BF16) for g in range(MP)], axis=1
     )
+    return dot(row, w_next()).astype(BF16)
+
+
+def first_layer_kernel(meta, o, state, gains, w_own, a1, a2, a3, other, w_k, w_v, w_q, *rest):
+    new, kv_out, q_out, kept, sems = rest
+    copies = copies_of([(w_k, 1), (w_v, 1), (w_q, 1)], kept, sems)
     for copy in copies:
-        copy.wait()
-    result = dot(row, jnp.concatenate([kept[i] for i in range(len(weights))], axis=1)).astype(BF16)
+        copy.start()
+    heads = jnp.concatenate([o[source(meta, k)] for k in range(MP)], axis=1)
+    new[meta[0]] = state[...]
+    for k, a in enumerate((a1, a2, a3)):
+        new[source(meta, k + 1)] = a[0:2].reshape(2 * BLOCK, 256)
+    core = meta[1] % 2
+    for part in range(4):
+        at = 3 * (part % 2)
+        if part < 2:
+            g = 2 * core + part
+            fetched = [a[2 + at] for a in (a1, a2, a3)]
+        else:
+            g = 2 * (1 - core) + part - 2
+            fetched = [other[k, at] for k in range(MP - 1)]
+        own = w_own[0, :, pl.ds(pl.multiple_of(g * 256, 256), 256)]
+        new[g] = (new[g].astype(F32) + dot(heads, jnp.concatenate([own] + fetched, axis=0))).astype(BF16)
+
+    def w_next():
+        for copy in copies:
+            copy.wait()
+        return jnp.concatenate([kept[i] for i in range(3)], axis=1)
+
+    result = finish_layer(2, gains, new, w_next)
+    kv_out[...] = result[:, :256]
+    q_out[...] = result[:, 256:]
+
+
+def first_layer(meta, o, state, gains, w_own, fetched, other, weights):
+    rows = o.shape[1]
+    return pl.pallas_call(
+        first_layer_kernel,
+        in_specs=[smem()] + [vmem()] * 8 + [hbm()] * 3,
+        out_specs=[vmem()] * 3,
+        out_shape=[
+            jax.ShapeDtypeStruct((MP, rows, 256), BF16),
+            jax.ShapeDtypeStruct((rows, 256), BF16),
+            jax.ShapeDtypeStruct((rows, 128), BF16),
+        ],
+        scratch_shapes=[pltpu.VMEM((3, 1024, 128), BF16), pltpu.SemaphoreType.DMA((3,))],
+        compiler_params=PARAMS,
+        name="first_layer",
+    )(meta, o, state, gains, w_own, *fetched, other, *weights)
+
+
+def layer_kernel(gain_row, meta, o, state, gains, w_out, w_next, *rest):
+    last = gain_row == 5
+    state_out, kv_out, new = rest[0], rest[1], rest[-1]
+    heads = jnp.concatenate([o[source(meta, k)] for k in range(MP)], axis=1)
+    for g in range(MP):
+        new[g] = (state[g].astype(F32) + dot(heads, w_out[g])).astype(BF16)
+        if not last:
+            state_out[g] = new[g]
+    if last:
+        state_out[...] = new[meta[0]]
+    result = finish_layer(gain_row, gains, new, lambda: w_next[...])
     kv_out[...] = result[:, :256]
     if not last:
         rest[2][...] = result[:, 256:]
 
 
-def layer(index, gain_row, meta, o, state, w_own, fetched, other, gains, w_key, w_value, w_query):
+def layer(gain_row, meta, o, state, gains, prepared):
     def body(*refs):
-        layer_kernel(index, gain_row, *refs)
-
-    last = index == 2
+        layer_kernel(gain_row, *refs)
+
+    last = gain_row == 5
     rows = o.shape[1]
     shapes = [
         jax.ShapeDtypeStruct((rows, 256) if last else (MP, rows, 256), BF16),
@@ -309,23 +376,13 @@
         shapes.append(jax.ShapeDtypeStruct((rows, 128), BF16))
     return pl.pallas_call(
         body,
-        grid=(1,),
-        in_specs=[smem(), vmem(), vmem()]
-        + [pl.BlockSpec((2, BLOCK, 256), lambda i: (0, 0, 0))] * 3
-        + [vmem()]
-        + [hbm()] * 8,
+        in_specs=[smem()] + [vmem()] * 5,
         out_specs=[vmem()] * len(shapes),
         out_shape=shapes,
-        scratch_shapes=[
-            pltpu.VMEM((MP, rows, 256), BF16),
-            pltpu.VMEM((MP, 4 * BLOCK, 256), BF16),
-            pltpu.VMEM((3, 1024, 128), BF16),
-            pltpu.SemaphoreType.DMA((MP, MP)),
-            pltpu.SemaphoreType.DMA((3,)),
-        ],
+        scratch_shapes=[pltpu.VMEM((MP, rows, 256), BF16)],
         compiler_params=PARAMS,
         name="mesh_layer",
-    )(meta, o, state, *fetched, gains, w_own, *fetched, other, w_key, w_value, w_query)
+    )(meta, o, state, gains, *prepared)
 
 
 def final_kernel(meta, counts, o, w_out, grid_in, out):
@@ -405,15 +462,15 @@
     sent[0] = sent[1]
     arrived = gathered(sent, "w")[1:]
 
-    kv, grid_q = grid_project(meta, grid_pieces, gains, w_key, w_value, w_query)
+    kv = grid_project(1, 0, meta, grid_pieces, gains, w_key, w_value)
     grid_windows = window(kv)
+    grid_q = grid_project(4, 3, meta, grid_pieces, gains, w_query)
+    w_own = pltpu.with_memory_space_constraint(w_out, pltpu.HBM)
     mesh_q = mesh_start(meta, mesh_in, arrived, gains, w_query)
     o = enc_attend(meta, enc_list, grid_count, mesh_q, grid_windows)
 
     arrived = lax.optimization_barrier((*arrived, o))[:3]
     other = swap_cores(jnp.stack([a[2:8] for a in arrived]))
-    other = pltpu.with_memory_space_constraint(other, pltpu.HBM)
-    w_own = pltpu.with_memory_space_constraint(w_out, pltpu.HBM)
     w_last = jnp.concatenate(
         [lax.dynamic_slice_in_dim(w_out[3:], own_mp * 256, 256, axis=2)] + [a[8:] for a in arrived], axis=0
     ).reshape(512, 256)
@@ -421,12 +478,15 @@
     state = mesh_in
     for index in range(3):
         heads = gather_heads(o)
-        made = layer(
-            index, index + 2 if index < 2 else 5, meta, heads, state, w_own, arrived, other, gains, w_key, w_value, w_query
-        )
+        if index == 0:
+            made = first_layer(meta, heads, state, gains, w_out, arrived, other, (w_key, w_value, w_query))
+        else:
+            made = layer(3 if index == 1 else 5, meta, heads, state, gains, prepared)
         state, kv = made[0], made[1]
         near = window(kv)
         if index < 2:
+            weights = (w_key, w_value, w_query) if index == 0 else (w_key, w_value)
+            prepared = prepare(index + 1, meta, w_own, arrived, other, weights)
             o = near_attend(PROC0, 3, meta, made[2], near)
     o = near_attend(DEC0, 2, meta, grid_q, near)
     heads = gather_heads(o)

time: 209 us -> 222 us (1.062)
  the two profiles are of different devices: /device:TPU:102 before, /device:TPU:230 now
where the time goes in v4:
time: 222 us; the launch traced here: 220 us
  starting transfers between devices  80 us (36%)
  waiting for transfers between devices  70.6 us (32%)
  Pallas kernels  37.2 us (17%)
  local copies, waits for them, and re-layouts  14.5 us (7%)
  blocking collectives  11.5 us (5%)
  other arithmetic  4.55 us (2%)
    ppermute x6, waiting for transfers between devices, shift_mp(): return lax.ppermute(value, 'mp', [(s, (s + steps) % MP) for s in range(MP)])  32.1 us
    ppermute x8, starting transfers between devices, from_node(): return lax.ppermute(value, 'nodes', pairs)  27.5 us
    ppermute x6, starting transfers between devices, shift_mp(): return lax.ppermute(value, 'mp', [(s, (s + steps) % MP) for s in range(MP)])  23 us
    all_to_all x3, waiting for transfers between devices, gather_heads(): return lax.all_to_all(copies, 'mp', split_axis=0, concat_axis=0, tiled=True)  20.6 us
    ppermute x9, starting transfers between devices, swap_cores(): return lax.ppermute(value, 'nodes', [(s, s ^ 1) for s in range(count)])  17.6 us
    ppermute x8, waiting for transfers between devices, from_node(): return lax.ppermute(value, 'nodes', pairs)  15.3 us
    unnamed x46, local copies, waits for them, and re-layouts  12.1 us
    all_to_all x3, starting transfers between devices, gather_heads(): return lax.all_to_all(copies, 'mp', split_axis=0, concat_axis=0, tiled=True)  11.8 us
  transfers between devices with their start and end apart: 26, of which 15 were waited for; matrix products, arithmetic and copies ran while one was open for 3% of the time, Pallas kernels for 6%

profile of v4, /device:TPU:230, one launch (start us, length us, event | category | flops | bytes accessed | tf_op | source)
XLA Modules:
  0.0 219.7 jit_solution(752187528574622249)
XLA Ops:
  0.6 3.5 %collective-permute-start = (bf16[1024,256]{1,0:T(8,128)(2,1)}, bf16[1024,256]{1,0:T(8,128)(2,1)S(1)}, u32[]{:S(2)}, u32[]{:S(2)}) collective-permute-start(bf16[1024,256]{1,0:T(8,128)(2,1)} %grid_in.1), channel_id=1, source_target_pairs={{0,1},{1,2},{2,3},{3,0},{4,5},{5,6},{6,7},{7,4},{8,9},{9,10},{10,1... | collective-permute-start | bytes 1572872 | tf_op jit(solution)/shard_map/ppermute | solution.py:23
  4.1 4.8 %collective-permute-start.1 = (bf16[1024,256]{1,0:T(8,128)(2,1)}, bf16[1024,256]{1,0:T(8,128)(2,1)S(1)}, u32[]{:S(2)}, u32[]{:S(2)}) collective-permute-start(bf16[1024,256]{1,0:T(8,128)(2,1)} %grid_in.1), channel_id=1, source_target_pairs={{0,2},{1,3},{2,0},{3,1},{4,6},{5,7},{6,4},{7,5},{8,10},{9,11},{10,... | collective-permute-start | bytes 1572872 | tf_op jit(solution)/shard_map/ppermute | solution.py:23
  8.9 3.3 %collective-permute-start.2 = (bf16[1024,256]{1,0:T(8,128)(2,1)}, bf16[1024,256]{1,0:T(8,128)(2,1)S(1)}, u32[]{:S(2)}, u32[]{:S(2)}) collective-permute-start(bf16[1024,256]{1,0:T(8,128)(2,1)} %grid_in.1), channel_id=1, source_target_pairs={{0,3},{1,0},{2,1},{3,2},{4,7},{5,4},{6,5},{7,6},{8,11},{9,8},{10,9... | collective-permute-start | bytes 1572872 | tf_op jit(solution)/shard_map/ppermute | solution.py:23
  15.5 2.2 %collective-permute-done.refs_2_ = bf16[1024,256]{1,0:T(8,128)(2,1)S(1)} collective-permute-done((bf16[1024,256]{1,0:T(8,128)(2,1)}, bf16[1024,256]{1,0:T(8,128)(2,1)S(1)}, u32[]{:S(2)}, u32[]{:S(2)}) %collective-permute-start) | collective-permute-done | bytes 524320 | tf_op jit(solution)/shard_map/ppermute | solution.py:23
  17.7 12.4 %collective-permute-done.1.refs_3_ = bf16[1024,256]{1,0:T(8,128)(2,1)S(1)} collective-permute-done((bf16[1024,256]{1,0:T(8,128)(2,1)}, bf16[1024,256]{1,0:T(8,128)(2,1)S(1)}, u32[]{:S(2)}, u32[]{:S(2)}) %collective-permute-start.1) | collective-permute-done | bytes 524320 | tf_op jit(solution)/shard_map/ppermute | solution.py:23
  31.5 5.6 %grid_project.3.a1 = bf16[1024,256]{1,0:T(8,128)(2,1)} custom-call(s32[32]{0:T(128)S(1)} %concatenate.15.refs_0_.meta, bf16[1024,256]{1,0:T(8,128)(2,1)} %grid_in.1, bf16[1024,256]{1,0:T(8,128)(2,1)S(1)} %collective-permute-done.refs_2_, bf16[1024,256]{1,0:T(8,128)(2,1)S(1)} %collective-permute-done.1.refs_3_, ...), custom_call_target="tpu_custom_call" | custom-call | flops 536870912 | bytes 4194304 | tf_op jit(solution)/shard_map/grid_project/pallas_call | solution.py:108
  37.9 5.1 %collective-permute-start.6 = (bf16[1024,256]{1,0:T(8,128)(2,1)}, bf16[1024,256]{1,0:T(8,128)(2,1)}, u32[]{:S(2)}, u32[]{:S(2)}) collective-permute-start(bf16[1024,256]{1,0:T(8,128)(2,1)} %grid_project.3.a1), channel_id=1, source_target_pairs={{0,8},{4,12},{8,16},{12,20},{16,24},{20,28},{24,32},{28,36},{32,40... | collective-permute-start | bytes 1572872 | tf_op jit(solution)/shard_map/ppermute | solution.py:29
  43.0 1.9 collective-permute-start.7
  47.4 4.4 %collective-permute-start.3 = (bf16[9,128,256]{2,1,0:T(8,128)(2,1)}, bf16[9,128,256]{2,1,0:T(8,128)(2,1)S(1)}, u32[]{:S(2)}, u32[]{:S(2)}) collective-permute-start(bf16[9,128,256]{2,1,0:T(8,128)(2,1)} %get-tuple-element.36), channel_id=1, source_target_pairs={{0,1},{1,2},{2,3},{3,0},{4,5},{5,6},{6,7},{7,4},{8,9},{9,10},{10,1... | collective-permute-start | bytes 1769480 | tf_op jit(solution)/shard_map/ppermute | solution.py:23
  51.7 3.5 %collective-permute-start.4 = (bf16[9,128,256]{2,1,0:T(8,128)(2,1)}, bf16[9,128,256]{2,1,0:T(8,128)(2,1)S(1)}, u32[]{:S(2)}, u32[]{:S(2)}) collective-permute-start(bf16[9,128,256]{2,1,0:T(8,128)(2,1)} %get-tuple-element.35), channel_id=1, source_target_pairs={{0,2},{1,3},{2,0},{3,1},{4,6},{5,7},{6,4},{7,5},{8,10},{9,11},{10,... | collective-permute-start | bytes 1769480 | tf_op jit(solution)/shard_map/ppermute | solution.py:23
  55.3 3.6 %collective-permute-start.5 = (bf16[9,128,256]{2,1,0:T(8,128)(2,1)S(1)}, bf16[9,128,256]{2,1,0:T(8,128)(2,1)S(1)}, u32[]{:S(2)}, u32[]{:S(2)}) collective-permute-start(bf16[9,128,256]{2,1,0:T(8,128)(2,1)S(1)} %get-tuple-element.34), channel_id=1, source_target_pairs={{0,3},{1,0},{2,1},{3,2},{4,7},{5,4},{6,5},{7,6},{8,11},{9,8},{10,9... | collective-permute-start | bytes 1769480 | tf_op jit(solution)/shard_map/ppermute | solution.py:23
  58.9 1.9 collective-permute-start.8
  62.2 2.1 collective-permute-start.9
  65.8 13.4 %collective-permute-done.4.a2.refs_3_ = bf16[9,128,256]{2,1,0:T(8,128)(2,1)S(1)} collective-permute-done((bf16[9,128,256]{2,1,0:T(8,128)(2,1)}, bf16[9,128,256]{2,1,0:T(8,128)(2,1)S(1)}, u32[]{:S(2)}, u32[]{:S(2)}) %collective-permute-start.4) | collective-permute-done | bytes 589856 | tf_op jit(solution)/shard_map/ppermute | solution.py:23
  80.5 1.9 mesh_start.1.q
  82.5 3.6 %enc_attend.1 = bf16[4,256,128]{2,1,0:T(8,128)(2,1)} custom-call(s32[32]{0:T(128)S(1)} %concatenate.15.refs_0_.meta, s32[2,4]{1,0:T(2,128)S(1)} %copy-done.20, s32[1024]{0:T(1024)S(1)} %copy-done.19, bf16[256,128]{1,0:T(8,128)(2,1)S(1)} %mesh_start.1.q, bf16[1024,256]{1,0:T(8,128)(2,1)} %collective-permute-done.6.a0, bf16[1024,256]{1,0:T(8,128)(2,1)} %grid_project.3.a1, ...), custom_call_target="tpu_custom_call" | custom-call | tf_op jit(solution)/shard_map/enc_attend/pallas_call | solution.py:208
  86.3 2.1 collective-permute-start.10
  88.4 11.5 %all_to_all.20.o = bf16[4,256,128]{2,1,0:T(8,128)(2,1)S(1)} all-to-all(bf16[4,256,128]{2,1,0:T(8,128)(2,1)S(1)} %copy-done.21), channel_id=1, replica_groups=mesh['nodes'=128,'mp'=4] {'mp'}, dimensions={0} | all-to-all | bytes 524288 | tf_op jit(solution)/shard_map/all_to_all | solution.py:420
  99.9 2.4 %first_layer.1 = (bf16[4,256,256]{2,1,0:T(8,128)(2,1)S(1)}, bf16[256,256]{1,0:T(8,128)(2,1)S(1)}, bf16[256,128]{1,0:T(8,128)(2,1)S(1)}) custom-call(s32[32]{0:T(128)S(1)} %concatenate.15.refs_0_.meta, bf16[4,256,128]{2,1,0:T(8,128)(2,1)S(1)} %all_to_all.20.o, bf16[256,256]{1,0:T(8,128)(2,1)S(1)} %copy-done.10, ...), custom_call_target="tpu_custom_call" | custom-call | tf_op jit(solution)/shard_map/first_layer/pallas_call | solution.py:334
  103.2 7.0 %collective-permute-start.11 = (bf16[256,256]{1,0:T(8,128)(2,1)S(1)}, bf16[256,256]{1,0:T(8,128)(2,1)S(1)}, u32[]{:S(2)}, u32[]{:S(2)}) collective-permute-start(bf16[256,256]{1,0:T(8,128)(2,1)S(1)} %get-tuple-element.21.refs_3_), channel_id=1, source_target_pairs={{0,8},{4,12},{8,16},{12,20},{16,24},{20,28},{24,32},{28,36},{32,40... | collective-permute-start | bytes 393224 | tf_op jit(solution)/shard_map/ppermute | solution.py:29
  110.1 1.9 collective-permute-start.12
  112.0 1.9 collective-permute-start.13
  114.0 6.3 %collective-permute-done.12.refs_4_ = bf16[256,256]{1,0:T(8,128)(2,1)S(1)} collective-permute-done((bf16[256,256]{1,0:T(8,128)(2,1)S(1)}, bf16[256,256]{1,0:T(8,128)(2,1)S(1)}, u32[]{:S(2)}, u32[]{:S(2)}) %collective-permute-start.12) | collective-permute-done | bytes 131104 | tf_op jit(solution)/shard_map/ppermute | solution.py:29
  120.3 1.9 collective-permute-start.14
  123.6 2.5 %near_attend.3 = bf16[4,256,128]{2,1,0:T(8,128)(2,1)} custom-call(s32[32]{0:T(128)S(1)} %concatenate.15.refs_0_.meta, bf16[256,128]{1,0:T(8,128)(2,1)S(1)} %get-tuple-element.20.refs_1_, bf16[256,256]{1,0:T(8,128)(2,1)S(1)} %collective-permute-done.11.refs_2_, bf16[256,256]{1,0:T(8,128)(2,1)S(1)} %get-tuple-element.21.refs_3_, ...), custom_call_target="tpu_custom_call" | custom-call | tf_op jit(solution)/shard_map/near_attend/pallas_call | solution.py:236
  126.0 3.4 %all-to-all-start.1 = ((bf16[4,256,128]{2,1,0:T(8,128)(2,1)}), bf16[4,256,128]{2,1,0:T(8,128)(2,1)S(1)}, u32[]{:S(2)}, u32[]{:S(2)}) async-start(bf16[4,256,128]{2,1,0:T(8,128)(2,1)} %near_attend.3), calls=%async_computation.1 | async-start | bytes 524288 | tf_op jit(solution)/shard_map/all_to_all | solution.py:420
  130.7 2.8 %layer_weights.2 = (bf16[4,512,256]{2,1,0:T(8,128)(2,1)S(1)}, bf16[1024,384]{1,0:T(8,128)(2,1)S(1)}) custom-call(s32[32]{0:T(128)S(1)} %concatenate.15.refs_0_.meta, bf16[4,128,1024]{2,1,0:T(8,128)(2,1)} %refs_1_.7, bf16[9,128,256]{2,1,0:T(8,128)(2,1)S(1)} %collective-permute-done.3.a1.refs_2_, bf16[9,128,256]{2,1,0:T(8,128)(2,1)S(1)} %collective-permute-done.4.a2.refs_3_, ...), custom_call_target="tpu_custom_call" | custom-call | tf_op jit(solution)/shard_map/layer_weights/pallas_call | solution.py:279
  134.5 2.1 all-to-all-done.1.refs_1_
  141.4 1.9 collective-permute-start.15
  143.3 3.9 %collective-permute-start.16 = (bf16[256,256]{1,0:T(8,128)(2,1)S(1)}, bf16[256,256]{1,0:T(8,128)(2,1)S(1)}, u32[]{:S(2)}, u32[]{:S(2)}) collective-permute-start(bf16[256,256]{1,0:T(8,128)(2,1)S(1)} %get-tuple-element.26.refs_3_), channel_id=1, source_target_pairs={{8,0},{12,4},{16,8},{20,12},{24,16},{28,20},{32,24},{36,28},{40,32... | collective-permute-start | bytes 393224 | tf_op jit(solution)/shard_map/ppermute | solution.py:29
  147.2 1.9 collective-permute-start.17
  149.2 4.3 %collective-permute-done.16.refs_4_ = bf16[256,256]{1,0:T(8,128)(2,1)S(1)} collective-permute-done((bf16[256,256]{1,0:T(8,128)(2,1)S(1)}, bf16[256,256]{1,0:T(8,128)(2,1)S(1)}, u32[]{:S(2)}, u32[]{:S(2)}) %collective-permute-start.16) | collective-permute-done | bytes 131104 | tf_op jit(solution)/shard_map/ppermute | solution.py:29
  153.5 1.9 collective-permute-start.18
  156.7 2.5 %near_attend.4 = bf16[4,256,128]{2,1,0:T(8,128)(2,1)} custom-call(s32[32]{0:T(128)S(1)} %concatenate.15.refs_0_.meta, bf16[256,128]{1,0:T(8,128)(2,1)S(1)} %get-tuple-element.25.refs_1_, bf16[256,256]{1,0:T(8,128)(2,1)S(1)} %collective-permute-done.15.refs_2_, bf16[256,256]{1,0:T(8,128)(2,1)S(1)} %get-tuple-element.26.refs_3_, ...), custom_call_target="tpu_custom_call" | custom-call | tf_op jit(solution)/shard_map/near_attend/pallas_call | solution.py:236
  159.2 4.0 %all-to-all-start.2 = ((bf16[4,256,128]{2,1,0:T(8,128)(2,1)}), bf16[4,256,128]{2,1,0:T(8,128)(2,1)}, u32[]{:S(2)}, u32[]{:S(2)}) async-start(bf16[4,256,128]{2,1,0:T(8,128)(2,1)} %near_attend.4), calls=%async_computation.2 | async-start | bytes 524288 | tf_op jit(solution)/shard_map/all_to_all | solution.py:420
  164.5 2.8 %layer_weights.3 = (bf16[4,512,256]{2,1,0:T(8,128)(2,1)S(1)}, bf16[1024,256]{1,0:T(8,128)(2,1)S(1)}) custom-call(s32[32]{0:T(128)S(1)} %concatenate.15.refs_0_.meta, bf16[4,128,1024]{2,1,0:T(8,128)(2,1)} %refs_1_.7, bf16[9,128,256]{2,1,0:T(8,128)(2,1)S(1)} %collective-permute-done.3.a1.refs_2_, bf16[9,128,256]{2,1,0:T(8,128)(2,1)S(1)} %collective-permute-done.4.a2.refs_3_, ...), custom_call_target="tpu_custom_call" | custom-call | tf_op jit(solution)/shard_map/layer_weights/pallas_call | solution.py:279
  168.1 2.5 %all-to-all-done.2.refs_1_ = bf16[4,256,128]{2,1,0:T(8,128)(2,1)} async-done(((bf16[4,256,128]{2,1,0:T(8,128)(2,1)}), bf16[4,256,128]{2,1,0:T(8,128)(2,1)}, u32[]{:S(2)}, u32[]{:S(2)}) %all-to-all-start.2) | async-done | bytes 262176 | tf_op jit(solution)/shard_map/all_to_all | solution.py:420
  172.6 2.7 %mesh_layer.3 = (bf16[256,256]{1,0:T(8,128)(2,1)}, bf16[256,256]{1,0:T(8,128)(2,1)S(1)}) custom-call(s32[32]{0:T(128)S(1)} %concatenate.15.refs_0_.meta, bf16[4,256,128]{2,1,0:T(8,128)(2,1)} %all-to-all-done.2.refs_1_, bf16[4,256,256]{2,1,0:T(8,128)(2,1)S(1)} %copy-done.14, f32[6,4,256]{2,1,0:T(4,128)S(1)} %reshape.24.refs_5_.gains.refs_3_, ...), custom_call_target="tpu_custom_call" | custom-call | tf_op jit(solution)/shard_map/mesh_layer/pallas_call | solution.py:377
  175.3 1.9 collective-permute-start.19
  177.2 3.9 %collective-permute-start.20 = (bf16[256,256]{1,0:T(8,128)(2,1)S(1)}, bf16[256,256]{1,0:T(8,128)(2,1)S(1)}, u32[]{:S(2)}, u32[]{:S(2)}) collective-permute-start(bf16[256,256]{1,0:T(8,128)(2,1)S(1)} %get-tuple-element.30.refs_3_), channel_id=1, source_target_pairs={{8,0},{12,4},{16,8},{20,12},{24,16},{28,20},{32,24},{36,28},{40,32... | collective-permute-start | bytes 393224 | tf_op jit(solution)/shard_map/ppermute | solution.py:29
  181.2 1.9 collective-permute-start.21
  183.1 4.3 %collective-permute-done.20.refs_4_ = bf16[256,256]{1,0:T(8,128)(2,1)S(1)} collective-permute-done((bf16[256,256]{1,0:T(8,128)(2,1)S(1)}, bf16[256,256]{1,0:T(8,128)(2,1)S(1)}, u32[]{:S(2)}, u32[]{:S(2)}) %collective-permute-start.20) | collective-permute-done | bytes 131104 | tf_op jit(solution)/shard_map/ppermute | solution.py:29
  187.4 1.9 collective-permute-start.22
  189.4 4.7 %grid_project.2.refs_1_ = bf16[1024,128]{1,0:T(8,128)(2,1)S(1)} custom-call(s32[32]{0:T(128)S(1)} %concatenate.15.refs_0_.meta, bf16[1024,256]{1,0:T(8,128)(2,1)} %grid_in.1, bf16[1024,256]{1,0:T(8,128)(2,1)S(1)} %collective-permute-done.refs_2_, bf16[1024,256]{1,0:T(8,128)(2,1)S(1)} %copy-done.7, bf16[1024,256]{1,0:T(8,128)(2,1)S(1)} %copy-done.9, ...), custom_call_target="tpu_custom_call" | custom-call | flops 268435456 | bytes 4194304 | tf_op jit(solution)/shard_map/grid_project/pallas_call | solution.py:108
  194.1 1.7 near_attend.5
  196.8 4.4 %all-to-all-start.3 = ((bf16[4,1024,128]{2,1,0:T(8,128)(2,1)}), bf16[4,1024,128]{2,1,0:T(8,128)(2,1)}, u32[]{:S(2)}, u32[]{:S(2)}) async-start(bf16[4,1024,128]{2,1,0:T(8,128)(2,1)} %copy-done.5), calls=%async_computation.3 | async-start | bytes 2097152 | tf_op jit(solution)/shard_map/all_to_all | solution.py:420
  201.3 16.0 %all-to-all-done.3.o = bf16[4,1024,128]{2,1,0:T(8,128)(2,1)} async-done(((bf16[4,1024,128]{2,1,0:T(8,128)(2,1)}), bf16[4,1024,128]{2,1,0:T(8,128)(2,1)}, u32[]{:S(2)}, u32[]{:S(2)}) %all-to-all-start.3) | async-done | bytes 1048608 | tf_op jit(solution)/shard_map/all_to_all | solution.py:420
  217.3 2.4 %grid_final.1 = bf16[1024,256]{1,0:T(8,128)(2,1)} custom-call(s32[32]{0:T(128)S(1)} %concatenate.15.refs_0_.meta, s32[1024]{0:T(1024)S(1)} %copy-done.19, bf16[4,1024,128]{2,1,0:T(8,128)(2,1)} %all-to-all-done.3.o, bf16[512,256]{1,0:T(8,128)(2,1)S(1)} %bitcast.11, bf16[1024,256]{1,0:T(8,128)(2,1)S(1)} %copy-done.4), custom_call_target="tpu_custom_call" | custom-call | tf_op jit(solution)/shard_map/grid_final/pallas_call | solution.py:402
  (91 shorter events, 27.8 us)
Async XLA Ops:
  0.6 17.1 %collective-permute-start = (bf16[1024,256]{1,0:T(8,128)(2,1)}, bf16[1024,256]{1,0:T(8,128)(2,1)S(1)}, u32[]{:S(2)}, u32[]{:S(2)}) collective-permute-start(bf16[1024,256]{1,0:T(8,128)(2,1)} %grid_in.1), channel_id=1, source_target_pairs={{0,1},{1,2},{2,3},{3,0},{4,5},{5,6},{6,7},{7,4},{8,9},{9,10},{10,1... | collective-permute-start | bytes 1572872 | tf_op jit(solution)/shard_map/ppermute | solution.py:23
  4.1 26.0 %collective-permute-start.1 = (bf16[1024,256]{1,0:T(8,128)(2,1)}, bf16[1024,256]{1,0:T(8,128)(2,1)S(1)}, u32[]{:S(2)}, u32[]{:S(2)}) collective-permute-start(bf16[1024,256]{1,0:T(8,128)(2,1)} %grid_in.1), channel_id=1, source_target_pairs={{0,2},{1,3},{2,0},{3,1},{4,6},{5,7},{6,4},{7,5},{8,10},{9,11},{10,... | collective-permute-start | bytes 1572872 | tf_op jit(solution)/shard_map/ppermute | solution.py:23
  8.9 22.5 %collective-permute-start.2 = (bf16[1024,256]{1,0:T(8,128)(2,1)}, bf16[1024,256]{1,0:T(8,128)(2,1)S(1)}, u32[]{:S(2)}, u32[]{:S(2)}) collective-permute-start(bf16[1024,256]{1,0:T(8,128)(2,1)} %grid_in.1), channel_id=1, source_target_pairs={{0,3},{1,0},{2,1},{3,2},{4,7},{5,4},{6,5},{7,6},{8,11},{9,8},{10,9... | collective-permute-start | bytes 1572872 | tf_op jit(solution)/shard_map/ppermute | solution.py:23
  31.5 5.6 %copy-start.8 = (bf16[1024,256]{1,0:T(8,128)(2,1)}, bf16[1024,256]{1,0:T(8,128)(2,1)S(1)}, u32[]{:S(2)}) copy-start(bf16[1024,256]{1,0:T(8,128)(2,1)S(1)} %collective-permute-done.2.refs_4_) | copy-start | bytes 1572868
  37.9 7.1 %slice-start = ((bf16[4,128,1024]{2,1,0:T(8,128)(2,1)}), bf16[1,128,1024]{2,1,0:T(8,128)(2,1)S(1)}, s32[]{:S(2)}) async-start(bf16[4,128,1024]{2,1,0:T(8,128)(2,1)} %refs_1_.7), calls=%async_computation.4 | async-start | bytes 524288 | tf_op jit(solution)/shard_map/slice | solution.py:460
  37.9 21.0 %collective-permute-start.6 = (bf16[1024,256]{1,0:T(8,128)(2,1)}, bf16[1024,256]{1,0:T(8,128)(2,1)}, u32[]{:S(2)}, u32[]{:S(2)}) collective-permute-start(bf16[1024,256]{1,0:T(8,128)(2,1)} %grid_project.3.a1), channel_id=1, source_target_pairs={{0,8},{4,12},{8,16},{12,20},{16,24},{20,28},{24,32},{28,36},{32,40... | collective-permute-start | bytes 1572872 | tf_op jit(solution)/shard_map/ppermute | solution.py:29
  43.0 18.1 %collective-permute-start.7 = (bf16[1024,256]{1,0:T(8,128)(2,1)}, bf16[1024,256]{1,0:T(8,128)(2,1)}, u32[]{:S(2)}, u32[]{:S(2)}) collective-permute-start(bf16[1024,256]{1,0:T(8,128)(2,1)} %grid_project.3.a1), channel_id=1, source_target_pairs={{8,0},{12,4},{16,8},{20,12},{24,16},{28,20},{32,24},{36,28},{40,32... | collective-permute-start | bytes 1572872 | tf_op jit(solution)/shard_map/ppermute | solution.py:29
  44.9 1.2 slice-start.1
  45.0 1.2 copy-start.10
  47.4 18.4 %collective-permute-start.3 = (bf16[9,128,256]{2,1,0:T(8,128)(2,1)}, bf16[9,128,256]{2,1,0:T(8,128)(2,1)S(1)}, u32[]{:S(2)}, u32[]{:S(2)}) collective-permute-start(bf16[9,128,256]{2,1,0:T(8,128)(2,1)} %get-tuple-element.36), channel_id=1, source_target_pairs={{0,1},{1,2},{2,3},{3,0},{4,5},{5,6},{6,7},{7,4},{8,9},{9,10},{10,1... | collective-permute-start | bytes 1769480 | tf_op jit(solution)/shard_map/ppermute | solution.py:23
  51.7 27.4 %collective-permute-start.4 = (bf16[9,128,256]{2,1,0:T(8,128)(2,1)}, bf16[9,128,256]{2,1,0:T(8,128)(2,1)S(1)}, u32[]{:S(2)}, u32[]{:S(2)}) collective-permute-start(bf16[9,128,256]{2,1,0:T(8,128)(2,1)} %get-tuple-element.35), channel_id=1, source_target_pairs={{0,2},{1,3},{2,0},{3,1},{4,6},{5,7},{6,4},{7,5},{8,10},{9,11},{10,... | collective-permute-start | bytes 1769480 | tf_op jit(solution)/shard_map/ppermute | solution.py:23
  55.3 25.2 %collective-permute-start.5 = (bf16[9,128,256]{2,1,0:T(8,128)(2,1)S(1)}, bf16[9,128,256]{2,1,0:T(8,128)(2,1)S(1)}, u32[]{:S(2)}, u32[]{:S(2)}) collective-permute-start(bf16[9,128,256]{2,1,0:T(8,128)(2,1)S(1)} %get-tuple-element.34), channel_id=1, source_target_pairs={{0,3},{1,0},{2,1},{3,2},{4,7},{5,4},{6,5},{7,6},{8,11},{9,8},{10,9... | collective-permute-start | bytes 1769480 | tf_op jit(solution)/shard_map/ppermute | solution.py:23
  58.9 23.6 %collective-permute-start.8 = (bf16[1024,256]{1,0:T(8,128)(2,1)}, bf16[1024,256]{1,0:T(8,128)(2,1)S(1)}, u32[]{:S(2)}, u32[]{:S(2)}) collective-permute-start(bf16[1024,256]{1,0:T(8,128)(2,1)} %grid_project.3.a1), channel_id=1, source_target_pairs={{0,4},{4,0},{8,12},{12,8},{16,20},{20,16},{24,28},{28,24},{32,36},... | collective-permute-start | bytes 1572872 | tf_op jit(solution)/shard_map/ppermute | solution.py:34
  62.2 20.2 %copy-start.19 = (s32[1024]{0:T(1024)S(1)}, s32[1024]{0:T(1024)}, u32[]{:S(2)}) copy-start(s32[1024]{0:T(1024)} %counts.3) | copy-start | bytes 12292
  62.2 20.2 %copy-start.20 = (s32[2,4]{1,0:T(2,128)S(1)}, s32[2,4]{1,0:T(2,128)}, u32[]{:S(2)}) copy-start(s32[2,4]{1,0:T(2,128)} %listed.1) | copy-start | bytes 100
  62.2 20.2 %collective-permute-start.9 = (bf16[1024,256]{1,0:T(8,128)(2,1)S(1)}, bf16[1024,256]{1,0:T(8,128)(2,1)S(1)}, u32[]{:S(2)}, u32[]{:S(2)}) collective-permute-start(bf16[1024,256]{1,0:T(8,128)(2,1)S(1)} %broadcast_select_fusion), channel_id=1, source_target_pairs={{0,4},{4,0},{8,12},{12,8},{16,20},{20,16},{24,28},{28,24},{32,36},... | collective-permute-start | bytes 1572872 | tf_op jit(solution)/shard_map/ppermute | solution.py:34
  86.1 2.2 %copy-start.21 = (bf16[4,256,128]{2,1,0:T(8,128)(2,1)S(1)}, bf16[4,256,128]{2,1,0:T(8,128)(2,1)}, u32[]{:S(2)}) copy-start(bf16[4,256,128]{2,1,0:T(8,128)(2,1)} %enc_attend.1) | copy-start | bytes 786436
  86.1 13.8 %copy-start = (bf16[4,128,1024]{2,1,0:T(8,128)(2,1)S(1)}, bf16[4,128,1024]{2,1,0:T(8,128)(2,1)}, u32[]{:S(2)}) copy-start(bf16[4,128,1024]{2,1,0:T(8,128)(2,1)} %refs_1_.7) | copy-start | bytes 3145732
  86.3 13.6 %collective-permute-start.10 = (bf16[3,6,128,256]{3,2,1,0:T(8,128)(2,1)S(1)}, bf16[3,6,128,256]{3,2,1,0:T(8,128)(2,1)S(1)}, u32[]{:S(2)}, u32[]{:S(2)}) collective-permute-start(bf16[3,6,128,256]{3,2,1,0:T(8,128)(2,1)S(1)} %pad_maximum_fusion), channel_id=1, source_target_pairs={{0,4},{4,0},{8,12},{12,8},{16,20},{20,16},{24,28},{28,24},{32,36},... | collective-permute-start | bytes 3538952 | tf_op jit(solution)/shard_map/ppermute | solution.py:34
  99.9 2.5 %copy-start.1 = (bf16[3,6,128,256]{3,2,1,0:T(8,128)(2,1)}, bf16[3,6,128,256]{3,2,1,0:T(8,128)(2,1)S(1)}, u32[]{:S(2)}) copy-start(bf16[3,6,128,256]{3,2,1,0:T(8,128)(2,1)S(1)} %collective-permute-done.10.other.refs_5_) | copy-start | bytes 3538948
  103.2 10.8 %collective-permute-start.11 = (bf16[256,256]{1,0:T(8,128)(2,1)S(1)}, bf16[256,256]{1,0:T(8,128)(2,1)S(1)}, u32[]{:S(2)}, u32[]{:S(2)}) collective-permute-start(bf16[256,256]{1,0:T(8,128)(2,1)S(1)} %get-tuple-element.21.refs_3_), channel_id=1, source_target_pairs={{0,8},{4,12},{8,16},{12,20},{16,24},{20,28},{24,32},{28,36},{32,40... | collective-permute-start | bytes 393224 | tf_op jit(solution)/shard_map/ppermute | solution.py:29
  110.1 10.2 %collective-permute-start.12 = (bf16[256,256]{1,0:T(8,128)(2,1)S(1)}, bf16[256,256]{1,0:T(8,128)(2,1)S(1)}, u32[]{:S(2)}, u32[]{:S(2)}) collective-permute-start(bf16[256,256]{1,0:T(8,128)(2,1)S(1)} %get-tuple-element.21.refs_3_), channel_id=1, source_target_pairs={{8,0},{12,4},{16,8},{20,12},{24,16},{28,20},{32,24},{36,28},{40,32... | collective-permute-start | bytes 393224 | tf_op jit(solution)/shard_map/ppermute | solution.py:29
  112.0 10.2 %collective-permute-start.13 = (bf16[256,256]{1,0:T(8,128)(2,1)S(1)}, bf16[256,256]{1,0:T(8,128)(2,1)S(1)}, u32[]{:S(2)}, u32[]{:S(2)}) collective-permute-start(bf16[256,256]{1,0:T(8,128)(2,1)S(1)} %get-tuple-element.21.refs_3_), channel_id=1, source_target_pairs={{0,4},{4,0},{8,12},{12,8},{16,20},{20,16},{24,28},{28,24},{32,36},... | collective-permute-start | bytes 393224 | tf_op jit(solution)/shard_map/ppermute | solution.py:34
  120.3 3.2 %collective-permute-start.14 = (bf16[256,256]{1,0:T(8,128)(2,1)S(1)}, bf16[256,256]{1,0:T(8,128)(2,1)S(1)}, u32[]{:S(2)}, u32[]{:S(2)}) collective-permute-start(bf16[256,256]{1,0:T(8,128)(2,1)S(1)} %broadcast_select_fusion.3), channel_id=1, source_target_pairs={{0,4},{4,0},{8,12},{12,8},{16,20},{20,16},{24,28},{28,24},{32,36},... | collective-permute-start | bytes 393224 | tf_op jit(solution)/shard_map/ppermute | solution.py:34
  126.0 10.6 %all-to-all-start.1 = ((bf16[4,256,128]{2,1,0:T(8,128)(2,1)}), bf16[4,256,128]{2,1,0:T(8,128)(2,1)S(1)}, u32[]{:S(2)}, u32[]{:S(2)}) async-start(bf16[4,256,128]{2,1,0:T(8,128)(2,1)} %near_attend.3), calls=%async_computation.1 | async-start | bytes 524288 | tf_op jit(solution)/shard_map/all_to_all | solution.py:420
  129.4 1.3 copy-start.2
  133.6 1.0 copy-start.11
  136.7 1.2 copy-start.12
  137.9 1.0 copy-start.16
  140.6 0.8 copy-start.13
  141.4 7.8 %collective-permute-start.15 = (bf16[256,256]{1,0:T(8,128)(2,1)S(1)}, bf16[256,256]{1,0:T(8,128)(2,1)S(1)}, u32[]{:S(2)}, u32[]{:S(2)}) collective-permute-start(bf16[256,256]{1,0:T(8,128)(2,1)S(1)} %get-tuple-element.26.refs_3_), channel_id=1, source_target_pairs={{0,8},{4,12},{8,16},{12,20},{16,24},{20,28},{24,32},{28,36},{32,40... | collective-permute-start | bytes 393224 | tf_op jit(solution)/shard_map/ppermute | solution.py:29
  143.3 10.2 %collective-permute-start.16 = (bf16[256,256]{1,0:T(8,128)(2,1)S(1)}, bf16[256,256]{1,0:T(8,128)(2,1)S(1)}, u32[]{:S(2)}, u32[]{:S(2)}) collective-permute-start(bf16[256,256]{1,0:T(8,128)(2,1)S(1)} %get-tuple-element.26.refs_3_), channel_id=1, source_target_pairs={{8,0},{12,4},{16,8},{20,12},{24,16},{28,20},{32,24},{36,28},{40,32... | collective-permute-start | bytes 393224 | tf_op jit(solution)/shard_map/ppermute | solution.py:29
  147.2 8.2 %collective-permute-start.17 = (bf16[256,256]{1,0:T(8,128)(2,1)S(1)}, bf16[256,256]{1,0:T(8,128)(2,1)S(1)}, u32[]{:S(2)}, u32[]{:S(2)}) collective-permute-start(bf16[256,256]{1,0:T(8,128)(2,1)S(1)} %get-tuple-element.26.refs_3_), channel_id=1, source_target_pairs={{0,4},{4,0},{8,12},{12,8},{16,20},{20,16},{24,28},{28,24},{32,36},... | collective-permute-start | bytes 393224 | tf_op jit(solution)/shard_map/ppermute | solution.py:34
  153.5 3.2 %collective-permute-start.18 = (bf16[256,256]{1,0:T(8,128)(2,1)S(1)}, bf16[256,256]{1,0:T(8,128)(2,1)S(1)}, u32[]{:S(2)}, u32[]{:S(2)}) collective-permute-start(bf16[256,256]{1,0:T(8,128)(2,1)S(1)} %broadcast_select_fusion.2), channel_id=1, source_target_pairs={{0,4},{4,0},{8,12},{12,8},{16,20},{20,16},{24,28},{28,24},{32,36},... | collective-permute-start | bytes 393224 | tf_op jit(solution)/shard_map/ppermute | solution.py:34
  159.2 11.4 %all-to-all-start.2 = ((bf16[4,256,128]{2,1,0:T(8,128)(2,1)}), bf16[4,256,128]{2,1,0:T(8,128)(2,1)}, u32[]{:S(2)}, u32[]{:S(2)}) async-start(bf16[4,256,128]{2,1,0:T(8,128)(2,1)} %near_attend.4), calls=%async_computation.2 | async-start | bytes 524288 | tf_op jit(solution)/shard_map/all_to_all | solution.py:420
  163.2 1.3 copy-start.3
  170.6 1.0 copy-start.14
  171.6 1.0 copy-start.18
  172.6 16.7 %copy-start.7 = (bf16[1024,256]{1,0:T(8,128)(2,1)S(1)}, bf16[1024,256]{1,0:T(8,128)(2,1)}, u32[]{:S(2)}) copy-start(bf16[1024,256]{1,0:T(8,128)(2,1)} %copy-done.6) | copy-start | bytes 1572868
  172.6 16.7 %copy-start.9 = (bf16[1024,256]{1,0:T(8,128)(2,1)S(1)}, bf16[1024,256]{1,0:T(8,128)(2,1)}, u32[]{:S(2)}) copy-start(bf16[1024,256]{1,0:T(8,128)(2,1)} %copy-done.8) | copy-start | bytes 1572868
  175.3 7.8 %collective-permute-start.19 = (bf16[256,256]{1,0:T(8,128)(2,1)S(1)}, bf16[256,256]{1,0:T(8,128)(2,1)S(1)}, u32[]{:S(2)}, u32[]{:S(2)}) collective-permute-start(bf16[256,256]{1,0:T(8,128)(2,1)S(1)} %get-tuple-element.30.refs_3_), channel_id=1, source_target_pairs={{0,8},{4,12},{8,16},{12,20},{16,24},{20,28},{24,32},{28,36},{32,40... | collective-permute-start | bytes 393224 | tf_op jit(solution)/shard_map/ppermute | solution.py:29
  177.2 10.2 %collective-permute-start.20 = (bf16[256,256]{1,0:T(8,128)(2,1)S(1)}, bf16[256,256]{1,0:T(8,128)(2,1)S(1)}, u32[]{:S(2)}, u32[]{:S(2)}) collective-permute-start(bf16[256,256]{1,0:T(8,128)(2,1)S(1)} %get-tuple-element.30.refs_3_), channel_id=1, source_target_pairs={{8,0},{12,4},{16,8},{20,12},{24,16},{28,20},{32,24},{36,28},{40,32... | collective-permute-start | bytes 393224 | tf_op jit(solution)/shard_map/ppermute | solution.py:29
  181.2 12.9 %collective-permute-start.21 = (bf16[256,256]{1,0:T(8,128)(2,1)S(1)}, bf16[256,256]{1,0:T(8,128)(2,1)S(1)}, u32[]{:S(2)}, u32[]{:S(2)}) collective-permute-start(bf16[256,256]{1,0:T(8,128)(2,1)S(1)} %get-tuple-element.30.refs_3_), channel_id=1, source_target_pairs={{0,4},{4,0},{8,12},{12,8},{16,20},{20,16},{24,28},{28,24},{32,36},... | collective-permute-start | bytes 393224 | tf_op jit(solution)/shard_map/ppermute | solution.py:34
  187.4 6.7 %collective-permute-start.22 = (bf16[256,256]{1,0:T(8,128)(2,1)S(1)}, bf16[256,256]{1,0:T(8,128)(2,1)S(1)}, u32[]{:S(2)}, u32[]{:S(2)}) collective-permute-start(bf16[256,256]{1,0:T(8,128)(2,1)S(1)} %broadcast_select_fusion.1), channel_id=1, source_target_pairs={{0,4},{4,0},{8,12},{12,8},{16,20},{20,16},{24,28},{28,24},{32,36},... | collective-permute-start | bytes 393224 | tf_op jit(solution)/shard_map/ppermute | solution.py:34
  195.8 1.0 copy-start.5
  196.8 4.4 %copy-start.22 = (bf16[1,128,256]{2,1,0:T(8,128)(2,1)S(1)}, bf16[1,128,256]{2,1,0:T(8,128)(2,1)}, u32[]{:S(2)}) copy-start(bf16[1,128,256]{2,1,0:T(8,128)(2,1)} %get-tuple-element.37) | copy-start | bytes 196612
  196.8 20.5 %copy-start.4 = (bf16[1024,256]{1,0:T(8,128)(2,1)S(1)}, bf16[1024,256]{1,0:T(8,128)(2,1)}, u32[]{:S(2)}) copy-start(bf16[1024,256]{1,0:T(8,128)(2,1)} %grid_in.1) | copy-start | bytes 1572868
  196.8 20.5 %all-to-all-start.3 = ((bf16[4,1024,128]{2,1,0:T(8,128)(2,1)}), bf16[4,1024,128]{2,1,0:T(8,128)(2,1)}, u32[]{:S(2)}, u32[]{:S(2)}) async-start(bf16[4,1024,128]{2,1,0:T(8,128)(2,1)} %copy-done.5), calls=%async_computation.3 | async-start | bytes 2097152 | tf_op jit(solution)/shard_map/all_to_all | solution.py:420
  (3 other events, 2.4 us)

commit v5 on v4

--- a/solution.py
+++ b/solution.py
@@ -71,7 +71,42 @@
     return jnp.dot(a, b, preferred_element_type=F32)
 
 
-def grid_kernel(gain_row, count, layer_index, meta, x0, x1, x2, x3, gains, *rest):
+def grid_kernel(gain_row, count, meta, x0, x1, x2, x3, gains, *rest):
+    weights, out = rest[:count], rest[count]
+    rows = normed([x[...] for x in (x0, x1, x2, x3)])
+    total = None
+    for k in range(MP):
+        src = source(meta, k)
+        at = pl.ds(pl.multiple_of(src * 256, 256), 256)
+        row = (rows[k] * gains[gain_row, pl.ds(src, 1), :]).astype(BF16)
+        part = dot(row, jnp.concatenate([w[at, :] for w in weights], axis=1))
+        total = part if total is None else total + part
+    out[...] = total.astype(BF16)
+
+
+def grid_project(gain_row, meta, pieces, gains, *weights):
+    count = len(weights)
+
+    def body(*refs):
+        grid_kernel(gain_row, count, *refs)
+
+    rows = pieces[0].shape[0]
+    tile = 256
+    return pl.pallas_call(
+        body,
+        grid=(rows // tile,),
+        in_specs=[smem()]
+        + [pl.BlockSpec((tile, 256), lambda i: (i, 0))] * MP
+        + [vmem()] * (1 + count),
+        out_specs=pl.BlockSpec((tile, 128 * count), lambda i: (i, 0)),
+        out_shape=jax.ShapeDtypeStruct((rows, 128 * count), BF16),
+        cost_estimate=pl.CostEstimate(flops=rows * 1024 * 128 * count * 2, transcendentals=0, bytes_accessed=rows * 4096),
+        compiler_params=PARAMS,
+        name="grid_project",
+    )(meta, *pieces, gains, *weights)
+
+
+def grid_query_kernel(gain_row, count, layer_index, meta, x0, x1, x2, x3, gains, *rest):
     weights, (out, kept, sems) = rest[:count], rest[count:]
     copies = copies_of([(w, layer_index) for w in weights], kept, sems)
 
@@ -97,11 +132,11 @@
     out[...] = total.astype(BF16)
 
 
-def grid_project(gain_row, layer_index, meta, pieces, gains, *weights):
+def grid_query(gain_row, layer_index, meta, pieces, gains, *weights):
     count = len(weights)
 
     def body(*refs):
-        grid_kernel(gain_row, count, layer_index, *refs)
+        grid_query_kernel(gain_row, count, layer_index, *refs)
 
     rows = pieces[0].shape[0]
     tile = 256
@@ -117,7 +152,7 @@
         scratch_shapes=[pltpu.VMEM((count, 1024, 128), BF16), pltpu.SemaphoreType.DMA((count,))],
         cost_estimate=pl.CostEstimate(flops=rows * 1024 * 128 * count * 2, transcendentals=0, bytes_accessed=rows * 4096),
         compiler_params=PARAMS,
-        name="grid_project",
+        name="grid_query",
     )(meta, *pieces, gains, *weights)
 
 
@@ -434,6 +469,7 @@
         dec_list.reshape(-1) - (own_node - REACH) * 2,
     ])
     gains = norm_gains.reshape(6, MP, 256)
+    w_first = (w_key[0], w_value[0])
     w_query, w_key, w_value = (
         pltpu.with_memory_space_constraint(w, pltpu.HBM) for w in (w_query, w_key, w_value)
     )
@@ -462,9 +498,9 @@
     sent[0] = sent[1]
     arrived = gathered(sent, "w")[1:]
 
-    kv = grid_project(1, 0, meta, grid_pieces, gains, w_key, w_value)
+    kv = grid_project(1, meta, grid_pieces, gains, *w_first)
     grid_windows = window(kv)
-    grid_q = grid_project(4, 3, meta, grid_pieces, gains, w_query)
+    grid_q = grid_query(4, 3, meta, grid_pieces, gains, w_query)
     w_own = pltpu.with_memory_space_constraint(w_out, pltpu.HBM)
     mesh_q = mesh_start(meta, mesh_in, arrived, gains, w_query)
     o = enc_attend(meta, enc_list, grid_count, mesh_q, grid_windows)
@@ -488,6 +524,7 @@
             weights = (w_key, w_value, w_query) if index == 0 else (w_key, w_value)
             prepared = prepare(index + 1, meta, w_own, arrived, other, weights)
             o = near_attend(PROC0, 3, meta, made[2], near)
+    grid_q, w_last = lax.optimization_barrier((grid_q, w_last))
     o = near_attend(DEC0, 2, meta, grid_q, near)
     heads = gather_heads(o)
     grid_out = final(meta, grid_count, heads, w_last, grid_in)

time: 222 us -> 216 us (0.973)
  blocking collectives: 11.5 us -> 30.1 us
  waiting for transfers between devices: 70.6 us -> 53.7 us
  starting transfers between devices: 80 us -> 74.9 us
    all_to_all x1 -> x2, blocking collectives: 11.5 us -> 30.1 us  [gather_heads(): return lax.all_to_all(copies, 'mp', split_axis=0, concat_axis=0, tiled=True)]
    all_to_all x3 -> x2, waiting for transfers between devices: 20.6 us -> 4.59 us  [gather_heads(): return lax.all_to_all(copies, 'mp', split_axis=0, concat_axis=0, tiled=True)]
    pallas_call x2 -> x1, Pallas kernels: 10.3 us -> 4.48 us  [grid_project(): pl.pallas_call(body, grid=(rows // tile,), in_specs=[smem()] + [pl.BlockS...]
    all_to_all x3 -> x2, starting transfers between devices: 11.8 us -> 6.81 us  [gather_heads(): return lax.all_to_all(copies, 'mp', split_axis=0, concat_axis=0, tiled=True)]
    pallas_call x0 -> x1, Pallas kernels: none -> 4.7 us  [grid_query(): pl.pallas_call(body, grid=(rows // tile,), in_specs=[smem()] + [pl.BlockS...]
    unnamed x46 -> x48, local copies, waits for them, and re-layouts: 12.1 us -> 10.9 us
  transfers between devices with their start and end apart: 26 -> 25, of which waited for: 15 -> 14; matrix products, arithmetic and copies ran while one was open for 3% -> 3% of each run, Pallas kernels for 6% -> 6%
where the time goes in v5:
time: 216 us; the launch traced here: 214 us
  starting transfers between devices  74.9 us (35%)
  waiting for transfers between devices  53.7 us (25%)
  Pallas kernels  35 us (16%)
  blocking collectives  30.1 us (14%)
  local copies, waits for them, and re-layouts  14.4 us (7%)
  other arithmetic  4.56 us (2%)
    ppermute x6, waiting for transfers between devices, shift_mp(): return lax.ppermute(value, 'mp', [(s, (s + steps) % MP) for s in range(MP)])  31.3 us
    all_to_all x2, blocking collectives, gather_heads(): return lax.all_to_all(copies, 'mp', split_axis=0, concat_axis=0, tiled=True)  30.1 us
    ppermute x8, starting transfers between devices, from_node(): return lax.ppermute(value, 'nodes', pairs)  27.5 us
    ppermute x6, starting transfers between devices, shift_mp(): return lax.ppermute(value, 'mp', [(s, (s + steps) % MP) for s in range(MP)])  23 us
    ppermute x9, starting transfers between devices, swap_cores(): return lax.ppermute(value, 'nodes', [(s, s ^ 1) for s in range(count)])  17.5 us
    ppermute x8, waiting for transfers between devices, from_node(): return lax.ppermute(value, 'nodes', pairs)  15.3 us
    unnamed x48, local copies, waits for them, and re-layouts  10.9 us
    all_to_all x2, starting transfers between devices, gather_heads(): return lax.all_to_all(copies, 'mp', split_axis=0, concat_axis=0, tiled=True)  6.81 us
  transfers between devices with their start and end apart: 25, of which 14 were waited for; matrix products, arithmetic and copies ran while one was open for 3% of the time, Pallas kernels for 6%

profile of v5, /device:TPU:230, one launch (start us, length us, event | category | flops | bytes accessed | tf_op | source)
XLA Modules:
  0.0 214.1 jit_solution(18021741829575977611)
XLA Ops:
  0.6 3.5 %collective-permute-start = (bf16[1024,256]{1,0:T(8,128)(2,1)}, bf16[1024,256]{1,0:T(8,128)(2,1)S(1)}, u32[]{:S(2)}, u32[]{:S(2)}) collective-permute-start(bf16[1024,256]{1,0:T(8,128)(2,1)} %grid_in.1), channel_id=1, source_target_pairs={{0,1},{1,2},{2,3},{3,0},{4,5},{5,6},{6,7},{7,4},{8,9},{9,10},{10,1... | collective-permute-start | bytes 1572872 | tf_op jit(solution)/shard_map/ppermute | solution.py:23
  4.1 4.8 %collective-permute-start.1 = (bf16[1024,256]{1,0:T(8,128)(2,1)}, bf16[1024,256]{1,0:T(8,128)(2,1)S(1)}, u32[]{:S(2)}, u32[]{:S(2)}) collective-permute-start(bf16[1024,256]{1,0:T(8,128)(2,1)} %grid_in.1), channel_id=1, source_target_pairs={{0,2},{1,3},{2,0},{3,1},{4,6},{5,7},{6,4},{7,5},{8,10},{9,11},{10,... | collective-permute-start | bytes 1572872 | tf_op jit(solution)/shard_map/ppermute | solution.py:23
  8.9 3.3 %collective-permute-start.2 = (bf16[1024,256]{1,0:T(8,128)(2,1)}, bf16[1024,256]{1,0:T(8,128)(2,1)S(1)}, u32[]{:S(2)}, u32[]{:S(2)}) collective-permute-start(bf16[1024,256]{1,0:T(8,128)(2,1)} %grid_in.1), channel_id=1, source_target_pairs={{0,3},{1,0},{2,1},{3,2},{4,7},{5,4},{6,5},{7,6},{8,11},{9,8},{10,9... | collective-permute-start | bytes 1572872 | tf_op jit(solution)/shard_map/ppermute | solution.py:23
  17.7 12.4 %collective-permute-done.1.refs_3_ = bf16[1024,256]{1,0:T(8,128)(2,1)S(1)} collective-permute-done((bf16[1024,256]{1,0:T(8,128)(2,1)}, bf16[1024,256]{1,0:T(8,128)(2,1)S(1)}, u32[]{:S(2)}, u32[]{:S(2)}) %collective-permute-start.1) | collective-permute-done | bytes 524320 | tf_op jit(solution)/shard_map/ppermute | solution.py:23
  31.5 4.5 %grid_project.1.a1 = bf16[1024,256]{1,0:T(8,128)(2,1)} custom-call(s32[32]{0:T(128)S(1)} %concatenate.15.refs_0_.meta, bf16[1024,256]{1,0:T(8,128)(2,1)} %grid_in.1, bf16[1024,256]{1,0:T(8,128)(2,1)S(1)} %collective-permute-done.refs_2_, bf16[1024,256]{1,0:T(8,128)(2,1)S(1)} %collective-permute-done.1.refs_3_, ...), custom_call_target="tpu_custom_call" | custom-call | flops 536870912 | bytes 4194304 | tf_op jit(solution)/shard_map/grid_project/pallas_call | solution.py:95
  36.7 5.1 %collective-permute-start.6 = (bf16[1024,256]{1,0:T(8,128)(2,1)}, bf16[1024,256]{1,0:T(8,128)(2,1)S(1)}, u32[]{:S(2)}, u32[]{:S(2)}) collective-permute-start(bf16[1024,256]{1,0:T(8,128)(2,1)} %grid_project.1.a1), channel_id=1, source_target_pairs={{0,8},{4,12},{8,16},{12,20},{16,24},{20,28},{24,32},{28,36},{32,40... | collective-permute-start | bytes 1572872 | tf_op jit(solution)/shard_map/ppermute | solution.py:29
  41.8 1.9 collective-permute-start.7
  46.2 4.4 %collective-permute-start.3 = (bf16[9,128,256]{2,1,0:T(8,128)(2,1)}, bf16[9,128,256]{2,1,0:T(8,128)(2,1)S(1)}, u32[]{:S(2)}, u32[]{:S(2)}) collective-permute-start(bf16[9,128,256]{2,1,0:T(8,128)(2,1)} %get-tuple-element.40), channel_id=1, source_target_pairs={{0,1},{1,2},{2,3},{3,0},{4,5},{5,6},{6,7},{7,4},{8,9},{9,10},{10,1... | collective-permute-start | bytes 1769480 | tf_op jit(solution)/shard_map/ppermute | solution.py:23
  50.6 3.5 %collective-permute-start.4 = (bf16[9,128,256]{2,1,0:T(8,128)(2,1)}, bf16[9,128,256]{2,1,0:T(8,128)(2,1)S(1)}, u32[]{:S(2)}, u32[]{:S(2)}) collective-permute-start(bf16[9,128,256]{2,1,0:T(8,128)(2,1)} %get-tuple-element.39), channel_id=1, source_target_pairs={{0,2},{1,3},{2,0},{3,1},{4,6},{5,7},{6,4},{7,5},{8,10},{9,11},{10,... | collective-permute-start | bytes 1769480 | tf_op jit(solution)/shard_map/ppermute | solution.py:23
  54.1 3.6 %collective-permute-start.5 = (bf16[9,128,256]{2,1,0:T(8,128)(2,1)S(1)}, bf16[9,128,256]{2,1,0:T(8,128)(2,1)S(1)}, u32[]{:S(2)}, u32[]{:S(2)}) collective-permute-start(bf16[9,128,256]{2,1,0:T(8,128)(2,1)S(1)} %get-tuple-element.38), channel_id=1, source_target_pairs={{0,3},{1,0},{2,1},{3,2},{4,7},{5,4},{6,5},{7,6},{8,11},{9,8},{10,9... | collective-permute-start | bytes 1769480 | tf_op jit(solution)/shard_map/ppermute | solution.py:23
  57.7 1.9 collective-permute-start.8
  61.1 1.9 collective-permute-start.9
  63.0 1.6 collective-permute-done.3.a1.refs_2_
  64.6 13.4 %collective-permute-done.4.a2.refs_3_ = bf16[9,128,256]{2,1,0:T(8,128)(2,1)S(1)} collective-permute-done((bf16[9,128,256]{2,1,0:T(8,128)(2,1)}, bf16[9,128,256]{2,1,0:T(8,128)(2,1)S(1)}, u32[]{:S(2)}, u32[]{:S(2)}) %collective-permute-start.4) | collective-permute-done | bytes 589856 | tf_op jit(solution)/shard_map/ppermute | solution.py:23
  79.3 1.9 mesh_start.1.q
  81.3 3.4 %enc_attend.1 = bf16[4,256,128]{2,1,0:T(8,128)(2,1)} custom-call(s32[32]{0:T(128)S(1)} %concatenate.15.refs_0_.meta, s32[2,4]{1,0:T(2,128)S(1)} %copy-done.21, s32[1024]{0:T(1024)S(1)} %copy-done.20, bf16[256,128]{1,0:T(8,128)(2,1)S(1)} %mesh_start.1.q, bf16[1024,256]{1,0:T(8,128)(2,1)S(1)} %collective-permute-done.6.a0, bf16[1024,256]{1,0:T(8,128)(2,1)} %grid_project.1.a1, ...), custom_call_target="tpu_custom_call" | custom-call | tf_op jit(solution)/shard_map/enc_attend/pallas_call | solution.py:243
  85.0 2.1 collective-permute-start.10
  87.1 11.5 %all_to_all.20.o = bf16[4,256,128]{2,1,0:T(8,128)(2,1)S(1)} all-to-all(bf16[4,256,128]{2,1,0:T(8,128)(2,1)S(1)} %copy-done.22), channel_id=1, replica_groups=mesh['nodes'=128,'mp'=4] {'mp'}, dimensions={0} | all-to-all | bytes 524288 | tf_op jit(solution)/shard_map/all_to_all | solution.py:455
  98.6 2.4 %first_layer.1 = (bf16[4,256,256]{2,1,0:T(8,128)(2,1)S(1)}, bf16[256,256]{1,0:T(8,128)(2,1)S(1)}, bf16[256,128]{1,0:T(8,128)(2,1)S(1)}) custom-call(s32[32]{0:T(128)S(1)} %concatenate.15.refs_0_.meta, bf16[4,256,128]{2,1,0:T(8,128)(2,1)S(1)} %all_to_all.20.o, bf16[256,256]{1,0:T(8,128)(2,1)S(1)} %copy-done.11, ...), custom_call_target="tpu_custom_call" | custom-call | tf_op jit(solution)/shard_map/first_layer/pallas_call | solution.py:369
  101.9 6.9 %collective-permute-start.11 = (bf16[256,256]{1,0:T(8,128)(2,1)S(1)}, bf16[256,256]{1,0:T(8,128)(2,1)S(1)}, u32[]{:S(2)}, u32[]{:S(2)}) collective-permute-start(bf16[256,256]{1,0:T(8,128)(2,1)S(1)} %get-tuple-element.24.refs_3_), channel_id=1, source_target_pairs={{0,8},{4,12},{8,16},{12,20},{16,24},{20,28},{24,32},{28,36},{32,40... | collective-permute-start | bytes 393224 | tf_op jit(solution)/shard_map/ppermute | solution.py:29
  108.8 1.9 collective-permute-start.12
  110.7 1.9 collective-permute-start.13
  112.7 6.3 %collective-permute-done.12.refs_4_ = bf16[256,256]{1,0:T(8,128)(2,1)S(1)} collective-permute-done((bf16[256,256]{1,0:T(8,128)(2,1)S(1)}, bf16[256,256]{1,0:T(8,128)(2,1)S(1)}, u32[]{:S(2)}, u32[]{:S(2)}) %collective-permute-start.12) | collective-permute-done | bytes 131104 | tf_op jit(solution)/shard_map/ppermute | solution.py:29
  119.0 1.9 collective-permute-start.14
  122.3 2.5 %near_attend.3 = bf16[4,256,128]{2,1,0:T(8,128)(2,1)} custom-call(s32[32]{0:T(128)S(1)} %concatenate.15.refs_0_.meta, bf16[256,128]{1,0:T(8,128)(2,1)S(1)} %get-tuple-element.23.refs_1_, bf16[256,256]{1,0:T(8,128)(2,1)S(1)} %collective-permute-done.11.refs_2_, bf16[256,256]{1,0:T(8,128)(2,1)S(1)} %get-tuple-element.24.refs_3_, ...), custom_call_target="tpu_custom_call" | custom-call | tf_op jit(solution)/shard_map/near_attend/pallas_call | solution.py:271
  124.7 3.4 %all-to-all-start.1 = ((bf16[4,256,128]{2,1,0:T(8,128)(2,1)}), bf16[4,256,128]{2,1,0:T(8,128)(2,1)S(1)}, u32[]{:S(2)}, u32[]{:S(2)}) async-start(bf16[4,256,128]{2,1,0:T(8,128)(2,1)} %near_attend.3), calls=%async_computation.1 | async-start | bytes 524288 | tf_op jit(solution)/shard_map/all_to_all | solution.py:455
  129.4 2.8 %layer_weights.2 = (bf16[4,512,256]{2,1,0:T(8,128)(2,1)S(1)}, bf16[1024,384]{1,0:T(8,128)(2,1)S(1)}) custom-call(s32[32]{0:T(128)S(1)} %concatenate.15.refs_0_.meta, bf16[4,128,1024]{2,1,0:T(8,128)(2,1)} %refs_1_.7, bf16[9,128,256]{2,1,0:T(8,128)(2,1)S(1)} %collective-permute-done.3.a1.refs_2_, bf16[9,128,256]{2,1,0:T(8,128)(2,1)S(1)} %collective-permute-done.4.a2.refs_3_, ...), custom_call_target="tpu_custom_call" | custom-call | tf_op jit(solution)/shard_map/layer_weights/pallas_call | solution.py:314
  133.1 2.2 %all-to-all-done.1.refs_1_ = bf16[4,256,128]{2,1,0:T(8,128)(2,1)S(1)} async-done(((bf16[4,256,128]{2,1,0:T(8,128)(2,1)}), bf16[4,256,128]{2,1,0:T(8,128)(2,1)S(1)}, u32[]{:S(2)}, u32[]{:S(2)}) %all-to-all-start.1) | async-done | bytes 262176 | tf_op jit(solution)/shard_map/all_to_all | solution.py:455
  137.5 1.6 mesh_layer.2
  140.0 1.9 collective-permute-start.15
  141.9 3.9 %collective-permute-start.16 = (bf16[256,256]{1,0:T(8,128)(2,1)S(1)}, bf16[256,256]{1,0:T(8,128)(2,1)S(1)}, u32[]{:S(2)}, u32[]{:S(2)}) collective-permute-start(bf16[256,256]{1,0:T(8,128)(2,1)S(1)} %get-tuple-element.29.refs_3_), channel_id=1, source_target_pairs={{8,0},{12,4},{16,8},{20,12},{24,16},{28,20},{32,24},{36,28},{40,32... | collective-permute-start | bytes 393224 | tf_op jit(solution)/shard_map/ppermute | solution.py:29
  145.8 1.9 collective-permute-start.17
  147.8 4.3 %collective-permute-done.16.refs_4_ = bf16[256,256]{1,0:T(8,128)(2,1)S(1)} collective-permute-done((bf16[256,256]{1,0:T(8,128)(2,1)S(1)}, bf16[256,256]{1,0:T(8,128)(2,1)S(1)}, u32[]{:S(2)}, u32[]{:S(2)}) %collective-permute-start.16) | collective-permute-done | bytes 131104 | tf_op jit(solution)/shard_map/ppermute | solution.py:29
  152.1 1.9 collective-permute-start.18
  155.3 2.5 %near_attend.4 = bf16[4,256,128]{2,1,0:T(8,128)(2,1)} custom-call(s32[32]{0:T(128)S(1)} %concatenate.15.refs_0_.meta, bf16[256,128]{1,0:T(8,128)(2,1)S(1)} %get-tuple-element.28.refs_1_, bf16[256,256]{1,0:T(8,128)(2,1)S(1)} %collective-permute-done.15.refs_2_, bf16[256,256]{1,0:T(8,128)(2,1)S(1)} %get-tuple-element.29.refs_3_, ...), custom_call_target="tpu_custom_call" | custom-call | tf_op jit(solution)/shard_map/near_attend/pallas_call | solution.py:271
  157.8 3.4 %all-to-all-start.2 = ((bf16[4,256,128]{2,1,0:T(8,128)(2,1)}), bf16[4,256,128]{2,1,0:T(8,128)(2,1)S(1)}, u32[]{:S(2)}, u32[]{:S(2)}) async-start(bf16[4,256,128]{2,1,0:T(8,128)(2,1)} %near_attend.4), calls=%async_computation.2 | async-start | bytes 524288 | tf_op jit(solution)/shard_map/all_to_all | solution.py:455
  162.5 2.8 %layer_weights.3 = (bf16[4,512,256]{2,1,0:T(8,128)(2,1)S(1)}, bf16[1024,256]{1,0:T(8,128)(2,1)S(1)}) custom-call(s32[32]{0:T(128)S(1)} %concatenate.15.refs_0_.meta, bf16[4,128,1024]{2,1,0:T(8,128)(2,1)} %refs_1_.7, bf16[9,128,256]{2,1,0:T(8,128)(2,1)S(1)} %collective-permute-done.3.a1.refs_2_, bf16[9,128,256]{2,1,0:T(8,128)(2,1)S(1)} %collective-permute-done.4.a2.refs_3_, ...), custom_call_target="tpu_custom_call" | custom-call | tf_op jit(solution)/shard_map/layer_weights/pallas_call | solution.py:314
  166.1 2.4 %all-to-all-done.2.refs_1_ = bf16[4,256,128]{2,1,0:T(8,128)(2,1)S(1)} async-done(((bf16[4,256,128]{2,1,0:T(8,128)(2,1)}), bf16[4,256,128]{2,1,0:T(8,128)(2,1)S(1)}, u32[]{:S(2)}, u32[]{:S(2)}) %all-to-all-start.2) | async-done | bytes 262176 | tf_op jit(solution)/shard_map/all_to_all | solution.py:455
  170.5 2.2 %mesh_layer.3 = (bf16[256,256]{1,0:T(8,128)(2,1)}, bf16[256,256]{1,0:T(8,128)(2,1)S(1)}) custom-call(s32[32]{0:T(128)S(1)} %concatenate.15.refs_0_.meta, bf16[4,256,128]{2,1,0:T(8,128)(2,1)S(1)} %all-to-all-done.2.refs_1_, bf16[4,256,256]{2,1,0:T(8,128)(2,1)S(1)} %copy-done.15, f32[6,4,256]{2,1,0:T(4,128)S(1)} %reshape.24.refs_5_.gains.refs_3_, ...), custom_call_target="tpu_custom_call" | custom-call | tf_op jit(solution)/shard_map/mesh_layer/pallas_call | solution.py:412
  172.7 1.9 collective-permute-start.19
  174.6 3.9 %collective-permute-start.20 = (bf16[256,256]{1,0:T(8,128)(2,1)S(1)}, bf16[256,256]{1,0:T(8,128)(2,1)S(1)}, u32[]{:S(2)}, u32[]{:S(2)}) collective-permute-start(bf16[256,256]{1,0:T(8,128)(2,1)S(1)} %get-tuple-element.33.refs_3_), channel_id=1, source_target_pairs={{8,0},{12,4},{16,8},{20,12},{24,16},{28,20},{32,24},{36,28},{40,32... | collective-permute-start | bytes 393224 | tf_op jit(solution)/shard_map/ppermute | solution.py:29
  178.6 1.9 collective-permute-start.21
  180.5 4.3 %collective-permute-done.20.refs_4_ = bf16[256,256]{1,0:T(8,128)(2,1)S(1)} collective-permute-done((bf16[256,256]{1,0:T(8,128)(2,1)S(1)}, bf16[256,256]{1,0:T(8,128)(2,1)S(1)}, u32[]{:S(2)}, u32[]{:S(2)}) %collective-permute-start.20) | collective-permute-done | bytes 131104 | tf_op jit(solution)/shard_map/ppermute | solution.py:29
  184.8 2.1 collective-permute-start.22
  186.9 4.7 %grid_query.1.refs_1_ = bf16[1024,128]{1,0:T(8,128)(2,1)S(1)} custom-call(s32[32]{0:T(128)S(1)} %concatenate.15.refs_0_.meta, bf16[1024,256]{1,0:T(8,128)(2,1)} %grid_in.1, bf16[1024,256]{1,0:T(8,128)(2,1)S(1)} %copy-done.6, bf16[1024,256]{1,0:T(8,128)(2,1)S(1)} %copy-done.8, bf16[1024,256]{1,0:T(8,128)(2,1)S(1)} %copy-done.10, ...), custom_call_target="tpu_custom_call" | custom-call | flops 268435456 | bytes 4194304 | tf_op jit(solution)/shard_map/grid_query/pallas_call | solution.py:143
  191.8 1.7 near_attend.5
  193.5 18.6 %all_to_all.21.o = bf16[4,1024,128]{2,1,0:T(8,128)(2,1)S(1)} all-to-all(bf16[4,1024,128]{2,1,0:T(8,128)(2,1)S(1)} %near_attend.5), channel_id=1, replica_groups=mesh['nodes'=128,'mp'=4] {'mp'}, dimensions={0} | all-to-all | bytes 2097152 | tf_op jit(solution)/shard_map/all_to_all | solution.py:455
  212.1 2.0 grid_final.1
  (94 shorter events, 25.8 us)
Async XLA Ops:
  0.6 17.1 %collective-permute-start = (bf16[1024,256]{1,0:T(8,128)(2,1)}, bf16[1024,256]{1,0:T(8,128)(2,1)S(1)}, u32[]{:S(2)}, u32[]{:S(2)}) collective-permute-start(bf16[1024,256]{1,0:T(8,128)(2,1)} %grid_in.1), channel_id=1, source_target_pairs={{0,1},{1,2},{2,3},{3,0},{4,5},{5,6},{6,7},{7,4},{8,9},{9,10},{10,1... | collective-permute-start | bytes 1572872 | tf_op jit(solution)/shard_map/ppermute | solution.py:23
  4.1 26.0 %collective-permute-start.1 = (bf16[1024,256]{1,0:T(8,128)(2,1)}, bf16[1024,256]{1,0:T(8,128)(2,1)S(1)}, u32[]{:S(2)}, u32[]{:S(2)}) collective-permute-start(bf16[1024,256]{1,0:T(8,128)(2,1)} %grid_in.1), channel_id=1, source_target_pairs={{0,2},{1,3},{2,0},{3,1},{4,6},{5,7},{6,4},{7,5},{8,10},{9,11},{10,... | collective-permute-start | bytes 1572872 | tf_op jit(solution)/shard_map/ppermute | solution.py:23
  8.9 22.5 %collective-permute-start.2 = (bf16[1024,256]{1,0:T(8,128)(2,1)}, bf16[1024,256]{1,0:T(8,128)(2,1)S(1)}, u32[]{:S(2)}, u32[]{:S(2)}) collective-permute-start(bf16[1024,256]{1,0:T(8,128)(2,1)} %grid_in.1), channel_id=1, source_target_pairs={{0,3},{1,0},{2,1},{3,2},{4,7},{5,4},{6,5},{7,6},{8,11},{9,8},{10,9... | collective-permute-start | bytes 1572872 | tf_op jit(solution)/shard_map/ppermute | solution.py:23
  30.1 5.9 %copy-start.7 = (bf16[1024,256]{1,0:T(8,128)(2,1)}, bf16[1024,256]{1,0:T(8,128)(2,1)S(1)}, u32[]{:S(2)}) copy-start(bf16[1024,256]{1,0:T(8,128)(2,1)S(1)} %collective-permute-done.1.refs_3_) | copy-start | bytes 1572868
  31.5 4.5 %copy-start.9 = (bf16[1024,256]{1,0:T(8,128)(2,1)}, bf16[1024,256]{1,0:T(8,128)(2,1)S(1)}, u32[]{:S(2)}) copy-start(bf16[1024,256]{1,0:T(8,128)(2,1)S(1)} %collective-permute-done.2.refs_4_) | copy-start | bytes 1572868
  36.7 7.1 %slice-start = ((bf16[4,128,1024]{2,1,0:T(8,128)(2,1)}), bf16[1,128,1024]{2,1,0:T(8,128)(2,1)S(1)}, s32[]{:S(2)}) async-start(bf16[4,128,1024]{2,1,0:T(8,128)(2,1)} %refs_1_.7), calls=%async_computation.4 | async-start | bytes 524288 | tf_op jit(solution)/shard_map/slice | solution.py:511
  36.7 21.0 %collective-permute-start.6 = (bf16[1024,256]{1,0:T(8,128)(2,1)}, bf16[1024,256]{1,0:T(8,128)(2,1)S(1)}, u32[]{:S(2)}, u32[]{:S(2)}) collective-permute-start(bf16[1024,256]{1,0:T(8,128)(2,1)} %grid_project.1.a1), channel_id=1, source_target_pairs={{0,8},{4,12},{8,16},{12,20},{16,24},{20,28},{24,32},{28,36},{32,40... | collective-permute-start | bytes 1572872 | tf_op jit(solution)/shard_map/ppermute | solution.py:29
  41.8 18.1 %collective-permute-start.7 = (bf16[1024,256]{1,0:T(8,128)(2,1)}, bf16[1024,256]{1,0:T(8,128)(2,1)}, u32[]{:S(2)}, u32[]{:S(2)}) collective-permute-start(bf16[1024,256]{1,0:T(8,128)(2,1)} %grid_project.1.a1), channel_id=1, source_target_pairs={{8,0},{12,4},{16,8},{20,12},{24,16},{28,20},{32,24},{36,28},{40,32... | collective-permute-start | bytes 1572872 | tf_op jit(solution)/shard_map/ppermute | solution.py:29
  43.8 1.2 slice-start.1
  43.8 1.2 copy-start.11
  46.2 18.4 %collective-permute-start.3 = (bf16[9,128,256]{2,1,0:T(8,128)(2,1)}, bf16[9,128,256]{2,1,0:T(8,128)(2,1)S(1)}, u32[]{:S(2)}, u32[]{:S(2)}) collective-permute-start(bf16[9,128,256]{2,1,0:T(8,128)(2,1)} %get-tuple-element.40), channel_id=1, source_target_pairs={{0,1},{1,2},{2,3},{3,0},{4,5},{5,6},{6,7},{7,4},{8,9},{9,10},{10,1... | collective-permute-start | bytes 1769480 | tf_op jit(solution)/shard_map/ppermute | solution.py:23
  50.6 27.4 %collective-permute-start.4 = (bf16[9,128,256]{2,1,0:T(8,128)(2,1)}, bf16[9,128,256]{2,1,0:T(8,128)(2,1)S(1)}, u32[]{:S(2)}, u32[]{:S(2)}) collective-permute-start(bf16[9,128,256]{2,1,0:T(8,128)(2,1)} %get-tuple-element.39), channel_id=1, source_target_pairs={{0,2},{1,3},{2,0},{3,1},{4,6},{5,7},{6,4},{7,5},{8,10},{9,11},{10,... | collective-permute-start | bytes 1769480 | tf_op jit(solution)/shard_map/ppermute | solution.py:23
  54.1 25.2 %collective-permute-start.5 = (bf16[9,128,256]{2,1,0:T(8,128)(2,1)S(1)}, bf16[9,128,256]{2,1,0:T(8,128)(2,1)S(1)}, u32[]{:S(2)}, u32[]{:S(2)}) collective-permute-start(bf16[9,128,256]{2,1,0:T(8,128)(2,1)S(1)} %get-tuple-element.38), channel_id=1, source_target_pairs={{0,3},{1,0},{2,1},{3,2},{4,7},{5,4},{6,5},{7,6},{8,11},{9,8},{10,9... | collective-permute-start | bytes 1769480 | tf_op jit(solution)/shard_map/ppermute | solution.py:23
  57.7 23.6 %collective-permute-start.8 = (bf16[1024,256]{1,0:T(8,128)(2,1)}, bf16[1024,256]{1,0:T(8,128)(2,1)S(1)}, u32[]{:S(2)}, u32[]{:S(2)}) collective-permute-start(bf16[1024,256]{1,0:T(8,128)(2,1)} %grid_project.1.a1), channel_id=1, source_target_pairs={{0,4},{4,0},{8,12},{12,8},{16,20},{20,16},{24,28},{28,24},{32,36},... | collective-permute-start | bytes 1572872 | tf_op jit(solution)/shard_map/ppermute | solution.py:34
  61.1 20.2 %copy-start.20 = (s32[1024]{0:T(1024)S(1)}, s32[1024]{0:T(1024)}, u32[]{:S(2)}) copy-start(s32[1024]{0:T(1024)} %counts.3) | copy-start | bytes 12292
  61.1 20.2 %copy-start.21 = (s32[2,4]{1,0:T(2,128)S(1)}, s32[2,4]{1,0:T(2,128)}, u32[]{:S(2)}) copy-start(s32[2,4]{1,0:T(2,128)} %listed.1) | copy-start | bytes 100
  61.1 20.2 %collective-permute-start.9 = (bf16[1024,256]{1,0:T(8,128)(2,1)S(1)}, bf16[1024,256]{1,0:T(8,128)(2,1)S(1)}, u32[]{:S(2)}, u32[]{:S(2)}) collective-permute-start(bf16[1024,256]{1,0:T(8,128)(2,1)S(1)} %broadcast_select_fusion), channel_id=1, source_target_pairs={{0,4},{4,0},{8,12},{12,8},{16,20},{20,16},{24,28},{28,24},{32,36},... | collective-permute-start | bytes 1572872 | tf_op jit(solution)/shard_map/ppermute | solution.py:34
  84.8 2.2 %copy-start.22 = (bf16[4,256,128]{2,1,0:T(8,128)(2,1)S(1)}, bf16[4,256,128]{2,1,0:T(8,128)(2,1)}, u32[]{:S(2)}) copy-start(bf16[4,256,128]{2,1,0:T(8,128)(2,1)} %enc_attend.1) | copy-start | bytes 786436
  84.8 13.8 %copy-start = (bf16[4,128,1024]{2,1,0:T(8,128)(2,1)S(1)}, bf16[4,128,1024]{2,1,0:T(8,128)(2,1)}, u32[]{:S(2)}) copy-start(bf16[4,128,1024]{2,1,0:T(8,128)(2,1)} %refs_1_.7) | copy-start | bytes 3145732
  85.0 13.6 %collective-permute-start.10 = (bf16[3,6,128,256]{3,2,1,0:T(8,128)(2,1)S(1)}, bf16[3,6,128,256]{3,2,1,0:T(8,128)(2,1)S(1)}, u32[]{:S(2)}, u32[]{:S(2)}) collective-permute-start(bf16[3,6,128,256]{3,2,1,0:T(8,128)(2,1)S(1)} %pad_maximum_fusion), channel_id=1, source_target_pairs={{0,4},{4,0},{8,12},{12,8},{16,20},{20,16},{24,28},{28,24},{32,36},... | collective-permute-start | bytes 3538952 | tf_op jit(solution)/shard_map/ppermute | solution.py:34
  98.6 2.5 %copy-start.1 = (bf16[3,6,128,256]{3,2,1,0:T(8,128)(2,1)}, bf16[3,6,128,256]{3,2,1,0:T(8,128)(2,1)S(1)}, u32[]{:S(2)}) copy-start(bf16[3,6,128,256]{3,2,1,0:T(8,128)(2,1)S(1)} %collective-permute-done.10.other.refs_5_) | copy-start | bytes 3538948
  101.9 10.8 %collective-permute-start.11 = (bf16[256,256]{1,0:T(8,128)(2,1)S(1)}, bf16[256,256]{1,0:T(8,128)(2,1)S(1)}, u32[]{:S(2)}, u32[]{:S(2)}) collective-permute-start(bf16[256,256]{1,0:T(8,128)(2,1)S(1)} %get-tuple-element.24.refs_3_), channel_id=1, source_target_pairs={{0,8},{4,12},{8,16},{12,20},{16,24},{20,28},{24,32},{28,36},{32,40... | collective-permute-start | bytes 393224 | tf_op jit(solution)/shard_map/ppermute | solution.py:29
  108.8 10.2 %collective-permute-start.12 = (bf16[256,256]{1,0:T(8,128)(2,1)S(1)}, bf16[256,256]{1,0:T(8,128)(2,1)S(1)}, u32[]{:S(2)}, u32[]{:S(2)}) collective-permute-start(bf16[256,256]{1,0:T(8,128)(2,1)S(1)} %get-tuple-element.24.refs_3_), channel_id=1, source_target_pairs={{8,0},{12,4},{16,8},{20,12},{24,16},{28,20},{32,24},{36,28},{40,32... | collective-permute-start | bytes 393224 | tf_op jit(solution)/shard_map/ppermute | solution.py:29
  110.7 10.2 %collective-permute-start.13 = (bf16[256,256]{1,0:T(8,128)(2,1)S(1)}, bf16[256,256]{1,0:T(8,128)(2,1)S(1)}, u32[]{:S(2)}, u32[]{:S(2)}) collective-permute-start(bf16[256,256]{1,0:T(8,128)(2,1)S(1)} %get-tuple-element.24.refs_3_), channel_id=1, source_target_pairs={{0,4},{4,0},{8,12},{12,8},{16,20},{20,16},{24,28},{28,24},{32,36},... | collective-permute-start | bytes 393224 | tf_op jit(solution)/shard_map/ppermute | solution.py:34
  119.0 3.2 %collective-permute-start.14 = (bf16[256,256]{1,0:T(8,128)(2,1)S(1)}, bf16[256,256]{1,0:T(8,128)(2,1)S(1)}, u32[]{:S(2)}, u32[]{:S(2)}) collective-permute-start(bf16[256,256]{1,0:T(8,128)(2,1)S(1)} %broadcast_select_fusion.3), channel_id=1, source_target_pairs={{0,4},{4,0},{8,12},{12,8},{16,20},{20,16},{24,28},{28,24},{32,36},... | collective-permute-start | bytes 393224 | tf_op jit(solution)/shard_map/ppermute | solution.py:34
  124.7 10.6 %all-to-all-start.1 = ((bf16[4,256,128]{2,1,0:T(8,128)(2,1)}), bf16[4,256,128]{2,1,0:T(8,128)(2,1)S(1)}, u32[]{:S(2)}, u32[]{:S(2)}) async-start(bf16[4,256,128]{2,1,0:T(8,128)(2,1)} %near_attend.3), calls=%async_computation.1 | async-start | bytes 524288 | tf_op jit(solution)/shard_map/all_to_all | solution.py:455
  128.1 1.3 copy-start.2
  132.3 0.9 copy-start.12
  135.4 1.1 copy-start.13
  136.5 1.0 copy-start.17
  140.0 7.8 %collective-permute-start.15 = (bf16[256,256]{1,0:T(8,128)(2,1)S(1)}, bf16[256,256]{1,0:T(8,128)(2,1)S(1)}, u32[]{:S(2)}, u32[]{:S(2)}) collective-permute-start(bf16[256,256]{1,0:T(8,128)(2,1)S(1)} %get-tuple-element.29.refs_3_), channel_id=1, source_target_pairs={{0,8},{4,12},{8,16},{12,20},{16,24},{20,28},{24,32},{28,36},{32,40... | collective-permute-start | bytes 393224 | tf_op jit(solution)/shard_map/ppermute | solution.py:29
  141.9 10.2 %collective-permute-start.16 = (bf16[256,256]{1,0:T(8,128)(2,1)S(1)}, bf16[256,256]{1,0:T(8,128)(2,1)S(1)}, u32[]{:S(2)}, u32[]{:S(2)}) collective-permute-start(bf16[256,256]{1,0:T(8,128)(2,1)S(1)} %get-tuple-element.29.refs_3_), channel_id=1, source_target_pairs={{8,0},{12,4},{16,8},{20,12},{24,16},{28,20},{32,24},{36,28},{40,32... | collective-permute-start | bytes 393224 | tf_op jit(solution)/shard_map/ppermute | solution.py:29
  145.8 8.2 %collective-permute-start.17 = (bf16[256,256]{1,0:T(8,128)(2,1)S(1)}, bf16[256,256]{1,0:T(8,128)(2,1)S(1)}, u32[]{:S(2)}, u32[]{:S(2)}) collective-permute-start(bf16[256,256]{1,0:T(8,128)(2,1)S(1)} %get-tuple-element.29.refs_3_), channel_id=1, source_target_pairs={{0,4},{4,0},{8,12},{12,8},{16,20},{20,16},{24,28},{28,24},{32,36},... | collective-permute-start | bytes 393224 | tf_op jit(solution)/shard_map/ppermute | solution.py:34
  152.1 3.2 %collective-permute-start.18 = (bf16[256,256]{1,0:T(8,128)(2,1)S(1)}, bf16[256,256]{1,0:T(8,128)(2,1)S(1)}, u32[]{:S(2)}, u32[]{:S(2)}) collective-permute-start(bf16[256,256]{1,0:T(8,128)(2,1)S(1)} %broadcast_select_fusion.2), channel_id=1, source_target_pairs={{0,4},{4,0},{8,12},{12,8},{16,20},{20,16},{24,28},{28,24},{32,36},... | collective-permute-start | bytes 393224 | tf_op jit(solution)/shard_map/ppermute | solution.py:34
  157.8 10.6 %all-to-all-start.2 = ((bf16[4,256,128]{2,1,0:T(8,128)(2,1)}), bf16[4,256,128]{2,1,0:T(8,128)(2,1)S(1)}, u32[]{:S(2)}, u32[]{:S(2)}) async-start(bf16[4,256,128]{2,1,0:T(8,128)(2,1)} %near_attend.4), calls=%async_computation.2 | async-start | bytes 524288 | tf_op jit(solution)/shard_map/all_to_all | solution.py:455
  161.2 1.3 copy-start.3
  165.3 0.8 copy-start.18
  168.4 1.0 copy-start.15
  169.5 1.0 copy-start.19
  170.5 16.4 %copy-start.6 = (bf16[1024,256]{1,0:T(8,128)(2,1)S(1)}, bf16[1024,256]{1,0:T(8,128)(2,1)}, u32[]{:S(2)}) copy-start(bf16[1024,256]{1,0:T(8,128)(2,1)} %copy-done.5) | copy-start | bytes 1572868
  170.5 16.4 %copy-start.8 = (bf16[1024,256]{1,0:T(8,128)(2,1)S(1)}, bf16[1024,256]{1,0:T(8,128)(2,1)}, u32[]{:S(2)}) copy-start(bf16[1024,256]{1,0:T(8,128)(2,1)} %copy-done.7) | copy-start | bytes 1572868
  170.5 16.4 %copy-start.10 = (bf16[1024,256]{1,0:T(8,128)(2,1)S(1)}, bf16[1024,256]{1,0:T(8,128)(2,1)}, u32[]{:S(2)}) copy-start(bf16[1024,256]{1,0:T(8,128)(2,1)} %copy-done.9) | copy-start | bytes 1572868
  172.7 7.8 %collective-permute-start.19 = (bf16[256,256]{1,0:T(8,128)(2,1)S(1)}, bf16[256,256]{1,0:T(8,128)(2,1)S(1)}, u32[]{:S(2)}, u32[]{:S(2)}) collective-permute-start(bf16[256,256]{1,0:T(8,128)(2,1)S(1)} %get-tuple-element.33.refs_3_), channel_id=1, source_target_pairs={{0,8},{4,12},{8,16},{12,20},{16,24},{20,28},{24,32},{28,36},{32,40... | collective-permute-start | bytes 393224 | tf_op jit(solution)/shard_map/ppermute | solution.py:29
  174.6 10.2 %collective-permute-start.20 = (bf16[256,256]{1,0:T(8,128)(2,1)S(1)}, bf16[256,256]{1,0:T(8,128)(2,1)S(1)}, u32[]{:S(2)}, u32[]{:S(2)}) collective-permute-start(bf16[256,256]{1,0:T(8,128)(2,1)S(1)} %get-tuple-element.33.refs_3_), channel_id=1, source_target_pairs={{8,0},{12,4},{16,8},{20,12},{24,16},{28,20},{32,24},{36,28},{40,32... | collective-permute-start | bytes 393224 | tf_op jit(solution)/shard_map/ppermute | solution.py:29
  178.6 13.2 %collective-permute-start.21 = (bf16[256,256]{1,0:T(8,128)(2,1)S(1)}, bf16[256,256]{1,0:T(8,128)(2,1)S(1)}, u32[]{:S(2)}, u32[]{:S(2)}) collective-permute-start(bf16[256,256]{1,0:T(8,128)(2,1)S(1)} %get-tuple-element.33.refs_3_), channel_id=1, source_target_pairs={{0,4},{4,0},{8,12},{12,8},{16,20},{20,16},{24,28},{28,24},{32,36},... | collective-permute-start | bytes 393224 | tf_op jit(solution)/shard_map/ppermute | solution.py:34
  184.8 6.8 %copy-start.23 = (bf16[1,128,256]{2,1,0:T(8,128)(2,1)S(1)}, bf16[1,128,256]{2,1,0:T(8,128)(2,1)}, u32[]{:S(2)}) copy-start(bf16[1,128,256]{2,1,0:T(8,128)(2,1)} %get-tuple-element.41) | copy-start | bytes 196612
  184.8 6.9 %collective-permute-start.22 = (bf16[256,256]{1,0:T(8,128)(2,1)S(1)}, bf16[256,256]{1,0:T(8,128)(2,1)S(1)}, u32[]{:S(2)}, u32[]{:S(2)}) collective-permute-start(bf16[256,256]{1,0:T(8,128)(2,1)S(1)} %broadcast_select_fusion.1), channel_id=1, source_target_pairs={{0,4},{4,0},{8,12},{12,8},{16,20},{20,16},{24,28},{28,24},{32,36},... | collective-permute-start | bytes 393224 | tf_op jit(solution)/shard_map/ppermute | solution.py:34
  193.5 18.6 %copy-start.4 = (bf16[1024,256]{1,0:T(8,128)(2,1)S(1)}, bf16[1024,256]{1,0:T(8,128)(2,1)}, u32[]{:S(2)}) copy-start(bf16[1024,256]{1,0:T(8,128)(2,1)} %grid_in.1) | copy-start | bytes 1572868
  (3 other events, 2.4 us)

commit v6 on v5

--- a/solution.py
+++ b/solution.py
@@ -19,13 +19,16 @@
 PARAMS = pltpu.CompilerParams(vmem_limit_bytes=16 * 1024 * 1024)
 
 
-def shift_mp(value, steps):
-    return lax.ppermute(value, "mp", [(s, (s + steps) % MP) for s in range(MP)])
-
-
-def from_node(value, offset):
-    count = lax.axis_size("nodes")
-    pairs = [(s, s - offset) for s in range(count) if 0 <= s - offset < count]
+def swap_mp(value, k):
+    return lax.ppermute(value, "mp", [(s, s ^ k) for s in range(MP)])
+
+
+def swap_chips(value, first):
+    count = lax.axis_size("nodes") // 2
+    pairs = []
+    for c in range(first, count - 1, 2):
+        for core in range(2):
+            pairs += [(2 * c + core, 2 * c + 2 + core), (2 * c + 2 + core, 2 * c + core)]
     return lax.ppermute(value, "nodes", pairs)
 
 
@@ -54,7 +57,7 @@
 
 
 def source(meta, k):
-    return (meta[0] + MP - k) % MP
+    return meta[0] ^ k
 
 
 def normed(pieces):
@@ -212,7 +215,8 @@
 
 def window_places(meta):
     core = meta[1] % 2
-    return 0, 2, 4, 3 - 2 * core, 1 + 2 * core
+    odd = meta[1] // 2 % 2
+    return 4 * odd, 2, 4 - 4 * odd, 3 - 2 * core, 1 + 2 * core
 
 
 def enc_kernel(meta, listed, counts, q, a0, a1, a2, a3, a4, o_out, kept):
@@ -477,15 +481,15 @@
     def gathered(part, name):
         pieces = [part, None, None, None]
         for k in (1, 3, 2):
-            pieces[k] = shift_mp(part if name != "w" else part[k], k)
+            pieces[k] = swap_mp(part if name != "w" else part[k], k)
         return pieces
 
     def window(part):
-        low = from_node(part, -2)
-        high = from_node(part, 2)
+        across = swap_chips(part, 1)
+        within = swap_chips(part, 0)
         beside = swap_cores(part)
-        beyond = swap_cores(jnp.where(core == 0, high, low))
-        return [low, part, high, beside, beyond]
+        beyond = swap_cores(jnp.where((core == 0) == (own_node // 2 % 2 == 0), within, across))
+        return [across, part, within, beside, beyond]
 
     grid_pieces = gathered(grid_in, "g")
     grid_pieces[0] = pltpu.with_memory_space_constraint(grid_in, pltpu.HBM)
@@ -493,7 +497,7 @@
     halves = [lax.dynamic_slice_in_dim(w_out[:3], core * 512 + part * 256, 256, axis=2) for part in range(2)]
     sent = [None] * MP
     for k in (1, 2, 3):
-        last = lax.dynamic_slice_in_dim(w_out[3:], (own_mp + k) % MP * 256, 256, axis=2)
+        last = lax.dynamic_slice_in_dim(w_out[3:], (own_mp ^ k) * 256, 256, axis=2)
         sent[k] = jnp.concatenate([mesh_in.reshape(2, BLOCK, 256)] + halves + [last], axis=0)
     sent[0] = sent[1]
     arrived = gathered(sent, "w")[1:]

time: 216 us -> 215 us (level)
  the two profiles are of different devices: /device:TPU:230 before, /device:TPU:384 now
where the time goes in v6:
time: 215 us; the launch traced here: 213 us
  starting transfers between devices  72.1 us (34%)
  waiting for transfers between devices  55.8 us (26%)
  Pallas kernels  35 us (16%)
  blocking collectives  29.9 us (14%)
  local copies, waits for them, and re-layouts  14.4 us (7%)
  other arithmetic  4.57 us (2%)
    ppermute x6, waiting for transfers between devices, swap_mp(): return lax.ppermute(value, 'mp', [(s, s ^ k) for s in range(MP)])  39.9 us
    all_to_all x2, blocking collectives, gather_heads(): return lax.all_to_all(copies, 'mp', split_axis=0, concat_axis=0, tiled=True)  29.9 us
    ppermute x8, starting transfers between devices, swap_chips(): return lax.ppermute(value, 'nodes', pairs)  26.9 us
    ppermute x6, starting transfers between devices, swap_mp(): return lax.ppermute(value, 'mp', [(s, s ^ k) for s in range(MP)])  20.8 us
    ppermute x9, starting transfers between devices, swap_cores(): return lax.ppermute(value, 'nodes', [(s, s ^ 1) for s in range(count)])  17.5 us
    unnamed x48, local copies, waits for them, and re-layouts  10.9 us
    ppermute x8, waiting for transfers between devices, swap_chips(): return lax.ppermute(value, 'nodes', pairs)  8.69 us
    all_to_all x2, starting transfers between devices, gather_heads(): return lax.all_to_all(copies, 'mp', split_axis=0, concat_axis=0, tiled=True)  6.81 us
  transfers between devices with their start and end apart: 25, of which 14 were waited for; matrix products, arithmetic and copies ran while one was open for 3% of the time, Pallas kernels for 6%

profile of v6, /device:TPU:384, one launch (start us, length us, event | category | flops | bytes accessed | tf_op | source)
XLA Modules:
  0.0 213.1 jit_solution(9903353327163673654)
XLA Ops:
  0.6 3.5 %collective-permute-start = (bf16[1024,256]{1,0:T(8,128)(2,1)}, bf16[1024,256]{1,0:T(8,128)(2,1)S(1)}, u32[]{:S(2)}, u32[]{:S(2)}) collective-permute-start(bf16[1024,256]{1,0:T(8,128)(2,1)} %grid_in.1), channel_id=1, source_target_pairs={{0,1},{1,0},{2,3},{3,2},{4,5},{5,4},{6,7},{7,6},{8,9},{9,8},{10,11... | collective-permute-start | bytes 1572872 | tf_op jit(solution)/shard_map/ppermute | solution.py:23
  4.1 4.8 %collective-permute-start.1 = (bf16[1024,256]{1,0:T(8,128)(2,1)}, bf16[1024,256]{1,0:T(8,128)(2,1)S(1)}, u32[]{:S(2)}, u32[]{:S(2)}) collective-permute-start(bf16[1024,256]{1,0:T(8,128)(2,1)} %grid_in.1), channel_id=1, source_target_pairs={{0,2},{1,3},{2,0},{3,1},{4,6},{5,7},{6,4},{7,5},{8,10},{9,11},{10,... | collective-permute-start | bytes 1572872 | tf_op jit(solution)/shard_map/ppermute | solution.py:23
  8.9 2.1 %collective-permute-start.2 = (bf16[1024,256]{1,0:T(8,128)(2,1)}, bf16[1024,256]{1,0:T(8,128)(2,1)S(1)}, u32[]{:S(2)}, u32[]{:S(2)}) collective-permute-start(bf16[1024,256]{1,0:T(8,128)(2,1)} %grid_in.1), channel_id=1, source_target_pairs={{0,3},{1,2},{2,1},{3,0},{4,7},{5,6},{6,5},{7,4},{8,11},{9,10},{10,... | collective-permute-start | bytes 1572872 | tf_op jit(solution)/shard_map/ppermute | solution.py:23
  15.4 2.1 collective-permute-done.refs_2_
  17.5 12.7 %collective-permute-done.1.refs_3_ = bf16[1024,256]{1,0:T(8,128)(2,1)S(1)} collective-permute-done((bf16[1024,256]{1,0:T(8,128)(2,1)}, bf16[1024,256]{1,0:T(8,128)(2,1)S(1)}, u32[]{:S(2)}, u32[]{:S(2)}) %collective-permute-start.1) | collective-permute-done | bytes 524320 | tf_op jit(solution)/shard_map/ppermute | solution.py:23
  30.2 6.4 %collective-permute-done.2.refs_4_ = bf16[1024,256]{1,0:T(8,128)(2,1)S(1)} collective-permute-done((bf16[1024,256]{1,0:T(8,128)(2,1)}, bf16[1024,256]{1,0:T(8,128)(2,1)S(1)}, u32[]{:S(2)}, u32[]{:S(2)}) %collective-permute-start.2) | collective-permute-done | bytes 524320 | tf_op jit(solution)/shard_map/ppermute | solution.py:23
  36.6 4.5 %grid_project.1.a1 = bf16[1024,256]{1,0:T(8,128)(2,1)} custom-call(s32[32]{0:T(128)S(1)} %concatenate.15.refs_0_.meta, bf16[1024,256]{1,0:T(8,128)(2,1)} %grid_in.1, bf16[1024,256]{1,0:T(8,128)(2,1)S(1)} %collective-permute-done.refs_2_, bf16[1024,256]{1,0:T(8,128)(2,1)S(1)} %collective-permute-done.1.refs_3_, ...), custom_call_target="tpu_custom_call" | custom-call | flops 536870912 | bytes 4194304 | tf_op jit(solution)/shard_map/grid_project/pallas_call | solution.py:98
  41.9 6.4 %collective-permute-start.6 = (bf16[1024,256]{1,0:T(8,128)(2,1)}, bf16[1024,256]{1,0:T(8,128)(2,1)S(1)}, u32[]{:S(2)}, u32[]{:S(2)}) collective-permute-start(bf16[1024,256]{1,0:T(8,128)(2,1)} %grid_project.1.a1), channel_id=1, source_target_pairs={{8,16},{16,8},{12,20},{20,12},{24,32},{32,24},{28,36},{36,28},{40,... | collective-permute-start | bytes 1572872 | tf_op jit(solution)/shard_map/ppermute | solution.py:32
  48.3 1.9 collective-permute-start.7
  54.6 3.7 %collective-permute-start.4 = (bf16[9,128,256]{2,1,0:T(8,128)(2,1)}, bf16[9,128,256]{2,1,0:T(8,128)(2,1)S(1)}, u32[]{:S(2)}, u32[]{:S(2)}) collective-permute-start(bf16[9,128,256]{2,1,0:T(8,128)(2,1)} %get-tuple-element.39), channel_id=1, source_target_pairs={{0,2},{1,3},{2,0},{3,1},{4,6},{5,7},{6,4},{7,5},{8,10},{9,11},{10,... | collective-permute-start | bytes 1769480 | tf_op jit(solution)/shard_map/ppermute | solution.py:23
  58.3 4.8 %collective-permute-start.5 = (bf16[9,128,256]{2,1,0:T(8,128)(2,1)S(1)}, bf16[9,128,256]{2,1,0:T(8,128)(2,1)S(1)}, u32[]{:S(2)}, u32[]{:S(2)}) collective-permute-start(bf16[9,128,256]{2,1,0:T(8,128)(2,1)S(1)} %get-tuple-element.38), channel_id=1, source_target_pairs={{0,3},{1,2},{2,1},{3,0},{4,7},{5,6},{6,5},{7,4},{8,11},{9,10},{10,... | collective-permute-start | bytes 1769480 | tf_op jit(solution)/shard_map/ppermute | solution.py:23
  63.2 1.9 collective-permute-start.8
  66.3 1.9 collective-permute-start.9
  68.2 2.8 %collective-permute-done.3.a1.refs_2_ = bf16[9,128,256]{2,1,0:T(8,128)(2,1)S(1)} collective-permute-done((bf16[9,128,256]{2,1,0:T(8,128)(2,1)}, bf16[9,128,256]{2,1,0:T(8,128)(2,1)S(1)}, u32[]{:S(2)}, u32[]{:S(2)}) %collective-permute-start.3) | collective-permute-done | bytes 589856 | tf_op jit(solution)/shard_map/ppermute | solution.py:23
  71.0 9.7 %collective-permute-done.4.a2.refs_3_ = bf16[9,128,256]{2,1,0:T(8,128)(2,1)S(1)} collective-permute-done((bf16[9,128,256]{2,1,0:T(8,128)(2,1)}, bf16[9,128,256]{2,1,0:T(8,128)(2,1)S(1)}, u32[]{:S(2)}, u32[]{:S(2)}) %collective-permute-start.4) | collective-permute-done | bytes 589856 | tf_op jit(solution)/shard_map/ppermute | solution.py:23
  80.7 6.2 %collective-permute-done.5.a3.refs_4_ = bf16[9,128,256]{2,1,0:T(8,128)(2,1)S(1)} collective-permute-done((bf16[9,128,256]{2,1,0:T(8,128)(2,1)S(1)}, bf16[9,128,256]{2,1,0:T(8,128)(2,1)S(1)}, u32[]{:S(2)}, u32[]{:S(2)}) %collective-permute-start.5) | collective-permute-done | bytes 589856 | tf_op jit(solution)/shard_map/ppermute | solution.py:23
  86.9 1.9 mesh_start.1.q
  88.9 3.4 %enc_attend.1 = bf16[4,256,128]{2,1,0:T(8,128)(2,1)} custom-call(s32[32]{0:T(128)S(1)} %concatenate.15.refs_0_.meta, s32[2,4]{1,0:T(2,128)S(1)} %copy-done.21, s32[1024]{0:T(1024)S(1)} %copy-done.20, bf16[256,128]{1,0:T(8,128)(2,1)S(1)} %mesh_start.1.q, bf16[1024,256]{1,0:T(8,128)(2,1)S(1)} %collective-permute-done.6.a0, bf16[1024,256]{1,0:T(8,128)(2,1)} %grid_project.1.a1, ...), custom_call_target="tpu_custom_call" | custom-call | tf_op jit(solution)/shard_map/enc_attend/pallas_call | solution.py:247
  92.6 2.1 collective-permute-start.10
  94.6 11.3 %all_to_all.20.o = bf16[4,256,128]{2,1,0:T(8,128)(2,1)S(1)} all-to-all(bf16[4,256,128]{2,1,0:T(8,128)(2,1)S(1)} %copy-done.22), channel_id=1, replica_groups=mesh['nodes'=128,'mp'=4] {'mp'}, dimensions={0} | all-to-all | bytes 524288 | tf_op jit(solution)/shard_map/all_to_all | solution.py:459
  105.9 2.4 %first_layer.1 = (bf16[4,256,256]{2,1,0:T(8,128)(2,1)S(1)}, bf16[256,256]{1,0:T(8,128)(2,1)S(1)}, bf16[256,128]{1,0:T(8,128)(2,1)S(1)}) custom-call(s32[32]{0:T(128)S(1)} %concatenate.15.refs_0_.meta, bf16[4,256,128]{2,1,0:T(8,128)(2,1)S(1)} %all_to_all.20.o, bf16[256,256]{1,0:T(8,128)(2,1)S(1)} %copy-done.11, ...), custom_call_target="tpu_custom_call" | custom-call | tf_op jit(solution)/shard_map/first_layer/pallas_call | solution.py:373
  109.2 3.0 %collective-permute-start.11 = (bf16[256,256]{1,0:T(8,128)(2,1)S(1)}, bf16[256,256]{1,0:T(8,128)(2,1)S(1)}, u32[]{:S(2)}, u32[]{:S(2)}) collective-permute-start(bf16[256,256]{1,0:T(8,128)(2,1)S(1)} %get-tuple-element.24.refs_3_), channel_id=1, source_target_pairs={{8,16},{16,8},{12,20},{20,12},{24,32},{32,24},{28,36},{36,28},{40,... | collective-permute-start | bytes 393224 | tf_op jit(solution)/shard_map/ppermute | solution.py:32
  112.1 2.6 %collective-permute-start.12 = (bf16[256,256]{1,0:T(8,128)(2,1)S(1)}, bf16[256,256]{1,0:T(8,128)(2,1)S(1)}, u32[]{:S(2)}, u32[]{:S(2)}) collective-permute-start(bf16[256,256]{1,0:T(8,128)(2,1)S(1)} %get-tuple-element.24.refs_3_), channel_id=1, source_target_pairs={{0,8},{8,0},{4,12},{12,4},{16,24},{24,16},{20,28},{28,20},{32,40},... | collective-permute-start | bytes 393224 | tf_op jit(solution)/shard_map/ppermute | solution.py:32
  114.7 1.9 collective-permute-start.13
  116.7 2.7 %collective-permute-done.11.refs_2_ = bf16[256,256]{1,0:T(8,128)(2,1)S(1)} collective-permute-done((bf16[256,256]{1,0:T(8,128)(2,1)S(1)}, bf16[256,256]{1,0:T(8,128)(2,1)S(1)}, u32[]{:S(2)}, u32[]{:S(2)}) %collective-permute-start.11) | collective-permute-done | bytes 131104 | tf_op jit(solution)/shard_map/ppermute | solution.py:32
  119.4 1.9 collective-permute-start.14
  122.6 2.5 %near_attend.3 = bf16[4,256,128]{2,1,0:T(8,128)(2,1)} custom-call(s32[32]{0:T(128)S(1)} %concatenate.15.refs_0_.meta, bf16[256,128]{1,0:T(8,128)(2,1)S(1)} %get-tuple-element.23.refs_1_, bf16[256,256]{1,0:T(8,128)(2,1)S(1)} %collective-permute-done.11.refs_2_, bf16[256,256]{1,0:T(8,128)(2,1)S(1)} %get-tuple-element.24.refs_3_, ...), custom_call_target="tpu_custom_call" | custom-call | tf_op jit(solution)/shard_map/near_attend/pallas_call | solution.py:275
  125.1 3.4 %all-to-all-start.1 = ((bf16[4,256,128]{2,1,0:T(8,128)(2,1)}), bf16[4,256,128]{2,1,0:T(8,128)(2,1)S(1)}, u32[]{:S(2)}, u32[]{:S(2)}) async-start(bf16[4,256,128]{2,1,0:T(8,128)(2,1)} %near_attend.3), calls=%async_computation.1 | async-start | bytes 524288 | tf_op jit(solution)/shard_map/all_to_all | solution.py:459
  129.8 2.8 %layer_weights.2 = (bf16[4,512,256]{2,1,0:T(8,128)(2,1)S(1)}, bf16[1024,384]{1,0:T(8,128)(2,1)S(1)}) custom-call(s32[32]{0:T(128)S(1)} %concatenate.15.refs_0_.meta, bf16[4,128,1024]{2,1,0:T(8,128)(2,1)} %refs_1_.7, bf16[9,128,256]{2,1,0:T(8,128)(2,1)S(1)} %collective-permute-done.3.a1.refs_2_, bf16[9,128,256]{2,1,0:T(8,128)(2,1)S(1)} %collective-permute-done.4.a2.refs_3_, ...), custom_call_target="tpu_custom_call" | custom-call | tf_op jit(solution)/shard_map/layer_weights/pallas_call | solution.py:318
  133.5 2.2 %all-to-all-done.1.refs_1_ = bf16[4,256,128]{2,1,0:T(8,128)(2,1)S(1)} async-done(((bf16[4,256,128]{2,1,0:T(8,128)(2,1)}), bf16[4,256,128]{2,1,0:T(8,128)(2,1)S(1)}, u32[]{:S(2)}, u32[]{:S(2)}) %all-to-all-start.1) | async-done | bytes 262176 | tf_op jit(solution)/shard_map/all_to_all | solution.py:459
  140.3 5.8 %collective-permute-start.15 = (bf16[256,256]{1,0:T(8,128)(2,1)S(1)}, bf16[256,256]{1,0:T(8,128)(2,1)S(1)}, u32[]{:S(2)}, u32[]{:S(2)}) collective-permute-start(bf16[256,256]{1,0:T(8,128)(2,1)S(1)} %get-tuple-element.29.refs_3_), channel_id=1, source_target_pairs={{8,16},{16,8},{12,20},{20,12},{24,32},{32,24},{28,36},{36,28},{40,... | collective-permute-start | bytes 393224 | tf_op jit(solution)/shard_map/ppermute | solution.py:32
  146.2 1.9 collective-permute-start.16
  148.1 1.9 collective-permute-start.17
  150.5 2.5 %collective-permute-done.16.refs_4_ = bf16[256,256]{1,0:T(8,128)(2,1)S(1)} collective-permute-done((bf16[256,256]{1,0:T(8,128)(2,1)S(1)}, bf16[256,256]{1,0:T(8,128)(2,1)S(1)}, u32[]{:S(2)}, u32[]{:S(2)}) %collective-permute-start.16) | collective-permute-done | bytes 131104 | tf_op jit(solution)/shard_map/ppermute | solution.py:32
  153.1 1.9 collective-permute-start.18
  156.3 2.5 %near_attend.4 = bf16[4,256,128]{2,1,0:T(8,128)(2,1)} custom-call(s32[32]{0:T(128)S(1)} %concatenate.15.refs_0_.meta, bf16[256,128]{1,0:T(8,128)(2,1)S(1)} %get-tuple-element.28.refs_1_, bf16[256,256]{1,0:T(8,128)(2,1)S(1)} %collective-permute-done.15.refs_2_, bf16[256,256]{1,0:T(8,128)(2,1)S(1)} %get-tuple-element.29.refs_3_, ...), custom_call_target="tpu_custom_call" | custom-call | tf_op jit(solution)/shard_map/near_attend/pallas_call | solution.py:275
  158.8 3.4 %all-to-all-start.2 = ((bf16[4,256,128]{2,1,0:T(8,128)(2,1)}), bf16[4,256,128]{2,1,0:T(8,128)(2,1)S(1)}, u32[]{:S(2)}, u32[]{:S(2)}) async-start(bf16[4,256,128]{2,1,0:T(8,128)(2,1)} %near_attend.4), calls=%async_computation.2 | async-start | bytes 524288 | tf_op jit(solution)/shard_map/all_to_all | solution.py:459
  163.5 2.8 %layer_weights.3 = (bf16[4,512,256]{2,1,0:T(8,128)(2,1)S(1)}, bf16[1024,256]{1,0:T(8,128)(2,1)S(1)}) custom-call(s32[32]{0:T(128)S(1)} %concatenate.15.refs_0_.meta, bf16[4,128,1024]{2,1,0:T(8,128)(2,1)} %refs_1_.7, bf16[9,128,256]{2,1,0:T(8,128)(2,1)S(1)} %collective-permute-done.3.a1.refs_2_, bf16[9,128,256]{2,1,0:T(8,128)(2,1)S(1)} %collective-permute-done.4.a2.refs_3_, ...), custom_call_target="tpu_custom_call" | custom-call | tf_op jit(solution)/shard_map/layer_weights/pallas_call | solution.py:318
  167.1 2.4 %all-to-all-done.2.refs_1_ = bf16[4,256,128]{2,1,0:T(8,128)(2,1)S(1)} async-done(((bf16[4,256,128]{2,1,0:T(8,128)(2,1)}), bf16[4,256,128]{2,1,0:T(8,128)(2,1)S(1)}, u32[]{:S(2)}, u32[]{:S(2)}) %all-to-all-start.2) | async-done | bytes 262176 | tf_op jit(solution)/shard_map/all_to_all | solution.py:459
  171.5 2.2 %mesh_layer.3 = (bf16[256,256]{1,0:T(8,128)(2,1)}, bf16[256,256]{1,0:T(8,128)(2,1)S(1)}) custom-call(s32[32]{0:T(128)S(1)} %concatenate.15.refs_0_.meta, bf16[4,256,128]{2,1,0:T(8,128)(2,1)S(1)} %all-to-all-done.2.refs_1_, bf16[4,256,256]{2,1,0:T(8,128)(2,1)S(1)} %copy-done.15, f32[6,4,256]{2,1,0:T(4,128)S(1)} %reshape.24.refs_5_.gains.refs_3_, ...), custom_call_target="tpu_custom_call" | custom-call | tf_op jit(solution)/shard_map/mesh_layer/pallas_call | solution.py:416
  173.7 3.3 %collective-permute-start.19 = (bf16[256,256]{1,0:T(8,128)(2,1)S(1)}, bf16[256,256]{1,0:T(8,128)(2,1)S(1)}, u32[]{:S(2)}, u32[]{:S(2)}) collective-permute-start(bf16[256,256]{1,0:T(8,128)(2,1)S(1)} %get-tuple-element.33.refs_3_), channel_id=1, source_target_pairs={{8,16},{16,8},{12,20},{20,12},{24,32},{32,24},{28,36},{36,28},{40,... | collective-permute-start | bytes 393224 | tf_op jit(solution)/shard_map/ppermute | solution.py:32
  177.0 1.9 collective-permute-start.20
  178.9 1.9 collective-permute-start.21
  180.9 3.0 %collective-permute-done.19.refs_2_ = bf16[256,256]{1,0:T(8,128)(2,1)S(1)} collective-permute-done((bf16[256,256]{1,0:T(8,128)(2,1)S(1)}, bf16[256,256]{1,0:T(8,128)(2,1)S(1)}, u32[]{:S(2)}, u32[]{:S(2)}) %collective-permute-start.19) | collective-permute-done | bytes 131104 | tf_op jit(solution)/shard_map/ppermute | solution.py:32
  183.9 2.1 collective-permute-start.22
  186.0 4.7 %grid_query.1.refs_1_ = bf16[1024,128]{1,0:T(8,128)(2,1)S(1)} custom-call(s32[32]{0:T(128)S(1)} %concatenate.15.refs_0_.meta, bf16[1024,256]{1,0:T(8,128)(2,1)} %grid_in.1, bf16[1024,256]{1,0:T(8,128)(2,1)S(1)} %copy-done.6, bf16[1024,256]{1,0:T(8,128)(2,1)S(1)} %copy-done.8, bf16[1024,256]{1,0:T(8,128)(2,1)S(1)} %copy-done.10, ...), custom_call_target="tpu_custom_call" | custom-call | flops 268435456 | bytes 4194304 | tf_op jit(solution)/shard_map/grid_query/pallas_call | solution.py:146
  192.5 18.6 %all_to_all.21.o = bf16[4,1024,128]{2,1,0:T(8,128)(2,1)S(1)} all-to-all(bf16[4,1024,128]{2,1,0:T(8,128)(2,1)S(1)} %near_attend.5), channel_id=1, replica_groups=mesh['nodes'=128,'mp'=4] {'mp'}, dimensions={0} | all-to-all | bytes 2097152 | tf_op jit(solution)/shard_map/all_to_all | solution.py:459
  211.1 2.0 grid_final.1
  (94 shorter events, 27.3 us)
Async XLA Ops:
  0.6 16.9 %collective-permute-start = (bf16[1024,256]{1,0:T(8,128)(2,1)}, bf16[1024,256]{1,0:T(8,128)(2,1)S(1)}, u32[]{:S(2)}, u32[]{:S(2)}) collective-permute-start(bf16[1024,256]{1,0:T(8,128)(2,1)} %grid_in.1), channel_id=1, source_target_pairs={{0,1},{1,0},{2,3},{3,2},{4,5},{5,4},{6,7},{7,6},{8,9},{9,8},{10,11... | collective-permute-start | bytes 1572872 | tf_op jit(solution)/shard_map/ppermute | solution.py:23
  4.1 26.1 %collective-permute-start.1 = (bf16[1024,256]{1,0:T(8,128)(2,1)}, bf16[1024,256]{1,0:T(8,128)(2,1)S(1)}, u32[]{:S(2)}, u32[]{:S(2)}) collective-permute-start(bf16[1024,256]{1,0:T(8,128)(2,1)} %grid_in.1), channel_id=1, source_target_pairs={{0,2},{1,3},{2,0},{3,1},{4,6},{5,7},{6,4},{7,5},{8,10},{9,11},{10,... | collective-permute-start | bytes 1572872 | tf_op jit(solution)/shard_map/ppermute | solution.py:23
  8.9 27.7 %collective-permute-start.2 = (bf16[1024,256]{1,0:T(8,128)(2,1)}, bf16[1024,256]{1,0:T(8,128)(2,1)S(1)}, u32[]{:S(2)}, u32[]{:S(2)}) collective-permute-start(bf16[1024,256]{1,0:T(8,128)(2,1)} %grid_in.1), channel_id=1, source_target_pairs={{0,3},{1,2},{2,1},{3,0},{4,7},{5,6},{6,5},{7,4},{8,11},{9,10},{10,... | collective-permute-start | bytes 1572872 | tf_op jit(solution)/shard_map/ppermute | solution.py:23
  30.2 10.9 %copy-start.7 = (bf16[1024,256]{1,0:T(8,128)(2,1)}, bf16[1024,256]{1,0:T(8,128)(2,1)S(1)}, u32[]{:S(2)}) copy-start(bf16[1024,256]{1,0:T(8,128)(2,1)S(1)} %collective-permute-done.1.refs_3_) | copy-start | bytes 1572868
  36.6 4.5 %copy-start.9 = (bf16[1024,256]{1,0:T(8,128)(2,1)}, bf16[1024,256]{1,0:T(8,128)(2,1)S(1)}, u32[]{:S(2)}) copy-start(bf16[1024,256]{1,0:T(8,128)(2,1)S(1)} %collective-permute-done.2.refs_4_) | copy-start | bytes 1572868
  41.9 8.4 %slice-start = ((bf16[4,128,1024]{2,1,0:T(8,128)(2,1)}), bf16[1,128,1024]{2,1,0:T(8,128)(2,1)S(1)}, s32[]{:S(2)}) async-start(bf16[4,128,1024]{2,1,0:T(8,128)(2,1)} %refs_1_.7), calls=%async_computation.4 | async-start | bytes 524288 | tf_op jit(solution)/shard_map/slice | solution.py:515
  41.9 21.3 %collective-permute-start.6 = (bf16[1024,256]{1,0:T(8,128)(2,1)}, bf16[1024,256]{1,0:T(8,128)(2,1)S(1)}, u32[]{:S(2)}, u32[]{:S(2)}) collective-permute-start(bf16[1024,256]{1,0:T(8,128)(2,1)} %grid_project.1.a1), channel_id=1, source_target_pairs={{8,16},{16,8},{12,20},{20,12},{24,32},{32,24},{28,36},{36,28},{40,... | collective-permute-start | bytes 1572872 | tf_op jit(solution)/shard_map/ppermute | solution.py:32
  48.3 16.8 %collective-permute-start.7 = (bf16[1024,256]{1,0:T(8,128)(2,1)}, bf16[1024,256]{1,0:T(8,128)(2,1)}, u32[]{:S(2)}, u32[]{:S(2)}) collective-permute-start(bf16[1024,256]{1,0:T(8,128)(2,1)} %grid_project.1.a1), channel_id=1, source_target_pairs={{0,8},{8,0},{4,12},{12,4},{16,24},{24,16},{20,28},{28,20},{32,40},... | collective-permute-start | bytes 1572872 | tf_op jit(solution)/shard_map/ppermute | solution.py:32
  50.3 1.2 slice-start.1
  50.3 1.2 copy-start.11
  52.7 18.3 %collective-permute-start.3 = (bf16[9,128,256]{2,1,0:T(8,128)(2,1)}, bf16[9,128,256]{2,1,0:T(8,128)(2,1)S(1)}, u32[]{:S(2)}, u32[]{:S(2)}) collective-permute-start(bf16[9,128,256]{2,1,0:T(8,128)(2,1)} %get-tuple-element.40), channel_id=1, source_target_pairs={{0,1},{1,0},{2,3},{3,2},{4,5},{5,4},{6,7},{7,6},{8,9},{9,8},{10,11... | collective-permute-start | bytes 1769480 | tf_op jit(solution)/shard_map/ppermute | solution.py:23
  54.6 26.1 %collective-permute-start.4 = (bf16[9,128,256]{2,1,0:T(8,128)(2,1)}, bf16[9,128,256]{2,1,0:T(8,128)(2,1)S(1)}, u32[]{:S(2)}, u32[]{:S(2)}) collective-permute-start(bf16[9,128,256]{2,1,0:T(8,128)(2,1)} %get-tuple-element.39), channel_id=1, source_target_pairs={{0,2},{1,3},{2,0},{3,1},{4,6},{5,7},{6,4},{7,5},{8,10},{9,11},{10,... | collective-permute-start | bytes 1769480 | tf_op jit(solution)/shard_map/ppermute | solution.py:23
  58.3 28.6 %collective-permute-start.5 = (bf16[9,128,256]{2,1,0:T(8,128)(2,1)S(1)}, bf16[9,128,256]{2,1,0:T(8,128)(2,1)S(1)}, u32[]{:S(2)}, u32[]{:S(2)}) collective-permute-start(bf16[9,128,256]{2,1,0:T(8,128)(2,1)S(1)} %get-tuple-element.38), channel_id=1, source_target_pairs={{0,3},{1,2},{2,1},{3,0},{4,7},{5,6},{6,5},{7,4},{8,11},{9,10},{10,... | collective-permute-start | bytes 1769480 | tf_op jit(solution)/shard_map/ppermute | solution.py:23
  63.2 25.7 %collective-permute-start.8 = (bf16[1024,256]{1,0:T(8,128)(2,1)}, bf16[1024,256]{1,0:T(8,128)(2,1)S(1)}, u32[]{:S(2)}, u32[]{:S(2)}) collective-permute-start(bf16[1024,256]{1,0:T(8,128)(2,1)} %grid_project.1.a1), channel_id=1, source_target_pairs={{0,4},{4,0},{8,12},{12,8},{16,20},{20,16},{24,28},{28,24},{32,36},... | collective-permute-start | bytes 1572872 | tf_op jit(solution)/shard_map/ppermute | solution.py:37
  66.2 22.6 %copy-start.20 = (s32[1024]{0:T(1024)S(1)}, s32[1024]{0:T(1024)}, u32[]{:S(2)}) copy-start(s32[1024]{0:T(1024)} %counts.3) | copy-start | bytes 12292
  66.2 22.6 %copy-start.21 = (s32[2,4]{1,0:T(2,128)S(1)}, s32[2,4]{1,0:T(2,128)}, u32[]{:S(2)}) copy-start(s32[2,4]{1,0:T(2,128)} %listed.1) | copy-start | bytes 100
  66.3 22.6 %collective-permute-start.9 = (bf16[1024,256]{1,0:T(8,128)(2,1)S(1)}, bf16[1024,256]{1,0:T(8,128)(2,1)S(1)}, u32[]{:S(2)}, u32[]{:S(2)}) collective-permute-start(bf16[1024,256]{1,0:T(8,128)(2,1)S(1)} %broadcast_select_fusion), channel_id=1, source_target_pairs={{0,4},{4,0},{8,12},{12,8},{16,20},{20,16},{24,28},{28,24},{32,36},... | collective-permute-start | bytes 1572872 | tf_op jit(solution)/shard_map/ppermute | solution.py:37
  92.4 2.2 %copy-start.22 = (bf16[4,256,128]{2,1,0:T(8,128)(2,1)S(1)}, bf16[4,256,128]{2,1,0:T(8,128)(2,1)}, u32[]{:S(2)}) copy-start(bf16[4,256,128]{2,1,0:T(8,128)(2,1)} %enc_attend.1) | copy-start | bytes 786436
  92.4 13.5 %copy-start = (bf16[4,128,1024]{2,1,0:T(8,128)(2,1)S(1)}, bf16[4,128,1024]{2,1,0:T(8,128)(2,1)}, u32[]{:S(2)}) copy-start(bf16[4,128,1024]{2,1,0:T(8,128)(2,1)} %refs_1_.7) | copy-start | bytes 3145732
  92.6 13.3 %collective-permute-start.10 = (bf16[3,6,128,256]{3,2,1,0:T(8,128)(2,1)S(1)}, bf16[3,6,128,256]{3,2,1,0:T(8,128)(2,1)S(1)}, u32[]{:S(2)}, u32[]{:S(2)}) collective-permute-start(bf16[3,6,128,256]{3,2,1,0:T(8,128)(2,1)S(1)} %pad_maximum_fusion), channel_id=1, source_target_pairs={{0,4},{4,0},{8,12},{12,8},{16,20},{20,16},{24,28},{28,24},{32,36},... | collective-permute-start | bytes 3538952 | tf_op jit(solution)/shard_map/ppermute | solution.py:37
  105.9 2.5 %copy-start.1 = (bf16[3,6,128,256]{3,2,1,0:T(8,128)(2,1)}, bf16[3,6,128,256]{3,2,1,0:T(8,128)(2,1)S(1)}, u32[]{:S(2)}) copy-start(bf16[3,6,128,256]{3,2,1,0:T(8,128)(2,1)S(1)} %collective-permute-done.10.other.refs_5_) | copy-start | bytes 3538948
  109.2 10.2 %collective-permute-start.11 = (bf16[256,256]{1,0:T(8,128)(2,1)S(1)}, bf16[256,256]{1,0:T(8,128)(2,1)S(1)}, u32[]{:S(2)}, u32[]{:S(2)}) collective-permute-start(bf16[256,256]{1,0:T(8,128)(2,1)S(1)} %get-tuple-element.24.refs_3_), channel_id=1, source_target_pairs={{8,16},{16,8},{12,20},{20,12},{24,32},{32,24},{28,36},{36,28},{40,... | collective-permute-start | bytes 393224 | tf_op jit(solution)/shard_map/ppermute | solution.py:32
  112.1 7.2 %collective-permute-start.12 = (bf16[256,256]{1,0:T(8,128)(2,1)S(1)}, bf16[256,256]{1,0:T(8,128)(2,1)S(1)}, u32[]{:S(2)}, u32[]{:S(2)}) collective-permute-start(bf16[256,256]{1,0:T(8,128)(2,1)S(1)} %get-tuple-element.24.refs_3_), channel_id=1, source_target_pairs={{0,8},{8,0},{4,12},{12,4},{16,24},{24,16},{20,28},{28,20},{32,40},... | collective-permute-start | bytes 393224 | tf_op jit(solution)/shard_map/ppermute | solution.py:32
  114.7 6.6 %collective-permute-start.13 = (bf16[256,256]{1,0:T(8,128)(2,1)S(1)}, bf16[256,256]{1,0:T(8,128)(2,1)S(1)}, u32[]{:S(2)}, u32[]{:S(2)}) collective-permute-start(bf16[256,256]{1,0:T(8,128)(2,1)S(1)} %get-tuple-element.24.refs_3_), channel_id=1, source_target_pairs={{0,4},{4,0},{8,12},{12,8},{16,20},{20,16},{24,28},{28,24},{32,36},... | collective-permute-start | bytes 393224 | tf_op jit(solution)/shard_map/ppermute | solution.py:37
  119.4 3.2 %collective-permute-start.14 = (bf16[256,256]{1,0:T(8,128)(2,1)S(1)}, bf16[256,256]{1,0:T(8,128)(2,1)S(1)}, u32[]{:S(2)}, u32[]{:S(2)}) collective-permute-start(bf16[256,256]{1,0:T(8,128)(2,1)S(1)} %broadcast_select_fusion.3), channel_id=1, source_target_pairs={{0,4},{4,0},{8,12},{12,8},{16,20},{20,16},{24,28},{28,24},{32,36},... | collective-permute-start | bytes 393224 | tf_op jit(solution)/shard_map/ppermute | solution.py:37
  125.1 10.6 %all-to-all-start.1 = ((bf16[4,256,128]{2,1,0:T(8,128)(2,1)}), bf16[4,256,128]{2,1,0:T(8,128)(2,1)S(1)}, u32[]{:S(2)}, u32[]{:S(2)}) async-start(bf16[4,256,128]{2,1,0:T(8,128)(2,1)} %near_attend.3), calls=%async_computation.1 | async-start | bytes 524288 | tf_op jit(solution)/shard_map/all_to_all | solution.py:459
  128.5 1.3 copy-start.2
  132.6 0.9 copy-start.12
  135.7 1.1 copy-start.13
  136.9 1.0 copy-start.17
  140.3 10.2 %collective-permute-start.15 = (bf16[256,256]{1,0:T(8,128)(2,1)S(1)}, bf16[256,256]{1,0:T(8,128)(2,1)S(1)}, u32[]{:S(2)}, u32[]{:S(2)}) collective-permute-start(bf16[256,256]{1,0:T(8,128)(2,1)S(1)} %get-tuple-element.29.refs_3_), channel_id=1, source_target_pairs={{8,16},{16,8},{12,20},{20,12},{24,32},{32,24},{28,36},{36,28},{40,... | collective-permute-start | bytes 393224 | tf_op jit(solution)/shard_map/ppermute | solution.py:32
  146.2 6.9 %collective-permute-start.16 = (bf16[256,256]{1,0:T(8,128)(2,1)S(1)}, bf16[256,256]{1,0:T(8,128)(2,1)S(1)}, u32[]{:S(2)}, u32[]{:S(2)}) collective-permute-start(bf16[256,256]{1,0:T(8,128)(2,1)S(1)} %get-tuple-element.29.refs_3_), channel_id=1, source_target_pairs={{0,8},{8,0},{4,12},{12,4},{16,24},{24,16},{20,28},{28,20},{32,40},... | collective-permute-start | bytes 393224 | tf_op jit(solution)/shard_map/ppermute | solution.py:32
  148.1 6.9 %collective-permute-start.17 = (bf16[256,256]{1,0:T(8,128)(2,1)S(1)}, bf16[256,256]{1,0:T(8,128)(2,1)S(1)}, u32[]{:S(2)}, u32[]{:S(2)}) collective-permute-start(bf16[256,256]{1,0:T(8,128)(2,1)S(1)} %get-tuple-element.29.refs_3_), channel_id=1, source_target_pairs={{0,4},{4,0},{8,12},{12,8},{16,20},{20,16},{24,28},{28,24},{32,36},... | collective-permute-start | bytes 393224 | tf_op jit(solution)/shard_map/ppermute | solution.py:37
  153.1 3.2 %collective-permute-start.18 = (bf16[256,256]{1,0:T(8,128)(2,1)S(1)}, bf16[256,256]{1,0:T(8,128)(2,1)S(1)}, u32[]{:S(2)}, u32[]{:S(2)}) collective-permute-start(bf16[256,256]{1,0:T(8,128)(2,1)S(1)} %broadcast_select_fusion.2), channel_id=1, source_target_pairs={{0,4},{4,0},{8,12},{12,8},{16,20},{20,16},{24,28},{28,24},{32,36},... | collective-permute-start | bytes 393224 | tf_op jit(solution)/shard_map/ppermute | solution.py:37
  158.8 10.6 %all-to-all-start.2 = ((bf16[4,256,128]{2,1,0:T(8,128)(2,1)}), bf16[4,256,128]{2,1,0:T(8,128)(2,1)S(1)}, u32[]{:S(2)}, u32[]{:S(2)}) async-start(bf16[4,256,128]{2,1,0:T(8,128)(2,1)} %near_attend.4), calls=%async_computation.2 | async-start | bytes 524288 | tf_op jit(solution)/shard_map/all_to_all | solution.py:459
  162.2 1.3 copy-start.3
  166.2 0.8 copy-start.18
  169.4 1.0 copy-start.15
  170.5 1.0 copy-start.19
  171.5 14.4 %copy-start.6 = (bf16[1024,256]{1,0:T(8,128)(2,1)S(1)}, bf16[1024,256]{1,0:T(8,128)(2,1)}, u32[]{:S(2)}) copy-start(bf16[1024,256]{1,0:T(8,128)(2,1)} %copy-done.5) | copy-start | bytes 1572868
  171.5 14.5 %copy-start.8 = (bf16[1024,256]{1,0:T(8,128)(2,1)S(1)}, bf16[1024,256]{1,0:T(8,128)(2,1)}, u32[]{:S(2)}) copy-start(bf16[1024,256]{1,0:T(8,128)(2,1)} %copy-done.7) | copy-start | bytes 1572868
  171.5 14.5 %copy-start.10 = (bf16[1024,256]{1,0:T(8,128)(2,1)S(1)}, bf16[1024,256]{1,0:T(8,128)(2,1)}, u32[]{:S(2)}) copy-start(bf16[1024,256]{1,0:T(8,128)(2,1)} %copy-done.9) | copy-start | bytes 1572868
  173.7 10.2 %collective-permute-start.19 = (bf16[256,256]{1,0:T(8,128)(2,1)S(1)}, bf16[256,256]{1,0:T(8,128)(2,1)S(1)}, u32[]{:S(2)}, u32[]{:S(2)}) collective-permute-start(bf16[256,256]{1,0:T(8,128)(2,1)S(1)} %get-tuple-element.33.refs_3_), channel_id=1, source_target_pairs={{8,16},{16,8},{12,20},{20,12},{24,32},{32,24},{28,36},{36,28},{40,... | collective-permute-start | bytes 393224 | tf_op jit(solution)/shard_map/ppermute | solution.py:32
  177.0 6.9 %collective-permute-start.20 = (bf16[256,256]{1,0:T(8,128)(2,1)S(1)}, bf16[256,256]{1,0:T(8,128)(2,1)S(1)}, u32[]{:S(2)}, u32[]{:S(2)}) collective-permute-start(bf16[256,256]{1,0:T(8,128)(2,1)S(1)} %get-tuple-element.33.refs_3_), channel_id=1, source_target_pairs={{0,8},{8,0},{4,12},{12,4},{16,24},{24,16},{20,28},{28,20},{32,40},... | collective-permute-start | bytes 393224 | tf_op jit(solution)/shard_map/ppermute | solution.py:32
  178.9 11.9 %collective-permute-start.21 = (bf16[256,256]{1,0:T(8,128)(2,1)S(1)}, bf16[256,256]{1,0:T(8,128)(2,1)S(1)}, u32[]{:S(2)}, u32[]{:S(2)}) collective-permute-start(bf16[256,256]{1,0:T(8,128)(2,1)S(1)} %get-tuple-element.33.refs_3_), channel_id=1, source_target_pairs={{0,4},{4,0},{8,12},{12,8},{16,20},{20,16},{24,28},{28,24},{32,36},... | collective-permute-start | bytes 393224 | tf_op jit(solution)/shard_map/ppermute | solution.py:37
  183.9 6.8 %copy-start.23 = (bf16[1,128,256]{2,1,0:T(8,128)(2,1)S(1)}, bf16[1,128,256]{2,1,0:T(8,128)(2,1)}, u32[]{:S(2)}) copy-start(bf16[1,128,256]{2,1,0:T(8,128)(2,1)} %get-tuple-element.41) | copy-start | bytes 196612
  183.9 6.9 %collective-permute-start.22 = (bf16[256,256]{1,0:T(8,128)(2,1)S(1)}, bf16[256,256]{1,0:T(8,128)(2,1)S(1)}, u32[]{:S(2)}, u32[]{:S(2)}) collective-permute-start(bf16[256,256]{1,0:T(8,128)(2,1)S(1)} %broadcast_select_fusion.1), channel_id=1, source_target_pairs={{0,4},{4,0},{8,12},{12,8},{16,20},{20,16},{24,28},{28,24},{32,36},... | collective-permute-start | bytes 393224 | tf_op jit(solution)/shard_map/ppermute | solution.py:37
  192.5 18.6 %copy-start.4 = (bf16[1024,256]{1,0:T(8,128)(2,1)S(1)}, bf16[1024,256]{1,0:T(8,128)(2,1)}, u32[]{:S(2)}) copy-start(bf16[1024,256]{1,0:T(8,128)(2,1)} %grid_in.1) | copy-start | bytes 1572868
  (3 other events, 2.4 us)

commit v7 on v3

--- a/solution.py
+++ b/solution.py
@@ -19,13 +19,16 @@
 PARAMS = pltpu.CompilerParams(vmem_limit_bytes=16 * 1024 * 1024)
 
 
-def shift_mp(value, steps):
-    return lax.ppermute(value, "mp", [(s, (s + steps) % MP) for s in range(MP)])
-
-
-def from_node(value, offset):
-    count = lax.axis_size("nodes")
-    pairs = [(s, s - offset) for s in range(count) if 0 <= s - offset < count]
+def swap_mp(value, k):
+    return lax.ppermute(value, "mp", [(s, s ^ k) for s in range(MP)])
+
+
+def swap_chips(value, first):
+    count = lax.axis_size("nodes") // 2
+    pairs = []
+    for c in range(first, count - 1, 2):
+        for core in range(2):
+            pairs += [(2 * c + core, 2 * c + 2 + core), (2 * c + 2 + core, 2 * c + core)]
     return lax.ppermute(value, "nodes", pairs)
 
 
@@ -54,7 +57,7 @@
 
 
 def source(meta, k):
-    return (meta[0] + MP - k) % MP
+    return meta[0] ^ k
 
 
 def normed(pieces):
@@ -71,8 +74,9 @@
     return jnp.dot(a, b, preferred_element_type=F32)
 
 
-def grid_kernel(meta, x0, x1, x2, x3, gains, w_k, w_v, w_q, kv_out, q_out, kept, sems):
-    copies = copies_of([(w_k, 0), (w_v, 0), (w_q, 3)], kept, sems)
+def grid_kernel(gain_row, count, layer_index, meta, x0, x1, x2, x3, gains, *rest):
+    weights, (out, kept, sems) = rest[:count], rest[count:]
+    copies = copies_of([(w, layer_index) for w in weights], kept, sems)
 
     @pl.when(pl.program_id(0) == 0)
     def _():
@@ -86,42 +90,38 @@
         for copy in copies:
             copy.wait()
 
-    kv = q = None
+    total = None
     for k in range(MP):
         src = source(meta, k)
         at = pl.ds(pl.multiple_of(src * 256, 256), 256)
-        for_kv = (rows[k] * gains[1, pl.ds(src, 1), :]).astype(BF16)
-        for_q = (rows[k] * gains[4, pl.ds(src, 1), :]).astype(BF16)
-        kv_part = dot(for_kv, jnp.concatenate([kept[0, at, :], kept[1, at, :]], axis=1))
-        q_part = dot(for_q, kept[2, at, :])
-        kv = kv_part if kv is None else kv + kv_part
-        q = q_part if q is None else q + q_part
-    kv_out[...] = kv.astype(BF16)
-    q_out[...] = q.astype(BF16)
-
-
-def grid_project(meta, pieces, gains, w_k, w_v, w_q):
+        row = (rows[k] * gains[gain_row, pl.ds(src, 1), :]).astype(BF16)
+        part = dot(row, jnp.concatenate([kept[i, at, :] for i in range(count)], axis=1))
+        total = part if total is None else total + part
+    out[...] = total.astype(BF16)
+
+
+def grid_project(gain_row, layer_index, meta, pieces, gains, *weights):
+    count = len(weights)
+
+    def body(*refs):
+        grid_kernel(gain_row, count, layer_index, *refs)
+
     rows = pieces[0].shape[0]
     tile = 256
     return pl.pallas_call(
-        grid_kernel,
+        body,
         grid=(rows // tile,),
         in_specs=[smem()]
         + [pl.BlockSpec((tile, 256), lambda i: (i, 0))] * MP
-        + [vmem(), hbm(), hbm(), hbm()],
-        out_specs=[
-            pl.BlockSpec((tile, 256), lambda i: (i, 0)),
-            pl.BlockSpec((tile, 128), lambda i: (i, 0)),
-        ],
-        out_shape=[
-            jax.ShapeDtypeStruct((rows, 256), BF16),
-            jax.ShapeDtypeStruct((rows, 128), BF16),
-        ],
-        scratch_shapes=[pltpu.VMEM((3, 1024, 128), BF16), pltpu.SemaphoreType.DMA((3,))],
-        cost_estimate=pl.CostEstimate(flops=rows * 1024 * 384 * 2, transcendentals=0, bytes_accessed=rows * 4096),
+        + [vmem()]
+        + [hbm()] * count,
+        out_specs=pl.BlockSpec((tile, 128 * count), lambda i: (i, 0)),
+        out_shape=jax.ShapeDtypeStruct((rows, 128 * count), BF16),
+        scratch_shapes=[pltpu.VMEM((count, 1024, 128), BF16), pltpu.SemaphoreType.DMA((count,))],
+        cost_estimate=pl.CostEstimate(flops=rows * 1024 * 128 * count * 2, transcendentals=0, bytes_accessed=rows * 4096),
         compiler_params=PARAMS,
         name="grid_project",
-    )(meta, *pieces, gains, w_k, w_v, w_q)
+    )(meta, *pieces, gains, *weights)
 
 
 def mesh_kernel(meta, x0, a1, a2, a3, gains, w_q, q_out, kept, sems):
@@ -180,7 +180,8 @@
 
 def window_places(meta):
     core = meta[1] % 2
-    return 0, 2, 4, 3 - 2 * core, 1 + 2 * core
+    odd = meta[1] // 2 % 2
+    return 4 * odd, 2, 4 - 4 * odd, 3 - 2 * core, 1 + 2 * core
 
 
 def enc_kernel(meta, listed, counts, q, a0, a1, a2, a3, a4, o_out, kept):
@@ -212,7 +213,7 @@
         enc_kernel,
         in_specs=[smem(), smem(), smem()] + [vmem()] * 6,
         out_specs=vmem(),
-        out_shape=jax.ShapeDtypeStruct((MP,) + q.shape, BF16),
+        out_shape=pltpu.HBM((MP,) + q.shape, BF16),
         scratch_shapes=[pltpu.VMEM((8, BLOCK, 256), BF16)],
         compiler_params=PARAMS,
         name="enc_attend",
@@ -247,57 +248,56 @@
     )(meta, q, *windows)
 
 
-def layer_kernel(index, gain_row, meta, o, state, a1, a2, a3, gains, w_own, b1, b2, b3, other, w_k, w_v, w_q, *rest):
+def layer_kernel(index, meta, o, state, gains, w_own, lo1, lo2, lo3, hi1, hi2, hi3, other_lo, other_hi, *rest):
     last = index == 2
-    state_out, kv_out = rest[0], rest[1]
-    new, w_out, kept, w_sems, sems = rest[2 + (not last) :]
-    core = meta[1] % 2
-    for g in range(MP):
-        pltpu.make_async_copy(
-            w_own.at[index, :, g * 256 : (g + 1) * 256], w_out.at[g, 0:BLOCK, :], w_sems.at[g, 0]
-        ).start()
-    for part in range(2):
-        at = index + 3 * part
-        for k, b in enumerate((b1, b2, b3)):
-            rows = w_out.at[2 * core + part, (k + 1) * BLOCK : (k + 2) * BLOCK, :]
-            pltpu.make_async_copy(b.at[2 + at], rows, w_sems.at[2 * core + part, k + 1]).start()
-            rows = w_out.at[2 * (1 - core) + part, (k + 1) * BLOCK : (k + 2) * BLOCK, :]
-            pltpu.make_async_copy(other.at[k, at], rows, w_sems.at[2 * (1 - core) + part, k + 1]).start()
-    weights = (w_k, w_v) if last else (w_k, w_v, w_q)
+    mesh, rest = rest[: 3 * (index == 0)], rest[3 * (index == 0) :]
+    count = 2 if last else 3
+    weights, outs, (kept, sems) = rest[:count], rest[count:-2], rest[-2:]
+    new = outs[-1] if last else outs[0]
     copies = copies_of([(w, index + 1) for w in weights], kept, sems)
     for copy in copies:
         copy.start()
+    heads = jnp.concatenate([o[source(meta, k)] for k in range(MP)], axis=1)
     if index == 0:
         new[meta[0]] = state[...]
-        for k, a in enumerate((a1, a2, a3)):
+        for k, a in enumerate(mesh):
             new[source(meta, k + 1)] = a[...].reshape(2 * BLOCK, 256)
         state = new
-    heads = jnp.concatenate([o[source(meta, k)] for k in range(MP)], axis=1)
-    for g in range(MP):
-        for k in range(MP):
-            rows = w_out.at[g, k * BLOCK : (k + 1) * BLOCK, :]
-            pltpu.make_async_copy(other.at[0, 0], rows, w_sems.at[g, k]).wait()
-        new[g] = (state[g].astype(F32) + dot(heads, w_out[g])).astype(BF16)
+    core = meta[1] % 2
+    for part in range(4):
+        if part < 2:
+            g = 2 * core + part
+            fetched = [a[0] for a in ((lo1, lo2, lo3), (hi1, hi2, hi3))[part]]
+        else:
+            g = 2 * (1 - core) + part - 2
+            other = (other_lo, other_hi)[part - 2]
+            fetched = [other[k, 0] for k in range(MP - 1)]
+        own = w_own[0, :, pl.ds(pl.multiple_of(g * 256, 256), 256)]
+        new[g] = (state[g].astype(F32) + dot(heads, jnp.concatenate([own] + fetched, axis=0))).astype(BF16)
     if last:
-        state_out[...] = new[meta[0]]
-    else:
-        for g in range(MP):
-            state_out[g] = new[g]
+        outs[0][...] = new[meta[0]]
     rows = normed([new[g] for g in range(MP)])
+    gain_row = 5 if last else index + 2
     row = jnp.concatenate(
         [(rows[g] * gains[gain_row, g : g + 1, :]).astype(BF16) for g in range(MP)], axis=1
     )
     for copy in copies:
         copy.wait()
-    result = dot(row, jnp.concatenate([kept[i] for i in range(len(weights))], axis=1)).astype(BF16)
-    kv_out[...] = result[:, :256]
+    result = dot(row, jnp.concatenate([kept[i] for i in range(count)], axis=1)).astype(BF16)
+    outs[1][...] = result[:, :256]
     if not last:
-        rest[2][...] = result[:, 256:]
-
-
-def layer(index, gain_row, meta, o, state, w_own, fetched, other, gains, w_key, w_value, w_query):
+        outs[2][...] = result[:, 256:]
+
+
+def layer(index, meta, o, state, gains, w_own, fetched, other, weights):
     def body(*refs):
-        layer_kernel(index, gain_row, *refs)
+        layer_kernel(index, *refs)
+
+    def block(at):
+        return pl.BlockSpec((1, BLOCK, 256), lambda i: (at, 0, 0))
+
+    def other_block(at):
+        return pl.BlockSpec((MP - 1, 1, BLOCK, 256), lambda i: (0, at, 0, 0))
 
     last = index == 2
     rows = o.shape[1]
@@ -307,25 +307,26 @@
     ]
     if not last:
         shapes.append(jax.ShapeDtypeStruct((rows, 128), BF16))
+    mesh = fetched if index == 0 else ()
+    weights = weights[:2] if last else weights
+    scratch = [pltpu.VMEM((MP, rows, 256), BF16)] if last else []
     return pl.pallas_call(
         body,
         grid=(1,),
-        in_specs=[smem(), vmem(), vmem()]
-        + [pl.BlockSpec((2, BLOCK, 256), lambda i: (0, 0, 0))] * 3
-        + [vmem()]
-        + [hbm()] * 8,
+        in_specs=[smem()]
+        + [vmem()] * 3
+        + [pl.BlockSpec((1, BLOCK, 1024), lambda i: (index, 0, 0))]
+        + [block(2 + index)] * 3
+        + [block(5 + index)] * 3
+        + [other_block(index), other_block(3 + index)]
+        + [pl.BlockSpec((2, BLOCK, 256), lambda i: (0, 0, 0))] * len(mesh)
+        + [hbm()] * len(weights),
         out_specs=[vmem()] * len(shapes),
         out_shape=shapes,
-        scratch_shapes=[
-            pltpu.VMEM((MP, rows, 256), BF16),
-            pltpu.VMEM((MP, 4 * BLOCK, 256), BF16),
-            pltpu.VMEM((3, 1024, 128), BF16),
-            pltpu.SemaphoreType.DMA((MP, MP)),
-            pltpu.SemaphoreType.DMA((3,)),
-        ],
+        scratch_shapes=scratch + [pltpu.VMEM((3, 1024, 128), BF16), pltpu.SemaphoreType.DMA((3,))],
         compiler_params=PARAMS,
         name="mesh_layer",
-    )(meta, o, state, *fetched, gains, w_own, *fetched, other, w_key, w_value, w_query)
+    )(meta, o, state, gains, w_own, *fetched, *fetched, other, other, *mesh, *weights)
 
 
 def final_kernel(meta, counts, o, w_out, grid_in, out):
@@ -384,15 +385,15 @@
     def gathered(part, name):
         pieces = [part, None, None, None]
         for k in (1, 3, 2):
-            pieces[k] = shift_mp(part if name != "w" else part[k], k)
+            pieces[k] = swap_mp(part if name != "w" else part[k], k)
         return pieces
 
     def window(part):
-        low = from_node(part, -2)
-        high = from_node(part, 2)
+        across = swap_chips(part, 1)
+        within = swap_chips(part, 0)
         beside = swap_cores(part)
-        beyond = swap_cores(jnp.where(core == 0, high, low))
-        return [low, part, high, beside, beyond]
+        beyond = swap_cores(jnp.where((core == 0) == (own_node // 2 % 2 == 0), within, across))
+        return [across, part, within, beside, beyond]
 
     grid_pieces = gathered(grid_in, "g")
     grid_pieces[0] = pltpu.with_memory_space_constraint(grid_in, pltpu.HBM)
@@ -400,20 +401,20 @@
     halves = [lax.dynamic_slice_in_dim(w_out[:3], core * 512 + part * 256, 256, axis=2) for part in range(2)]
     sent = [None] * MP
     for k in (1, 2, 3):
-        last = lax.dynamic_slice_in_dim(w_out[3:], (own_mp + k) % MP * 256, 256, axis=2)
+        last = lax.dynamic_slice_in_dim(w_out[3:], (own_mp ^ k) * 256, 256, axis=2)
         sent[k] = jnp.concatenate([mesh_in.reshape(2, BLOCK, 256)] + halves + [last], axis=0)
     sent[0] = sent[1]
     arrived = gathered(sent, "w")[1:]
 
-    kv, grid_q = grid_project(meta, grid_pieces, gains, w_key, w_value, w_query)
+    kv = grid_project(1, 0, meta, grid_pieces, gains, w_key, w_value)
     grid_windows = window(kv)
+    grid_q = grid_project(4, 3, meta, grid_pieces, gains, w_query)
+    w_own = pltpu.with_memory_space_constraint(w_out, pltpu.HBM)
     mesh_q = mesh_start(meta, mesh_in, arrived, gains, w_query)
     o = enc_attend(meta, enc_list, grid_count, mesh_q, grid_windows)
 
     arrived = lax.optimization_barrier((*arrived, o))[:3]
     other = swap_cores(jnp.stack([a[2:8] for a in arrived]))
-    other = pltpu.with_memory_space_constraint(other, pltpu.HBM)
-    w_own = pltpu.with_memory_space_constraint(w_out, pltpu.HBM)
     w_last = jnp.concatenate(
         [lax.dynamic_slice_in_dim(w_out[3:], own_mp * 256, 256, axis=2)] + [a[8:] for a in arrived], axis=0
     ).reshape(512, 256)
@@ -421,13 +422,12 @@
     state = mesh_in
     for index in range(3):
         heads = gather_heads(o)
-        made = layer(
-            index, index + 2 if index < 2 else 5, meta, heads, state, w_own, arrived, other, gains, w_key, w_value, w_query
-        )
+        made = layer(index, meta, heads, state, gains, w_own, arrived, other, (w_key, w_value, w_query))
         state, kv = made[0], made[1]
         near = window(kv)
         if index < 2:
             o = near_attend(PROC0, 3, meta, made[2], near)
+    grid_q, w_last = lax.optimization_barrier((grid_q, w_last))
     o = near_attend(DEC0, 2, meta, grid_q, near)
     heads = gather_heads(o)
     grid_out = final(meta, grid_count, heads, w_last, grid_in)

time: 209 us -> 205 us (0.981)
  the two profiles are of different devices: /device:TPU:102 before, /device:TPU:384 now
where the time goes in v7:
time: 205 us; the launch traced here: 204 us
  starting transfers between devices  63 us (31%)
  waiting for transfers between devices  51.2 us (25%)
  blocking collectives  49.3 us (24%)
  Pallas kernels  31.8 us (16%)
  other arithmetic  4.7 us (2%)
  local copies, waits for them, and re-layouts  2.49 us (1%)
    all_to_all x4, blocking collectives, gather_heads(): return lax.all_to_all(copies, 'mp', split_axis=0, concat_axis=0, tiled=True)  49.3 us
    ppermute x6, waiting for transfers between devices, swap_mp(): return lax.ppermute(value, 'mp', [(s, s ^ k) for s in range(MP)])  34.3 us
    ppermute x8, starting transfers between devices, swap_chips(): return lax.ppermute(value, 'nodes', pairs)  25.5 us
    ppermute x6, starting transfers between devices, swap_mp(): return lax.ppermute(value, 'mp', [(s, s ^ k) for s in range(MP)])  19.6 us
    ppermute x9, starting transfers between devices, swap_cores(): return lax.ppermute(value, 'nodes', [(s, s ^ 1) for s in range(count)])  17.9 us
    ppermute x8, waiting for transfers between devices, swap_chips(): return lax.ppermute(value, 'nodes', pairs)  14.2 us
    pallas_call x2, Pallas kernels, grid_project(): pl.pallas_call(body, grid=(rows // tile,), in_specs=[smem()] + [pl.BlockS...  10.2 us
    pallas_call x3, Pallas kernels, layer(): pl.pallas_call(body, grid=(1,), in_specs=[smem()] + [vmem()] * 3 + [pl.Bl...  8.88 us
  transfers between devices with their start and end apart: 23, of which 9 were waited for; matrix products, arithmetic and copies ran while one was open for 3% of the time, Pallas kernels for 3%

profile of v7, /device:TPU:384, one launch (start us, length us, event | category | flops | bytes accessed | tf_op | source)
XLA Modules:
  0.0 203.8 jit_solution(14180859600176111078)
XLA Ops:
  0.6 4.9 %collective-permute-start.2 = (bf16[1024,256]{1,0:T(8,128)(2,1)}, bf16[1024,256]{1,0:T(8,128)(2,1)S(1)}, u32[]{:S(2)}, u32[]{:S(2)}) collective-permute-start(bf16[1024,256]{1,0:T(8,128)(2,1)} %grid_in.1), channel_id=1, source_target_pairs={{0,3},{1,2},{2,1},{3,0},{4,7},{5,6},{6,5},{7,4},{8,11},{9,10},{10,... | collective-permute-start | bytes 1572872 | tf_op jit(solution)/shard_map/ppermute | solution.py:23
  5.6 2.5 %collective-permute-start.1 = (bf16[1024,256]{1,0:T(8,128)(2,1)}, bf16[1024,256]{1,0:T(8,128)(2,1)S(1)}, u32[]{:S(2)}, u32[]{:S(2)}) collective-permute-start(bf16[1024,256]{1,0:T(8,128)(2,1)} %grid_in.1), channel_id=1, source_target_pairs={{0,2},{1,3},{2,0},{3,1},{4,6},{5,7},{6,4},{7,5},{8,10},{9,11},{10,... | collective-permute-start | bytes 1572872 | tf_op jit(solution)/shard_map/ppermute | solution.py:23
  8.1 2.4 %collective-permute-start = (bf16[1024,256]{1,0:T(8,128)(2,1)}, bf16[1024,256]{1,0:T(8,128)(2,1)S(1)}, u32[]{:S(2)}, u32[]{:S(2)}) collective-permute-start(bf16[1024,256]{1,0:T(8,128)(2,1)} %grid_in.1), channel_id=1, source_target_pairs={{0,1},{1,0},{2,3},{3,2},{4,5},{5,4},{6,7},{7,6},{8,9},{9,8},{10,11... | collective-permute-start | bytes 1572872 | tf_op jit(solution)/shard_map/ppermute | solution.py:23
  13.7 15.2 %collective-permute-done.2.refs_4_ = bf16[1024,256]{1,0:T(8,128)(2,1)S(1)} collective-permute-done((bf16[1024,256]{1,0:T(8,128)(2,1)}, bf16[1024,256]{1,0:T(8,128)(2,1)S(1)}, u32[]{:S(2)}, u32[]{:S(2)}) %collective-permute-start.2) | collective-permute-done | bytes 524320 | tf_op jit(solution)/shard_map/ppermute | solution.py:23
  28.9 2.5 %collective-permute-done.refs_2_ = bf16[1024,256]{1,0:T(8,128)(2,1)S(1)} collective-permute-done((bf16[1024,256]{1,0:T(8,128)(2,1)}, bf16[1024,256]{1,0:T(8,128)(2,1)S(1)}, u32[]{:S(2)}, u32[]{:S(2)}) %collective-permute-start) | collective-permute-done | bytes 524320 | tf_op jit(solution)/shard_map/ppermute | solution.py:23
  31.5 5.5 %grid_project.3.a1 = bf16[1024,256]{1,0:T(8,128)(2,1)} custom-call(s32[32]{0:T(128)S(1)} %concatenate.15.refs_0_.meta, bf16[1024,256]{1,0:T(8,128)(2,1)} %grid_in.1, bf16[1024,256]{1,0:T(8,128)(2,1)S(1)} %collective-permute-done.refs_2_, bf16[1024,256]{1,0:T(8,128)(2,1)S(1)} %collective-permute-done.1.refs_3_, ...), custom_call_target="tpu_custom_call" | custom-call | flops 536870912 | bytes 4194304 | tf_op jit(solution)/shard_map/grid_project/pallas_call | solution.py:111
  37.0 3.5 %collective-permute-start.7 = (bf16[1024,256]{1,0:T(8,128)(2,1)}, bf16[1024,256]{1,0:T(8,128)(2,1)}, u32[]{:S(2)}, u32[]{:S(2)}) collective-permute-start(bf16[1024,256]{1,0:T(8,128)(2,1)} %grid_project.3.a1), channel_id=1, source_target_pairs={{0,8},{8,0},{4,12},{12,4},{16,24},{24,16},{20,28},{28,20},{32,40},... | collective-permute-start | bytes 1572872 | tf_op jit(solution)/shard_map/ppermute | solution.py:32
  40.5 5.7 %collective-permute-start.6 = (bf16[1024,256]{1,0:T(8,128)(2,1)}, bf16[1024,256]{1,0:T(8,128)(2,1)}, u32[]{:S(2)}, u32[]{:S(2)}) collective-permute-start(bf16[1024,256]{1,0:T(8,128)(2,1)} %grid_project.3.a1), channel_id=1, source_target_pairs={{8,16},{16,8},{12,20},{20,12},{24,32},{32,24},{28,36},{36,28},{40,... | collective-permute-start | bytes 1572872 | tf_op jit(solution)/shard_map/ppermute | solution.py:32
  47.4 1.3 pad_maximum_fusion.4
  48.8 4.8 %collective-permute-start.5 = (bf16[9,128,256]{2,1,0:T(8,128)(2,1)}, bf16[9,128,256]{2,1,0:T(8,128)(2,1)S(1)}, u32[]{:S(2)}, u32[]{:S(2)}) collective-permute-start(bf16[9,128,256]{2,1,0:T(8,128)(2,1)} %get-tuple-element.30), channel_id=1, source_target_pairs={{0,3},{1,2},{2,1},{3,0},{4,7},{5,6},{6,5},{7,4},{8,11},{9,10},{10,... | collective-permute-start | bytes 1769480 | tf_op jit(solution)/shard_map/ppermute | solution.py:23
  53.6 2.5 %collective-permute-start.4 = (bf16[9,128,256]{2,1,0:T(8,128)(2,1)}, bf16[9,128,256]{2,1,0:T(8,128)(2,1)S(1)}, u32[]{:S(2)}, u32[]{:S(2)}) collective-permute-start(bf16[9,128,256]{2,1,0:T(8,128)(2,1)} %get-tuple-element.31), channel_id=1, source_target_pairs={{0,2},{1,3},{2,0},{3,1},{4,6},{5,7},{6,4},{7,5},{8,10},{9,11},{10,... | collective-permute-start | bytes 1769480 | tf_op jit(solution)/shard_map/ppermute | solution.py:23
  56.2 2.4 %collective-permute-start.3 = (bf16[9,128,256]{2,1,0:T(8,128)(2,1)}, bf16[9,128,256]{2,1,0:T(8,128)(2,1)S(1)}, u32[]{:S(2)}, u32[]{:S(2)}) collective-permute-start(bf16[9,128,256]{2,1,0:T(8,128)(2,1)} %get-tuple-element.32), channel_id=1, source_target_pairs={{0,1},{1,0},{2,3},{3,2},{4,5},{5,4},{6,7},{7,6},{8,9},{9,8},{10,11... | collective-permute-start | bytes 1769480 | tf_op jit(solution)/shard_map/ppermute | solution.py:23
  58.7 1.9 collective-permute-start.8
  61.7 2.4 %collective-permute-start.9 = (bf16[1024,256]{1,0:T(8,128)(2,1)S(1)}, bf16[1024,256]{1,0:T(8,128)(2,1)S(1)}, u32[]{:S(2)}, u32[]{:S(2)}) collective-permute-start(bf16[1024,256]{1,0:T(8,128)(2,1)S(1)} %broadcast_select_fusion), channel_id=1, source_target_pairs={{0,4},{4,0},{8,12},{12,8},{16,20},{20,16},{24,28},{28,24},{32,36},... | collective-permute-start | bytes 1572872 | tf_op jit(solution)/shard_map/ppermute | solution.py:37
  64.2 14.1 %collective-permute-done.5.a3.refs_7_.refs_10_.refs_15_ = bf16[9,128,256]{2,1,0:T(8,128)(2,1)S(1)} collective-permute-done((bf16[9,128,256]{2,1,0:T(8,128)(2,1)}, bf16[9,128,256]{2,1,0:T(8,128)(2,1)S(1)}, u32[]{:S(2)}, u32[]{:S(2)}) %collective-permute-start.5) | collective-permute-done | bytes 589856 | tf_op jit(solution)/shard_map/ppermute | solution.py:23
  78.2 2.5 %collective-permute-done.3.a1.refs_5_.refs_8_.refs_13_ = bf16[9,128,256]{2,1,0:T(8,128)(2,1)S(1)} collective-permute-done((bf16[9,128,256]{2,1,0:T(8,128)(2,1)}, bf16[9,128,256]{2,1,0:T(8,128)(2,1)S(1)}, u32[]{:S(2)}, u32[]{:S(2)}) %collective-permute-start.3) | collective-permute-done | bytes 589856 | tf_op jit(solution)/shard_map/ppermute | solution.py:23
  80.7 1.9 mesh_start.1.q
  82.7 3.6 %enc_attend.1 = bf16[4,256,128]{2,1,0:T(8,128)(2,1)} custom-call(s32[32]{0:T(128)S(1)} %concatenate.15.refs_0_.meta, s32[2,4]{1,0:T(2,128)S(1)} %copy-done.3, s32[1024]{0:T(1024)S(1)} %copy-done.2, bf16[256,128]{1,0:T(8,128)(2,1)S(1)} %mesh_start.1.q, bf16[1024,256]{1,0:T(8,128)(2,1)} %collective-permute-done.6.a0, bf16[1024,256]{1,0:T(8,128)(2,1)} %grid_project.3.a1, ...), custom_call_target="tpu_custom_call" | custom-call | tf_op jit(solution)/shard_map/enc_attend/pallas_call | solution.py:212
  86.5 1.9 collective-permute-start.10
  88.5 11.5 %all_to_all.20.refs_1_ = bf16[4,256,128]{2,1,0:T(8,128)(2,1)S(1)} all-to-all(bf16[4,256,128]{2,1,0:T(8,128)(2,1)S(1)} %copy-done.4), channel_id=1, replica_groups=mesh['nodes'=128,'mp'=4] {'mp'}, dimensions={0} | all-to-all | bytes 524288 | tf_op jit(solution)/shard_map/all_to_all | solution.py:364
  99.9 3.1 %mesh_layer.3 = (bf16[4,256,256]{2,1,0:T(8,128)(2,1)S(1)}, bf16[256,256]{1,0:T(8,128)(2,1)S(1)}, bf16[256,128]{1,0:T(8,128)(2,1)S(1)}) custom-call(s32[32]{0:T(128)S(1)} %concatenate.15.refs_0_.meta, bf16[4,256,128]{2,1,0:T(8,128)(2,1)S(1)} %all_to_all.20.refs_1_, bf16[256,256]{1,0:T(8,128)(2,1)S(1)} %copy-done.1, ...), custom_call_target="tpu_custom_call" | custom-call | tf_op jit(solution)/shard_map/mesh_layer/pallas_call | solution.py:313
  103.0 1.9 collective-permute-start.12
  105.0 3.5 %collective-permute-start.11 = (bf16[256,256]{1,0:T(8,128)(2,1)S(1)}, bf16[256,256]{1,0:T(8,128)(2,1)S(1)}, u32[]{:S(2)}, u32[]{:S(2)}) collective-permute-start(bf16[256,256]{1,0:T(8,128)(2,1)S(1)} %get-tuple-element.20.refs_3_), channel_id=1, source_target_pairs={{8,16},{16,8},{12,20},{20,12},{24,32},{32,24},{28,36},{36,28},{40,... | collective-permute-start | bytes 393224 | tf_op jit(solution)/shard_map/ppermute | solution.py:32
  108.5 1.9 collective-permute-start.13
  110.4 4.7 %collective-permute-done.11.refs_2_ = bf16[256,256]{1,0:T(8,128)(2,1)S(1)} collective-permute-done((bf16[256,256]{1,0:T(8,128)(2,1)S(1)}, bf16[256,256]{1,0:T(8,128)(2,1)S(1)}, u32[]{:S(2)}, u32[]{:S(2)}) %collective-permute-start.11) | collective-permute-done | bytes 131104 | tf_op jit(solution)/shard_map/ppermute | solution.py:32
  115.2 1.9 collective-permute-start.14
  117.1 1.3 collective-permute-done.14.refs_6_
  118.4 1.8 near_attend.3
  120.2 9.6 %all_to_all.21.refs_1_ = bf16[4,256,128]{2,1,0:T(8,128)(2,1)S(1)} all-to-all(bf16[4,256,128]{2,1,0:T(8,128)(2,1)S(1)} %near_attend.3), channel_id=1, replica_groups=mesh['nodes'=128,'mp'=4] {'mp'}, dimensions={0} | all-to-all | bytes 524288 | tf_op jit(solution)/shard_map/all_to_all | solution.py:364
  129.8 3.0 %mesh_layer.4 = (bf16[4,256,256]{2,1,0:T(8,128)(2,1)S(1)}, bf16[256,256]{1,0:T(8,128)(2,1)S(1)}, bf16[256,128]{1,0:T(8,128)(2,1)S(1)}) custom-call(s32[32]{0:T(128)S(1)} %concatenate.15.refs_0_.meta, bf16[4,256,128]{2,1,0:T(8,128)(2,1)S(1)} %all_to_all.21.refs_1_, bf16[4,256,256]{2,1,0:T(8,128)(2,1)S(1)} %get-tuple-element.21.refs_2_, ...), custom_call_target="tpu_custom_call" | custom-call | tf_op jit(solution)/shard_map/mesh_layer/pallas_call | solution.py:313
  132.9 1.9 collective-permute-start.16
  134.8 3.5 %collective-permute-start.15 = (bf16[256,256]{1,0:T(8,128)(2,1)S(1)}, bf16[256,256]{1,0:T(8,128)(2,1)S(1)}, u32[]{:S(2)}, u32[]{:S(2)}) collective-permute-start(bf16[256,256]{1,0:T(8,128)(2,1)S(1)} %get-tuple-element.23.refs_3_), channel_id=1, source_target_pairs={{8,16},{16,8},{12,20},{20,12},{24,32},{32,24},{28,36},{36,28},{40,... | collective-permute-start | bytes 393224 | tf_op jit(solution)/shard_map/ppermute | solution.py:32
  138.3 1.9 collective-permute-start.17
  140.2 4.7 %collective-permute-done.15.refs_2_ = bf16[256,256]{1,0:T(8,128)(2,1)S(1)} collective-permute-done((bf16[256,256]{1,0:T(8,128)(2,1)S(1)}, bf16[256,256]{1,0:T(8,128)(2,1)S(1)}, u32[]{:S(2)}, u32[]{:S(2)}) %collective-permute-start.15) | collective-permute-done | bytes 131104 | tf_op jit(solution)/shard_map/ppermute | solution.py:32
  145.0 1.9 collective-permute-start.18
  146.9 1.3 collective-permute-done.18.refs_6_
  148.2 1.8 near_attend.4
  150.0 9.6 %all_to_all.22.refs_1_ = bf16[4,256,128]{2,1,0:T(8,128)(2,1)S(1)} all-to-all(bf16[4,256,128]{2,1,0:T(8,128)(2,1)S(1)} %near_attend.4), channel_id=1, replica_groups=mesh['nodes'=128,'mp'=4] {'mp'}, dimensions={0} | all-to-all | bytes 524288 | tf_op jit(solution)/shard_map/all_to_all | solution.py:364
  159.7 2.7 %mesh_layer.5 = (bf16[256,256]{1,0:T(8,128)(2,1)}, bf16[256,256]{1,0:T(8,128)(2,1)S(1)}) custom-call(s32[32]{0:T(128)S(1)} %concatenate.15.refs_0_.meta, bf16[4,256,128]{2,1,0:T(8,128)(2,1)S(1)} %all_to_all.22.refs_1_, bf16[4,256,256]{2,1,0:T(8,128)(2,1)S(1)} %get-tuple-element.24.refs_2_, f32[6,4,256]{2,1,0:T(4,128)S(1)} %reshape.24.refs_5_.gains.refs_3_, ...), custom_call_target="tpu_custom_call" | custom-call | tf_op jit(solution)/shard_map/mesh_layer/pallas_call | solution.py:313
  162.4 1.9 collective-permute-start.20
  164.3 3.5 %collective-permute-start.19 = (bf16[256,256]{1,0:T(8,128)(2,1)S(1)}, bf16[256,256]{1,0:T(8,128)(2,1)S(1)}, u32[]{:S(2)}, u32[]{:S(2)}) collective-permute-start(bf16[256,256]{1,0:T(8,128)(2,1)S(1)} %get-tuple-element.25.refs_3_), channel_id=1, source_target_pairs={{8,16},{16,8},{12,20},{20,12},{24,32},{32,24},{28,36},{36,28},{40,... | collective-permute-start | bytes 393224 | tf_op jit(solution)/shard_map/ppermute | solution.py:32
  167.9 1.9 collective-permute-start.21
  169.8 4.7 %collective-permute-done.19.refs_2_ = bf16[256,256]{1,0:T(8,128)(2,1)S(1)} collective-permute-done((bf16[256,256]{1,0:T(8,128)(2,1)S(1)}, bf16[256,256]{1,0:T(8,128)(2,1)S(1)}, u32[]{:S(2)}, u32[]{:S(2)}) %collective-permute-start.19) | collective-permute-done | bytes 131104 | tf_op jit(solution)/shard_map/ppermute | solution.py:32
  174.6 2.1 %collective-permute-start.22 = (bf16[256,256]{1,0:T(8,128)(2,1)S(1)}, bf16[256,256]{1,0:T(8,128)(2,1)S(1)}, u32[]{:S(2)}, u32[]{:S(2)}) collective-permute-start(bf16[256,256]{1,0:T(8,128)(2,1)S(1)} %broadcast_select_fusion.1), channel_id=1, source_target_pairs={{0,4},{4,0},{8,12},{12,8},{16,20},{20,16},{24,28},{28,24},{32,36},... | collective-permute-start | bytes 393224 | tf_op jit(solution)/shard_map/ppermute | solution.py:37
  176.6 4.7 %grid_project.2.refs_1_ = bf16[1024,128]{1,0:T(8,128)(2,1)S(1)} custom-call(s32[32]{0:T(128)S(1)} %concatenate.15.refs_0_.meta, bf16[1024,256]{1,0:T(8,128)(2,1)} %grid_in.1, bf16[1024,256]{1,0:T(8,128)(2,1)S(1)} %collective-permute-done.refs_2_, bf16[1024,256]{1,0:T(8,128)(2,1)S(1)} %collective-permute-done.1.refs_3_, ...), custom_call_target="tpu_custom_call" | custom-call | flops 268435456 | bytes 4194304 | tf_op jit(solution)/shard_map/grid_project/pallas_call | solution.py:111
  181.4 1.7 near_attend.5
  183.2 18.6 %all_to_all.23.o = bf16[4,1024,128]{2,1,0:T(8,128)(2,1)S(1)} all-to-all(bf16[4,1024,128]{2,1,0:T(8,128)(2,1)S(1)} %near_attend.5), channel_id=1, replica_groups=mesh['nodes'=128,'mp'=4] {'mp'}, dimensions={0} | all-to-all | bytes 2097152 | tf_op jit(solution)/shard_map/all_to_all | solution.py:364
  201.8 2.0 grid_final.1
  (52 shorter events, 5.9 us)
Async XLA Ops:
  0.6 28.3 %collective-permute-start.2 = (bf16[1024,256]{1,0:T(8,128)(2,1)}, bf16[1024,256]{1,0:T(8,128)(2,1)S(1)}, u32[]{:S(2)}, u32[]{:S(2)}) collective-permute-start(bf16[1024,256]{1,0:T(8,128)(2,1)} %grid_in.1), channel_id=1, source_target_pairs={{0,3},{1,2},{2,1},{3,0},{4,7},{5,6},{6,5},{7,4},{8,11},{9,10},{10,... | collective-permute-start | bytes 1572872 | tf_op jit(solution)/shard_map/ppermute | solution.py:23
  5.6 23.4 %collective-permute-start.1 = (bf16[1024,256]{1,0:T(8,128)(2,1)}, bf16[1024,256]{1,0:T(8,128)(2,1)S(1)}, u32[]{:S(2)}, u32[]{:S(2)}) collective-permute-start(bf16[1024,256]{1,0:T(8,128)(2,1)} %grid_in.1), channel_id=1, source_target_pairs={{0,2},{1,3},{2,0},{3,1},{4,6},{5,7},{6,4},{7,5},{8,10},{9,11},{10,... | collective-permute-start | bytes 1572872 | tf_op jit(solution)/shard_map/ppermute | solution.py:23
  8.1 23.3 %collective-permute-start = (bf16[1024,256]{1,0:T(8,128)(2,1)}, bf16[1024,256]{1,0:T(8,128)(2,1)S(1)}, u32[]{:S(2)}, u32[]{:S(2)}) collective-permute-start(bf16[1024,256]{1,0:T(8,128)(2,1)} %grid_in.1), channel_id=1, source_target_pairs={{0,1},{1,0},{2,3},{3,2},{4,5},{5,4},{6,7},{7,6},{8,9},{9,8},{10,11... | collective-permute-start | bytes 1572872 | tf_op jit(solution)/shard_map/ppermute | solution.py:23
  37.0 9.3 %slice-start = ((bf16[4,128,1024]{2,1,0:T(8,128)(2,1)}), bf16[1,128,1024]{2,1,0:T(8,128)(2,1)S(1)}, s32[]{:S(2)}) async-start(bf16[4,128,1024]{2,1,0:T(8,128)(2,1)} %refs_4_.5), calls=%async_computation.4 | async-start | bytes 524288 | tf_op jit(solution)/shard_map/slice | solution.py:419
  37.0 21.7 %collective-permute-start.7 = (bf16[1024,256]{1,0:T(8,128)(2,1)}, bf16[1024,256]{1,0:T(8,128)(2,1)}, u32[]{:S(2)}, u32[]{:S(2)}) collective-permute-start(bf16[1024,256]{1,0:T(8,128)(2,1)} %grid_project.3.a1), channel_id=1, source_target_pairs={{0,8},{8,0},{4,12},{12,4},{16,24},{24,16},{20,28},{28,20},{32,40},... | collective-permute-start | bytes 1572872 | tf_op jit(solution)/shard_map/ppermute | solution.py:32
  40.5 20.1 %collective-permute-start.6 = (bf16[1024,256]{1,0:T(8,128)(2,1)}, bf16[1024,256]{1,0:T(8,128)(2,1)}, u32[]{:S(2)}, u32[]{:S(2)}) collective-permute-start(bf16[1024,256]{1,0:T(8,128)(2,1)} %grid_project.3.a1), channel_id=1, source_target_pairs={{8,16},{16,8},{12,20},{20,12},{24,32},{32,24},{28,36},{36,28},{40,... | collective-permute-start | bytes 1572872 | tf_op jit(solution)/shard_map/ppermute | solution.py:32
  46.2 1.2 slice-start.1
  46.2 1.2 copy-start.1
  48.8 29.4 %collective-permute-start.5 = (bf16[9,128,256]{2,1,0:T(8,128)(2,1)}, bf16[9,128,256]{2,1,0:T(8,128)(2,1)S(1)}, u32[]{:S(2)}, u32[]{:S(2)}) collective-permute-start(bf16[9,128,256]{2,1,0:T(8,128)(2,1)} %get-tuple-element.30), channel_id=1, source_target_pairs={{0,3},{1,2},{2,1},{3,0},{4,7},{5,6},{6,5},{7,4},{8,11},{9,10},{10,... | collective-permute-start | bytes 1769480 | tf_op jit(solution)/shard_map/ppermute | solution.py:23
  53.6 24.6 %collective-permute-start.4 = (bf16[9,128,256]{2,1,0:T(8,128)(2,1)}, bf16[9,128,256]{2,1,0:T(8,128)(2,1)S(1)}, u32[]{:S(2)}, u32[]{:S(2)}) collective-permute-start(bf16[9,128,256]{2,1,0:T(8,128)(2,1)} %get-tuple-element.31), channel_id=1, source_target_pairs={{0,2},{1,3},{2,0},{3,1},{4,6},{5,7},{6,4},{7,5},{8,10},{9,11},{10,... | collective-permute-start | bytes 1769480 | tf_op jit(solution)/shard_map/ppermute | solution.py:23
  56.2 24.6 %collective-permute-start.3 = (bf16[9,128,256]{2,1,0:T(8,128)(2,1)}, bf16[9,128,256]{2,1,0:T(8,128)(2,1)S(1)}, u32[]{:S(2)}, u32[]{:S(2)}) collective-permute-start(bf16[9,128,256]{2,1,0:T(8,128)(2,1)} %get-tuple-element.32), channel_id=1, source_target_pairs={{0,1},{1,0},{2,3},{3,2},{4,5},{5,4},{6,7},{7,6},{8,9},{9,8},{10,11... | collective-permute-start | bytes 1769480 | tf_op jit(solution)/shard_map/ppermute | solution.py:23
  58.7 24.0 %collective-permute-start.8 = (bf16[1024,256]{1,0:T(8,128)(2,1)}, bf16[1024,256]{1,0:T(8,128)(2,1)S(1)}, u32[]{:S(2)}, u32[]{:S(2)}) collective-permute-start(bf16[1024,256]{1,0:T(8,128)(2,1)} %grid_project.3.a1), channel_id=1, source_target_pairs={{0,4},{4,0},{8,12},{12,8},{16,20},{20,16},{24,28},{28,24},{32,36},... | collective-permute-start | bytes 1572872 | tf_op jit(solution)/shard_map/ppermute | solution.py:37
  61.7 21.0 %copy-start.2 = (s32[1024]{0:T(1024)S(1)}, s32[1024]{0:T(1024)}, u32[]{:S(2)}) copy-start(s32[1024]{0:T(1024)} %counts.3) | copy-start | bytes 12292
  61.7 21.0 %copy-start.3 = (s32[2,4]{1,0:T(2,128)S(1)}, s32[2,4]{1,0:T(2,128)}, u32[]{:S(2)}) copy-start(s32[2,4]{1,0:T(2,128)} %listed.1) | copy-start | bytes 100
  61.7 21.0 %collective-permute-start.9 = (bf16[1024,256]{1,0:T(8,128)(2,1)S(1)}, bf16[1024,256]{1,0:T(8,128)(2,1)S(1)}, u32[]{:S(2)}, u32[]{:S(2)}) collective-permute-start(bf16[1024,256]{1,0:T(8,128)(2,1)S(1)} %broadcast_select_fusion), channel_id=1, source_target_pairs={{0,4},{4,0},{8,12},{12,8},{16,20},{20,16},{24,28},{28,24},{32,36},... | collective-permute-start | bytes 1572872 | tf_op jit(solution)/shard_map/ppermute | solution.py:37
  86.4 2.1 %copy-start.4 = (bf16[4,256,128]{2,1,0:T(8,128)(2,1)S(1)}, bf16[4,256,128]{2,1,0:T(8,128)(2,1)}, u32[]{:S(2)}) copy-start(bf16[4,256,128]{2,1,0:T(8,128)(2,1)} %enc_attend.1) | copy-start | bytes 786436
  86.5 13.4 %collective-permute-start.10 = (bf16[3,6,128,256]{3,2,1,0:T(8,128)(2,1)S(1)}, bf16[3,6,128,256]{3,2,1,0:T(8,128)(2,1)S(1)}, u32[]{:S(2)}, u32[]{:S(2)}) collective-permute-start(bf16[3,6,128,256]{3,2,1,0:T(8,128)(2,1)S(1)} %pad_maximum_fusion), channel_id=1, source_target_pairs={{0,4},{4,0},{8,12},{12,8},{16,20},{20,16},{24,28},{28,24},{32,36},... | collective-permute-start | bytes 3538952 | tf_op jit(solution)/shard_map/ppermute | solution.py:37
  103.0 7.4 %collective-permute-start.12 = (bf16[256,256]{1,0:T(8,128)(2,1)S(1)}, bf16[256,256]{1,0:T(8,128)(2,1)S(1)}, u32[]{:S(2)}, u32[]{:S(2)}) collective-permute-start(bf16[256,256]{1,0:T(8,128)(2,1)S(1)} %get-tuple-element.20.refs_3_), channel_id=1, source_target_pairs={{0,8},{8,0},{4,12},{12,4},{16,24},{24,16},{20,28},{28,20},{32,40},... | collective-permute-start | bytes 393224 | tf_op jit(solution)/shard_map/ppermute | solution.py:32
  105.0 10.2 %collective-permute-start.11 = (bf16[256,256]{1,0:T(8,128)(2,1)S(1)}, bf16[256,256]{1,0:T(8,128)(2,1)S(1)}, u32[]{:S(2)}, u32[]{:S(2)}) collective-permute-start(bf16[256,256]{1,0:T(8,128)(2,1)S(1)} %get-tuple-element.20.refs_3_), channel_id=1, source_target_pairs={{8,16},{16,8},{12,20},{20,12},{24,32},{32,24},{28,36},{36,28},{40,... | collective-permute-start | bytes 393224 | tf_op jit(solution)/shard_map/ppermute | solution.py:32
  108.5 8.6 %collective-permute-start.13 = (bf16[256,256]{1,0:T(8,128)(2,1)S(1)}, bf16[256,256]{1,0:T(8,128)(2,1)S(1)}, u32[]{:S(2)}, u32[]{:S(2)}) collective-permute-start(bf16[256,256]{1,0:T(8,128)(2,1)S(1)} %get-tuple-element.20.refs_3_), channel_id=1, source_target_pairs={{0,4},{4,0},{8,12},{12,8},{16,20},{20,16},{24,28},{28,24},{32,36},... | collective-permute-start | bytes 393224 | tf_op jit(solution)/shard_map/ppermute | solution.py:37
  115.2 3.2 %collective-permute-start.14 = (bf16[256,256]{1,0:T(8,128)(2,1)S(1)}, bf16[256,256]{1,0:T(8,128)(2,1)S(1)}, u32[]{:S(2)}, u32[]{:S(2)}) collective-permute-start(bf16[256,256]{1,0:T(8,128)(2,1)S(1)} %broadcast_select_fusion.3), channel_id=1, source_target_pairs={{0,4},{4,0},{8,12},{12,8},{16,20},{20,16},{24,28},{28,24},{32,36},... | collective-permute-start | bytes 393224 | tf_op jit(solution)/shard_map/ppermute | solution.py:37
  132.9 7.4 %collective-permute-start.16 = (bf16[256,256]{1,0:T(8,128)(2,1)S(1)}, bf16[256,256]{1,0:T(8,128)(2,1)S(1)}, u32[]{:S(2)}, u32[]{:S(2)}) collective-permute-start(bf16[256,256]{1,0:T(8,128)(2,1)S(1)} %get-tuple-element.23.refs_3_), channel_id=1, source_target_pairs={{0,8},{8,0},{4,12},{12,4},{16,24},{24,16},{20,28},{28,20},{32,40},... | collective-permute-start | bytes 393224 | tf_op jit(solution)/shard_map/ppermute | solution.py:32
  134.8 10.2 %collective-permute-start.15 = (bf16[256,256]{1,0:T(8,128)(2,1)S(1)}, bf16[256,256]{1,0:T(8,128)(2,1)S(1)}, u32[]{:S(2)}, u32[]{:S(2)}) collective-permute-start(bf16[256,256]{1,0:T(8,128)(2,1)S(1)} %get-tuple-element.23.refs_3_), channel_id=1, source_target_pairs={{8,16},{16,8},{12,20},{20,12},{24,32},{32,24},{28,36},{36,28},{40,... | collective-permute-start | bytes 393224 | tf_op jit(solution)/shard_map/ppermute | solution.py:32
  138.3 8.6 %collective-permute-start.17 = (bf16[256,256]{1,0:T(8,128)(2,1)S(1)}, bf16[256,256]{1,0:T(8,128)(2,1)S(1)}, u32[]{:S(2)}, u32[]{:S(2)}) collective-permute-start(bf16[256,256]{1,0:T(8,128)(2,1)S(1)} %get-tuple-element.23.refs_3_), channel_id=1, source_target_pairs={{0,4},{4,0},{8,12},{12,8},{16,20},{20,16},{24,28},{28,24},{32,36},... | collective-permute-start | bytes 393224 | tf_op jit(solution)/shard_map/ppermute | solution.py:37
  145.0 3.2 %collective-permute-start.18 = (bf16[256,256]{1,0:T(8,128)(2,1)S(1)}, bf16[256,256]{1,0:T(8,128)(2,1)S(1)}, u32[]{:S(2)}, u32[]{:S(2)}) collective-permute-start(bf16[256,256]{1,0:T(8,128)(2,1)S(1)} %broadcast_select_fusion.2), channel_id=1, source_target_pairs={{0,4},{4,0},{8,12},{12,8},{16,20},{20,16},{24,28},{28,24},{32,36},... | collective-permute-start | bytes 393224 | tf_op jit(solution)/shard_map/ppermute | solution.py:37
  162.4 7.4 %collective-permute-start.20 = (bf16[256,256]{1,0:T(8,128)(2,1)S(1)}, bf16[256,256]{1,0:T(8,128)(2,1)S(1)}, u32[]{:S(2)}, u32[]{:S(2)}) collective-permute-start(bf16[256,256]{1,0:T(8,128)(2,1)S(1)} %get-tuple-element.25.refs_3_), channel_id=1, source_target_pairs={{0,8},{8,0},{4,12},{12,4},{16,24},{24,16},{20,28},{28,20},{32,40},... | collective-permute-start | bytes 393224 | tf_op jit(solution)/shard_map/ppermute | solution.py:32
  164.3 10.2 %collective-permute-start.19 = (bf16[256,256]{1,0:T(8,128)(2,1)S(1)}, bf16[256,256]{1,0:T(8,128)(2,1)S(1)}, u32[]{:S(2)}, u32[]{:S(2)}) collective-permute-start(bf16[256,256]{1,0:T(8,128)(2,1)S(1)} %get-tuple-element.25.refs_3_), channel_id=1, source_target_pairs={{8,16},{16,8},{12,20},{20,12},{24,32},{32,24},{28,36},{36,28},{40,... | collective-permute-start | bytes 393224 | tf_op jit(solution)/shard_map/ppermute | solution.py:32
  167.9 13.6 %collective-permute-start.21 = (bf16[256,256]{1,0:T(8,128)(2,1)S(1)}, bf16[256,256]{1,0:T(8,128)(2,1)S(1)}, u32[]{:S(2)}, u32[]{:S(2)}) collective-permute-start(bf16[256,256]{1,0:T(8,128)(2,1)S(1)} %get-tuple-element.25.refs_3_), channel_id=1, source_target_pairs={{0,4},{4,0},{8,12},{12,8},{16,20},{20,16},{24,28},{28,24},{32,36},... | collective-permute-start | bytes 393224 | tf_op jit(solution)/shard_map/ppermute | solution.py:37
  174.5 6.8 %copy-start.5 = (bf16[1,128,256]{2,1,0:T(8,128)(2,1)S(1)}, bf16[1,128,256]{2,1,0:T(8,128)(2,1)}, u32[]{:S(2)}) copy-start(bf16[1,128,256]{2,1,0:T(8,128)(2,1)} %get-tuple-element.33) | copy-start | bytes 196612
  174.6 6.9 %collective-permute-start.22 = (bf16[256,256]{1,0:T(8,128)(2,1)S(1)}, bf16[256,256]{1,0:T(8,128)(2,1)S(1)}, u32[]{:S(2)}, u32[]{:S(2)}) collective-permute-start(bf16[256,256]{1,0:T(8,128)(2,1)S(1)} %broadcast_select_fusion.1), channel_id=1, source_target_pairs={{0,4},{4,0},{8,12},{12,8},{16,20},{20,16},{24,28},{28,24},{32,36},... | collective-permute-start | bytes 393224 | tf_op jit(solution)/shard_map/ppermute | solution.py:37
  183.2 18.6 %copy-start = (bf16[1024,256]{1,0:T(8,128)(2,1)S(1)}, bf16[1024,256]{1,0:T(8,128)(2,1)}, u32[]{:S(2)}) copy-start(bf16[1024,256]{1,0:T(8,128)(2,1)} %grid_in.1) | copy-start | bytes 1572868

commit v8 on v6

--- a/solution.py
+++ b/solution.py
@@ -264,11 +264,11 @@
             [kept[meta[first_entry + b * per_block + j]] for j in range(per_block)], axis=0
         )
         o = attend_block(q[b * BLOCK : (b + 1) * BLOCK, :], kv[:, :128], kv[:, 128:], None)
-        for j in range(MP):
+        for j in range(o_out.shape[0]):
             o_out[j, b * BLOCK : (b + 1) * BLOCK, :] = o
 
 
-def near_attend(first_entry, per_block, meta, q, windows):
+def near_attend(first_entry, per_block, copies, meta, q, windows):
     def body(*refs):
         near_kernel(first_entry, per_block, *refs)
 
@@ -276,7 +276,7 @@
         body,
         in_specs=[smem()] + [vmem()] * 6,
         out_specs=vmem(),
-        out_shape=jax.ShapeDtypeStruct((MP,) + q.shape, BF16),
+        out_shape=jax.ShapeDtypeStruct((copies,) + q.shape, BF16),
         scratch_shapes=[pltpu.VMEM((10, BLOCK, 256), BF16)],
         compiler_params=PARAMS,
         name="near_attend",
@@ -385,23 +385,24 @@
     )(meta, o, state, gains, w_own, *fetched, other, *weights)
 
 
-def layer_kernel(gain_row, meta, o, state, gains, w_out, w_next, *rest):
+def layer_kernel(gain_row, o, state, gains, w_out, w_next, *rest):
     last = gain_row == 5
     state_out, kv_out, new = rest[0], rest[1], rest[-1]
-    heads = jnp.concatenate([o[source(meta, k)] for k in range(MP)], axis=1)
+    own = lax.axis_index("mp")
+    heads = jnp.concatenate([o[own ^ k] for k in range(MP)], axis=1)
     for g in range(MP):
         new[g] = (state[g].astype(F32) + dot(heads, w_out[g])).astype(BF16)
         if not last:
             state_out[g] = new[g]
     if last:
-        state_out[...] = new[meta[0]]
+        state_out[...] = new[own]
     result = finish_layer(gain_row, gains, new, lambda: w_next[...])
     kv_out[...] = result[:, :256]
     if not last:
         rest[2][...] = result[:, 256:]
 
 
-def layer(gain_row, meta, o, state, gains, prepared):
+def layer(gain_row, o, state, gains, prepared):
     def body(*refs):
         layer_kernel(gain_row, *refs)
 
@@ -415,18 +416,18 @@
         shapes.append(jax.ShapeDtypeStruct((rows, 128), BF16))
     return pl.pallas_call(
         body,
-        in_specs=[smem()] + [vmem()] * 5,
+        in_specs=[vmem()] * 5,
         out_specs=[vmem()] * len(shapes),
         out_shape=shapes,
         scratch_shapes=[pltpu.VMEM((MP, rows, 256), BF16)],
         compiler_params=PARAMS,
         name="mesh_layer",
-    )(meta, o, state, gains, *prepared)
-
-
-def final_kernel(meta, counts, o, w_out, grid_in, out):
+    )(o, state, gains, *prepared)
+
+
+def final_kernel(meta, counts, o0, o1, o2, o3, w_out, grid_in, out):
     tile = grid_in.shape[0]
-    heads = jnp.concatenate([o[source(meta, k)] for k in range(MP)], axis=1)
+    heads = jnp.concatenate([o[...] for o in (o0, o1, o2, o3)], axis=1)
     value = grid_in[...].astype(F32) + dot(heads, w_out[...])
     row = lax.broadcasted_iota(jnp.int32, (BLOCK, 256), 0)
     for b in range(tile // BLOCK):
@@ -444,7 +445,9 @@
         in_specs=[
             smem(),
             smem(),
-            pl.BlockSpec((MP, tile, 128), lambda i: (0, i, 0)),
+        ]
+        + [pl.BlockSpec((tile, 128), lambda i: (i, 0))] * MP
+        + [
             vmem(),
             pl.BlockSpec((tile, 256), lambda i: (i, 0)),
         ],
@@ -452,7 +455,7 @@
         out_shape=jax.ShapeDtypeStruct((rows, 256), BF16),
         compiler_params=PARAMS,
         name="grid_final",
-    )(meta, counts, o, w_out, grid_in)
+    )(meta, counts, *o, w_out, grid_in)
 
 
 def gather_heads(copies):
@@ -521,16 +524,16 @@
         if index == 0:
             made = first_layer(meta, heads, state, gains, w_out, arrived, other, (w_key, w_value, w_query))
         else:
-            made = layer(3 if index == 1 else 5, meta, heads, state, gains, prepared)
+            made = layer(3 if index == 1 else 5, heads, state, gains, prepared)
         state, kv = made[0], made[1]
         near = window(kv)
         if index < 2:
             weights = (w_key, w_value, w_query) if index == 0 else (w_key, w_value)
             prepared = prepare(index + 1, meta, w_own, arrived, other, weights)
-            o = near_attend(PROC0, 3, meta, made[2], near)
+            o = near_attend(PROC0, 3, MP, meta, made[2], near)
     grid_q, w_last = lax.optimization_barrier((grid_q, w_last))
-    o = near_attend(DEC0, 2, meta, grid_q, near)
-    heads = gather_heads(o)
+    o = near_attend(DEC0, 2, 1, meta, grid_q, near)
+    heads = gathered(o[0], "d")
     grid_out = final(meta, grid_count, heads, w_last, grid_in)
     return grid_out, state
 

time: 215 us -> 218 us (1.014)
  the two profiles are of different devices: /device:TPU:384 before, /device:TPU:385 now
where the time goes in v8:
time: 218 us; the launch traced here: 216 us
  starting transfers between devices  99.7 us (46%)
  waiting for transfers between devices  52.9 us (24%)
  Pallas kernels  33.9 us (16%)
  local copies, waits for them, and re-layouts  14.4 us (7%)
  blocking collectives  10.1 us (5%)
  other arithmetic  3.51 us (2%)
    ppermute x9, waiting for transfers between devices, swap_mp(): return lax.ppermute(value, 'mp', [(s, s ^ k) for s in range(MP)])  47.9 us
    ppermute x9, starting transfers between devices, swap_cores(): return lax.ppermute(value, 'nodes', [(s, s ^ 1) for s in range(count)])  38.3 us
    ppermute x9, starting transfers between devices, swap_mp(): return lax.ppermute(value, 'mp', [(s, s ^ k) for s in range(MP)])  28.8 us
    ppermute x8, starting transfers between devices, swap_chips(): return lax.ppermute(value, 'nodes', pairs)  25.8 us
    unnamed x48, local copies, waits for them, and re-layouts  10.9 us
    all_to_all x1, blocking collectives, gather_heads(): return lax.all_to_all(copies, 'mp', split_axis=0, concat_axis=0, tiled=True)  10.1 us
    all_to_all x2, starting transfers between devices, gather_heads(): return lax.all_to_all(copies, 'mp', split_axis=0, concat_axis=0, tiled=True)  6.81 us
    pallas_call x3, Pallas kernels, near_attend(): pl.pallas_call(body, in_specs=[smem()] + [vmem()] * 6, out_specs=vmem(),...  6.69 us
  transfers between devices with their start and end apart: 28, of which 15 were waited for; matrix products, arithmetic and copies ran while one was open for 3% of the time, Pallas kernels for 6%

profile of v8, /device:TPU:385, one launch (start us, length us, event | category | flops | bytes accessed | tf_op | source)
XLA Modules:
  0.0 216.0 jit_solution(10838450451401182354)
XLA Ops:
  0.6 3.2 %collective-permute-start = (bf16[1024,256]{1,0:T(8,128)(2,1)}, bf16[1024,256]{1,0:T(8,128)(2,1)S(1)}, u32[]{:S(2)}, u32[]{:S(2)}) collective-permute-start(bf16[1024,256]{1,0:T(8,128)(2,1)} %grid_in.1), channel_id=1, source_target_pairs={{0,1},{1,0},{2,3},{3,2},{4,5},{5,4},{6,7},{7,6},{8,9},{9,8},{10,11... | collective-permute-start | bytes 1572872 | tf_op jit(solution)/shard_map/ppermute | solution.py:23
  3.8 4.5 %collective-permute-start.1 = (bf16[1024,256]{1,0:T(8,128)(2,1)}, bf16[1024,256]{1,0:T(8,128)(2,1)S(1)}, u32[]{:S(2)}, u32[]{:S(2)}) collective-permute-start(bf16[1024,256]{1,0:T(8,128)(2,1)} %grid_in.1), channel_id=1, source_target_pairs={{0,2},{1,3},{2,0},{3,1},{4,6},{5,7},{6,4},{7,5},{8,10},{9,11},{10,... | collective-permute-start | bytes 1572872 | tf_op jit(solution)/shard_map/ppermute | solution.py:23
  8.4 1.9 collective-permute-start.2
  15.5 13.7 %collective-permute-done.1.refs_3_ = bf16[1024,256]{1,0:T(8,128)(2,1)S(1)} collective-permute-done((bf16[1024,256]{1,0:T(8,128)(2,1)}, bf16[1024,256]{1,0:T(8,128)(2,1)S(1)}, u32[]{:S(2)}, u32[]{:S(2)}) %collective-permute-start.1) | collective-permute-done | bytes 524320 | tf_op jit(solution)/shard_map/ppermute | solution.py:23
  29.3 5.9 %collective-permute-done.2.refs_4_ = bf16[1024,256]{1,0:T(8,128)(2,1)S(1)} collective-permute-done((bf16[1024,256]{1,0:T(8,128)(2,1)}, bf16[1024,256]{1,0:T(8,128)(2,1)S(1)}, u32[]{:S(2)}, u32[]{:S(2)}) %collective-permute-start.2) | collective-permute-done | bytes 524320 | tf_op jit(solution)/shard_map/ppermute | solution.py:23
  35.2 4.5 %grid_project.1.a1 = bf16[1024,256]{1,0:T(8,128)(2,1)} custom-call(s32[32]{0:T(128)S(1)} %concatenate.15.refs_0_.meta, bf16[1024,256]{1,0:T(8,128)(2,1)} %grid_in.1, bf16[1024,256]{1,0:T(8,128)(2,1)S(1)} %collective-permute-done.refs_2_, bf16[1024,256]{1,0:T(8,128)(2,1)S(1)} %collective-permute-done.1.refs_3_, ...), custom_call_target="tpu_custom_call" | custom-call | flops 536870912 | bytes 4194304 | tf_op jit(solution)/shard_map/grid_project/pallas_call | solution.py:98
  40.5 6.2 %collective-permute-start.6 = (bf16[1024,256]{1,0:T(8,128)(2,1)}, bf16[1024,256]{1,0:T(8,128)(2,1)S(1)}, u32[]{:S(2)}, u32[]{:S(2)}) collective-permute-start(bf16[1024,256]{1,0:T(8,128)(2,1)} %grid_project.1.a1), channel_id=1, source_target_pairs={{8,16},{16,8},{12,20},{20,12},{24,32},{32,24},{28,36},{36,28},{40,... | collective-permute-start | bytes 1572872 | tf_op jit(solution)/shard_map/ppermute | solution.py:32
  46.6 1.9 collective-permute-start.7
  51.0 1.9 collective-permute-start.3
  52.9 3.2 %collective-permute-start.4 = (bf16[9,128,256]{2,1,0:T(8,128)(2,1)}, bf16[9,128,256]{2,1,0:T(8,128)(2,1)S(1)}, u32[]{:S(2)}, u32[]{:S(2)}) collective-permute-start(bf16[9,128,256]{2,1,0:T(8,128)(2,1)} %get-tuple-element.39), channel_id=1, source_target_pairs={{0,2},{1,3},{2,0},{3,1},{4,6},{5,7},{6,4},{7,5},{8,10},{9,11},{10,... | collective-permute-start | bytes 1769480 | tf_op jit(solution)/shard_map/ppermute | solution.py:23
  56.1 4.5 %collective-permute-start.5 = (bf16[9,128,256]{2,1,0:T(8,128)(2,1)S(1)}, bf16[9,128,256]{2,1,0:T(8,128)(2,1)S(1)}, u32[]{:S(2)}, u32[]{:S(2)}) collective-permute-start(bf16[9,128,256]{2,1,0:T(8,128)(2,1)S(1)} %get-tuple-element.38), channel_id=1, source_target_pairs={{0,3},{1,2},{2,1},{3,0},{4,7},{5,6},{6,5},{7,4},{8,11},{9,10},{10,... | collective-permute-start | bytes 1769480 | tf_op jit(solution)/shard_map/ppermute | solution.py:23
  60.6 5.1 %collective-permute-start.8 = (bf16[1024,256]{1,0:T(8,128)(2,1)}, bf16[1024,256]{1,0:T(8,128)(2,1)S(1)}, u32[]{:S(2)}, u32[]{:S(2)}) collective-permute-start(bf16[1024,256]{1,0:T(8,128)(2,1)} %grid_project.1.a1), channel_id=1, source_target_pairs={{0,4},{4,0},{8,12},{12,8},{16,20},{20,16},{24,28},{28,24},{32,36},... | collective-permute-start | bytes 1572872 | tf_op jit(solution)/shard_map/ppermute | solution.py:37
  65.9 3.0 %collective-permute-start.9 = (bf16[1024,256]{1,0:T(8,128)(2,1)S(1)}, bf16[1024,256]{1,0:T(8,128)(2,1)S(1)}, u32[]{:S(2)}, u32[]{:S(2)}) collective-permute-start(bf16[1024,256]{1,0:T(8,128)(2,1)S(1)} %broadcast_select_fusion), channel_id=1, source_target_pairs={{0,4},{4,0},{8,12},{12,8},{16,20},{20,16},{24,28},{28,24},{32,36},... | collective-permute-start | bytes 1572872 | tf_op jit(solution)/shard_map/ppermute | solution.py:37
  68.9 9.3 %collective-permute-done.4.a2.refs_3_ = bf16[9,128,256]{2,1,0:T(8,128)(2,1)S(1)} collective-permute-done((bf16[9,128,256]{2,1,0:T(8,128)(2,1)}, bf16[9,128,256]{2,1,0:T(8,128)(2,1)S(1)}, u32[]{:S(2)}, u32[]{:S(2)}) %collective-permute-start.4) | collective-permute-done | bytes 589856 | tf_op jit(solution)/shard_map/ppermute | solution.py:23
  78.2 5.7 %collective-permute-done.5.a3.refs_4_ = bf16[9,128,256]{2,1,0:T(8,128)(2,1)S(1)} collective-permute-done((bf16[9,128,256]{2,1,0:T(8,128)(2,1)S(1)}, bf16[9,128,256]{2,1,0:T(8,128)(2,1)S(1)}, u32[]{:S(2)}, u32[]{:S(2)}) %collective-permute-start.5) | collective-permute-done | bytes 589856 | tf_op jit(solution)/shard_map/ppermute | solution.py:23
  83.9 1.9 mesh_start.1.q
  85.8 3.4 %enc_attend.1 = bf16[4,256,128]{2,1,0:T(8,128)(2,1)} custom-call(s32[32]{0:T(128)S(1)} %concatenate.15.refs_0_.meta, s32[2,4]{1,0:T(2,128)S(1)} %copy-done.21, s32[1024]{0:T(1024)S(1)} %copy-done.20, bf16[256,128]{1,0:T(8,128)(2,1)S(1)} %mesh_start.1.q, bf16[1024,256]{1,0:T(8,128)(2,1)S(1)} %collective-permute-done.6.a0, bf16[1024,256]{1,0:T(8,128)(2,1)} %grid_project.1.a1, ...), custom_call_target="tpu_custom_call" | custom-call | tf_op jit(solution)/shard_map/enc_attend/pallas_call | solution.py:247
  89.5 5.8 %collective-permute-start.10 = (bf16[3,6,128,256]{3,2,1,0:T(8,128)(2,1)S(1)}, bf16[3,6,128,256]{3,2,1,0:T(8,128)(2,1)S(1)}, u32[]{:S(2)}, u32[]{:S(2)}) collective-permute-start(bf16[3,6,128,256]{3,2,1,0:T(8,128)(2,1)S(1)} %pad_maximum_fusion), channel_id=1, source_target_pairs={{0,4},{4,0},{8,12},{12,8},{16,20},{20,16},{24,28},{28,24},{32,36},... | collective-permute-start | bytes 3538952 | tf_op jit(solution)/shard_map/ppermute | solution.py:37
  95.3 10.1 %all_to_all.15.o = bf16[4,256,128]{2,1,0:T(8,128)(2,1)S(1)} all-to-all(bf16[4,256,128]{2,1,0:T(8,128)(2,1)S(1)} %copy-done.22), channel_id=1, replica_groups=mesh['nodes'=128,'mp'=4] {'mp'}, dimensions={0} | all-to-all | bytes 524288 | tf_op jit(solution)/shard_map/all_to_all | solution.py:462
  105.4 2.5 %first_layer.1 = (bf16[4,256,256]{2,1,0:T(8,128)(2,1)S(1)}, bf16[256,256]{1,0:T(8,128)(2,1)S(1)}, bf16[256,128]{1,0:T(8,128)(2,1)S(1)}) custom-call(s32[32]{0:T(128)S(1)} %concatenate.15.refs_0_.meta, bf16[4,256,128]{2,1,0:T(8,128)(2,1)S(1)} %all_to_all.15.o, bf16[256,256]{1,0:T(8,128)(2,1)S(1)} %copy-done.11, ...), custom_call_target="tpu_custom_call" | custom-call | tf_op jit(solution)/shard_map/first_layer/pallas_call | solution.py:373
  108.7 2.7 %collective-permute-start.11 = (bf16[256,256]{1,0:T(8,128)(2,1)S(1)}, bf16[256,256]{1,0:T(8,128)(2,1)S(1)}, u32[]{:S(2)}, u32[]{:S(2)}) collective-permute-start(bf16[256,256]{1,0:T(8,128)(2,1)S(1)} %get-tuple-element.24.refs_3_), channel_id=1, source_target_pairs={{8,16},{16,8},{12,20},{20,12},{24,32},{32,24},{28,36},{36,28},{40,... | collective-permute-start | bytes 393224 | tf_op jit(solution)/shard_map/ppermute | solution.py:32
  111.4 2.6 %collective-permute-start.12 = (bf16[256,256]{1,0:T(8,128)(2,1)S(1)}, bf16[256,256]{1,0:T(8,128)(2,1)S(1)}, u32[]{:S(2)}, u32[]{:S(2)}) collective-permute-start(bf16[256,256]{1,0:T(8,128)(2,1)S(1)} %get-tuple-element.24.refs_3_), channel_id=1, source_target_pairs={{0,8},{8,0},{4,12},{12,4},{16,24},{24,16},{20,28},{28,20},{32,40},... | collective-permute-start | bytes 393224 | tf_op jit(solution)/shard_map/ppermute | solution.py:32
  113.9 3.3 %collective-permute-start.13 = (bf16[256,256]{1,0:T(8,128)(2,1)S(1)}, bf16[256,256]{1,0:T(8,128)(2,1)S(1)}, u32[]{:S(2)}, u32[]{:S(2)}) collective-permute-start(bf16[256,256]{1,0:T(8,128)(2,1)S(1)} %get-tuple-element.24.refs_3_), channel_id=1, source_target_pairs={{0,4},{4,0},{8,12},{12,8},{16,20},{20,16},{24,28},{28,24},{32,36},... | collective-permute-start | bytes 393224 | tf_op jit(solution)/shard_map/ppermute | solution.py:37
  117.7 4.2 %collective-permute-start.14 = (bf16[256,256]{1,0:T(8,128)(2,1)S(1)}, bf16[256,256]{1,0:T(8,128)(2,1)S(1)}, u32[]{:S(2)}, u32[]{:S(2)}) collective-permute-start(bf16[256,256]{1,0:T(8,128)(2,1)S(1)} %broadcast_select_fusion.3), channel_id=1, source_target_pairs={{0,4},{4,0},{8,12},{12,8},{16,20},{20,16},{24,28},{28,24},{32,36},... | collective-permute-start | bytes 393224 | tf_op jit(solution)/shard_map/ppermute | solution.py:37
  122.9 2.5 %near_attend.3 = bf16[4,256,128]{2,1,0:T(8,128)(2,1)} custom-call(s32[32]{0:T(128)S(1)} %concatenate.15.refs_0_.meta, bf16[256,128]{1,0:T(8,128)(2,1)S(1)} %get-tuple-element.23.refs_1_, bf16[256,256]{1,0:T(8,128)(2,1)S(1)} %collective-permute-done.11.refs_2_, bf16[256,256]{1,0:T(8,128)(2,1)S(1)} %get-tuple-element.24.refs_3_, ...), custom_call_target="tpu_custom_call" | custom-call | tf_op jit(solution)/shard_map/near_attend/pallas_call | solution.py:275
  125.4 3.4 %all-to-all-start.1 = ((bf16[4,256,128]{2,1,0:T(8,128)(2,1)}), bf16[4,256,128]{2,1,0:T(8,128)(2,1)S(1)}, u32[]{:S(2)}, u32[]{:S(2)}) async-start(bf16[4,256,128]{2,1,0:T(8,128)(2,1)} %near_attend.3), calls=%async_computation.1 | async-start | bytes 524288 | tf_op jit(solution)/shard_map/all_to_all | solution.py:462
  128.8 1.3 copy-done.2
  130.1 2.8 %layer_weights.2 = (bf16[4,512,256]{2,1,0:T(8,128)(2,1)S(1)}, bf16[1024,384]{1,0:T(8,128)(2,1)S(1)}) custom-call(s32[32]{0:T(128)S(1)} %concatenate.15.refs_0_.meta, bf16[4,128,1024]{2,1,0:T(8,128)(2,1)} %refs_1_.7, bf16[9,128,256]{2,1,0:T(8,128)(2,1)S(1)} %collective-permute-done.3.a1.refs_2_, bf16[9,128,256]{2,1,0:T(8,128)(2,1)S(1)} %collective-permute-done.4.a2.refs_3_, ...), custom_call_target="tpu_custom_call" | custom-call | tf_op jit(solution)/shard_map/layer_weights/pallas_call | solution.py:318
  138.9 5.6 %collective-permute-start.15 = (bf16[256,256]{1,0:T(8,128)(2,1)S(1)}, bf16[256,256]{1,0:T(8,128)(2,1)S(1)}, u32[]{:S(2)}, u32[]{:S(2)}) collective-permute-start(bf16[256,256]{1,0:T(8,128)(2,1)S(1)} %get-tuple-element.29.refs_3_), channel_id=1, source_target_pairs={{8,16},{16,8},{12,20},{20,12},{24,32},{32,24},{28,36},{36,28},{40,... | collective-permute-start | bytes 393224 | tf_op jit(solution)/shard_map/ppermute | solution.py:32
  144.5 1.9 collective-permute-start.16
  146.4 3.7 %collective-permute-start.17 = (bf16[256,256]{1,0:T(8,128)(2,1)S(1)}, bf16[256,256]{1,0:T(8,128)(2,1)S(1)}, u32[]{:S(2)}, u32[]{:S(2)}) collective-permute-start(bf16[256,256]{1,0:T(8,128)(2,1)S(1)} %get-tuple-element.29.refs_3_), channel_id=1, source_target_pairs={{0,4},{4,0},{8,12},{12,8},{16,20},{20,16},{24,28},{28,24},{32,36},... | collective-permute-start | bytes 393224 | tf_op jit(solution)/shard_map/ppermute | solution.py:37
  150.3 4.8 %collective-permute-start.18 = (bf16[256,256]{1,0:T(8,128)(2,1)S(1)}, bf16[256,256]{1,0:T(8,128)(2,1)S(1)}, u32[]{:S(2)}, u32[]{:S(2)}) collective-permute-start(bf16[256,256]{1,0:T(8,128)(2,1)S(1)} %broadcast_select_fusion.2), channel_id=1, source_target_pairs={{0,4},{4,0},{8,12},{12,8},{16,20},{20,16},{24,28},{28,24},{32,36},... | collective-permute-start | bytes 393224 | tf_op jit(solution)/shard_map/ppermute | solution.py:37
  156.1 2.5 %near_attend.4 = bf16[4,256,128]{2,1,0:T(8,128)(2,1)} custom-call(s32[32]{0:T(128)S(1)} %concatenate.15.refs_0_.meta, bf16[256,128]{1,0:T(8,128)(2,1)S(1)} %get-tuple-element.28.refs_1_, bf16[256,256]{1,0:T(8,128)(2,1)S(1)} %collective-permute-done.15.refs_2_, bf16[256,256]{1,0:T(8,128)(2,1)S(1)} %get-tuple-element.29.refs_3_, ...), custom_call_target="tpu_custom_call" | custom-call | tf_op jit(solution)/shard_map/near_attend/pallas_call | solution.py:275
  158.5 3.4 %all-to-all-start.2 = ((bf16[4,256,128]{2,1,0:T(8,128)(2,1)}), bf16[4,256,128]{2,1,0:T(8,128)(2,1)S(1)}, u32[]{:S(2)}, u32[]{:S(2)}) async-start(bf16[4,256,128]{2,1,0:T(8,128)(2,1)} %near_attend.4), calls=%async_computation.2 | async-start | bytes 524288 | tf_op jit(solution)/shard_map/all_to_all | solution.py:462
  163.2 2.8 %layer_weights.3 = (bf16[4,512,256]{2,1,0:T(8,128)(2,1)S(1)}, bf16[1024,256]{1,0:T(8,128)(2,1)S(1)}) custom-call(s32[32]{0:T(128)S(1)} %concatenate.15.refs_0_.meta, bf16[4,128,1024]{2,1,0:T(8,128)(2,1)} %refs_1_.7, bf16[9,128,256]{2,1,0:T(8,128)(2,1)S(1)} %collective-permute-done.3.a1.refs_2_, bf16[9,128,256]{2,1,0:T(8,128)(2,1)S(1)} %collective-permute-done.4.a2.refs_3_, ...), custom_call_target="tpu_custom_call" | custom-call | tf_op jit(solution)/shard_map/layer_weights/pallas_call | solution.py:318
  170.1 1.7 mesh_layer.3
  171.8 3.0 %collective-permute-start.19 = (bf16[256,256]{1,0:T(8,128)(2,1)S(1)}, bf16[256,256]{1,0:T(8,128)(2,1)S(1)}, u32[]{:S(2)}, u32[]{:S(2)}) collective-permute-start(bf16[256,256]{1,0:T(8,128)(2,1)S(1)} %get-tuple-element.33.refs_3_), channel_id=1, source_target_pairs={{8,16},{16,8},{12,20},{20,12},{24,32},{32,24},{28,36},{36,28},{40,... | collective-permute-start | bytes 393224 | tf_op jit(solution)/shard_map/ppermute | solution.py:32
  174.8 1.9 collective-permute-start.20
  176.7 3.7 %collective-permute-start.21 = (bf16[256,256]{1,0:T(8,128)(2,1)S(1)}, bf16[256,256]{1,0:T(8,128)(2,1)S(1)}, u32[]{:S(2)}, u32[]{:S(2)}) collective-permute-start(bf16[256,256]{1,0:T(8,128)(2,1)S(1)} %get-tuple-element.33.refs_3_), channel_id=1, source_target_pairs={{0,4},{4,0},{8,12},{12,8},{16,20},{20,16},{24,28},{28,24},{32,36},... | collective-permute-start | bytes 393224 | tf_op jit(solution)/shard_map/ppermute | solution.py:37
  180.8 4.7 %collective-permute-start.22 = (bf16[256,256]{1,0:T(8,128)(2,1)S(1)}, bf16[256,256]{1,0:T(8,128)(2,1)S(1)}, u32[]{:S(2)}, u32[]{:S(2)}) collective-permute-start(bf16[256,256]{1,0:T(8,128)(2,1)S(1)} %broadcast_select_fusion.1), channel_id=1, source_target_pairs={{0,4},{4,0},{8,12},{12,8},{16,20},{20,16},{24,28},{28,24},{32,36},... | collective-permute-start | bytes 393224 | tf_op jit(solution)/shard_map/ppermute | solution.py:37
  185.6 4.7 %grid_query.1.refs_1_ = bf16[1024,128]{1,0:T(8,128)(2,1)S(1)} custom-call(s32[32]{0:T(128)S(1)} %concatenate.15.refs_0_.meta, bf16[1024,256]{1,0:T(8,128)(2,1)} %grid_in.1, bf16[1024,256]{1,0:T(8,128)(2,1)S(1)} %copy-done.6, bf16[1024,256]{1,0:T(8,128)(2,1)S(1)} %copy-done.8, bf16[1024,256]{1,0:T(8,128)(2,1)S(1)} %copy-done.10, ...), custom_call_target="tpu_custom_call" | custom-call | flops 268435456 | bytes 4194304 | tf_op jit(solution)/shard_map/grid_query/pallas_call | solution.py:146
  190.4 1.7 near_attend.5
  192.1 2.2 %collective-permute-start.23 = (bf16[1024,128]{1,0:T(8,128)(2,1)S(1)}, bf16[1024,128]{1,0:T(8,128)(2,1)S(1)}, u32[]{:S(2)}, u32[]{:S(2)}) collective-permute-start(bf16[1024,128]{1,0:T(8,128)(2,1)S(1)} %bitcast.17), channel_id=1, source_target_pairs={{0,1},{1,0},{2,3},{3,2},{4,5},{5,4},{6,7},{7,6},{8,9},{9,8},{10,11... | collective-permute-start | bytes 786440 | tf_op jit(solution)/shard_map/ppermute | solution.py:23
  194.3 3.7 %collective-permute-start.24 = (bf16[1024,128]{1,0:T(8,128)(2,1)S(1)}, bf16[1024,128]{1,0:T(8,128)(2,1)S(1)}, u32[]{:S(2)}, u32[]{:S(2)}) collective-permute-start(bf16[1024,128]{1,0:T(8,128)(2,1)S(1)} %bitcast.18), channel_id=1, source_target_pairs={{0,2},{1,3},{2,0},{3,1},{4,6},{5,7},{6,4},{7,5},{8,10},{9,11},{10,... | collective-permute-start | bytes 786440 | tf_op jit(solution)/shard_map/ppermute | solution.py:23
  198.0 3.7 %collective-permute-start.25 = (bf16[1024,128]{1,0:T(8,128)(2,1)S(1)}, bf16[1024,128]{1,0:T(8,128)(2,1)S(1)}, u32[]{:S(2)}, u32[]{:S(2)}) collective-permute-start(bf16[1024,128]{1,0:T(8,128)(2,1)S(1)} %bitcast.19), channel_id=1, source_target_pairs={{0,3},{1,2},{2,1},{3,0},{4,7},{5,6},{6,5},{7,4},{8,11},{9,10},{10,... | collective-permute-start | bytes 786440 | tf_op jit(solution)/shard_map/ppermute | solution.py:23
  201.9 6.2 %collective-permute-done.24.o2 = bf16[1024,128]{1,0:T(8,128)(2,1)S(1)} collective-permute-done((bf16[1024,128]{1,0:T(8,128)(2,1)S(1)}, bf16[1024,128]{1,0:T(8,128)(2,1)S(1)}, u32[]{:S(2)}, u32[]{:S(2)}) %collective-permute-start.24) | collective-permute-done | bytes 262176 | tf_op jit(solution)/shard_map/ppermute | solution.py:23
  208.1 6.0 %collective-permute-done.25.o3 = bf16[1024,128]{1,0:T(8,128)(2,1)S(1)} collective-permute-done((bf16[1024,128]{1,0:T(8,128)(2,1)S(1)}, bf16[1024,128]{1,0:T(8,128)(2,1)S(1)}, u32[]{:S(2)}, u32[]{:S(2)}) %collective-permute-start.25) | collective-permute-done | bytes 262176 | tf_op jit(solution)/shard_map/ppermute | solution.py:23
  214.1 1.9 grid_final.1
  (99 shorter events, 23.8 us)
Async XLA Ops:
  0.6 14.9 %collective-permute-start = (bf16[1024,256]{1,0:T(8,128)(2,1)}, bf16[1024,256]{1,0:T(8,128)(2,1)S(1)}, u32[]{:S(2)}, u32[]{:S(2)}) collective-permute-start(bf16[1024,256]{1,0:T(8,128)(2,1)} %grid_in.1), channel_id=1, source_target_pairs={{0,1},{1,0},{2,3},{3,2},{4,5},{5,4},{6,7},{7,6},{8,9},{9,8},{10,11... | collective-permute-start | bytes 1572872 | tf_op jit(solution)/shard_map/ppermute | solution.py:23
  3.8 25.4 %collective-permute-start.1 = (bf16[1024,256]{1,0:T(8,128)(2,1)}, bf16[1024,256]{1,0:T(8,128)(2,1)S(1)}, u32[]{:S(2)}, u32[]{:S(2)}) collective-permute-start(bf16[1024,256]{1,0:T(8,128)(2,1)} %grid_in.1), channel_id=1, source_target_pairs={{0,2},{1,3},{2,0},{3,1},{4,6},{5,7},{6,4},{7,5},{8,10},{9,11},{10,... | collective-permute-start | bytes 1572872 | tf_op jit(solution)/shard_map/ppermute | solution.py:23
  8.4 26.8 %collective-permute-start.2 = (bf16[1024,256]{1,0:T(8,128)(2,1)}, bf16[1024,256]{1,0:T(8,128)(2,1)S(1)}, u32[]{:S(2)}, u32[]{:S(2)}) collective-permute-start(bf16[1024,256]{1,0:T(8,128)(2,1)} %grid_in.1), channel_id=1, source_target_pairs={{0,3},{1,2},{2,1},{3,0},{4,7},{5,6},{6,5},{7,4},{8,11},{9,10},{10,... | collective-permute-start | bytes 1572872 | tf_op jit(solution)/shard_map/ppermute | solution.py:23
  29.3 10.4 %copy-start.7 = (bf16[1024,256]{1,0:T(8,128)(2,1)}, bf16[1024,256]{1,0:T(8,128)(2,1)S(1)}, u32[]{:S(2)}) copy-start(bf16[1024,256]{1,0:T(8,128)(2,1)S(1)} %collective-permute-done.1.refs_3_) | copy-start | bytes 1572868
  35.2 4.5 %copy-start.9 = (bf16[1024,256]{1,0:T(8,128)(2,1)}, bf16[1024,256]{1,0:T(8,128)(2,1)S(1)}, u32[]{:S(2)}) copy-start(bf16[1024,256]{1,0:T(8,128)(2,1)S(1)} %collective-permute-done.2.refs_4_) | copy-start | bytes 1572868
  40.5 8.2 %slice-start = ((bf16[4,128,1024]{2,1,0:T(8,128)(2,1)}), bf16[1,128,1024]{2,1,0:T(8,128)(2,1)S(1)}, s32[]{:S(2)}) async-start(bf16[4,128,1024]{2,1,0:T(8,128)(2,1)} %refs_1_.7), calls=%async_computation.3 | async-start | bytes 524288 | tf_op jit(solution)/shard_map/slice | solution.py:518
  40.5 20.2 %collective-permute-start.6 = (bf16[1024,256]{1,0:T(8,128)(2,1)}, bf16[1024,256]{1,0:T(8,128)(2,1)S(1)}, u32[]{:S(2)}, u32[]{:S(2)}) collective-permute-start(bf16[1024,256]{1,0:T(8,128)(2,1)} %grid_project.1.a1), channel_id=1, source_target_pairs={{8,16},{16,8},{12,20},{20,12},{24,32},{32,24},{28,36},{36,28},{40,... | collective-permute-start | bytes 1572872 | tf_op jit(solution)/shard_map/ppermute | solution.py:32
  46.6 19.1 %collective-permute-start.7 = (bf16[1024,256]{1,0:T(8,128)(2,1)}, bf16[1024,256]{1,0:T(8,128)(2,1)}, u32[]{:S(2)}, u32[]{:S(2)}) collective-permute-start(bf16[1024,256]{1,0:T(8,128)(2,1)} %grid_project.1.a1), channel_id=1, source_target_pairs={{0,8},{8,0},{4,12},{12,4},{16,24},{24,16},{20,28},{28,20},{32,40},... | collective-permute-start | bytes 1572872 | tf_op jit(solution)/shard_map/ppermute | solution.py:32
  48.6 1.2 slice-start.1
  48.6 1.2 copy-start.11
  51.0 17.9 %collective-permute-start.3 = (bf16[9,128,256]{2,1,0:T(8,128)(2,1)}, bf16[9,128,256]{2,1,0:T(8,128)(2,1)S(1)}, u32[]{:S(2)}, u32[]{:S(2)}) collective-permute-start(bf16[9,128,256]{2,1,0:T(8,128)(2,1)} %get-tuple-element.40), channel_id=1, source_target_pairs={{0,1},{1,0},{2,3},{3,2},{4,5},{5,4},{6,7},{7,6},{8,9},{9,8},{10,11... | collective-permute-start | bytes 1769480 | tf_op jit(solution)/shard_map/ppermute | solution.py:23
  52.9 25.2 %collective-permute-start.4 = (bf16[9,128,256]{2,1,0:T(8,128)(2,1)}, bf16[9,128,256]{2,1,0:T(8,128)(2,1)S(1)}, u32[]{:S(2)}, u32[]{:S(2)}) collective-permute-start(bf16[9,128,256]{2,1,0:T(8,128)(2,1)} %get-tuple-element.39), channel_id=1, source_target_pairs={{0,2},{1,3},{2,0},{3,1},{4,6},{5,7},{6,4},{7,5},{8,10},{9,11},{10,... | collective-permute-start | bytes 1769480 | tf_op jit(solution)/shard_map/ppermute | solution.py:23
  56.1 27.8 %collective-permute-start.5 = (bf16[9,128,256]{2,1,0:T(8,128)(2,1)S(1)}, bf16[9,128,256]{2,1,0:T(8,128)(2,1)S(1)}, u32[]{:S(2)}, u32[]{:S(2)}) collective-permute-start(bf16[9,128,256]{2,1,0:T(8,128)(2,1)S(1)} %get-tuple-element.38), channel_id=1, source_target_pairs={{0,3},{1,2},{2,1},{3,0},{4,7},{5,6},{6,5},{7,4},{8,11},{9,10},{10,... | collective-permute-start | bytes 1769480 | tf_op jit(solution)/shard_map/ppermute | solution.py:23
  60.6 25.1 %collective-permute-start.8 = (bf16[1024,256]{1,0:T(8,128)(2,1)}, bf16[1024,256]{1,0:T(8,128)(2,1)S(1)}, u32[]{:S(2)}, u32[]{:S(2)}) collective-permute-start(bf16[1024,256]{1,0:T(8,128)(2,1)} %grid_project.1.a1), channel_id=1, source_target_pairs={{0,4},{4,0},{8,12},{12,8},{16,20},{20,16},{24,28},{28,24},{32,36},... | collective-permute-start | bytes 1572872 | tf_op jit(solution)/shard_map/ppermute | solution.py:37
  65.9 19.9 %copy-start.20 = (s32[1024]{0:T(1024)S(1)}, s32[1024]{0:T(1024)}, u32[]{:S(2)}) copy-start(s32[1024]{0:T(1024)} %counts.3) | copy-start | bytes 12292
  65.9 19.9 %copy-start.21 = (s32[2,4]{1,0:T(2,128)S(1)}, s32[2,4]{1,0:T(2,128)}, u32[]{:S(2)}) copy-start(s32[2,4]{1,0:T(2,128)} %listed.1) | copy-start | bytes 100
  65.9 19.9 %collective-permute-start.9 = (bf16[1024,256]{1,0:T(8,128)(2,1)S(1)}, bf16[1024,256]{1,0:T(8,128)(2,1)S(1)}, u32[]{:S(2)}, u32[]{:S(2)}) collective-permute-start(bf16[1024,256]{1,0:T(8,128)(2,1)S(1)} %broadcast_select_fusion), channel_id=1, source_target_pairs={{0,4},{4,0},{8,12},{12,8},{16,20},{20,16},{24,28},{28,24},{32,36},... | collective-permute-start | bytes 1572872 | tf_op jit(solution)/shard_map/ppermute | solution.py:37
  89.3 5.9 %copy-start.22 = (bf16[4,256,128]{2,1,0:T(8,128)(2,1)S(1)}, bf16[4,256,128]{2,1,0:T(8,128)(2,1)}, u32[]{:S(2)}) copy-start(bf16[4,256,128]{2,1,0:T(8,128)(2,1)} %enc_attend.1) | copy-start | bytes 786436
  89.3 16.1 %copy-start = (bf16[4,128,1024]{2,1,0:T(8,128)(2,1)S(1)}, bf16[4,128,1024]{2,1,0:T(8,128)(2,1)}, u32[]{:S(2)}) copy-start(bf16[4,128,1024]{2,1,0:T(8,128)(2,1)} %refs_1_.7) | copy-start | bytes 3145732
  89.5 15.9 %collective-permute-start.10 = (bf16[3,6,128,256]{3,2,1,0:T(8,128)(2,1)S(1)}, bf16[3,6,128,256]{3,2,1,0:T(8,128)(2,1)S(1)}, u32[]{:S(2)}, u32[]{:S(2)}) collective-permute-start(bf16[3,6,128,256]{3,2,1,0:T(8,128)(2,1)S(1)} %pad_maximum_fusion), channel_id=1, source_target_pairs={{0,4},{4,0},{8,12},{12,8},{16,20},{20,16},{24,28},{28,24},{32,36},... | collective-permute-start | bytes 3538952 | tf_op jit(solution)/shard_map/ppermute | solution.py:37
  105.4 2.5 %copy-start.1 = (bf16[3,6,128,256]{3,2,1,0:T(8,128)(2,1)}, bf16[3,6,128,256]{3,2,1,0:T(8,128)(2,1)S(1)}, u32[]{:S(2)}) copy-start(bf16[3,6,128,256]{3,2,1,0:T(8,128)(2,1)S(1)} %collective-permute-done.10.other.refs_5_) | copy-start | bytes 3538948
  108.7 9.0 %collective-permute-start.11 = (bf16[256,256]{1,0:T(8,128)(2,1)S(1)}, bf16[256,256]{1,0:T(8,128)(2,1)S(1)}, u32[]{:S(2)}, u32[]{:S(2)}) collective-permute-start(bf16[256,256]{1,0:T(8,128)(2,1)S(1)} %get-tuple-element.24.refs_3_), channel_id=1, source_target_pairs={{8,16},{16,8},{12,20},{20,12},{24,32},{32,24},{28,36},{36,28},{40,... | collective-permute-start | bytes 393224 | tf_op jit(solution)/shard_map/ppermute | solution.py:32
  111.4 6.3 %collective-permute-start.12 = (bf16[256,256]{1,0:T(8,128)(2,1)S(1)}, bf16[256,256]{1,0:T(8,128)(2,1)S(1)}, u32[]{:S(2)}, u32[]{:S(2)}) collective-permute-start(bf16[256,256]{1,0:T(8,128)(2,1)S(1)} %get-tuple-element.24.refs_3_), channel_id=1, source_target_pairs={{0,8},{8,0},{4,12},{12,4},{16,24},{24,16},{20,28},{28,20},{32,40},... | collective-permute-start | bytes 393224 | tf_op jit(solution)/shard_map/ppermute | solution.py:32
  113.9 8.0 %collective-permute-start.13 = (bf16[256,256]{1,0:T(8,128)(2,1)S(1)}, bf16[256,256]{1,0:T(8,128)(2,1)S(1)}, u32[]{:S(2)}, u32[]{:S(2)}) collective-permute-start(bf16[256,256]{1,0:T(8,128)(2,1)S(1)} %get-tuple-element.24.refs_3_), channel_id=1, source_target_pairs={{0,4},{4,0},{8,12},{12,8},{16,20},{20,16},{24,28},{28,24},{32,36},... | collective-permute-start | bytes 393224 | tf_op jit(solution)/shard_map/ppermute | solution.py:37
  117.7 5.2 %collective-permute-start.14 = (bf16[256,256]{1,0:T(8,128)(2,1)S(1)}, bf16[256,256]{1,0:T(8,128)(2,1)S(1)}, u32[]{:S(2)}, u32[]{:S(2)}) collective-permute-start(bf16[256,256]{1,0:T(8,128)(2,1)S(1)} %broadcast_select_fusion.3), channel_id=1, source_target_pairs={{0,4},{4,0},{8,12},{12,8},{16,20},{20,16},{24,28},{28,24},{32,36},... | collective-permute-start | bytes 393224 | tf_op jit(solution)/shard_map/ppermute | solution.py:37
  125.4 9.5 %all-to-all-start.1 = ((bf16[4,256,128]{2,1,0:T(8,128)(2,1)}), bf16[4,256,128]{2,1,0:T(8,128)(2,1)S(1)}, u32[]{:S(2)}, u32[]{:S(2)}) async-start(bf16[4,256,128]{2,1,0:T(8,128)(2,1)} %near_attend.3), calls=%async_computation.1 | async-start | bytes 524288 | tf_op jit(solution)/shard_map/all_to_all | solution.py:462
  128.8 1.3 copy-start.2
  134.9 1.1 copy-start.13
  136.0 1.0 copy-start.15
  138.9 11.2 %collective-permute-start.15 = (bf16[256,256]{1,0:T(8,128)(2,1)S(1)}, bf16[256,256]{1,0:T(8,128)(2,1)S(1)}, u32[]{:S(2)}, u32[]{:S(2)}) collective-permute-start(bf16[256,256]{1,0:T(8,128)(2,1)S(1)} %get-tuple-element.29.refs_3_), channel_id=1, source_target_pairs={{8,16},{16,8},{12,20},{20,12},{24,32},{32,24},{28,36},{36,28},{40,... | collective-permute-start | bytes 393224 | tf_op jit(solution)/shard_map/ppermute | solution.py:32
  144.5 5.7 %collective-permute-start.16 = (bf16[256,256]{1,0:T(8,128)(2,1)S(1)}, bf16[256,256]{1,0:T(8,128)(2,1)S(1)}, u32[]{:S(2)}, u32[]{:S(2)}) collective-permute-start(bf16[256,256]{1,0:T(8,128)(2,1)S(1)} %get-tuple-element.29.refs_3_), channel_id=1, source_target_pairs={{0,8},{8,0},{4,12},{12,4},{16,24},{24,16},{20,28},{28,20},{32,40},... | collective-permute-start | bytes 393224 | tf_op jit(solution)/shard_map/ppermute | solution.py:32
  146.4 8.7 %collective-permute-start.17 = (bf16[256,256]{1,0:T(8,128)(2,1)S(1)}, bf16[256,256]{1,0:T(8,128)(2,1)S(1)}, u32[]{:S(2)}, u32[]{:S(2)}) collective-permute-start(bf16[256,256]{1,0:T(8,128)(2,1)S(1)} %get-tuple-element.29.refs_3_), channel_id=1, source_target_pairs={{0,4},{4,0},{8,12},{12,8},{16,20},{20,16},{24,28},{28,24},{32,36},... | collective-permute-start | bytes 393224 | tf_op jit(solution)/shard_map/ppermute | solution.py:37
  150.3 5.8 %collective-permute-start.18 = (bf16[256,256]{1,0:T(8,128)(2,1)S(1)}, bf16[256,256]{1,0:T(8,128)(2,1)S(1)}, u32[]{:S(2)}, u32[]{:S(2)}) collective-permute-start(bf16[256,256]{1,0:T(8,128)(2,1)S(1)} %broadcast_select_fusion.2), channel_id=1, source_target_pairs={{0,4},{4,0},{8,12},{12,8},{16,20},{20,16},{24,28},{28,24},{32,36},... | collective-permute-start | bytes 393224 | tf_op jit(solution)/shard_map/ppermute | solution.py:37
  158.5 9.5 %all-to-all-start.2 = ((bf16[4,256,128]{2,1,0:T(8,128)(2,1)}), bf16[4,256,128]{2,1,0:T(8,128)(2,1)S(1)}, u32[]{:S(2)}, u32[]{:S(2)}) async-start(bf16[4,256,128]{2,1,0:T(8,128)(2,1)} %near_attend.4), calls=%async_computation.2 | async-start | bytes 524288 | tf_op jit(solution)/shard_map/all_to_all | solution.py:462
  161.9 1.3 copy-start.3
  168.0 1.0 copy-start.17
  170.1 15.4 %copy-start.6 = (bf16[1024,256]{1,0:T(8,128)(2,1)S(1)}, bf16[1024,256]{1,0:T(8,128)(2,1)}, u32[]{:S(2)}) copy-start(bf16[1024,256]{1,0:T(8,128)(2,1)} %copy-done.5) | copy-start | bytes 1572868
  170.1 15.5 %copy-start.8 = (bf16[1024,256]{1,0:T(8,128)(2,1)S(1)}, bf16[1024,256]{1,0:T(8,128)(2,1)}, u32[]{:S(2)}) copy-start(bf16[1024,256]{1,0:T(8,128)(2,1)} %copy-done.7) | copy-start | bytes 1572868
  170.1 15.5 %copy-start.10 = (bf16[1024,256]{1,0:T(8,128)(2,1)S(1)}, bf16[1024,256]{1,0:T(8,128)(2,1)}, u32[]{:S(2)}) copy-start(bf16[1024,256]{1,0:T(8,128)(2,1)} %copy-done.9) | copy-start | bytes 1572868
  171.8 9.0 %collective-permute-start.19 = (bf16[256,256]{1,0:T(8,128)(2,1)S(1)}, bf16[256,256]{1,0:T(8,128)(2,1)S(1)}, u32[]{:S(2)}, u32[]{:S(2)}) collective-permute-start(bf16[256,256]{1,0:T(8,128)(2,1)S(1)} %get-tuple-element.33.refs_3_), channel_id=1, source_target_pairs={{8,16},{16,8},{12,20},{20,12},{24,32},{32,24},{28,36},{36,28},{40,... | collective-permute-start | bytes 393224 | tf_op jit(solution)/shard_map/ppermute | solution.py:32
  174.8 6.0 %collective-permute-start.20 = (bf16[256,256]{1,0:T(8,128)(2,1)S(1)}, bf16[256,256]{1,0:T(8,128)(2,1)S(1)}, u32[]{:S(2)}, u32[]{:S(2)}) collective-permute-start(bf16[256,256]{1,0:T(8,128)(2,1)S(1)} %get-tuple-element.33.refs_3_), channel_id=1, source_target_pairs={{0,8},{8,0},{4,12},{12,4},{16,24},{24,16},{20,28},{28,20},{32,40},... | collective-permute-start | bytes 393224 | tf_op jit(solution)/shard_map/ppermute | solution.py:32
  176.7 13.7 %collective-permute-start.21 = (bf16[256,256]{1,0:T(8,128)(2,1)S(1)}, bf16[256,256]{1,0:T(8,128)(2,1)S(1)}, u32[]{:S(2)}, u32[]{:S(2)}) collective-permute-start(bf16[256,256]{1,0:T(8,128)(2,1)S(1)} %get-tuple-element.33.refs_3_), channel_id=1, source_target_pairs={{0,4},{4,0},{8,12},{12,8},{16,20},{20,16},{24,28},{28,24},{32,36},... | collective-permute-start | bytes 393224 | tf_op jit(solution)/shard_map/ppermute | solution.py:37
  180.8 9.5 %copy-start.23 = (bf16[1,128,256]{2,1,0:T(8,128)(2,1)S(1)}, bf16[1,128,256]{2,1,0:T(8,128)(2,1)}, u32[]{:S(2)}) copy-start(bf16[1,128,256]{2,1,0:T(8,128)(2,1)} %get-tuple-element.41) | copy-start | bytes 196612
  180.8 9.6 %collective-permute-start.22 = (bf16[256,256]{1,0:T(8,128)(2,1)S(1)}, bf16[256,256]{1,0:T(8,128)(2,1)S(1)}, u32[]{:S(2)}, u32[]{:S(2)}) collective-permute-start(bf16[256,256]{1,0:T(8,128)(2,1)S(1)} %broadcast_select_fusion.1), channel_id=1, source_target_pairs={{0,4},{4,0},{8,12},{12,8},{16,20},{20,16},{24,28},{28,24},{32,36},... | collective-permute-start | bytes 393224 | tf_op jit(solution)/shard_map/ppermute | solution.py:37
  190.3 23.8 %copy-start.4 = (bf16[1024,256]{1,0:T(8,128)(2,1)S(1)}, bf16[1024,256]{1,0:T(8,128)(2,1)}, u32[]{:S(2)}) copy-start(bf16[1024,256]{1,0:T(8,128)(2,1)} %grid_in.1) | copy-start | bytes 1572868
  192.1 9.7 %collective-permute-start.23 = (bf16[1024,128]{1,0:T(8,128)(2,1)S(1)}, bf16[1024,128]{1,0:T(8,128)(2,1)S(1)}, u32[]{:S(2)}, u32[]{:S(2)}) collective-permute-start(bf16[1024,128]{1,0:T(8,128)(2,1)S(1)} %bitcast.17), channel_id=1, source_target_pairs={{0,1},{1,0},{2,3},{3,2},{4,5},{5,4},{6,7},{7,6},{8,9},{9,8},{10,11... | collective-permute-start | bytes 786440 | tf_op jit(solution)/shard_map/ppermute | solution.py:23
  194.3 13.8 %collective-permute-start.24 = (bf16[1024,128]{1,0:T(8,128)(2,1)S(1)}, bf16[1024,128]{1,0:T(8,128)(2,1)S(1)}, u32[]{:S(2)}, u32[]{:S(2)}) collective-permute-start(bf16[1024,128]{1,0:T(8,128)(2,1)S(1)} %bitcast.18), channel_id=1, source_target_pairs={{0,2},{1,3},{2,0},{3,1},{4,6},{5,7},{6,4},{7,5},{8,10},{9,11},{10,... | collective-permute-start | bytes 786440 | tf_op jit(solution)/shard_map/ppermute | solution.py:23
  198.0 16.1 %collective-permute-start.25 = (bf16[1024,128]{1,0:T(8,128)(2,1)S(1)}, bf16[1024,128]{1,0:T(8,128)(2,1)S(1)}, u32[]{:S(2)}, u32[]{:S(2)}) collective-permute-start(bf16[1024,128]{1,0:T(8,128)(2,1)S(1)} %bitcast.19), channel_id=1, source_target_pairs={{0,3},{1,2},{2,1},{3,0},{4,7},{5,6},{6,5},{7,4},{8,11},{9,10},{10,... | collective-permute-start | bytes 786440 | tf_op jit(solution)/shard_map/ppermute | solution.py:23
  (6 other events, 5.1 us)

commit v9 on v6

--- a/solution.py
+++ b/solution.py
@@ -385,23 +385,24 @@
     )(meta, o, state, gains, w_own, *fetched, other, *weights)
 
 
-def layer_kernel(gain_row, meta, o, state, gains, w_out, w_next, *rest):
+def layer_kernel(gain_row, o, state, gains, w_out, w_next, *rest):
     last = gain_row == 5
     state_out, kv_out, new = rest[0], rest[1], rest[-1]
-    heads = jnp.concatenate([o[source(meta, k)] for k in range(MP)], axis=1)
+    own = lax.axis_index("mp")
+    heads = jnp.concatenate([o[own ^ k] for k in range(MP)], axis=1)
     for g in range(MP):
         new[g] = (state[g].astype(F32) + dot(heads, w_out[g])).astype(BF16)
         if not last:
             state_out[g] = new[g]
     if last:
-        state_out[...] = new[meta[0]]
+        state_out[...] = new[own]
     result = finish_layer(gain_row, gains, new, lambda: w_next[...])
     kv_out[...] = result[:, :256]
     if not last:
         rest[2][...] = result[:, 256:]
 
 
-def layer(gain_row, meta, o, state, gains, prepared):
+def layer(gain_row, o, state, gains, prepared):
     def body(*refs):
         layer_kernel(gain_row, *refs)
 
@@ -415,13 +416,13 @@
         shapes.append(jax.ShapeDtypeStruct((rows, 128), BF16))
     return pl.pallas_call(
         body,
-        in_specs=[smem()] + [vmem()] * 5,
+        in_specs=[vmem()] * 5,
         out_specs=[vmem()] * len(shapes),
         out_shape=shapes,
         scratch_shapes=[pltpu.VMEM((MP, rows, 256), BF16)],
         compiler_params=PARAMS,
         name="mesh_layer",
-    )(meta, o, state, gains, *prepared)
+    )(o, state, gains, *prepared)
 
 
 def final_kernel(meta, counts, o, w_out, grid_in, out):
@@ -521,7 +522,7 @@
         if index == 0:
             made = first_layer(meta, heads, state, gains, w_out, arrived, other, (w_key, w_value, w_query))
         else:
-            made = layer(3 if index == 1 else 5, meta, heads, state, gains, prepared)
+            made = layer(3 if index == 1 else 5, heads, state, gains, prepared)
         state, kv = made[0], made[1]
         near = window(kv)
         if index < 2:

time: 215 us -> 214 us (level)
  no operation moved by 1% of the time
where the time goes in v9:
time: 214 us; the launch traced here: 212 us
  starting transfers between devices  72.1 us (34%)
  waiting for transfers between devices  55.8 us (26%)
  Pallas kernels  34 us (16%)
  blocking collectives  29.9 us (14%)
  local copies, waits for them, and re-layouts  14.4 us (7%)
  other arithmetic  4.57 us (2%)
    ppermute x6, waiting for transfers between devices, swap_mp(): return lax.ppermute(value, 'mp', [(s, s ^ k) for s in range(MP)])  39.9 us
    all_to_all x2, blocking collectives, gather_heads(): return lax.all_to_all(copies, 'mp', split_axis=0, concat_axis=0, tiled=True)  29.9 us
    ppermute x8, starting transfers between devices, swap_chips(): return lax.ppermute(value, 'nodes', pairs)  26.9 us
    ppermute x6, starting transfers between devices, swap_mp(): return lax.ppermute(value, 'mp', [(s, s ^ k) for s in range(MP)])  20.8 us
    ppermute x9, starting transfers between devices, swap_cores(): return lax.ppermute(value, 'nodes', [(s, s ^ 1) for s in range(count)])  17.5 us
    unnamed x48, local copies, waits for them, and re-layouts  10.9 us
    ppermute x8, waiting for transfers between devices, swap_chips(): return lax.ppermute(value, 'nodes', pairs)  8.69 us
    all_to_all x2, starting transfers between devices, gather_heads(): return lax.all_to_all(copies, 'mp', split_axis=0, concat_axis=0, tiled=True)  6.81 us
  transfers between devices with their start and end apart: 25, of which 14 were waited for; matrix products, arithmetic and copies ran while one was open for 3% of the time, Pallas kernels for 6%

profile of v9, /device:TPU:384, one launch (start us, length us, event | category | flops | bytes accessed | tf_op | source)
XLA Modules:
  0.0 212.1 jit_solution(1261685608438820202)
XLA Ops:
  0.6 3.5 %collective-permute-start = (bf16[1024,256]{1,0:T(8,128)(2,1)}, bf16[1024,256]{1,0:T(8,128)(2,1)S(1)}, u32[]{:S(2)}, u32[]{:S(2)}) collective-permute-start(bf16[1024,256]{1,0:T(8,128)(2,1)} %grid_in.1), channel_id=1, source_target_pairs={{0,1},{1,0},{2,3},{3,2},{4,5},{5,4},{6,7},{7,6},{8,9},{9,8},{10,11... | collective-permute-start | bytes 1572872 | tf_op jit(solution)/shard_map/ppermute | solution.py:23
  4.1 4.8 %collective-permute-start.1 = (bf16[1024,256]{1,0:T(8,128)(2,1)}, bf16[1024,256]{1,0:T(8,128)(2,1)S(1)}, u32[]{:S(2)}, u32[]{:S(2)}) collective-permute-start(bf16[1024,256]{1,0:T(8,128)(2,1)} %grid_in.1), channel_id=1, source_target_pairs={{0,2},{1,3},{2,0},{3,1},{4,6},{5,7},{6,4},{7,5},{8,10},{9,11},{10,... | collective-permute-start | bytes 1572872 | tf_op jit(solution)/shard_map/ppermute | solution.py:23
  8.9 2.1 %collective-permute-start.2 = (bf16[1024,256]{1,0:T(8,128)(2,1)}, bf16[1024,256]{1,0:T(8,128)(2,1)S(1)}, u32[]{:S(2)}, u32[]{:S(2)}) collective-permute-start(bf16[1024,256]{1,0:T(8,128)(2,1)} %grid_in.1), channel_id=1, source_target_pairs={{0,3},{1,2},{2,1},{3,0},{4,7},{5,6},{6,5},{7,4},{8,11},{9,10},{10,... | collective-permute-start | bytes 1572872 | tf_op jit(solution)/shard_map/ppermute | solution.py:23
  15.4 2.1 %collective-permute-done.refs_2_ = bf16[1024,256]{1,0:T(8,128)(2,1)S(1)} collective-permute-done((bf16[1024,256]{1,0:T(8,128)(2,1)}, bf16[1024,256]{1,0:T(8,128)(2,1)S(1)}, u32[]{:S(2)}, u32[]{:S(2)}) %collective-permute-start) | collective-permute-done | bytes 524320 | tf_op jit(solution)/shard_map/ppermute | solution.py:23
  17.5 12.7 %collective-permute-done.1.refs_3_ = bf16[1024,256]{1,0:T(8,128)(2,1)S(1)} collective-permute-done((bf16[1024,256]{1,0:T(8,128)(2,1)}, bf16[1024,256]{1,0:T(8,128)(2,1)S(1)}, u32[]{:S(2)}, u32[]{:S(2)}) %collective-permute-start.1) | collective-permute-done | bytes 524320 | tf_op jit(solution)/shard_map/ppermute | solution.py:23
  30.2 6.4 %collective-permute-done.2.refs_4_ = bf16[1024,256]{1,0:T(8,128)(2,1)S(1)} collective-permute-done((bf16[1024,256]{1,0:T(8,128)(2,1)}, bf16[1024,256]{1,0:T(8,128)(2,1)S(1)}, u32[]{:S(2)}, u32[]{:S(2)}) %collective-permute-start.2) | collective-permute-done | bytes 524320 | tf_op jit(solution)/shard_map/ppermute | solution.py:23
  36.6 4.5 %grid_project.1.a1 = bf16[1024,256]{1,0:T(8,128)(2,1)} custom-call(s32[32]{0:T(128)S(1)} %concatenate.15.refs_0_.meta, bf16[1024,256]{1,0:T(8,128)(2,1)} %grid_in.1, bf16[1024,256]{1,0:T(8,128)(2,1)S(1)} %collective-permute-done.refs_2_, bf16[1024,256]{1,0:T(8,128)(2,1)S(1)} %collective-permute-done.1.refs_3_, ...), custom_call_target="tpu_custom_call" | custom-call | flops 536870912 | bytes 4194304 | tf_op jit(solution)/shard_map/grid_project/pallas_call | solution.py:98
  41.9 6.4 %collective-permute-start.6 = (bf16[1024,256]{1,0:T(8,128)(2,1)}, bf16[1024,256]{1,0:T(8,128)(2,1)S(1)}, u32[]{:S(2)}, u32[]{:S(2)}) collective-permute-start(bf16[1024,256]{1,0:T(8,128)(2,1)} %grid_project.1.a1), channel_id=1, source_target_pairs={{8,16},{16,8},{12,20},{20,12},{24,32},{32,24},{28,36},{36,28},{40,... | collective-permute-start | bytes 1572872 | tf_op jit(solution)/shard_map/ppermute | solution.py:32
  48.3 1.9 collective-permute-start.7
  52.7 1.9 collective-permute-start.3
  54.6 3.7 %collective-permute-start.4 = (bf16[9,128,256]{2,1,0:T(8,128)(2,1)}, bf16[9,128,256]{2,1,0:T(8,128)(2,1)S(1)}, u32[]{:S(2)}, u32[]{:S(2)}) collective-permute-start(bf16[9,128,256]{2,1,0:T(8,128)(2,1)} %get-tuple-element.39), channel_id=1, source_target_pairs={{0,2},{1,3},{2,0},{3,1},{4,6},{5,7},{6,4},{7,5},{8,10},{9,11},{10,... | collective-permute-start | bytes 1769480 | tf_op jit(solution)/shard_map/ppermute | solution.py:23
  58.3 4.8 %collective-permute-start.5 = (bf16[9,128,256]{2,1,0:T(8,128)(2,1)S(1)}, bf16[9,128,256]{2,1,0:T(8,128)(2,1)S(1)}, u32[]{:S(2)}, u32[]{:S(2)}) collective-permute-start(bf16[9,128,256]{2,1,0:T(8,128)(2,1)S(1)} %get-tuple-element.38), channel_id=1, source_target_pairs={{0,3},{1,2},{2,1},{3,0},{4,7},{5,6},{6,5},{7,4},{8,11},{9,10},{10,... | collective-permute-start | bytes 1769480 | tf_op jit(solution)/shard_map/ppermute | solution.py:23
  63.2 1.9 collective-permute-start.8
  66.3 1.9 collective-permute-start.9
  68.2 2.8 %collective-permute-done.3.a1.refs_2_ = bf16[9,128,256]{2,1,0:T(8,128)(2,1)S(1)} collective-permute-done((bf16[9,128,256]{2,1,0:T(8,128)(2,1)}, bf16[9,128,256]{2,1,0:T(8,128)(2,1)S(1)}, u32[]{:S(2)}, u32[]{:S(2)}) %collective-permute-start.3) | collective-permute-done | bytes 589856 | tf_op jit(solution)/shard_map/ppermute | solution.py:23
  71.0 9.7 %collective-permute-done.4.a2.refs_3_ = bf16[9,128,256]{2,1,0:T(8,128)(2,1)S(1)} collective-permute-done((bf16[9,128,256]{2,1,0:T(8,128)(2,1)}, bf16[9,128,256]{2,1,0:T(8,128)(2,1)S(1)}, u32[]{:S(2)}, u32[]{:S(2)}) %collective-permute-start.4) | collective-permute-done | bytes 589856 | tf_op jit(solution)/shard_map/ppermute | solution.py:23
  80.7 6.2 %collective-permute-done.5.a3.refs_4_ = bf16[9,128,256]{2,1,0:T(8,128)(2,1)S(1)} collective-permute-done((bf16[9,128,256]{2,1,0:T(8,128)(2,1)S(1)}, bf16[9,128,256]{2,1,0:T(8,128)(2,1)S(1)}, u32[]{:S(2)}, u32[]{:S(2)}) %collective-permute-start.5) | collective-permute-done | bytes 589856 | tf_op jit(solution)/shard_map/ppermute | solution.py:23
  86.9 1.9 mesh_start.1.q
  88.9 3.4 %enc_attend.1 = bf16[4,256,128]{2,1,0:T(8,128)(2,1)} custom-call(s32[32]{0:T(128)S(1)} %concatenate.15.refs_0_.meta, s32[2,4]{1,0:T(2,128)S(1)} %copy-done.21, s32[1024]{0:T(1024)S(1)} %copy-done.20, bf16[256,128]{1,0:T(8,128)(2,1)S(1)} %mesh_start.1.q, bf16[1024,256]{1,0:T(8,128)(2,1)S(1)} %collective-permute-done.6.a0, bf16[1024,256]{1,0:T(8,128)(2,1)} %grid_project.1.a1, ...), custom_call_target="tpu_custom_call" | custom-call | tf_op jit(solution)/shard_map/enc_attend/pallas_call | solution.py:247
  92.6 2.1 collective-permute-start.10
  94.6 11.3 %all_to_all.20.o = bf16[4,256,128]{2,1,0:T(8,128)(2,1)S(1)} all-to-all(bf16[4,256,128]{2,1,0:T(8,128)(2,1)S(1)} %copy-done.22), channel_id=1, replica_groups=mesh['nodes'=128,'mp'=4] {'mp'}, dimensions={0} | all-to-all | bytes 524288 | tf_op jit(solution)/shard_map/all_to_all | solution.py:460
  105.9 2.4 %first_layer.1 = (bf16[4,256,256]{2,1,0:T(8,128)(2,1)S(1)}, bf16[256,256]{1,0:T(8,128)(2,1)S(1)}, bf16[256,128]{1,0:T(8,128)(2,1)S(1)}) custom-call(s32[32]{0:T(128)S(1)} %concatenate.15.refs_0_.meta, bf16[4,256,128]{2,1,0:T(8,128)(2,1)S(1)} %all_to_all.20.o, bf16[256,256]{1,0:T(8,128)(2,1)S(1)} %copy-done.11, ...), custom_call_target="tpu_custom_call" | custom-call | tf_op jit(solution)/shard_map/first_layer/pallas_call | solution.py:373
  109.2 3.0 %collective-permute-start.11 = (bf16[256,256]{1,0:T(8,128)(2,1)S(1)}, bf16[256,256]{1,0:T(8,128)(2,1)S(1)}, u32[]{:S(2)}, u32[]{:S(2)}) collective-permute-start(bf16[256,256]{1,0:T(8,128)(2,1)S(1)} %get-tuple-element.24.refs_3_), channel_id=1, source_target_pairs={{8,16},{16,8},{12,20},{20,12},{24,32},{32,24},{28,36},{36,28},{40,... | collective-permute-start | bytes 393224 | tf_op jit(solution)/shard_map/ppermute | solution.py:32
  112.1 2.6 %collective-permute-start.12 = (bf16[256,256]{1,0:T(8,128)(2,1)S(1)}, bf16[256,256]{1,0:T(8,128)(2,1)S(1)}, u32[]{:S(2)}, u32[]{:S(2)}) collective-permute-start(bf16[256,256]{1,0:T(8,128)(2,1)S(1)} %get-tuple-element.24.refs_3_), channel_id=1, source_target_pairs={{0,8},{8,0},{4,12},{12,4},{16,24},{24,16},{20,28},{28,20},{32,40},... | collective-permute-start | bytes 393224 | tf_op jit(solution)/shard_map/ppermute | solution.py:32
  114.7 1.9 collective-permute-start.13
  116.7 2.7 %collective-permute-done.11.refs_2_ = bf16[256,256]{1,0:T(8,128)(2,1)S(1)} collective-permute-done((bf16[256,256]{1,0:T(8,128)(2,1)S(1)}, bf16[256,256]{1,0:T(8,128)(2,1)S(1)}, u32[]{:S(2)}, u32[]{:S(2)}) %collective-permute-start.11) | collective-permute-done | bytes 131104 | tf_op jit(solution)/shard_map/ppermute | solution.py:32
  119.4 1.9 collective-permute-start.14
  122.6 2.5 %near_attend.3 = bf16[4,256,128]{2,1,0:T(8,128)(2,1)} custom-call(s32[32]{0:T(128)S(1)} %concatenate.15.refs_0_.meta, bf16[256,128]{1,0:T(8,128)(2,1)S(1)} %get-tuple-element.23.refs_1_, bf16[256,256]{1,0:T(8,128)(2,1)S(1)} %collective-permute-done.11.refs_2_, bf16[256,256]{1,0:T(8,128)(2,1)S(1)} %get-tuple-element.24.refs_3_, ...), custom_call_target="tpu_custom_call" | custom-call | tf_op jit(solution)/shard_map/near_attend/pallas_call | solution.py:275
  125.1 3.4 %all-to-all-start.1 = ((bf16[4,256,128]{2,1,0:T(8,128)(2,1)}), bf16[4,256,128]{2,1,0:T(8,128)(2,1)S(1)}, u32[]{:S(2)}, u32[]{:S(2)}) async-start(bf16[4,256,128]{2,1,0:T(8,128)(2,1)} %near_attend.3), calls=%async_computation.1 | async-start | bytes 524288 | tf_op jit(solution)/shard_map/all_to_all | solution.py:460
  129.8 2.8 %layer_weights.2 = (bf16[4,512,256]{2,1,0:T(8,128)(2,1)S(1)}, bf16[1024,384]{1,0:T(8,128)(2,1)S(1)}) custom-call(s32[32]{0:T(128)S(1)} %concatenate.15.refs_0_.meta, bf16[4,128,1024]{2,1,0:T(8,128)(2,1)} %refs_1_.7, bf16[9,128,256]{2,1,0:T(8,128)(2,1)S(1)} %collective-permute-done.3.a1.refs_2_, bf16[9,128,256]{2,1,0:T(8,128)(2,1)S(1)} %collective-permute-done.4.a2.refs_3_, ...), custom_call_target="tpu_custom_call" | custom-call | tf_op jit(solution)/shard_map/layer_weights/pallas_call | solution.py:318
  133.5 2.2 %all-to-all-done.1.refs_0_ = bf16[4,256,128]{2,1,0:T(8,128)(2,1)S(1)} async-done(((bf16[4,256,128]{2,1,0:T(8,128)(2,1)}), bf16[4,256,128]{2,1,0:T(8,128)(2,1)S(1)}, u32[]{:S(2)}, u32[]{:S(2)}) %all-to-all-start.1) | async-done | bytes 262176 | tf_op jit(solution)/shard_map/all_to_all | solution.py:460
  139.8 5.8 %collective-permute-start.15 = (bf16[256,256]{1,0:T(8,128)(2,1)S(1)}, bf16[256,256]{1,0:T(8,128)(2,1)S(1)}, u32[]{:S(2)}, u32[]{:S(2)}) collective-permute-start(bf16[256,256]{1,0:T(8,128)(2,1)S(1)} %get-tuple-element.29.refs_3_), channel_id=1, source_target_pairs={{8,16},{16,8},{12,20},{20,12},{24,32},{32,24},{28,36},{36,28},{40,... | collective-permute-start | bytes 393224 | tf_op jit(solution)/shard_map/ppermute | solution.py:32
  145.7 1.9 collective-permute-start.16
  147.6 1.9 collective-permute-start.17
  150.0 2.5 %collective-permute-done.16.refs_4_ = bf16[256,256]{1,0:T(8,128)(2,1)S(1)} collective-permute-done((bf16[256,256]{1,0:T(8,128)(2,1)S(1)}, bf16[256,256]{1,0:T(8,128)(2,1)S(1)}, u32[]{:S(2)}, u32[]{:S(2)}) %collective-permute-start.16) | collective-permute-done | bytes 131104 | tf_op jit(solution)/shard_map/ppermute | solution.py:32
  152.5 1.9 collective-permute-start.18
  155.8 2.5 %near_attend.4 = bf16[4,256,128]{2,1,0:T(8,128)(2,1)} custom-call(s32[32]{0:T(128)S(1)} %concatenate.15.refs_0_.meta, bf16[256,128]{1,0:T(8,128)(2,1)S(1)} %get-tuple-element.28.refs_1_, bf16[256,256]{1,0:T(8,128)(2,1)S(1)} %collective-permute-done.15.refs_2_, bf16[256,256]{1,0:T(8,128)(2,1)S(1)} %get-tuple-element.29.refs_3_, ...), custom_call_target="tpu_custom_call" | custom-call | tf_op jit(solution)/shard_map/near_attend/pallas_call | solution.py:275
  158.2 3.4 %all-to-all-start.2 = ((bf16[4,256,128]{2,1,0:T(8,128)(2,1)}), bf16[4,256,128]{2,1,0:T(8,128)(2,1)S(1)}, u32[]{:S(2)}, u32[]{:S(2)}) async-start(bf16[4,256,128]{2,1,0:T(8,128)(2,1)} %near_attend.4), calls=%async_computation.2 | async-start | bytes 524288 | tf_op jit(solution)/shard_map/all_to_all | solution.py:460
  162.9 2.8 %layer_weights.3 = (bf16[4,512,256]{2,1,0:T(8,128)(2,1)S(1)}, bf16[1024,256]{1,0:T(8,128)(2,1)S(1)}) custom-call(s32[32]{0:T(128)S(1)} %concatenate.15.refs_0_.meta, bf16[4,128,1024]{2,1,0:T(8,128)(2,1)} %refs_1_.7, bf16[9,128,256]{2,1,0:T(8,128)(2,1)S(1)} %collective-permute-done.3.a1.refs_2_, bf16[9,128,256]{2,1,0:T(8,128)(2,1)S(1)} %collective-permute-done.4.a2.refs_3_, ...), custom_call_target="tpu_custom_call" | custom-call | tf_op jit(solution)/shard_map/layer_weights/pallas_call | solution.py:318
  166.5 2.4 %all-to-all-done.2.refs_0_ = bf16[4,256,128]{2,1,0:T(8,128)(2,1)S(1)} async-done(((bf16[4,256,128]{2,1,0:T(8,128)(2,1)}), bf16[4,256,128]{2,1,0:T(8,128)(2,1)S(1)}, u32[]{:S(2)}, u32[]{:S(2)}) %all-to-all-start.2) | async-done | bytes 262176 | tf_op jit(solution)/shard_map/all_to_all | solution.py:460
  172.6 3.3 %collective-permute-start.19 = (bf16[256,256]{1,0:T(8,128)(2,1)S(1)}, bf16[256,256]{1,0:T(8,128)(2,1)S(1)}, u32[]{:S(2)}, u32[]{:S(2)}) collective-permute-start(bf16[256,256]{1,0:T(8,128)(2,1)S(1)} %get-tuple-element.33.refs_3_), channel_id=1, source_target_pairs={{8,16},{16,8},{12,20},{20,12},{24,32},{32,24},{28,36},{36,28},{40,... | collective-permute-start | bytes 393224 | tf_op jit(solution)/shard_map/ppermute | solution.py:32
  176.0 1.9 collective-permute-start.20
  177.9 1.9 collective-permute-start.21
  179.8 3.0 %collective-permute-done.19.refs_2_ = bf16[256,256]{1,0:T(8,128)(2,1)S(1)} collective-permute-done((bf16[256,256]{1,0:T(8,128)(2,1)S(1)}, bf16[256,256]{1,0:T(8,128)(2,1)S(1)}, u32[]{:S(2)}, u32[]{:S(2)}) %collective-permute-start.19) | collective-permute-done | bytes 131104 | tf_op jit(solution)/shard_map/ppermute | solution.py:32
  182.8 2.1 collective-permute-start.22
  184.9 4.7 %grid_query.1.refs_1_ = bf16[1024,128]{1,0:T(8,128)(2,1)S(1)} custom-call(s32[32]{0:T(128)S(1)} %concatenate.15.refs_0_.meta, bf16[1024,256]{1,0:T(8,128)(2,1)} %grid_in.1, bf16[1024,256]{1,0:T(8,128)(2,1)S(1)} %copy-done.6, bf16[1024,256]{1,0:T(8,128)(2,1)S(1)} %copy-done.8, bf16[1024,256]{1,0:T(8,128)(2,1)S(1)} %copy-done.10, ...), custom_call_target="tpu_custom_call" | custom-call | flops 268435456 | bytes 4194304 | tf_op jit(solution)/shard_map/grid_query/pallas_call | solution.py:146
  191.5 18.6 %all_to_all.21.o = bf16[4,1024,128]{2,1,0:T(8,128)(2,1)S(1)} all-to-all(bf16[4,1024,128]{2,1,0:T(8,128)(2,1)S(1)} %near_attend.5), channel_id=1, replica_groups=mesh['nodes'=128,'mp'=4] {'mp'}, dimensions={0} | all-to-all | bytes 2097152 | tf_op jit(solution)/shard_map/all_to_all | solution.py:460
  210.1 2.0 grid_final.1
  (94 shorter events, 26.5 us)
Async XLA Ops:
  0.6 16.9 %collective-permute-start = (bf16[1024,256]{1,0:T(8,128)(2,1)}, bf16[1024,256]{1,0:T(8,128)(2,1)S(1)}, u32[]{:S(2)}, u32[]{:S(2)}) collective-permute-start(bf16[1024,256]{1,0:T(8,128)(2,1)} %grid_in.1), channel_id=1, source_target_pairs={{0,1},{1,0},{2,3},{3,2},{4,5},{5,4},{6,7},{7,6},{8,9},{9,8},{10,11... | collective-permute-start | bytes 1572872 | tf_op jit(solution)/shard_map/ppermute | solution.py:23
  4.1 26.1 %collective-permute-start.1 = (bf16[1024,256]{1,0:T(8,128)(2,1)}, bf16[1024,256]{1,0:T(8,128)(2,1)S(1)}, u32[]{:S(2)}, u32[]{:S(2)}) collective-permute-start(bf16[1024,256]{1,0:T(8,128)(2,1)} %grid_in.1), channel_id=1, source_target_pairs={{0,2},{1,3},{2,0},{3,1},{4,6},{5,7},{6,4},{7,5},{8,10},{9,11},{10,... | collective-permute-start | bytes 1572872 | tf_op jit(solution)/shard_map/ppermute | solution.py:23
  8.9 27.7 %collective-permute-start.2 = (bf16[1024,256]{1,0:T(8,128)(2,1)}, bf16[1024,256]{1,0:T(8,128)(2,1)S(1)}, u32[]{:S(2)}, u32[]{:S(2)}) collective-permute-start(bf16[1024,256]{1,0:T(8,128)(2,1)} %grid_in.1), channel_id=1, source_target_pairs={{0,3},{1,2},{2,1},{3,0},{4,7},{5,6},{6,5},{7,4},{8,11},{9,10},{10,... | collective-permute-start | bytes 1572872 | tf_op jit(solution)/shard_map/ppermute | solution.py:23
  30.2 10.9 %copy-start.7 = (bf16[1024,256]{1,0:T(8,128)(2,1)}, bf16[1024,256]{1,0:T(8,128)(2,1)S(1)}, u32[]{:S(2)}) copy-start(bf16[1024,256]{1,0:T(8,128)(2,1)S(1)} %collective-permute-done.1.refs_3_) | copy-start | bytes 1572868
  36.6 4.5 %copy-start.9 = (bf16[1024,256]{1,0:T(8,128)(2,1)}, bf16[1024,256]{1,0:T(8,128)(2,1)S(1)}, u32[]{:S(2)}) copy-start(bf16[1024,256]{1,0:T(8,128)(2,1)S(1)} %collective-permute-done.2.refs_4_) | copy-start | bytes 1572868
  41.9 8.4 %slice-start = ((bf16[4,128,1024]{2,1,0:T(8,128)(2,1)}), bf16[1,128,1024]{2,1,0:T(8,128)(2,1)S(1)}, s32[]{:S(2)}) async-start(bf16[4,128,1024]{2,1,0:T(8,128)(2,1)} %refs_1_.7), calls=%async_computation.4 | async-start | bytes 524288 | tf_op jit(solution)/shard_map/slice | solution.py:516
  41.9 21.3 %collective-permute-start.6 = (bf16[1024,256]{1,0:T(8,128)(2,1)}, bf16[1024,256]{1,0:T(8,128)(2,1)S(1)}, u32[]{:S(2)}, u32[]{:S(2)}) collective-permute-start(bf16[1024,256]{1,0:T(8,128)(2,1)} %grid_project.1.a1), channel_id=1, source_target_pairs={{8,16},{16,8},{12,20},{20,12},{24,32},{32,24},{28,36},{36,28},{40,... | collective-permute-start | bytes 1572872 | tf_op jit(solution)/shard_map/ppermute | solution.py:32
  48.3 16.8 %collective-permute-start.7 = (bf16[1024,256]{1,0:T(8,128)(2,1)}, bf16[1024,256]{1,0:T(8,128)(2,1)}, u32[]{:S(2)}, u32[]{:S(2)}) collective-permute-start(bf16[1024,256]{1,0:T(8,128)(2,1)} %grid_project.1.a1), channel_id=1, source_target_pairs={{0,8},{8,0},{4,12},{12,4},{16,24},{24,16},{20,28},{28,20},{32,40},... | collective-permute-start | bytes 1572872 | tf_op jit(solution)/shard_map/ppermute | solution.py:32
  50.3 1.2 slice-start.1
  50.3 1.2 copy-start.11
  52.7 18.3 %collective-permute-start.3 = (bf16[9,128,256]{2,1,0:T(8,128)(2,1)}, bf16[9,128,256]{2,1,0:T(8,128)(2,1)S(1)}, u32[]{:S(2)}, u32[]{:S(2)}) collective-permute-start(bf16[9,128,256]{2,1,0:T(8,128)(2,1)} %get-tuple-element.40), channel_id=1, source_target_pairs={{0,1},{1,0},{2,3},{3,2},{4,5},{5,4},{6,7},{7,6},{8,9},{9,8},{10,11... | collective-permute-start | bytes 1769480 | tf_op jit(solution)/shard_map/ppermute | solution.py:23
  54.6 26.1 %collective-permute-start.4 = (bf16[9,128,256]{2,1,0:T(8,128)(2,1)}, bf16[9,128,256]{2,1,0:T(8,128)(2,1)S(1)}, u32[]{:S(2)}, u32[]{:S(2)}) collective-permute-start(bf16[9,128,256]{2,1,0:T(8,128)(2,1)} %get-tuple-element.39), channel_id=1, source_target_pairs={{0,2},{1,3},{2,0},{3,1},{4,6},{5,7},{6,4},{7,5},{8,10},{9,11},{10,... | collective-permute-start | bytes 1769480 | tf_op jit(solution)/shard_map/ppermute | solution.py:23
  58.3 28.6 %collective-permute-start.5 = (bf16[9,128,256]{2,1,0:T(8,128)(2,1)S(1)}, bf16[9,128,256]{2,1,0:T(8,128)(2,1)S(1)}, u32[]{:S(2)}, u32[]{:S(2)}) collective-permute-start(bf16[9,128,256]{2,1,0:T(8,128)(2,1)S(1)} %get-tuple-element.38), channel_id=1, source_target_pairs={{0,3},{1,2},{2,1},{3,0},{4,7},{5,6},{6,5},{7,4},{8,11},{9,10},{10,... | collective-permute-start | bytes 1769480 | tf_op jit(solution)/shard_map/ppermute | solution.py:23
  63.2 25.7 %collective-permute-start.8 = (bf16[1024,256]{1,0:T(8,128)(2,1)}, bf16[1024,256]{1,0:T(8,128)(2,1)S(1)}, u32[]{:S(2)}, u32[]{:S(2)}) collective-permute-start(bf16[1024,256]{1,0:T(8,128)(2,1)} %grid_project.1.a1), channel_id=1, source_target_pairs={{0,4},{4,0},{8,12},{12,8},{16,20},{20,16},{24,28},{28,24},{32,36},... | collective-permute-start | bytes 1572872 | tf_op jit(solution)/shard_map/ppermute | solution.py:37
  66.2 22.6 %copy-start.20 = (s32[1024]{0:T(1024)S(1)}, s32[1024]{0:T(1024)}, u32[]{:S(2)}) copy-start(s32[1024]{0:T(1024)} %counts.3) | copy-start | bytes 12292
  66.2 22.6 %copy-start.21 = (s32[2,4]{1,0:T(2,128)S(1)}, s32[2,4]{1,0:T(2,128)}, u32[]{:S(2)}) copy-start(s32[2,4]{1,0:T(2,128)} %listed.1) | copy-start | bytes 100
  66.3 22.6 %collective-permute-start.9 = (bf16[1024,256]{1,0:T(8,128)(2,1)S(1)}, bf16[1024,256]{1,0:T(8,128)(2,1)S(1)}, u32[]{:S(2)}, u32[]{:S(2)}) collective-permute-start(bf16[1024,256]{1,0:T(8,128)(2,1)S(1)} %broadcast_select_fusion), channel_id=1, source_target_pairs={{0,4},{4,0},{8,12},{12,8},{16,20},{20,16},{24,28},{28,24},{32,36},... | collective-permute-start | bytes 1572872 | tf_op jit(solution)/shard_map/ppermute | solution.py:37
  92.4 2.2 %copy-start.22 = (bf16[4,256,128]{2,1,0:T(8,128)(2,1)S(1)}, bf16[4,256,128]{2,1,0:T(8,128)(2,1)}, u32[]{:S(2)}) copy-start(bf16[4,256,128]{2,1,0:T(8,128)(2,1)} %enc_attend.1) | copy-start | bytes 786436
  92.4 13.5 %copy-start = (bf16[4,128,1024]{2,1,0:T(8,128)(2,1)S(1)}, bf16[4,128,1024]{2,1,0:T(8,128)(2,1)}, u32[]{:S(2)}) copy-start(bf16[4,128,1024]{2,1,0:T(8,128)(2,1)} %refs_1_.7) | copy-start | bytes 3145732
  92.6 13.3 %collective-permute-start.10 = (bf16[3,6,128,256]{3,2,1,0:T(8,128)(2,1)S(1)}, bf16[3,6,128,256]{3,2,1,0:T(8,128)(2,1)S(1)}, u32[]{:S(2)}, u32[]{:S(2)}) collective-permute-start(bf16[3,6,128,256]{3,2,1,0:T(8,128)(2,1)S(1)} %pad_maximum_fusion), channel_id=1, source_target_pairs={{0,4},{4,0},{8,12},{12,8},{16,20},{20,16},{24,28},{28,24},{32,36},... | collective-permute-start | bytes 3538952 | tf_op jit(solution)/shard_map/ppermute | solution.py:37
  105.9 2.5 %copy-start.1 = (bf16[3,6,128,256]{3,2,1,0:T(8,128)(2,1)}, bf16[3,6,128,256]{3,2,1,0:T(8,128)(2,1)S(1)}, u32[]{:S(2)}) copy-start(bf16[3,6,128,256]{3,2,1,0:T(8,128)(2,1)S(1)} %collective-permute-done.10.other.refs_5_) | copy-start | bytes 3538948
  109.2 10.2 %collective-permute-start.11 = (bf16[256,256]{1,0:T(8,128)(2,1)S(1)}, bf16[256,256]{1,0:T(8,128)(2,1)S(1)}, u32[]{:S(2)}, u32[]{:S(2)}) collective-permute-start(bf16[256,256]{1,0:T(8,128)(2,1)S(1)} %get-tuple-element.24.refs_3_), channel_id=1, source_target_pairs={{8,16},{16,8},{12,20},{20,12},{24,32},{32,24},{28,36},{36,28},{40,... | collective-permute-start | bytes 393224 | tf_op jit(solution)/shard_map/ppermute | solution.py:32
  112.1 7.2 %collective-permute-start.12 = (bf16[256,256]{1,0:T(8,128)(2,1)S(1)}, bf16[256,256]{1,0:T(8,128)(2,1)S(1)}, u32[]{:S(2)}, u32[]{:S(2)}) collective-permute-start(bf16[256,256]{1,0:T(8,128)(2,1)S(1)} %get-tuple-element.24.refs_3_), channel_id=1, source_target_pairs={{0,8},{8,0},{4,12},{12,4},{16,24},{24,16},{20,28},{28,20},{32,40},... | collective-permute-start | bytes 393224 | tf_op jit(solution)/shard_map/ppermute | solution.py:32
  114.7 6.6 %collective-permute-start.13 = (bf16[256,256]{1,0:T(8,128)(2,1)S(1)}, bf16[256,256]{1,0:T(8,128)(2,1)S(1)}, u32[]{:S(2)}, u32[]{:S(2)}) collective-permute-start(bf16[256,256]{1,0:T(8,128)(2,1)S(1)} %get-tuple-element.24.refs_3_), channel_id=1, source_target_pairs={{0,4},{4,0},{8,12},{12,8},{16,20},{20,16},{24,28},{28,24},{32,36},... | collective-permute-start | bytes 393224 | tf_op jit(solution)/shard_map/ppermute | solution.py:37
  119.4 3.2 %collective-permute-start.14 = (bf16[256,256]{1,0:T(8,128)(2,1)S(1)}, bf16[256,256]{1,0:T(8,128)(2,1)S(1)}, u32[]{:S(2)}, u32[]{:S(2)}) collective-permute-start(bf16[256,256]{1,0:T(8,128)(2,1)S(1)} %broadcast_select_fusion.3), channel_id=1, source_target_pairs={{0,4},{4,0},{8,12},{12,8},{16,20},{20,16},{24,28},{28,24},{32,36},... | collective-permute-start | bytes 393224 | tf_op jit(solution)/shard_map/ppermute | solution.py:37
  125.1 10.6 %all-to-all-start.1 = ((bf16[4,256,128]{2,1,0:T(8,128)(2,1)}), bf16[4,256,128]{2,1,0:T(8,128)(2,1)S(1)}, u32[]{:S(2)}, u32[]{:S(2)}) async-start(bf16[4,256,128]{2,1,0:T(8,128)(2,1)} %near_attend.3), calls=%async_computation.1 | async-start | bytes 524288 | tf_op jit(solution)/shard_map/all_to_all | solution.py:460
  128.5 1.3 copy-start.2
  132.6 0.9 copy-start.12
  135.7 1.1 copy-start.13
  136.9 1.0 copy-start.15
  139.8 10.2 %collective-permute-start.15 = (bf16[256,256]{1,0:T(8,128)(2,1)S(1)}, bf16[256,256]{1,0:T(8,128)(2,1)S(1)}, u32[]{:S(2)}, u32[]{:S(2)}) collective-permute-start(bf16[256,256]{1,0:T(8,128)(2,1)S(1)} %get-tuple-element.29.refs_3_), channel_id=1, source_target_pairs={{8,16},{16,8},{12,20},{20,12},{24,32},{32,24},{28,36},{36,28},{40,... | collective-permute-start | bytes 393224 | tf_op jit(solution)/shard_map/ppermute | solution.py:32
  145.7 6.9 %collective-permute-start.16 = (bf16[256,256]{1,0:T(8,128)(2,1)S(1)}, bf16[256,256]{1,0:T(8,128)(2,1)S(1)}, u32[]{:S(2)}, u32[]{:S(2)}) collective-permute-start(bf16[256,256]{1,0:T(8,128)(2,1)S(1)} %get-tuple-element.29.refs_3_), channel_id=1, source_target_pairs={{0,8},{8,0},{4,12},{12,4},{16,24},{24,16},{20,28},{28,20},{32,40},... | collective-permute-start | bytes 393224 | tf_op jit(solution)/shard_map/ppermute | solution.py:32
  147.6 6.9 %collective-permute-start.17 = (bf16[256,256]{1,0:T(8,128)(2,1)S(1)}, bf16[256,256]{1,0:T(8,128)(2,1)S(1)}, u32[]{:S(2)}, u32[]{:S(2)}) collective-permute-start(bf16[256,256]{1,0:T(8,128)(2,1)S(1)} %get-tuple-element.29.refs_3_), channel_id=1, source_target_pairs={{0,4},{4,0},{8,12},{12,8},{16,20},{20,16},{24,28},{28,24},{32,36},... | collective-permute-start | bytes 393224 | tf_op jit(solution)/shard_map/ppermute | solution.py:37
  152.5 3.2 %collective-permute-start.18 = (bf16[256,256]{1,0:T(8,128)(2,1)S(1)}, bf16[256,256]{1,0:T(8,128)(2,1)S(1)}, u32[]{:S(2)}, u32[]{:S(2)}) collective-permute-start(bf16[256,256]{1,0:T(8,128)(2,1)S(1)} %broadcast_select_fusion.2), channel_id=1, source_target_pairs={{0,4},{4,0},{8,12},{12,8},{16,20},{20,16},{24,28},{28,24},{32,36},... | collective-permute-start | bytes 393224 | tf_op jit(solution)/shard_map/ppermute | solution.py:37
  158.2 10.6 %all-to-all-start.2 = ((bf16[4,256,128]{2,1,0:T(8,128)(2,1)}), bf16[4,256,128]{2,1,0:T(8,128)(2,1)S(1)}, u32[]{:S(2)}, u32[]{:S(2)}) async-start(bf16[4,256,128]{2,1,0:T(8,128)(2,1)} %near_attend.4), calls=%async_computation.2 | async-start | bytes 524288 | tf_op jit(solution)/shard_map/all_to_all | solution.py:460
  161.7 1.3 copy-start.3
  165.7 0.8 copy-start.18
  168.9 1.0 copy-start.17
  169.9 1.0 copy-start.19
  171.0 13.9 %copy-start.6 = (bf16[1024,256]{1,0:T(8,128)(2,1)S(1)}, bf16[1024,256]{1,0:T(8,128)(2,1)}, u32[]{:S(2)}) copy-start(bf16[1024,256]{1,0:T(8,128)(2,1)} %copy-done.5) | copy-start | bytes 1572868
  171.0 13.9 %copy-start.8 = (bf16[1024,256]{1,0:T(8,128)(2,1)S(1)}, bf16[1024,256]{1,0:T(8,128)(2,1)}, u32[]{:S(2)}) copy-start(bf16[1024,256]{1,0:T(8,128)(2,1)} %copy-done.7) | copy-start | bytes 1572868
  171.0 13.9 %copy-start.10 = (bf16[1024,256]{1,0:T(8,128)(2,1)S(1)}, bf16[1024,256]{1,0:T(8,128)(2,1)}, u32[]{:S(2)}) copy-start(bf16[1024,256]{1,0:T(8,128)(2,1)} %copy-done.9) | copy-start | bytes 1572868
  172.6 10.2 %collective-permute-start.19 = (bf16[256,256]{1,0:T(8,128)(2,1)S(1)}, bf16[256,256]{1,0:T(8,128)(2,1)S(1)}, u32[]{:S(2)}, u32[]{:S(2)}) collective-permute-start(bf16[256,256]{1,0:T(8,128)(2,1)S(1)} %get-tuple-element.33.refs_3_), channel_id=1, source_target_pairs={{8,16},{16,8},{12,20},{20,12},{24,32},{32,24},{28,36},{36,28},{40,... | collective-permute-start | bytes 393224 | tf_op jit(solution)/shard_map/ppermute | solution.py:32
  176.0 6.9 %collective-permute-start.20 = (bf16[256,256]{1,0:T(8,128)(2,1)S(1)}, bf16[256,256]{1,0:T(8,128)(2,1)S(1)}, u32[]{:S(2)}, u32[]{:S(2)}) collective-permute-start(bf16[256,256]{1,0:T(8,128)(2,1)S(1)} %get-tuple-element.33.refs_3_), channel_id=1, source_target_pairs={{0,8},{8,0},{4,12},{12,4},{16,24},{24,16},{20,28},{28,20},{32,40},... | collective-permute-start | bytes 393224 | tf_op jit(solution)/shard_map/ppermute | solution.py:32
  177.9 11.9 %collective-permute-start.21 = (bf16[256,256]{1,0:T(8,128)(2,1)S(1)}, bf16[256,256]{1,0:T(8,128)(2,1)S(1)}, u32[]{:S(2)}, u32[]{:S(2)}) collective-permute-start(bf16[256,256]{1,0:T(8,128)(2,1)S(1)} %get-tuple-element.33.refs_3_), channel_id=1, source_target_pairs={{0,4},{4,0},{8,12},{12,8},{16,20},{20,16},{24,28},{28,24},{32,36},... | collective-permute-start | bytes 393224 | tf_op jit(solution)/shard_map/ppermute | solution.py:37
  182.8 6.8 %copy-start.23 = (bf16[1,128,256]{2,1,0:T(8,128)(2,1)S(1)}, bf16[1,128,256]{2,1,0:T(8,128)(2,1)}, u32[]{:S(2)}) copy-start(bf16[1,128,256]{2,1,0:T(8,128)(2,1)} %get-tuple-element.41) | copy-start | bytes 196612
  182.8 6.9 %collective-permute-start.22 = (bf16[256,256]{1,0:T(8,128)(2,1)S(1)}, bf16[256,256]{1,0:T(8,128)(2,1)S(1)}, u32[]{:S(2)}, u32[]{:S(2)}) collective-permute-start(bf16[256,256]{1,0:T(8,128)(2,1)S(1)} %broadcast_select_fusion.1), channel_id=1, source_target_pairs={{0,4},{4,0},{8,12},{12,8},{16,20},{20,16},{24,28},{28,24},{32,36},... | collective-permute-start | bytes 393224 | tf_op jit(solution)/shard_map/ppermute | solution.py:37
  191.5 18.6 %copy-start.4 = (bf16[1024,256]{1,0:T(8,128)(2,1)S(1)}, bf16[1024,256]{1,0:T(8,128)(2,1)}, u32[]{:S(2)}) copy-start(bf16[1024,256]{1,0:T(8,128)(2,1)} %grid_in.1) | copy-start | bytes 1572868
  (3 other events, 2.4 us)
